TPU v7x, 128 devices: a whole 4x4x4 slice. The times are simulated.
128 devices in a mesh: gx: 2 (over core), gy: 4 (over x), gz: 16 (over z, y).
Axes of the slice: x: 4, y: 4, z: 4, core: 2. Of those that a mesh axis runs over, the one named last changes fastest.
Arguments:
- right_side: float32 [96, 192, 768], P('gx', 'gy', 'gz'), may hold values from -6 to 6
- start_guess: float32 [96, 192, 768], P('gx', 'gy', 'gz'), may hold values from -3 to 3
- reaction: float32 [96, 192, 768], P('gx', 'gy', 'gz'), may hold values from 0.0005 to 0.005
Outputs:
- solution_field: float32 [96, 192, 768], P('gx', 'gy', 'gz')
- residual: float32 [96, 192, 768], P('gx', 'gy', 'gz')
All inputs are finite; a program needn't handle non-finite values.
Results may differ from a plain program's by a relative error of at most 0.0003.
Values sent between devices are 32-bit elements.
No kernel may reach another device: no remote copies, remote signals or barrier semaphores. Data moves between devices by JAX's collectives and lax.ppermute only.
A program may use at most 128 MiB of HBM per device.

v0:
```python
import jax
import jax.numpy as jnp
from jax import lax
from jax.sharding import PartitionSpec as P

LEVELS = 5
BOTTOM_ITERS = 6


damping = 6.0 / 7.0


def extended(block, sides, width, periodic):
    for axis, dim in sides:
        count = lax.axis_size(axis)
        forward = [(i, i + 1) for i in range(count - 1)]
        if periodic:
            forward.append((count - 1, 0))
        backward = [(target, source) for source, target in forward]
        low = lax.ppermute(
            lax.slice_in_dim(block, block.shape[dim] - width, None, axis=dim), axis, forward
        )
        high = lax.ppermute(lax.slice_in_dim(block, 0, width, axis=dim), axis, backward)
        block = jnp.concatenate([low, block, high], axis=dim)
    return block


def laid_out(parts, dim):
    lengths = list(parts.shape[1:])
    lengths[dim] *= parts.shape[0]
    return jnp.moveaxis(parts, 0, dim).reshape(lengths)


def gather_together(arrays, axis, dims):
    flat = jnp.concatenate([a.reshape(-1) for a in arrays])
    lines, at, outs = lax.all_gather(flat, axis), 0, []
    for a, dim in zip(arrays, dims):
        parts = lines[:, at : at + a.size].reshape(-1, *a.shape)
        outs.append(laid_out(parts, dim))
        at += a.size
    return tuple(outs)


def stencil(padded, values, shifted, factor):
    beside = padded[2:, 1:-1, 1:-1] + padded[:-2, 1:-1, 1:-1]
    beside = beside + padded[1:-1, 2:, 1:-1] + padded[1:-1, :-2, 1:-1]
    beside = beside + padded[1:-1, 1:-1, 2:] + padded[1:-1, 1:-1, :-2]
    return factor * (6.0 * values - beside) + shifted * values


def operate_fine(values, shifted, factor):
    padded = extended(values, (("gx", 0), ("gy", 1), ("gz", 2)), 1, False)
    return stencil(padded, values, shifted, factor)


def operate_coarse(values, shifted, factor):
    padded = extended(values, (("gx", 0), ("gy", 1), ("gz", 2)), 1, False)
    return stencil(padded, values, shifted, factor)


def operate_whole(values, shifted, factor):
    return stencil(jnp.pad(values, 1), values, shifted, factor)


def coarsen(values):
    size_x, size_y, size_z = values.shape
    blocks = values.reshape(size_x // 2, 2, size_y // 2, 2, size_z // 2, 2)
    return jnp.mean(blocks, axis=(1, 3, 5))


def refine(values):
    size_x, size_y, size_z = values.shape
    spread = jnp.broadcast_to(values[:, None, :, None, :, None], (size_x, 2, size_y, 2, size_z, 2))
    return spread.reshape(2 * size_x, 2 * size_y, 2 * size_z)


def solve_whole(source, shifted, factor):
    estimate = jnp.zeros_like(source)
    leftover = source
    direction = source
    norm_now = jnp.sum(leftover * leftover)
    for repeat_index in range(BOTTOM_ITERS):
        applied = operate_whole(direction, shifted, factor)
        step_length = norm_now / jnp.sum(direction * applied)
        estimate = estimate + step_length * direction
        leftover = leftover - step_length * applied
        norm_next = jnp.sum(leftover * leftover)
        direction = leftover + norm_next / norm_now * direction
        norm_now = norm_next
    return estimate


def bottom(source, shifted, factor):
    gathered = (
        lax.all_gather(source, "gx", axis=0, tiled=True),
        lax.all_gather(shifted, "gx", axis=0, tiled=True),
    )
    gathered = gather_together((gathered[0], gathered[1]), "gy", (1, 1))
    gathered = (
        lax.all_gather(gathered[0], "gz", axis=2, tiled=True),
        lax.all_gather(gathered[1], "gz", axis=2, tiled=True),
    )
    answer = solve_whole(gathered[0], gathered[1], factor)
    size_x, size_y, size_z = source.shape
    corner = (
        lax.axis_index("gx") * size_x,
        lax.axis_index("gy") * size_y,
        lax.axis_index("gz") * size_z,
    )
    return lax.dynamic_slice(answer, corner, (size_x, size_y, size_z))


def vcycle_level(source, shifts, depth_index):
    factor = 0.25**depth_index
    shifted = shifts[depth_index]
    if depth_index == LEVELS - 1:
        return bottom(source, shifted, factor)
    operator = operate_fine if depth_index == 0 else operate_coarse
    diagonal = 6.0 * factor + shifted
    estimate = damping * source / diagonal
    estimate = estimate + damping * (source - operator(estimate, shifted, factor)) / diagonal
    leftover = source - operator(estimate, shifted, factor)
    estimate = estimate + refine(vcycle_level(coarsen(leftover), shifts, depth_index + 1))
    for repeat_index in range(2):
        estimate = estimate + damping * (source - operator(estimate, shifted, factor)) / diagonal
    return estimate


def body(right_side, start_guess, reaction):
    shifts = [reaction]
    for depth_index in range(LEVELS - 1):
        shifts.append(coarsen(shifts[-1]))
    start_residual = right_side - operate_fine(start_guess, reaction, 1.0)
    precond = vcycle_level(start_residual, shifts, 0)
    upper = lax.psum(jnp.sum(start_residual * precond), ("gx", "gy", "gz"))
    applied = operate_fine(precond, reaction, 1.0)
    step_length = upper / lax.psum(jnp.sum(precond * applied), ("gx", "gy", "gz"))
    solution_field = start_guess + step_length * precond
    residual = start_residual - step_length * applied
    return (solution_field, residual)


def solution(mesh):
    placed = (P("gx", "gy", "gz"), P("gx", "gy", "gz"), P("gx", "gy", "gz"))
    return jax.shard_map(
        body,
        mesh=mesh,
        in_specs=placed,
        out_specs=(P("gx", "gy", "gz"), P("gx", "gy", "gz")),
        check_vma=False,
    )
```

profile of v0, /device:TPU:1, one launch (start us, length us, event | category | flops | bytes accessed | tf_op | source)
XLA Modules:
  0.0 883.1 jit_solution(6199730012006355169)
XLA Ops:
  28.2 8.1 multiply_divide_fusion
  65.1 9.3 %fusion.43 = f32[48,48,48]{2,1,0:T(8,128)S(1)} fusion(f32[48,48,48]{2,1,0:T(8,128)} %copy-done.3, f32[48,48,48]{2,1,0:T(8,128)S(1)} %get-tuple-element.22, f32[50,50,1]{2,1,0:T(8,128)} %copy.44, f32[50,1,48]{2,1,0:T(1,128)} %copy-done.37, f32[50,1,48]{2,1,0:T(1,128)} %copy-done.43, f32[1,48,48]{2,1,0:T(8,128)} %copy-done.26, f32[1,48,48]{2,1,0:T(8,128)} %copy-done.30, ...), kind=kLoop, calls=%fused_computation.122 | loop fusion | flops 3538944 | bytes 1827104 | tf_op jit(solution)/shard_map/add | solution.py:121
  102.1 13.7 %reshape.66 = f32[24,2,24,2,24,2]{5,4,3,2,1,0:T(8,128)} reshape(f32[48,48,48]{2,1,0:T(8,128)S(1)} %copy-done) | data formatting | bytes 884736 | tf_op jit(solution)/shard_map/reshape | solution.py:67
  115.8 10.9 %reduce_sum.199 = f32[24,24,24]{2,1,0:T(8,128)} reduce(f32[24,2,24,2,24,2]{5,4,3,2,1,0:T(8,128)} %reshape.66, f32[]{:T(128)} %constant.24.clone.1), dimensions={1,3,5}, to_apply=%region_1.0 | reduce | flops 96768 | bytes 497668 | tf_op jit(solution)/shard_map/reduce_sum | solution.py:68
  138.4 15.3 %reshape.65 = f32[24,2,24,2,24,2]{5,4,3,2,1,0:T(8,128)} reshape(f32[48,48,48]{2,1,0:T(8,128)} %fusion.32) | data formatting | bytes 884736 | tf_op jit(solution)/shard_map/reshape | solution.py:67
  153.7 10.9 %reduce_sum.198 = f32[24,24,24]{2,1,0:T(8,128)} reduce(f32[24,2,24,2,24,2]{5,4,3,2,1,0:T(8,128)} %reshape.65, f32[]{:T(128)} %constant.24.clone.1), dimensions={1,3,5}, to_apply=%region_0.0 | reduce | flops 96768 | bytes 497668 | tf_op jit(solution)/shard_map/reduce_sum | solution.py:68
  185.6 7.2 collective-permute-done.22
  210.5 7.3 collective-permute-start.29
  280.9 7.2 collective-permute-start.41
  316.8 7.1 collective-permute-start.47
  345.7 7.6 collective-permute-start.53
  363.3 9.9 %all-reduce.6 = f32[432]{0:T(512)S(1)} all-reduce(f32[432]{0:T(512)S(1)} %maximum_dynamic-update-slice_fusion), channel_id=2, replica_groups=mesh['gx'=2,'gy'=4,'gz'=16] {'gy'}, use_global_device_ids=true, to_apply=%add.6 | all-reduce | flops 432 | bytes 3456
  376.5 32.1 %all_gather.22 = f32[6,12,48]{1,0,2:T(8,128)} all-gather(f32[6,12,3]{1,0,2:T(8,128)S(1)} %copy.50), channel_id=1, replica_groups=mesh['gx'=2,'gy'=4,'gz'=16] {'gz'}, dimensions={2}, use_global_device_ids=true | all-gather | bytes 14688 | tf_op jit(solution)/shard_map/all_gather | solution.py:100
  414.8 17.9 %all_gather.23 = f32[6,12,48]{1,0,2:T(8,128)} all-gather(f32[6,12,3]{1,0,2:T(8,128)S(1)} %copy.54), channel_id=1, replica_groups=mesh['gx'=2,'gy'=4,'gz'=16] {'gz'}, dimensions={2}, use_global_device_ids=true | all-gather | bytes 14688 | tf_op jit(solution)/shard_map/all_gather | solution.py:101
  481.8 14.6 %collective-permute-start.54 = (f32[1,6,6]{2,1,0:T(8,128)S(1)}, f32[1,6,6]{2,1,0:T(8,128)S(1)}, u32[]{:S(2)}, u32[]{:S(2)}) collective-permute-start(f32[1,6,6]{2,1,0:T(8,128)S(1)} %get-tuple-element.130), channel_id=1, source_target_pairs={{64,0},{65,1},{66,2},{67,3},{68,4},{69,5},{70,6},{71,7},{72,8},{73... | collective-permute-start | bytes 440 | tf_op jit(solution)/shard_map/ppermute | solution.py:23
  610.7 7.2 collective-permute-done.82
  641.1 7.0 collective-permute-done.88
  649.4 9.7 %broadcast_in_dim.11 = f32[24,2,24,2,24,2]{5,4,3,2,1,0:T(8,128)} broadcast(f32[24,24,24]{2,1,0:T(8,128)S(1)} %fusion.63), dimensions={0,2,4} | broadcast | bytes 497664 | tf_op jit(solution)/shard_map/broadcast_in_dim | solution.py:73
  659.1 17.3 %reshape.79 = f32[48,48,48]{2,1,0:T(8,128)} reshape(f32[24,2,24,2,24,2]{5,4,3,2,1,0:T(8,128)} %broadcast_in_dim.11) | data formatting | bytes 884736 | tf_op jit(solution)/shard_map/reshape | solution.py:74
  700.2 7.5 collective-permute-start.95
  749.6 9.3 %fusion.13 = f32[48,48,48]{2,1,0:T(8,128)S(1)} fusion(f32[48,48,48]{2,1,0:T(8,128)} %copy-done.4, f32[48,48,48]{2,1,0:T(8,128)S(1)} %get-tuple-element.22, f32[50,50,1]{2,1,0:T(8,128)} %copy.73, f32[50,1,48]{2,1,0:T(1,128)} %copy-done.39, f32[50,1,48]{2,1,0:T(1,128)} %copy-done.45, f32[1,48,48]{2,1,0:T(8,128)} %copy-done.28, f32[1,48,48]{2,1,0:T(8,128)} %copy-done.32, ...), kind=kLoop, calls=%fused_computation.38 | loop fusion | flops 3538944 | bytes 1827104 | tf_op jit(solution)/shard_map/add | solution.py:125
  781.2 7.7 collective-permute-start.107
  793.8 7.7 multiply_reduce_fusion
  801.5 76.6 %all-reduce.7 = (f32[]{:T(128)}, f32[]{:T(128)}) all-reduce(f32[]{:T(128)} %get-tuple-element.3, f32[]{:T(128)} %get-tuple-element.2), channel_id=1, replica_groups=mesh['gx'=2,'gy'=4,'gz'=16] {'gx','gy','gz'}, use_global_device_ids=true, to_apply=%region_21.22 | all-reduce | flops 2 | bytes 16 | tf_op jit(solution)/shard_map/psum | solution.py:135
  (484 shorter events, 534.5 us)
Async XLA Ops:
  92.9 33.8 %collective-permute-start.16 = (f32[50,50,1]{1,2,0:T(1,128)}, f32[50,50,1]{1,2,0:T(1,128)}, u32[]{:S(2)}, u32[]{:S(2)}) collective-permute-start(f32[50,50,1]{1,2,0:T(1,128)} %copy.45), channel_id=1, source_target_pairs={{1,0},{2,1},{3,2},{4,3},{5,4},{6,5},{7,6},{8,7},{9,8},{10,9},{11,1... | collective-permute-start | bytes 30008 | tf_op jit(solution)/shard_map/ppermute | solution.py:23
  96.7 32.4 %collective-permute-start.17 = (f32[50,50,1]{1,2,0:T(1,128)}, f32[50,50,1]{1,2,0:T(1,128)}, u32[]{:S(2)}, u32[]{:S(2)}) collective-permute-start(f32[50,50,1]{1,2,0:T(1,128)} %copy.47), channel_id=1, source_target_pairs={{0,1},{1,2},{2,3},{3,4},{4,5},{5,6},{6,7},{7,8},{8,9},{9,10},{10,1... | collective-permute-start | bytes 30008 | tf_op jit(solution)/shard_map/ppermute | solution.py:20
  179.9 13.0 %collective-permute-start.22 = (f32[26,26,1]{2,1,0:T(8,128)S(1)}, f32[26,26,1]{2,1,0:T(8,128)S(1)}, u32[]{:S(2)}, u32[]{:S(2)}) collective-permute-start(f32[26,26,1]{2,1,0:T(8,128)S(1)} %get-tuple-element.65), channel_id=1, source_target_pairs={{1,0},{2,1},{3,2},{4,3},{5,4},{6,5},{7,6},{8,7},{9,8},{10,9},{11,1... | collective-permute-start | bytes 8120 | tf_op jit(solution)/shard_map/ppermute | solution.py:23
  181.2 12.6 %collective-permute-start.23 = (f32[26,26,1]{2,1,0:T(8,128)S(1)}, f32[26,26,1]{2,1,0:T(8,128)S(1)}, u32[]{:S(2)}, u32[]{:S(2)}) collective-permute-start(f32[26,26,1]{2,1,0:T(8,128)S(1)} %get-tuple-element.66), channel_id=1, source_target_pairs={{0,1},{1,2},{2,3},{3,4},{4,5},{5,6},{6,7},{7,8},{8,9},{9,10},{10,1... | collective-permute-start | bytes 8120 | tf_op jit(solution)/shard_map/ppermute | solution.py:20
  209.2 16.2 %collective-permute-start.28 = (f32[26,26,1]{2,1,0:T(8,128)}, f32[26,26,1]{2,1,0:T(8,128)}, u32[]{:S(2)}, u32[]{:S(2)}) collective-permute-start(f32[26,26,1]{2,1,0:T(8,128)} %get-tuple-element.63), channel_id=1, source_target_pairs={{1,0},{2,1},{3,2},{4,3},{5,4},{6,5},{7,6},{8,7},{9,8},{10,9},{11,1... | collective-permute-start | bytes 8120 | tf_op jit(solution)/shard_map/ppermute | solution.py:23
  210.5 14.9 %collective-permute-start.29 = (f32[26,26,1]{2,1,0:T(8,128)}, f32[26,26,1]{2,1,0:T(8,128)}, u32[]{:S(2)}, u32[]{:S(2)}) collective-permute-start(f32[26,26,1]{2,1,0:T(8,128)} %get-tuple-element.64), channel_id=1, source_target_pairs={{0,1},{1,2},{2,3},{3,4},{4,5},{5,6},{6,7},{7,8},{8,9},{9,10},{10,1... | collective-permute-start | bytes 8120 | tf_op jit(solution)/shard_map/ppermute | solution.py:20
  251.6 8.3 collective-permute-start.34
  252.9 8.3 collective-permute-start.35
  279.6 12.1 %collective-permute-start.40 = (f32[14,14,1]{2,1,0:T(8,128)}, f32[14,14,1]{2,1,0:T(8,128)}, u32[]{:S(2)}, u32[]{:S(2)}) collective-permute-start(f32[14,14,1]{2,1,0:T(8,128)} %get-tuple-element.93), channel_id=1, source_target_pairs={{1,0},{2,1},{3,2},{4,3},{5,4},{6,5},{7,6},{8,7},{9,8},{10,9},{11,1... | collective-permute-start | bytes 2360 | tf_op jit(solution)/shard_map/ppermute | solution.py:23
  280.9 10.9 %collective-permute-start.41 = (f32[14,14,1]{2,1,0:T(8,128)}, f32[14,14,1]{2,1,0:T(8,128)}, u32[]{:S(2)}, u32[]{:S(2)}) collective-permute-start(f32[14,14,1]{2,1,0:T(8,128)} %get-tuple-element.94), channel_id=1, source_target_pairs={{0,1},{1,2},{2,3},{3,4},{4,5},{5,6},{6,7},{7,8},{8,9},{9,10},{10,1... | collective-permute-start | bytes 2360 | tf_op jit(solution)/shard_map/ppermute | solution.py:20
  315.5 9.1 %collective-permute-start.46 = (f32[8,8,1]{2,1,0:T(8,128)}, f32[8,8,1]{2,1,0:T(8,128)}, u32[]{:S(2)}, u32[]{:S(2)}) collective-permute-start(f32[8,8,1]{2,1,0:T(8,128)} %get-tuple-element.123), channel_id=1, source_target_pairs={{1,0},{2,1},{3,2},{4,3},{5,4},{6,5},{7,6},{8,7},{9,8},{10,9},{11,1... | collective-permute-start | bytes 776 | tf_op jit(solution)/shard_map/ppermute | solution.py:23
  334.1 8.9 %collective-permute-start.50 = (f32[8,1,6]{2,1,0:T(1,128)}, f32[8,1,6]{2,1,0:T(1,128)}, u32[]{:S(2)}, u32[]{:S(2)}) collective-permute-start(f32[8,1,6]{2,1,0:T(1,128)} %get-tuple-element.122), channel_id=1, source_target_pairs={{16,0},{32,16},{48,32},{17,1},{33,17},{49,33},{18,2},{34,18},{50,3... | collective-permute-start | bytes 584 | tf_op jit(solution)/shard_map/ppermute | solution.py:23
  344.4 11.7 %collective-permute-start.52 = (f32[8,8,1]{2,1,0:T(8,128)}, f32[8,8,1]{2,1,0:T(8,128)}, u32[]{:S(2)}, u32[]{:S(2)}) collective-permute-start(f32[8,8,1]{2,1,0:T(8,128)} %get-tuple-element.119), channel_id=1, source_target_pairs={{1,0},{2,1},{3,2},{4,3},{5,4},{6,5},{7,6},{8,7},{9,8},{10,9},{11,1... | collective-permute-start | bytes 776 | tf_op jit(solution)/shard_map/ppermute | solution.py:23
  345.7 10.5 %collective-permute-start.53 = (f32[8,8,1]{2,1,0:T(8,128)}, f32[8,8,1]{2,1,0:T(8,128)}, u32[]{:S(2)}, u32[]{:S(2)}) collective-permute-start(f32[8,8,1]{2,1,0:T(8,128)} %get-tuple-element.120), channel_id=1, source_target_pairs={{0,1},{1,2},{2,3},{3,4},{4,5},{5,6},{6,7},{7,8},{8,9},{9,10},{10,1... | collective-permute-start | bytes 776 | tf_op jit(solution)/shard_map/ppermute | solution.py:20
  481.8 15.9 %collective-permute-start.54 = (f32[1,6,6]{2,1,0:T(8,128)S(1)}, f32[1,6,6]{2,1,0:T(8,128)S(1)}, u32[]{:S(2)}, u32[]{:S(2)}) collective-permute-start(f32[1,6,6]{2,1,0:T(8,128)S(1)} %get-tuple-element.130), channel_id=1, source_target_pairs={{64,0},{65,1},{66,2},{67,3},{68,4},{69,5},{70,6},{71,7},{72,8},{73... | collective-permute-start | bytes 440 | tf_op jit(solution)/shard_map/ppermute | solution.py:23
  603.6 14.3 %collective-permute-start.82 = (f32[26,26,1]{2,1,0:T(8,128)S(1)}, f32[26,26,1]{2,1,0:T(8,128)S(1)}, u32[]{:S(2)}, u32[]{:S(2)}) collective-permute-start(f32[26,26,1]{2,1,0:T(8,128)S(1)} %get-tuple-element.61), channel_id=1, source_target_pairs={{1,0},{2,1},{3,2},{4,3},{5,4},{6,5},{7,6},{8,7},{9,8},{10,9},{11,1... | collective-permute-start | bytes 8120 | tf_op jit(solution)/shard_map/ppermute | solution.py:23
  604.9 13.9 %collective-permute-start.83 = (f32[26,26,1]{2,1,0:T(8,128)S(1)}, f32[26,26,1]{2,1,0:T(8,128)S(1)}, u32[]{:S(2)}, u32[]{:S(2)}) collective-permute-start(f32[26,26,1]{2,1,0:T(8,128)S(1)} %get-tuple-element.62), channel_id=1, source_target_pairs={{0,1},{1,2},{2,3},{3,4},{4,5},{5,6},{6,7},{7,8},{8,9},{9,10},{10,1... | collective-permute-start | bytes 8120 | tf_op jit(solution)/shard_map/ppermute | solution.py:20
  632.9 15.2 %collective-permute-start.88 = (f32[26,26,1]{2,1,0:T(8,128)S(1)}, f32[26,26,1]{2,1,0:T(8,128)S(1)}, u32[]{:S(2)}, u32[]{:S(2)}) collective-permute-start(f32[26,26,1]{2,1,0:T(8,128)S(1)} %get-tuple-element.59), channel_id=1, source_target_pairs={{1,0},{2,1},{3,2},{4,3},{5,4},{6,5},{7,6},{8,7},{9,8},{10,9},{11,1... | collective-permute-start | bytes 8120 | tf_op jit(solution)/shard_map/ppermute | solution.py:23
  634.2 14.8 %collective-permute-start.89 = (f32[26,26,1]{2,1,0:T(8,128)S(1)}, f32[26,26,1]{2,1,0:T(8,128)S(1)}, u32[]{:S(2)}, u32[]{:S(2)}) collective-permute-start(f32[26,26,1]{2,1,0:T(8,128)S(1)} %get-tuple-element.60), channel_id=1, source_target_pairs={{0,1},{1,2},{2,3},{3,4},{4,5},{5,6},{6,7},{7,8},{8,9},{9,10},{10,1... | collective-permute-start | bytes 8120 | tf_op jit(solution)/shard_map/ppermute | solution.py:20
  696.4 11.3 %collective-permute-start.94 = (f32[50,50,1]{1,2,0:T(1,128)}, f32[50,50,1]{1,2,0:T(1,128)}, u32[]{:S(2)}, u32[]{:S(2)}) collective-permute-start(f32[50,50,1]{1,2,0:T(1,128)} %copy.66), channel_id=1, source_target_pairs={{1,0},{2,1},{3,2},{4,3},{5,4},{6,5},{7,6},{8,7},{9,8},{10,9},{11,1... | collective-permute-start | bytes 30008 | tf_op jit(solution)/shard_map/ppermute | solution.py:23
  700.2 9.9 %collective-permute-start.95 = (f32[50,50,1]{1,2,0:T(1,128)}, f32[50,50,1]{1,2,0:T(1,128)}, u32[]{:S(2)}, u32[]{:S(2)}) collective-permute-start(f32[50,50,1]{1,2,0:T(1,128)} %copy.68), channel_id=1, source_target_pairs={{0,1},{1,2},{2,3},{3,4},{4,5},{5,6},{6,7},{7,8},{8,9},{9,10},{10,1... | collective-permute-start | bytes 30008 | tf_op jit(solution)/shard_map/ppermute | solution.py:20
  736.5 9.7 %collective-permute-start.100 = (f32[50,50,1]{1,2,0:T(1,128)S(1)}, f32[50,50,1]{1,2,0:T(1,128)S(1)}, u32[]{:S(2)}, u32[]{:S(2)}) collective-permute-start(f32[50,50,1]{1,2,0:T(1,128)S(1)} %copy.70), channel_id=1, source_target_pairs={{1,0},{2,1},{3,2},{4,3},{5,4},{6,5},{7,6},{8,7},{9,8},{10,9},{11,1... | collective-permute-start | bytes 30008 | tf_op jit(solution)/shard_map/ppermute | solution.py:23
  777.4 11.5 %collective-permute-start.106 = (f32[50,50,1]{1,2,0:T(1,128)}, f32[50,50,1]{1,2,0:T(1,128)}, u32[]{:S(2)}, u32[]{:S(2)}) collective-permute-start(f32[50,50,1]{1,2,0:T(1,128)} %copy.74), channel_id=1, source_target_pairs={{1,0},{2,1},{3,2},{4,3},{5,4},{6,5},{7,6},{8,7},{9,8},{10,9},{11,1... | collective-permute-start | bytes 30008 | tf_op jit(solution)/shard_map/ppermute | solution.py:23
  781.2 10.2 %collective-permute-start.107 = (f32[50,50,1]{1,2,0:T(1,128)}, f32[50,50,1]{1,2,0:T(1,128)}, u32[]{:S(2)}, u32[]{:S(2)}) collective-permute-start(f32[50,50,1]{1,2,0:T(1,128)} %copy.76), channel_id=1, source_target_pairs={{0,1},{1,2},{2,3},{3,4},{4,5},{5,6},{6,7},{7,8},{8,9},{9,10},{10,1... | collective-permute-start | bytes 30008 | tf_op jit(solution)/shard_map/ppermute | solution.py:20
  (135 other events, 807.4 us)
where the time goes:
time: 898 us; the launch traced here: 883 us
  starting transfers between devices  332 us (37%)
  local copies, waits for them, and re-layouts  172 us (19%)
  other arithmetic  144 us (16%)
  blocking collectives  140 us (16%)
  waiting for transfers between devices  74.2 us (8%)
  between operations  19.6 us (2%)
    ppermute x54, starting transfers between devices, extended(): lax.ppermute(lax.slice_in_dim(block, block.shape[dim] - width, None, axis...  211 us
    ppermute x54, starting transfers between devices, extended(): lax.ppermute(lax.slice_in_dim(block, 0, width, axis=dim), axis, backward)  121 us
    psum x1, blocking collectives, body(): upper = lax.psum(jnp.sum(start_residual * precond), ('gx', 'gy', 'gz'))  76.6 us
    ppermute x54, waiting for transfers between devices, extended(): lax.ppermute(lax.slice_in_dim(block, block.shape[dim] - width, None, axis...  51 us
    reshape x5, local copies, waits for them, and re-layouts, coarsen(): blocks = values.reshape(size_x // 2, 2, size_y // 2, 2, size_z // 2, 2)  36.5 us
    reduce_sum x8, other arithmetic, coarsen(): return jnp.mean(blocks, axis=(1, 3, 5))  34.2 us
    all_gather x1, blocking collectives, bottom(): lax.all_gather(gathered[0], 'gz', axis=2, tiled=True)  32.1 us
    add x12, other arithmetic, vcycle_level(): estimate + damping * (source - operator(estimate, shifted, factor)) / dia...  30 us
  transfers between devices with their start and end apart: 108, of which 47 were waited for; matrix products, arithmetic and copies ran while one was open for 7% of the time, Pallas kernels for 0%

commit v1 on v0

v1 whole, which is shorter than its diff:
```python
import functools
import jax
import jax.numpy as jnp
from jax import lax
from jax.experimental import pallas as pl
from jax.experimental.pallas import tpu as pltpu
from jax.sharding import PartitionSpec as P

W = 6.0 / 7.0
BOTTOM_ITERS = 6
N0 = 48
F32 = jnp.float32
HI = lax.Precision.HIGHEST
LIMIT = 56 * 1024 * 1024


class Spec:
    def __init__(self, n, h, na, gp, r0, R, hx):
        self.n, self.h, self.na, self.gp, self.r0, self.R, self.hx = n, h, na, gp, r0, R, hx
        self.lw = 128 // gp
        self.zshape = (n // gp, n, 128)
        self.yrows = -(-na * h // 8) * 8
        self.yshape = (n // 2, self.yrows, 128)
        self.xshape = (hx, na, R, 128)
        self.nx = n + hx


L0 = Spec(48, 5, 3, 8, 8, 64, 6)
L1 = Spec(24, 12, 2, 4, 16, 56, 12)


def sds(*shape):
    return jax.ShapeDtypeStruct(shape, F32)


def run(kernel, outs, args, scratch=()):
    smem = pl.BlockSpec(memory_space=pltpu.SMEM)
    vmem = pl.BlockSpec(memory_space=pltpu.VMEM)
    specs = [smem if a.dtype == jnp.int32 else vmem for a in args]
    return pl.pallas_call(
        kernel,
        out_shape=outs,
        in_specs=specs,
        out_specs=jax.tree.map(lambda _: vmem, outs),
        scratch_shapes=[pltpu.VMEM(s, F32) for s in scratch],
        compiler_params=pltpu.CompilerParams(vmem_limit_bytes=LIMIT),
    )(*args)


def lanes(rows):
    return lax.broadcasted_iota(jnp.int32, (rows, 128), 1)


def roll(v, shift, axis):
    if isinstance(shift, int):
        shift = shift % v.shape[axis]
        if shift == 0:
            return v
    return pltpu.roll(v, shift, axis)


def loop(n, f):
    lax.fori_loop(0, n, lambda i, c: (f(i), c)[1], 0)


def widen(dst, src, rows=N0):
    def one(x):
        dst[x, :, :] = jnp.zeros(dst.shape[1:], F32)
        dst[x, :, 0:rows] = src[x]

    loop(src.shape[0], one)


def zpack(sp, get, hi_ref, lo_ref):
    ln = lanes(sp.n)

    def group(g):
        hi = jnp.zeros((sp.n, 128), F32)
        lo = hi
        for j in range(sp.gp):
            for a in range(sp.na):
                v = get(g * sp.gp + j, a, 0, sp.n)
                at = sp.lw * j + sp.h * a
                here = (ln >= at) & (ln < at + sp.h)
                hi = jnp.where(here, roll(v, at - (sp.n - sp.h), 1), hi)
                lo = jnp.where(here, roll(v, at, 1), lo)
        hi_ref[g] = hi
        lo_ref[g] = lo

    loop(sp.n // sp.gp, group)


def ypack(sp, get, zl, zh, up_ref, dn_ref):
    n, h = sp.n, sp.h
    up0 = (n - h) // 8 * 8
    dn1 = -(-h // 8) * 8

    def fold(x, g, j, a, b, e):
        o = 64 * (j % 2)
        ln = lanes(e - b)
        at = sp.lw * j + h * a
        own = roll(get(x, a, b, e), o, 1)
        high = roll(zh[g, b:e, :], o + n - at, 1)
        low = roll(zl[g, b:e, :], o + 64 - h - at, 1)
        return jnp.where(ln < o + n, own, jnp.where(ln < o + n + h, high, low))

    def group(g):
        for q in range(sp.gp // 2):
            p = g * (sp.gp // 2) + q
            for a in range(sp.na):
                for ref, b, e, s, t in ((up_ref, up0, n, n - h - up0, n - up0), (dn_ref, 0, dn1, 0, h)):
                    even = fold(g * sp.gp + 2 * q, g, 2 * q, a, b, e)
                    odd = fold(g * sp.gp + 2 * q + 1, g, 2 * q + 1, a, b, e)
                    both = jnp.where(lanes(e - b) < 64, even, odd)
                    ref[p, a * h : (a + 1) * h, :] = both[s:t]
            if sp.yrows > sp.na * h:
                pad = jnp.zeros((sp.yrows - sp.na * h, 128), F32)
                up_ref[p, sp.na * h :, :] = pad
                dn_ref[p, sp.na * h :, :] = pad

    loop(n // sp.gp, group)


def plane(sp, get, zl, zh, yl, yh, x, g, j, a, dst, xw):
    n, h, r0 = sp.n, sp.h, sp.r0
    at = sp.lw * j + h * a
    ln = lanes(n)
    static = isinstance(j, int)

    def amount(k):
        return k - at if static else lax.rem(k + 128 - at, 128)

    high = roll(zh[g], amount(n), 1)
    low = roll(zl[g], amount(128 - h), 1)
    v = jnp.where(ln < n, get(x, a, 0, n), jnp.where(ln < n + h, high, jnp.where(ln >= 128 - h, low, 0.0)))
    dst[xw, r0 : r0 + n, :] = v
    lh = lanes(h)
    half = g * (sp.gp // 2) + j // 2
    for ref, r in ((yl, r0 - h), (yh, r0 + n)):
        u = ref[half, a * h : (a + 1) * h, :]
        if static:
            near, far = (u, roll(u, 64, 1)) if j % 2 == 0 else (roll(u, 64, 1), u)
        else:
            s = 64 * lax.rem(j, 2)
            near, far = roll(u, s, 1), roll(u, 64 - s, 1)
        dst[xw, r : r + h, :] = jnp.where(lh < n + h, near, jnp.where(lh >= 128 - h, far, 0.0))
    dst[xw, 0 : r0 - h, :] = jnp.zeros((r0 - h, 128), F32)
    dst[xw, r0 + n + h :, :] = jnp.zeros((sp.R - r0 - n - h, 128), F32)


def domain(sp, n, h, r0, R, ids):
    row = lax.broadcasted_iota(jnp.int32, (R, 128), 0) - r0
    ln = lanes(R)
    z = jnp.where(ln < 64, ln, ln - 128)
    gy, gz, ny, nz = ids[1], ids[2], ids[3], ids[4]
    y_at, z_at = row + gy * n, z + gz * n
    ok = (row >= -h) & (row < n + h) & (z >= -h) & (z < n + h)
    return ok & (y_at >= 0) & (y_at < ny * n) & (z_at >= 0) & (z_at < nz * n)


def neighbours(ref, x):
    c = ref[x + 1]
    R = c.shape[0]
    s = ref[x] + ref[x + 2]
    s = s + (roll(c, 1, 0) + roll(c, R - 1, 0))
    return s + (roll(c, 1, 1) + roll(c, 127, 1))


def zero_ends(ref, n):
    ref[0] = jnp.zeros(ref.shape[1:], F32)
    ref[n + 1] = jnp.zeros(ref.shape[1:], F32)


def relax(src, dst, f, c, n, factor):
    def one(x):
        dst[x + 1] = (1.0 - W) * src[x + 1] + c[x] * (f[x] + factor * neighbours(src, x))

    loop(n, one)


def lane_map(signed, value):
    l = lax.broadcasted_iota(jnp.int32, (128, 128), 0)
    m = lax.broadcasted_iota(jnp.int32, (128, 128), 1)
    c = l // 2
    if signed:
        c = jnp.where(l < 64, c, c + 64)
    return jnp.where(c == m, value, 0.0).astype(F32)


def spread_map(signed):
    m = lax.broadcasted_iota(jnp.int32, (128, 128), 0)
    l = lax.broadcasted_iota(jnp.int32, (128, 128), 1)
    c = l // 2
    if signed:
        c = jnp.where(l < 64, c, c + 64)
    return jnp.where(c == m, 1.0, 0.0).astype(F32)


def coarsen_planes(pair, n, tmp, acc, signed):
    half = tmp.shape[0] // 2

    def one(x):
        tmp[...] = pair(x)
        acc[x] = tmp[pl.ds(0, half, stride=2), :] + tmp[pl.ds(1, half, stride=2), :]

    loop(n, one)
    m = lane_map(signed, 0.125)

    def two(x):
        acc[x] = jnp.dot(acc[x], m, precision=HI, preferred_element_type=F32)

    loop(n, two)


def add_refined(coarse, r, n, dst, tmp, m):
    rows = tmp.shape[0] // 2

    def one(i):
        v = jnp.dot(coarse(i)[r : r + rows], m, precision=HI, preferred_element_type=F32)
        tmp[pl.ds(0, rows, stride=2), :] = v
        tmp[pl.ds(1, rows, stride=2), :] = v
        t = tmp[...]
        dst[2 * i + 1] = dst[2 * i + 1] + t
        dst[2 * i + 2] = dst[2 * i + 2] + t

    loop(n, one)


def wide_get(s):
    return lambda x, a, b, e: s[a, x, b:e, :]


def k_zpack0(x0, b, rea, hi, lo, s):
    for a, ref in enumerate((x0, b, rea)):
        widen(s.at[a], ref)
    zpack(L0, wide_get(s), hi, lo)


def k_ypack0(x0, b, rea, zl, zh, up, dn, s):
    for a, ref in enumerate((x0, b, rea)):
        widen(s.at[a], ref)
    ypack(L0, wide_get(s), zl, zh, up, dn)


def k_xpack(sp, ids, get, zl, zh, yl, yh, out):
    start = (1 - ids[0]) * (sp.n - sp.hx)

    def one(i):
        x = start + i
        g, j = lax.div(x, sp.gp), lax.rem(x, sp.gp)
        for a in range(sp.na):
            plane(sp, get, zl, zh, yl, yh, x, g, j, a, out.at[i], a)

    loop(sp.hx, one)


def k_xpack0(ids, x0, b, rea, zl, zh, yl, yh, out, s):
    for a, ref in enumerate((x0, b, rea)):
        widen(s.at[a], ref)
    k_xpack(L0, ids, wide_get(s), zl, zh, yl, yh, out)


def assemble(sp, ids, get, zl, zh, yl, yh, xr, dsts):
    shift = ids[0] * sp.hx

    def group(g):
        for j in range(sp.gp):
            x = g * sp.gp + j
            for a, (dst, off) in enumerate(dsts):
                plane(sp, get, zl, zh, yl, yh, x, g, j, a, dst, x + shift + off)

    loop(sp.n // sp.gp, group)
    other = (1 - ids[0]) * sp.n

    def take(i):
        for a, (dst, off) in enumerate(dsts):
            dst[other + i + off] = xr[i, a]

    loop(sp.hx, take)


def k_down0(ids, x0, b, rea, zl, zh, yl, yh, xr, f_out, c_out, e_out, f1, r1, z1h, z1l, s, xw, bw, rw, ew, tmp):
    for a, ref in enumerate((x0, b, rea)):
        widen(s.at[a], ref)
    assemble(L0, ids, wide_get(s), zl, zh, yl, yh, xr, ((xw, 1), (bw, 0), (rw, 0)))
    n = L0.nx
    ok = domain(L0, 48, 5, 8, 64, ids)
    zero_ends(xw, n)
    zero_ends(ew, n)
    zero_ends(e_out, n)

    def mask(x):
        xw[x + 1] = jnp.where(ok, xw[x + 1], 0.0)

    loop(n, mask)

    def first(x):
        d = 6.0 + rw[x]
        c = jnp.where(ok, W / d, 0.0)
        f = bw[x] - d * xw[x + 1] + neighbours(xw, x)
        f_out[x] = f
        c_out[x] = c
        ew[x + 1] = c * f

    loop(n, first)
    relax(ew, e_out, f_out, c_out, n, 1.0)
    shift = ids[0] * L0.hx

    def left(x):
        r = f_out[x] - (6.0 + rw[x]) * e_out[x + 1] + neighbours(e_out, x)
        return r[8:56]

    inner = lanes(48) < 48
    coarsen_planes(lambda x: jnp.where(inner, left(2 * x + shift) + left(2 * x + shift + 1), 0.0), 24, tmp, f1, True)
    coarsen_planes(lambda x: s[2, 2 * x] + s[2, 2 * x + 1], 24, tmp, r1, True)
    both = (f1, r1)
    zpack(L1, lambda x, a, p, q: both[a][x, p:q, :], z1h, z1l)


def k_ypack1(f1, r1, zl, zh, up, dn):
    both = (f1, r1)
    ypack(L1, lambda x, a, p, q: both[a][x, p:q, :], zl, zh, up, dn)


def k_xpack1(ids, f1, r1, zl, zh, yl, yh, out):
    both = (f1, r1)

    def get(x, a, p, q):
        return both[a][x, p:q, :]

    k_xpack(L1, ids, get, zl, zh, yl, yh, out)


def k_down1(ids, f1, r1, zl, zh, yl, yh, xr, fw, cw, e_out, f2, c2, e2, out3, rw, ew, tmp, r2, ew2, tmp2, t3):
    both = (f1, r1)
    assemble(L1, ids, lambda x, a, p, q: both[a][x, p:q, :], zl, zh, yl, yh, xr, ((fw, 0), (rw, 0)))
    n = L1.nx
    ok = domain(L1, 24, 12, 16, 56, ids)
    zero_ends(ew, n)
    zero_ends(e_out, n)

    def first(x):
        c = jnp.where(ok, W / (1.5 + rw[x]), 0.0)
        cw[x] = c
        ew[x + 1] = c * fw[x]

    loop(n, first)
    relax(ew, e_out, fw, cw, n, 0.25)

    def left(x):
        return fw[x] - (1.5 + rw[x]) * e_out[x + 1] + 0.25 * neighbours(e_out, x)

    def keep(ref):
        def one(x):
            ref[x, 28:32, :] = jnp.zeros((4, 128), F32)

        loop(18, one)

    keep(f2)
    keep(r2)
    coarsen_planes(lambda x: left(2 * x) + left(2 * x + 1), 18, tmp, f2.at[:, 0:28, :], True)
    coarsen_planes(lambda x: rw[2 * x] + rw[2 * x + 1], 18, tmp, r2.at[:, 0:28, :], True)
    ok2 = domain(None, 12, 6, 8, 32, ids)
    zero_ends(ew2, 18)
    zero_ends(e2, 18)

    def second(x):
        c = jnp.where(ok2, W / (0.375 + r2[x]), 0.0)
        c2[x] = c
        ew2[x + 1] = c * f2[x]

    loop(18, second)
    relax(ew2, e2, f2, c2, 18, 0.0625)

    def left2(x):
        return f2[x] - (0.375 + r2[x]) * e2[x + 1] + 0.0625 * neighbours(e2, x)

    coarsen_planes(lambda x: left2(2 * x) + left2(2 * x + 1), 9, tmp2, t3.at[0], True)
    coarsen_planes(lambda x: r2[2 * x] + r2[2 * x + 1], 9, tmp2, t3.at[1], True)
    shift = ids[0] * 3

    def give(x):
        for a in range(2):
            out3[a, x] = t3[a, x + shift, 4:10, 0:6]

    loop(6, give)


def sum_all(v):
    s = jnp.sum(v, axis=0)
    return jnp.sum(jnp.sum(s, axis=1, keepdims=True), axis=0, keepdims=True)


def coarse_solve(g3, e3, s3, f3, c3, r3, tmp, f4, r4):
    nx, ny, nz = g3.shape[1:]
    R = f3.shape[1]
    for ref in (f3, r3):
        ref[...] = jnp.zeros(ref.shape, F32)
    f3[:, 0:ny, 0:nz] = g3[0]
    r3[:, 0:ny, 0:nz] = g3[1]
    factor = 0.25**3
    ok = (lax.broadcasted_iota(jnp.int32, (R, 128), 0) < ny) & (lanes(R) < nz)
    for ref in (e3, s3):
        zero_ends(ref, nx)

    def first(x):
        c = jnp.where(ok, W / (6.0 * factor + r3[x]), 0.0)
        c3[x] = c
        s3[x + 1] = c * f3[x]

    loop(nx, first)
    relax(s3, e3, f3, c3, nx, factor)

    def left(x):
        v = f3[x] - (6.0 * factor + r3[x]) * e3[x + 1] + factor * neighbours(e3, x)
        return jnp.where(ok, v, 0.0)

    coarsen_planes(lambda x: left(2 * x) + left(2 * x + 1), nx // 2, tmp, f4, False)
    coarsen_planes(lambda x: r3[2 * x] + r3[2 * x + 1], nx // 2, tmp, r4, False)
    f4k = 0.25**4
    H = R // 2
    row = lax.broadcasted_iota(jnp.int32, (nx // 2, H, 128), 1)
    lane = lax.broadcasted_iota(jnp.int32, (nx // 2, H, 128), 2)
    inside = (row < ny // 2) & (lane < nz // 2)
    diag = 6.0 * f4k + r4[...]
    zero = jnp.zeros((1, H, 128), F32)

    def apply(p):
        s = jnp.concatenate([zero, p[:-1]], axis=0) + jnp.concatenate([p[1:], zero], axis=0)
        s = s + roll(p, 1, 1) + roll(p, H - 1, 1) + roll(p, 1, 2) + roll(p, 127, 2)
        return jnp.where(inside, diag * p - f4k * s, 0.0)

    r = jnp.where(inside, f4[...], 0.0)
    p = r
    e = jnp.zeros_like(r)
    rr = sum_all(r * r)
    for i in range(BOTTOM_ITERS):
        q = apply(p)
        a = rr / sum_all(p * q)
        e = e + a * p
        if i + 1 < BOTTOM_ITERS:
            r = r - a * q
            new = sum_all(r * r)
            p = r + (new / rr) * p
            rr = new
    f4[...] = e
    add_refined(lambda i: f4[i], 0, nx // 2, e3, tmp, spread_map(False))
    relax(e3, s3, f3, c3, nx, factor)
    relax(s3, e3, f3, c3, nx, factor)


def k_up(ids, g3, f2, c2, e2i, f1, c1, e1i, f0, c0, e0i, rea, z_out, az_out, f_own, sums,
         e3, s3, f3, c3, r3, tmp3, f4, r4, w3, e2, s2, tmp2, e1, s1, tmp1, e0, s0, tmp0):
    coarse_solve(g3, e3, s3, f3, c3, r3, tmp3, f4, r4)
    gx, gy, gz = ids[0], ids[1], ids[2]
    for dst, src in ((e2, e2i), (e1, e1i), (e0, e0i)):
        def copy(x, dst=dst, src=src):
            dst[x] = src[x]
        loop(src.shape[0], copy)
    for ref, n in ((s2, 18), (s1, 36), (s0, 54)):
        zero_ends(ref, n)
    R3 = e3.shape[1]
    pick = lax.broadcasted_iota(jnp.int32, (16, R3), 1) == lax.broadcasted_iota(jnp.int32, (16, R3), 0) + (gy * 6 - 4)
    pick = pick.astype(F32)
    c = lax.broadcasted_iota(jnp.int32, (128, 128), 0)
    l = lanes(128)
    half = l // 2
    spread = (c == gz * 6 + jnp.where(l < 64, half, half - 64)).astype(F32)
    ok2 = domain(None, 12, 6, 8, 32, ids)

    def window(i):
        w3[i] = jnp.dot(pick, e3[i + 1 + gx * 3], precision=HI, preferred_element_type=F32)

    loop(9, window)
    add_refined(lambda i: w3[i], 0, 9, e2, tmp2, spread)
    relax(e2, s2, f2, c2, 18, 0.0625)
    relax(s2, e2, f2, c2, 18, 0.0625)
    m = spread_map(True)
    add_refined(lambda i: e2[i + 1], 0, 18, e1, tmp1, m)
    relax(e1, s1, f1, c1, 36, 0.25)
    relax(s1, e1, f1, c1, 36, 0.25)
    ok0 = domain(L0, 48, 5, 8, 64, ids)
    m0 = m
    add_refined(lambda i: e1[i + 1 + gx * 9], 12, 27, e0, tmp0, m0)

    def mask(x):
        e0[x + 1] = jnp.where(ok0, e0[x + 1], 0.0)

    loop(54, mask)
    relax(e0, s0, f0, c0, 54, 1.0)
    relax(s0, e0, f0, c0, 54, 1.0)
    shift = gx * 6

    def last(x, carry):
        u, v = carry
        z = e0[x + shift + 1][8:56, 0:48]
        nb = neighbours(e0, x + shift)[8:56, 0:48]
        az = (6.0 + rea[x]) * z - nb
        f = f0[x + shift][8:56, 0:48]
        z_out[x] = z
        az_out[x] = az
        f_own[x] = f
        return u + f * z, v + z * az

    zero = jnp.zeros((48, 48), F32)
    u, v = lax.fori_loop(0, 48, last, (zero, zero))

    def total(t):
        return jnp.sum(jnp.sum(t, axis=1, keepdims=True), axis=0, keepdims=True)

    ln = lanes(8)
    sums[...] = jnp.where(ln == 0, total(u), jnp.where(ln == 1, total(v), 0.0))


def k_last(sums, x0, z, az, f, sol, res):
    s = jnp.sum(sums[...], axis=0, keepdims=True)
    ln = lanes(1)
    upper = jnp.sum(jnp.where(ln == 0, s, 0.0), axis=1, keepdims=True)
    lower = jnp.sum(jnp.where(ln == 1, s, 0.0), axis=1, keepdims=True)
    step = upper / lower

    def one(x):
        sol[x] = x0[x] + step * z[x]
        res[x] = f[x] - step * az[x]

    loop(48, one)


def ring(up, dn, axis):
    n = lax.axis_size(axis)
    low = lax.ppermute(up, axis, [(i, (i + 1) % n) for i in range(n)])
    high = lax.ppermute(dn, axis, [(i, (i - 1) % n) for i in range(n)])
    return low, high


def swap(v):
    return lax.ppermute(v, "gx", [(0, 1), (1, 0)])


def body(b, x0, rea):
    ALL = ("gx", "gy", "gz")
    sizes = [lax.axis_size(a) for a in ALL]
    count = sizes[0] * sizes[1] * sizes[2]
    ids = jnp.stack([lax.axis_index(a) for a in ALL] + [jnp.int32(sizes[1]), jnp.int32(sizes[2])]).astype(jnp.int32)
    wide = (3, 48, 48, 128)
    hi, lo = run(k_zpack0, (sds(*L0.zshape),) * 2, (x0, b, rea), [wide])
    zl, zh = ring(hi, lo, "gz")
    up, dn = run(k_ypack0, (sds(*L0.yshape),) * 2, (x0, b, rea, zl, zh), [wide])
    yl, yh = ring(up, dn, "gy")
    xs = run(k_xpack0, sds(*L0.xshape), (ids, x0, b, rea, zl, zh, yl, yh), [wide])
    xr = swap(xs)
    p0 = (54, 64, 128)
    q0 = (56, 64, 128)
    f0, c0, e0, f1, r1, z1h, z1l = run(
        k_down0,
        (sds(*p0), sds(*p0), sds(*q0), sds(24, 24, 128), sds(24, 24, 128), sds(*L1.zshape), sds(*L1.zshape)),
        (ids, x0, b, rea, zl, zh, yl, yh, xr),
        [wide, q0, p0, p0, q0, (48, 128)],
    )
    zl, zh = ring(z1h, z1l, "gz")
    up, dn = run(k_ypack1, (sds(*L1.yshape),) * 2, (f1, r1, zl, zh))
    yl, yh = ring(up, dn, "gy")
    xs = run(k_xpack1, sds(*L1.xshape), (ids, f1, r1, zl, zh, yl, yh))
    xr = swap(xs)
    p1, q1, p2, q2 = (36, 56, 128), (38, 56, 128), (18, 32, 128), (20, 32, 128)
    f1w, c1w, e1w, f2w, c2w, e2w, g = run(
        k_down1,
        (sds(*p1), sds(*p1), sds(*q1), sds(*p2), sds(*p2), sds(*q2), sds(2, 6, 6, 6)),
        (ids, f1, r1, zl, zh, yl, yh, xr),
        [p1, q1, (56, 128), p2, q2, (32, 128), (2, 9, 16, 128)],
    )
    g = jnp.broadcast_to(g.reshape(1, 432), (count, 432))
    g = lax.all_to_all(g, ALL, 0, 0)
    g = g.reshape(sizes[0], sizes[1], sizes[2], 2, 6, 6, 6).transpose(3, 0, 4, 1, 5, 2, 6)
    n3 = [6 * s for s in sizes]
    g = g.reshape(2, *n3)
    R3 = (n3[1] + 8) // 8 * 8
    if R3 % 16:
        R3 += 8
    p3, q3, p4 = (n3[0], R3, 128), (n3[0] + 2, R3, 128), (n3[0] // 2, R3 // 2, 128)
    z, az, f, sums = run(
        k_up,
        (sds(48, 48, 48), sds(48, 48, 48), sds(48, 48, 48), sds(8, 128)),
        (ids, g, f2w, c2w, e2w, f1w, c1w, e1w, f0, c0, e0, rea),
        [q3, q3, p3, p3, p3, (R3, 128), p4, p4, (9, 16, 128), q2, q2, (32, 128), q1, q1, (56, 128), q0, q0, (64, 128)],
    )
    sums = lax.all_to_all(jnp.broadcast_to(sums[:1], (count, 128)), ALL, 0, 0)
    return run(k_last, (sds(48, 48, 48), sds(48, 48, 48)), (sums, x0, z, az, f))


def solution(mesh):
    spec = P("gx", "gy", "gz")
    return jax.shard_map(body, mesh=mesh, in_specs=(spec, spec, spec), out_specs=(spec, spec), check_vma=False)
```

time: 898 us -> 219 us (0.24); the launches traced: 883 us -> 219 us
  starting transfers between devices: 332 us -> 22.3 us
  local copies, waits for them, and re-layouts: 172 us -> 19.4 us
  other arithmetic: 144 us -> 0 us
  Pallas kernels: 0 us -> 128 us
  blocking collectives: 140 us -> 33.6 us
  waiting for transfers between devices: 74.2 us -> 15.4 us
  between operations: 19.6 us -> 0.69 us
    ppermute x108 -> x10, starting transfers between devices: 332 us -> 22.3 us  [the longest x4 13.1 us: ring(): high = lax.ppermute(dn, axis, [(i, (i - 1) % n) for i in range(n)])]
    pallas_call x0 -> x9, Pallas kernels: none -> 128 us  [run(): pl.pallas_call(kernel, out_shape=outs, in_specs=specs, out_specs=jax.tree...]
    psum x1 -> x0, blocking collectives: 76.6 us -> none  [body(): upper = lax.psum(jnp.sum(start_residual * precond), ('gx', 'gy', 'gz'))]
    reduce_sum x21 -> x0, other arithmetic: 64.9 us -> none  [the longest x8 34.2 us: coarsen(): return jnp.mean(blocks, axis=(1, 3, 5))]
    reshape x15 -> x2, local copies, waits for them, and re-layouts: 65.4 us -> 5.79 us  [the longest x1 4.6 us: body(): g = g.reshape(2, *n3)]
    ppermute x108 -> x10, waiting for transfers between devices: 74.2 us -> 15.4 us  [the longest x4 11.5 us: ring(): low = lax.ppermute(up, axis, [(i, (i + 1) % n) for i in range(n)])]
    all_gather x4 -> x0, blocking collectives: 54 us -> none  [the longest x1 32.1 us: bottom(): lax.all_gather(gathered[0], 'gz', axis=2, tiled=True)]
    slice x50 -> x1, local copies, waits for them, and re-layouts: 42.3 us -> 0.68 us  [body(): sums = lax.all_to_all(jnp.broadcast_to(sums[:1], (count, 128)), ALL, 0, 0)]
  transfers between devices with their start and end apart: 108 -> 10, of which waited for: 47 -> 6; matrix products, arithmetic and copies ran while one was open for 7% -> 0% of each run, Pallas kernels for 0% -> 0%
where the time goes in v1:
time: 219 us
  Pallas kernels  128 us (58%)
  blocking collectives  33.6 us (15%)
  starting transfers between devices  22.3 us (10%)
  local copies, waits for them, and re-layouts  19.4 us (9%)
  waiting for transfers between devices  15.4 us (7%)
    pallas_call x9, Pallas kernels, run(): pl.pallas_call(kernel, out_shape=outs, in_specs=specs, out_specs=jax.tree...  128 us
    all_to_all x1, blocking collectives, body(): g = lax.all_to_all(g, ALL, 0, 0)  19.2 us
    all_to_all x1, blocking collectives, body(): sums = lax.all_to_all(jnp.broadcast_to(sums[:1], (count, 128)), ALL, 0, 0)  14.4 us
    ppermute x4, starting transfers between devices, ring(): high = lax.ppermute(dn, axis, [(i, (i - 1) % n) for i in range(n)])  13.1 us
    ppermute x4, waiting for transfers between devices, ring(): low = lax.ppermute(up, axis, [(i, (i + 1) % n) for i in range(n)])  11.5 us
    unnamed x20, local copies, waits for them, and re-layouts  6.28 us
    ppermute x2, starting transfers between devices, swap(): return lax.ppermute(v, 'gx', [(0, 1), (1, 0)])  5.09 us
    transpose x1, local copies, waits for them, and re-layouts, body(): g.reshape(sizes[0], sizes[1], sizes[2], 2, 6, 6, 6)  4.86 us
  transfers between devices with their start and end apart: 10, of which 6 were waited for; matrix products, arithmetic and copies ran while one was open for 0% of the time, Pallas kernels for 0%

profile of v1, /device:TPU:1, one launch (start us, length us, event | category | flops | bytes accessed | tf_op | source)
XLA Modules:
  0.0 219.0 jit_solution(7512506620322301143)
XLA Ops:
  0.6 5.6 %shard_map.50 = (f32[6,48,128]{2,1,0:T(8,128)}, f32[6,48,128]{2,1,0:T(8,128)}) custom-call(f32[48,48,48]{2,1,0:T(8,128)} %x0.9, f32[48,48,48]{2,1,0:T(8,128)} %b.7, f32[48,48,48]{2,1,0:T(8,128)} %rea.9), custom_call_target="tpu_custom_call" | custom-call | tf_op jit(solution)/shard_map/pallas_call | solution.py:40
  6.3 2.1 collective-permute-start
  8.4 4.9 %collective-permute-start.1 = (f32[6,48,128]{2,1,0:T(8,128)}, f32[6,48,128]{2,1,0:T(8,128)S(1)}, u32[]{:S(2)}, u32[]{:S(2)}) collective-permute-start(f32[6,48,128]{2,1,0:T(8,128)} %get-tuple-element.27), channel_id=1, source_target_pairs={{0,15},{1,0},{2,1},{3,2},{4,3},{5,4},{6,5},{7,6},{8,7},{9,8},{10,9... | collective-permute-start | bytes 442376 | tf_op jit(solution)/shard_map/ppermute | solution.py:532
  13.3 3.8 %collective-permute-done.zl = f32[6,48,128]{2,1,0:T(8,128)S(1)} collective-permute-done((f32[6,48,128]{2,1,0:T(8,128)}, f32[6,48,128]{2,1,0:T(8,128)S(1)}, u32[]{:S(2)}, u32[]{:S(2)}) %collective-permute-start) | collective-permute-done | bytes 147488 | tf_op jit(solution)/shard_map/ppermute | solution.py:531
  18.4 4.7 %shard_map.51 = (f32[24,16,128]{2,1,0:T(8,128)}, f32[24,16,128]{2,1,0:T(8,128)}) custom-call(f32[48,48,48]{2,1,0:T(8,128)} %x0.9, f32[48,48,48]{2,1,0:T(8,128)} %b.7, f32[48,48,48]{2,1,0:T(8,128)} %rea.9, f32[6,48,128]{2,1,0:T(8,128)} %copy-done, f32[6,48,128]{2,1,0:T(8,128)} %copy-done.1), custom_call_target="tpu_custom_call" | custom-call | tf_op jit(solution)/shard_map/pallas_call | solution.py:40
  26.3 3.1 %collective-permute-done.2.yl = f32[24,16,128]{2,1,0:T(8,128)S(1)} collective-permute-done((f32[24,16,128]{2,1,0:T(8,128)}, f32[24,16,128]{2,1,0:T(8,128)S(1)}, u32[]{:S(2)}, u32[]{:S(2)}) %collective-permute-start.2) | collective-permute-done | bytes 196640 | tf_op jit(solution)/shard_map/ppermute | solution.py:531
  30.7 4.5 %shard_map.52 = f32[6,3,64,128]{3,2,1,0:T(8,128)} custom-call(s32[5]{0:T(128)} %stack.15.ids, f32[48,48,48]{2,1,0:T(8,128)} %x0.9, f32[48,48,48]{2,1,0:T(8,128)} %b.7, f32[48,48,48]{2,1,0:T(8,128)} %rea.9, f32[6,48,128]{2,1,0:T(8,128)} %copy-done, f32[6,48,128]{2,1,0:T(8,128)} %copy-done.1, f32[24,16,128]{2,1,0:T(8,128)} %copy-done.2, f32[24,16,128]{2,1,0:T(8,128)} %copy-done.3), custom_call_target="tpu_custom_call" | custom-call | tf_op jit(solution)/shard_map/pallas_call | solution.py:40
  35.2 2.4 %collective-permute-start.4 = (f32[6,3,64,128]{3,2,1,0:T(8,128)}, f32[6,3,64,128]{3,2,1,0:T(8,128)S(1)}, u32[]{:S(2)}, u32[]{:S(2)}) collective-permute-start(f32[6,3,64,128]{3,2,1,0:T(8,128)} %shard_map.52), channel_id=1, source_target_pairs={{0,64},{64,0},{1,65},{65,1},{2,66},{66,2},{3,67},{67,3},{4,68},{68... | collective-permute-start | bytes 1769480 | tf_op jit(solution)/shard_map/ppermute | solution.py:537
  40.3 29.9 %shard_map.53 = (f32[54,64,128]{2,1,0:T(8,128)}, f32[54,64,128]{2,1,0:T(8,128)}, f32[56,64,128]{2,1,0:T(8,128)}, f32[24,24,128]{2,1,0:T(8,128)}, f32[24,24,128]{...) custom-call(s32[5]{0:T(128)} %stack.15.ids, f32[48,48,48]{2,1,0:T(8,128)} %x0.9, f32[48,48,48]{2,1,0:T(8,128)} %b.7, ...), custom_call_target="tpu_custom_call" | custom-call | tf_op jit(solution)/shard_map/pallas_call | solution.py:40
  70.1 4.8 %collective-permute-start.6 = (f32[6,24,128]{2,1,0:T(8,128)}, f32[6,24,128]{2,1,0:T(8,128)S(1)}, u32[]{:S(2)}, u32[]{:S(2)}) collective-permute-start(f32[6,24,128]{2,1,0:T(8,128)} %get-tuple-element.33), channel_id=1, source_target_pairs={{0,15},{1,0},{2,1},{3,2},{4,3},{5,4},{6,5},{7,6},{8,7},{9,8},{10,9... | collective-permute-start | bytes 221192 | tf_op jit(solution)/shard_map/ppermute | solution.py:532
  74.9 1.9 collective-permute-done.5.zl
  77.5 2.7 %shard_map.54 = (f32[12,24,128]{2,1,0:T(8,128)}, f32[12,24,128]{2,1,0:T(8,128)}) custom-call(f32[24,24,128]{2,1,0:T(8,128)} %get-tuple-element.30.f1, f32[24,24,128]{2,1,0:T(8,128)} %get-tuple-element.31.r1, f32[6,24,128]{2,1,0:T(8,128)} %copy-done.5, f32[6,24,128]{2,1,0:T(8,128)} %copy-done.6), custom_call_target="tpu_custom_call" | custom-call | tf_op jit(solution)/shard_map/pallas_call | solution.py:40
  81.0 1.9 collective-permute-start.8
  82.9 2.7 %collective-permute-done.7.yl = f32[12,24,128]{2,1,0:T(8,128)S(1)} collective-permute-done((f32[12,24,128]{2,1,0:T(8,128)}, f32[12,24,128]{2,1,0:T(8,128)S(1)}, u32[]{:S(2)}, u32[]{:S(2)}) %collective-permute-start.7) | collective-permute-done | bytes 147488 | tf_op jit(solution)/shard_map/ppermute | solution.py:531
  87.0 3.3 %shard_map.55 = f32[12,2,56,128]{3,2,1,0:T(8,128)} custom-call(s32[5]{0:T(128)} %stack.15.ids, f32[24,24,128]{2,1,0:T(8,128)} %get-tuple-element.30.f1, f32[24,24,128]{2,1,0:T(8,128)} %get-tuple-element.31.r1, f32[6,24,128]{2,1,0:T(8,128)} %copy-done.5, f32[6,24,128]{2,1,0:T(8,128)} %copy-done.6, f32[12,24,128]{2,1,0:T(8,128)} %copy-done.8, ...), custom_call_target="tpu_custom_call" | custom-call | tf_op jit(solution)/shard_map/pallas_call | solution.py:40
  90.2 2.7 %collective-permute-start.9 = (f32[12,2,56,128]{3,2,1,0:T(8,128)}, f32[12,2,56,128]{3,2,1,0:T(8,128)S(1)}, u32[]{:S(2)}, u32[]{:S(2)}) collective-permute-start(f32[12,2,56,128]{3,2,1,0:T(8,128)} %shard_map.55), channel_id=1, source_target_pairs={{0,64},{64,0},{1,65},{65,1},{2,66},{66,2},{3,67},{67,3},{4,68},{68... | collective-permute-start | bytes 2064392 | tf_op jit(solution)/shard_map/ppermute | solution.py:537
  92.9 2.0 collective-permute-done.9.xr
  95.7 22.7 %shard_map.56 = (f32[36,56,128]{2,1,0:T(8,128)}, f32[36,56,128]{2,1,0:T(8,128)}, f32[38,56,128]{2,1,0:T(8,128)}, f32[18,32,128]{2,1,0:T(8,128)}, f32[18,32,128]{...) custom-call(s32[5]{0:T(128)} %stack.15.ids, f32[24,24,128]{2,1,0:T(8,128)} %get-tuple-element.30.f1, ...), custom_call_target="tpu_custom_call" | custom-call | tf_op jit(solution)/shard_map/pallas_call | solution.py:40
  119.5 19.2 %all_to_all.14 = f32[128,1,432]{2,1,0:T(1,128)S(1)} all-to-all(f32[128,1,432]{2,1,0:T(1,128)S(1)} %broadcast_in_dim.13), channel_id=1, replica_groups=mesh['gx'=2,'gy'=4,'gz'=16] {'gx','gy','gz'}, dimensions={0} | all-to-all | bytes 442368 | tf_op jit(solution)/shard_map/all_to_all | solution.py:573
  140.0 4.9 %copy.7 = f32[2,2,6,4,6,16,6]{6,5,4,3,2,1,0:T(8,128)} copy(f32[2,2,6,4,6,16,6]{5,3,1,6,4,2,0:T(4,128)S(1)} %bitcast.11) | data formatting | bytes 442368 | tf_op jit(solution)/shard_map/transpose | solution.py:574
  144.9 4.6 %reshape.27.g3 = f32[2,12,24,96]{3,2,1,0:T(8,128)} reshape(f32[2,2,6,4,6,16,6]{6,5,4,3,2,1,0:T(8,128)} %copy.7) | data formatting | bytes 442368 | tf_op jit(solution)/shard_map/reshape | solution.py:576
  149.5 50.1 %shard_map.57 = (f32[48,48,48]{2,1,0:T(8,128)}, f32[48,48,48]{2,1,0:T(8,128)}, f32[48,48,48]{2,1,0:T(8,128)}, f32[8,128]{1,0:T(8,128)}) custom-call(s32[5]{0:T(128)} %stack.15.ids, f32[2,12,24,96]{3,2,1,0:T(8,128)} %reshape.27.g3, f32[18,32,128]{2,1,0:T(8,128)} %get-tuple-element.37.f2, f32[18,32,128]{2,1,0:T(8,128)} %get-tuple-element.38.c2, ...), custom_call_target="tpu_custom_call" | custom-call | tf_op jit(solution)/shard_map/pallas_call | solution.py:40
  200.3 14.4 %all_to_all.15 = f32[128,1,128]{2,1,0:T(1,128)} all-to-all(f32[128,1,128]{2,1,0:T(1,128)S(1)} %broadcast_in_dim.14), channel_id=1, replica_groups=mesh['gx'=2,'gy'=4,'gz'=16] {'gx','gy','gz'}, dimensions={0} | all-to-all | bytes 131072 | tf_op jit(solution)/shard_map/all_to_all | solution.py:587
  214.8 4.3 %shard_map.58 = (f32[48,48,48]{2,1,0:T(8,128)}, f32[48,48,48]{2,1,0:T(8,128)}) custom-call(f32[128,128]{1,0:T(8,128)} %bitcast.12, f32[48,48,48]{2,1,0:T(8,128)} %x0.9, f32[48,48,48]{2,1,0:T(8,128)} %get-tuple-element.47.z, f32[48,48,48]{2,1,0:T(8,128)} %get-tuple-element.48.az, f32[48,48,48]{2,1,0:T(8,128)} %get-tuple-element.49.f), custom_call_target="tpu_custom_call" | custom-call | tf_op jit(solution)/shard_map/pallas_call | solution.py:40
  (36 shorter events, 15.2 us)
Async XLA Ops:
  6.3 10.8 %collective-permute-start = (f32[6,48,128]{2,1,0:T(8,128)}, f32[6,48,128]{2,1,0:T(8,128)S(1)}, u32[]{:S(2)}, u32[]{:S(2)}) collective-permute-start(f32[6,48,128]{2,1,0:T(8,128)} %get-tuple-element.26), channel_id=1, source_target_pairs={{0,1},{1,2},{2,3},{3,4},{4,5},{5,6},{6,7},{7,8},{8,9},{9,10},{10,1... | collective-permute-start | bytes 442376 | tf_op jit(solution)/shard_map/ppermute | solution.py:531
  8.4 8.7 %collective-permute-start.1 = (f32[6,48,128]{2,1,0:T(8,128)}, f32[6,48,128]{2,1,0:T(8,128)S(1)}, u32[]{:S(2)}, u32[]{:S(2)}) collective-permute-start(f32[6,48,128]{2,1,0:T(8,128)} %get-tuple-element.27), channel_id=1, source_target_pairs={{0,15},{1,0},{2,1},{3,2},{4,3},{5,4},{6,5},{7,6},{8,7},{9,8},{10,9... | collective-permute-start | bytes 442376 | tf_op jit(solution)/shard_map/ppermute | solution.py:532
  17.1 0.7 copy-start
  17.7 0.7 copy-start.1
  23.1 6.3 %collective-permute-start.2 = (f32[24,16,128]{2,1,0:T(8,128)}, f32[24,16,128]{2,1,0:T(8,128)S(1)}, u32[]{:S(2)}, u32[]{:S(2)}) collective-permute-start(f32[24,16,128]{2,1,0:T(8,128)} %get-tuple-element.28), channel_id=1, source_target_pairs={{0,16},{16,32},{32,48},{48,0},{1,17},{17,33},{33,49},{49,1},{2,18}... | collective-permute-start | bytes 589832 | tf_op jit(solution)/shard_map/ppermute | solution.py:531
  24.3 5.1 %collective-permute-start.3 = (f32[24,16,128]{2,1,0:T(8,128)}, f32[24,16,128]{2,1,0:T(8,128)S(1)}, u32[]{:S(2)}, u32[]{:S(2)}) collective-permute-start(f32[24,16,128]{2,1,0:T(8,128)} %get-tuple-element.29), channel_id=1, source_target_pairs={{0,48},{16,0},{32,16},{48,32},{1,49},{17,1},{33,17},{49,33},{2,50}... | collective-permute-start | bytes 589832 | tf_op jit(solution)/shard_map/ppermute | solution.py:532
  29.4 0.7 copy-start.2
  30.1 0.7 copy-start.3
  35.2 4.3 %collective-permute-start.4 = (f32[6,3,64,128]{3,2,1,0:T(8,128)}, f32[6,3,64,128]{3,2,1,0:T(8,128)S(1)}, u32[]{:S(2)}, u32[]{:S(2)}) collective-permute-start(f32[6,3,64,128]{3,2,1,0:T(8,128)} %shard_map.52), channel_id=1, source_target_pairs={{0,64},{64,0},{1,65},{65,1},{2,66},{66,2},{3,67},{67,3},{4,68},{68... | collective-permute-start | bytes 1769480 | tf_op jit(solution)/shard_map/ppermute | solution.py:537
  39.4 0.8 copy-start.7
  70.1 6.7 %collective-permute-start.5 = (f32[6,24,128]{2,1,0:T(8,128)}, f32[6,24,128]{2,1,0:T(8,128)S(1)}, u32[]{:S(2)}, u32[]{:S(2)}) collective-permute-start(f32[6,24,128]{2,1,0:T(8,128)} %get-tuple-element.32), channel_id=1, source_target_pairs={{0,1},{1,2},{2,3},{3,4},{4,5},{5,6},{6,7},{7,8},{8,9},{9,10},{10,1... | collective-permute-start | bytes 221192 | tf_op jit(solution)/shard_map/ppermute | solution.py:531
  70.1 6.7 %collective-permute-start.6 = (f32[6,24,128]{2,1,0:T(8,128)}, f32[6,24,128]{2,1,0:T(8,128)S(1)}, u32[]{:S(2)}, u32[]{:S(2)}) collective-permute-start(f32[6,24,128]{2,1,0:T(8,128)} %get-tuple-element.33), channel_id=1, source_target_pairs={{0,15},{1,0},{2,1},{3,2},{4,3},{5,4},{6,5},{7,6},{8,7},{9,8},{10,9... | collective-permute-start | bytes 221192 | tf_op jit(solution)/shard_map/ppermute | solution.py:532
  76.9 0.6 copy-start.5
  76.9 0.6 copy-start.6
  80.2 5.4 %collective-permute-start.7 = (f32[12,24,128]{2,1,0:T(8,128)}, f32[12,24,128]{2,1,0:T(8,128)S(1)}, u32[]{:S(2)}, u32[]{:S(2)}) collective-permute-start(f32[12,24,128]{2,1,0:T(8,128)} %get-tuple-element.34), channel_id=1, source_target_pairs={{0,16},{16,32},{32,48},{48,0},{1,17},{17,33},{33,49},{49,1},{2,18}... | collective-permute-start | bytes 442376 | tf_op jit(solution)/shard_map/ppermute | solution.py:531
  81.0 4.7 %collective-permute-start.8 = (f32[12,24,128]{2,1,0:T(8,128)}, f32[12,24,128]{2,1,0:T(8,128)S(1)}, u32[]{:S(2)}, u32[]{:S(2)}) collective-permute-start(f32[12,24,128]{2,1,0:T(8,128)} %get-tuple-element.35), channel_id=1, source_target_pairs={{0,48},{16,0},{32,16},{48,32},{1,49},{17,1},{33,17},{49,33},{2,50}... | collective-permute-start | bytes 442376 | tf_op jit(solution)/shard_map/ppermute | solution.py:532
  85.7 0.7 copy-start.8
  86.3 0.7 copy-start.9
  90.2 4.7 %collective-permute-start.9 = (f32[12,2,56,128]{3,2,1,0:T(8,128)}, f32[12,2,56,128]{3,2,1,0:T(8,128)S(1)}, u32[]{:S(2)}, u32[]{:S(2)}) collective-permute-start(f32[12,2,56,128]{3,2,1,0:T(8,128)} %shard_map.55), channel_id=1, source_target_pairs={{0,64},{64,0},{1,65},{65,1},{2,66},{66,2},{3,67},{67,3},{4,68},{68... | collective-permute-start | bytes 2064392 | tf_op jit(solution)/shard_map/ppermute | solution.py:537
  94.9 0.9 copy-start.4

commit v2 on v1

v2 whole, which is shorter than its diff:
```python
import functools
import jax
import jax.numpy as jnp
from jax import lax
from jax.experimental import pallas as pl
from jax.experimental.pallas import tpu as pltpu
from jax.sharding import PartitionSpec as P

W = 6.0 / 7.0
BOTTOM_ITERS = 6
N0 = 48
F32 = jnp.float32
HI = lax.Precision.HIGHEST
M0, M1, M2 = 20, 12, 20


class Spec:
    def __init__(self, n, h, na, gp, r0, R, hx):
        self.n, self.h, self.na, self.gp, self.r0, self.R, self.hx = n, h, na, gp, r0, R, hx
        self.lw = 128 // gp
        self.zshape = (n // gp, n, 128)
        self.yrows = -(-na * h // 8) * 8
        self.yshape = (n // 2, self.yrows, 128)
        self.xshape = (hx, na, R, 128)
        self.nx = n + hx


L0 = Spec(48, 5, 3, 8, 8, 64, 6)
L1 = Spec(24, 12, 2, 4, 16, 56, 12)


def sds(*shape):
    return jax.ShapeDtypeStruct(shape, F32)


def run(kernel, outs, args, scratch=(), mib=12):
    vmem = pl.BlockSpec(memory_space=pltpu.VMEM)
    return pl.pallas_call(
        kernel,
        out_shape=outs,
        in_specs=[vmem] * len(args),
        out_specs=jax.tree.map(lambda _: vmem, outs),
        scratch_shapes=[pltpu.VMEM(s, F32) for s in scratch],
        compiler_params=pltpu.CompilerParams(vmem_limit_bytes=mib * 1024 * 1024),
    )(*args)


def place():
    return [lax.axis_index(a) for a in ("gx", "gy", "gz")] + [lax.axis_size(a) for a in ("gy", "gz")]


def lanes(rows):
    return lax.broadcasted_iota(jnp.int32, (rows, 128), 1)


def roll(v, shift, axis):
    if isinstance(shift, int):
        shift = shift % v.shape[axis]
        if shift == 0:
            return v
    return pltpu.roll(v, shift, axis)


def loop(n, f, u=1):
    u = max(d for d in range(1, u + 1) if n % d == 0)

    def some(i, c):
        for k in range(u):
            f(i * u + k)
        return c

    lax.fori_loop(0, n // u, some, 0)


def edge(sp, ids):
    _, gy, gz, ny, nz = ids
    high = jnp.where(gz < nz - 1, sp.n + sp.h, sp.n)
    low = jnp.where(gz > 0, 128 - sp.h, 128)
    return high, low, jnp.where(gy > 0, 1.0, 0.0), jnp.where(gy < ny - 1, 1.0, 0.0)


def zpack(sp, get, hi_ref, lo_ref):
    ln = lanes(sp.n)

    def group(g):
        hi = jnp.zeros((sp.n, 128), F32)
        lo = hi
        for j in range(sp.gp):
            for a in range(sp.na):
                v = get(g * sp.gp + j, a, 0, sp.n)
                at = sp.lw * j + sp.h * a
                here = (ln >= at) & (ln < at + sp.h)
                hi = jnp.where(here, roll(v, at - (sp.n - sp.h), 1), hi)
                lo = jnp.where(here, roll(v, at, 1), lo)
        hi_ref[g] = hi
        lo_ref[g] = lo

    loop(sp.n // sp.gp, group)


def ypack(sp, get, zl, zh, up_ref, dn_ref):
    n, h = sp.n, sp.h
    up0 = (n - h) // 8 * 8
    dn1 = -(-h // 8) * 8

    def fold(x, g, j, a, b, e):
        o = 64 * (j % 2)
        ln = lanes(e - b)
        at = sp.lw * j + h * a
        own = roll(get(x, a, b, e), o, 1)
        high = roll(zh[g, b:e, :], o + n - at, 1)
        low = roll(zl[g, b:e, :], o + 64 - h - at, 1)
        return jnp.where(ln < o + n, own, jnp.where(ln < o + n + h, high, low))

    def group(g):
        for q in range(sp.gp // 2):
            p = g * (sp.gp // 2) + q
            for a in range(sp.na):
                for ref, b, e, s, t in ((up_ref, up0, n, n - h - up0, n - up0), (dn_ref, 0, dn1, 0, h)):
                    even = fold(g * sp.gp + 2 * q, g, 2 * q, a, b, e)
                    odd = fold(g * sp.gp + 2 * q + 1, g, 2 * q + 1, a, b, e)
                    both = jnp.where(lanes(e - b) < 64, even, odd)
                    ref[p, a * h : (a + 1) * h, :] = both[s:t]
            if sp.yrows > sp.na * h:
                pad = jnp.zeros((sp.yrows - sp.na * h, 128), F32)
                up_ref[p, sp.na * h :, :] = pad
                dn_ref[p, sp.na * h :, :] = pad

    loop(n // sp.gp, group)


def plane(sp, own, zl, zh, yl, yh, x, g, j, a, dst, xw, ends):
    n, h, r0 = sp.n, sp.h, sp.r0
    at = sp.lw * j + h * a
    ln = lanes(n)
    top, bottom, below, above = ends
    static = isinstance(j, int)

    def amount(k):
        return k - at if static else lax.rem(k + 128 - at, 128)

    high = roll(zh[g], amount(n), 1)
    low = roll(zl[g], amount(128 - h), 1)
    dst[xw, r0 : r0 + n, :] = jnp.where(ln < top, high, jnp.where(ln >= bottom, low, 0.0))
    dst[xw, r0 : r0 + n, 0:n] = own(x, a)
    lh = lanes(h)
    half = g * (sp.gp // 2) + j // 2
    dst[xw, 0:r0, :] = jnp.zeros((r0, 128), F32)
    dst[xw, r0 + n :, :] = jnp.zeros((sp.R - r0 - n, 128), F32)
    for ref, r, weight in ((yl, r0 - h, below), (yh, r0 + n, above)):
        u = ref[half, a * h : (a + 1) * h, :] * weight
        if static:
            near, far = (u, roll(u, 64, 1)) if j % 2 == 0 else (roll(u, 64, 1), u)
        else:
            t = 64 * lax.rem(j, 2)
            near, far = roll(u, t, 1), roll(u, 64 - t, 1)
        dst[xw, r : r + h, :] = jnp.where(lh < top, near, jnp.where(lh >= bottom, far, 0.0))


def domain(sp, n, h, r0, R, ids):
    row = lax.broadcasted_iota(jnp.int32, (R, 128), 0) - r0
    ln = lanes(R)
    z = jnp.where(ln < 64, ln, ln - 128)
    gy, gz, ny, nz = ids[1], ids[2], ids[3], ids[4]
    y_at, z_at = row + gy * n, z + gz * n
    ok = (row >= -h) & (row < n + h) & (z >= -h) & (z < n + h)
    return ok & (y_at >= 0) & (y_at < ny * n) & (z_at >= 0) & (z_at < nz * n)


def neighbours(ref, x):
    c = ref[x + 1]
    R = c.shape[0]
    s = ref[x] + ref[x + 2]
    s = s + (roll(c, 1, 0) + roll(c, R - 1, 0))
    return s + (roll(c, 1, 1) + roll(c, 127, 1))


def zero_ends(ref, n):
    ref[0] = jnp.zeros(ref.shape[1:], F32)
    ref[n + 1] = jnp.zeros(ref.shape[1:], F32)


def relax(src, dst, f, c, n, factor, u=3):
    def one(x):
        dst[x + 1] = (1.0 - W) * src[x + 1] + c[x] * (f[x] + factor * neighbours(src, x))

    loop(n, one, u)


def coarse_lane(l, signed):
    c = l // 2
    return jnp.where(l < 64, c, c + 64) if signed else c


def lane_map(signed, value):
    l = lax.broadcasted_iota(jnp.int32, (256, 128), 0) % 128
    m = lax.broadcasted_iota(jnp.int32, (256, 128), 1)
    return jnp.where(coarse_lane(l, signed) == m, value, 0.0).astype(jnp.bfloat16)


def spread_map(pick):
    m = lax.broadcasted_iota(jnp.int32, (256, 128), 0) % 128
    l = lax.broadcasted_iota(jnp.int32, (256, 128), 1)
    return jnp.where(pick(l) == m, 1.0, 0.0).astype(jnp.bfloat16)


def times(v, m):
    big = v.astype(jnp.bfloat16)
    rest = (v - big.astype(F32)).astype(jnp.bfloat16)
    return jnp.dot(jnp.concatenate([big, rest], axis=1), m, preferred_element_type=F32)


def coarsen_planes(pair, n, tmp, acc, signed, rows=None, u=2):
    half = acc.shape[1]
    rows = rows or 2 * half

    def one(x):
        tmp[x, 0:rows, :] = pair(x)
        acc[x] = tmp[x, pl.ds(0, half, stride=2), :] + tmp[x, pl.ds(1, half, stride=2), :]

    loop(n, one, u)
    v = acc[...].reshape(n * half, 128)
    acc[...] = times(v, lane_map(signed, 0.125)).reshape(n, half, 128)


def add_refined(coarse, n, src, dst, wide, m, u=3):
    rows = coarse.shape[1]
    wide[0:n, 0:rows, :] = times(coarse[...].reshape(n * rows, 128), m).reshape(n, rows, 128)
    R = dst.shape[1]

    def one(i):
        v = wide[i, 0 : R // 2, :]
        for k in range(2):
            dst[2 * i + 1, pl.ds(k, R // 2, stride=2), :] = v
        t = dst[2 * i + 1]
        dst[2 * i + 1] = src[2 * i + 1] + t
        dst[2 * i + 2] = src[2 * i + 2] + t

    loop(n, one, u)


def k_zpack0(x0, b, rea, hi, lo, s):
    for a, ref in enumerate((x0, b, rea)):
        def one(x, a=a, ref=ref):
            s[a, x, :, 0:48] = ref[x]
        loop(48, one, 4)
    zpack(L0, lambda x, a, p, q: s[a, x, p:q, :], hi, lo)


def k_ypack0(x0, b, rea, zl, zh, up, dn, s):
    for a, ref in enumerate((x0, b, rea)):
        def one(x, a=a, ref=ref):
            s[a, x, 0:8, 0:48] = ref[x, 0:8]
            s[a, x, 8:16, 0:48] = ref[x, 40:48]
        loop(48, one, 8)
    ypack(L0, lambda x, a, p, q: s[a, x, 0:8, :] if p == 0 else s[a, x, 8:16, :], zl, zh, up, dn)


def k_xpack(sp, own, zl, zh, yl, yh, out):
    ids = place()
    ends = edge(sp, ids)
    start = (1 - ids[0]) * (sp.n - sp.hx)

    def one(i):
        x = start + i
        g, j = lax.div(x, sp.gp), lax.rem(x, sp.gp)
        for a in range(sp.na):
            plane(sp, own, zl, zh, yl, yh, x, g, j, a, out.at[i], a, ends)

    loop(sp.hx, one, 2)


def k_xpack0(x0, b, rea, zl, zh, yl, yh, out):
    refs = (x0, b, rea)
    k_xpack(L0, lambda x, a: refs[a][x], zl, zh, yl, yh, out)


def assemble(sp, ids, own, zl, zh, yl, yh, xr, dsts):
    shift = ids[0] * sp.hx
    ends = edge(sp, ids)

    def group(g):
        for j in range(sp.gp):
            x = g * sp.gp + j
            for a, (dst, off) in enumerate(dsts):
                plane(sp, own, zl, zh, yl, yh, x, g, j, a, dst, x + shift + off, ends)

    loop(sp.n // sp.gp, group)
    other = (1 - ids[0]) * sp.n

    def take(i):
        for a, (dst, off) in enumerate(dsts):
            dst[other + i + off] = xr[i, a]

    loop(sp.hx, take, 2)


def k_down0(x0, b, rea, zl, zh, yl, yh, xr, f_out, c_out, e_out, f1, r1, z1h, z1l, xw, bw, rw, ew, tmp):
    ids = place()
    refs = (x0, b, rea)
    assemble(L0, ids, lambda x, a: refs[a][x], zl, zh, yl, yh, xr, ((xw, 1), (bw, 0), (rw, 0)))
    n = L0.nx
    ok = domain(L0, 48, 5, 8, 64, ids)
    zero_ends(xw, n)
    zero_ends(ew, n)
    zero_ends(e_out, n)

    def first(x):
        d = 6.0 + rw[x]
        c = jnp.where(ok, W / d, 0.0)
        f = bw[x] - d * xw[x + 1] + neighbours(xw, x)
        f_out[x] = f
        c_out[x] = c
        ew[x + 1] = c * f

    loop(n, first, 3)
    relax(ew, e_out, f_out, c_out, n, 1.0)
    shift = ids[0] * L0.hx

    def left(x):
        r = f_out[x] - (6.0 + rw[x]) * e_out[x + 1] + neighbours(e_out, x)
        return r[8:56]

    inner = lanes(48) < 48
    coarsen_planes(lambda x: jnp.where(inner, left(2 * x + shift) + left(2 * x + shift + 1), 0.0), 24, tmp, f1, True)

    def react(x):
        return jnp.where(inner, rw[2 * x + shift, 8:56, :] + rw[2 * x + shift + 1, 8:56, :], 0.0)

    coarsen_planes(react, 24, tmp, r1, True)
    both = (f1, r1)
    zpack(L1, lambda x, a, p, q: both[a][x, p:q, :], z1h, z1l)


def k_ypack1(f1, r1, zl, zh, up, dn):
    both = (f1, r1)
    ypack(L1, lambda x, a, p, q: both[a][x, p:q, :], zl, zh, up, dn)


def k_xpack1(f1, r1, zl, zh, yl, yh, out):
    both = (f1, r1)
    k_xpack(L1, lambda x, a: both[a][x, :, 0:24], zl, zh, yl, yh, out)


def k_down1(f1, r1, zl, zh, yl, yh, xr, fw, cw, e_out, f2, c2, e2, out3, rw, ew, tmp, r2, ew2, tmp2, t3, sq):
    ids = place()
    both = (f1, r1)
    assemble(L1, ids, lambda x, a: both[a][x, :, 0:24], zl, zh, yl, yh, xr, ((fw, 0), (rw, 0)))
    n = L1.nx
    ok = domain(L1, 24, 12, 16, 56, ids)
    zero_ends(ew, n)
    zero_ends(e_out, n)

    def first(x):
        c = jnp.where(ok, W / (1.5 + rw[x]), 0.0)
        cw[x] = c
        ew[x + 1] = c * fw[x]

    loop(n, first, 4)
    relax(ew, e_out, fw, cw, n, 0.25)

    def left(x):
        return fw[x] - (1.5 + rw[x]) * e_out[x + 1] + 0.25 * neighbours(e_out, x)

    def pad(x):
        tmp[x, 56:64, :] = jnp.zeros((8, 128), F32)

    loop(18, pad, 3)
    coarsen_planes(lambda x: left(2 * x) + left(2 * x + 1), 18, tmp, f2, True, 56)
    coarsen_planes(lambda x: rw[2 * x] + rw[2 * x + 1], 18, tmp, r2, True, 56)
    ok2 = domain(None, 12, 6, 8, 32, ids)
    zero_ends(ew2, 18)
    zero_ends(e2, 18)

    def second(x):
        c = jnp.where(ok2, W / (0.375 + r2[x]), 0.0)
        c2[x] = c
        ew2[x + 1] = c * f2[x]

    loop(18, second, 6)
    relax(ew2, e2, f2, c2, 18, 0.0625, 6)

    def left2(x):
        return f2[x] - (0.375 + r2[x]) * e2[x + 1] + 0.0625 * neighbours(e2, x)

    coarsen_planes(lambda x: left2(2 * x) + left2(2 * x + 1), 9, tmp2, t3.at[0], True, u=3)
    coarsen_planes(lambda x: r2[2 * x] + r2[2 * x + 1], 9, tmp2, t3.at[1], True, u=3)
    shift = ids[0] * 3
    sq[...] = jnp.zeros((128, 128), F32)
    for a in range(2):
        for x in range(6):
            at = a * 36 + x * 6
            sq[at : at + 6, :] = t3[a, x + shift, 4:10, :]
    t = sq[...].T[0:8]
    out3[...] = jnp.broadcast_to(t[None], out3.shape)


def sum_all(v):
    s = jnp.sum(v, axis=0)
    return jnp.sum(jnp.sum(s, axis=1, keepdims=True), axis=0, keepdims=True)


def coarse_solve(g3, nx, ny, nz, e3, s3, f3, c3, r3, tmp, f4, r4, wide, sq):
    R = f3.shape[1]
    for ref in (f3, r3):
        ref[...] = jnp.zeros(ref.shape, F32)
    kx, ky, kz = nx // 6, ny // 6, nz // 6
    for bx in range(kx):
        for by in range(ky):
            k = bx * ky + by
            if kz * 6 < 128:
                sq[k, kz * 6 :, :] = jnp.zeros((128 - kz * 6, 128), F32)
            for bz in range(kz):
                sq[k, bz * 6 : bz * 6 + 6, :] = g3[k * kz + bz, 0:6, :]
            t = sq[k].T
            for x in range(6):
                f3[bx * 6 + x, by * 6 : by * 6 + 6, :] = t[x * 6 : x * 6 + 6]
                r3[bx * 6 + x, by * 6 : by * 6 + 6, :] = t[36 + x * 6 : 42 + x * 6]
    factor = 0.25**3
    ok = (lax.broadcasted_iota(jnp.int32, (R, 128), 0) < ny) & (lanes(R) < nz)
    for ref in (e3, s3):
        zero_ends(ref, nx)

    def first(x):
        c = jnp.where(ok, W / (6.0 * factor + r3[x]), 0.0)
        c3[x] = c
        s3[x + 1] = c * f3[x]

    loop(nx, first, 6)
    relax(s3, e3, f3, c3, nx, factor, 6)

    def left(x):
        v = f3[x] - (6.0 * factor + r3[x]) * e3[x + 1] + factor * neighbours(e3, x)
        return jnp.where(ok, v, 0.0)

    coarsen_planes(lambda x: left(2 * x) + left(2 * x + 1), nx // 2, tmp, f4, False, u=3)
    coarsen_planes(lambda x: r3[2 * x] + r3[2 * x + 1], nx // 2, tmp, r4, False, u=3)
    f4k = 0.25**4
    H = R // 2
    row = lax.broadcasted_iota(jnp.int32, (nx // 2, H, 128), 1)
    lane = lax.broadcasted_iota(jnp.int32, (nx // 2, H, 128), 2)
    inside = (row < ny // 2) & (lane < nz // 2)
    diag = 6.0 * f4k + r4[...]
    zero = jnp.zeros((1, H, 128), F32)

    def apply(p):
        s = jnp.concatenate([zero, p[:-1]], axis=0) + jnp.concatenate([p[1:], zero], axis=0)
        s = s + roll(p, 1, 1) + roll(p, H - 1, 1) + roll(p, 1, 2) + roll(p, 127, 2)
        return jnp.where(inside, diag * p - f4k * s, 0.0)

    r = jnp.where(inside, f4[...], 0.0)
    p = r
    e = jnp.zeros_like(r)
    rr = sum_all(r * r)
    for i in range(BOTTOM_ITERS):
        q = apply(p)
        a = rr / sum_all(p * q)
        e = e + a * p
        if i + 1 < BOTTOM_ITERS:
            r = r - a * q
            new = sum_all(r * r)
            p = r + (new / rr) * p
            rr = new
    f4[...] = e
    add_refined(f4, nx // 2, e3, s3, wide, spread_map(lambda l: coarse_lane(l, False)))
    relax(s3, e3, f3, c3, nx, factor, 6)
    relax(e3, s3, f3, c3, nx, factor, 6)


def k_up(g3, f2, c2, e2i, f1, c1, e1i, f0, c0, e0i, rea, z_out, az_out, f_own, sums,
         e3, s3, f3, c3, r3, tmp3, f4, r4, sq, w3, w2, n1, w1, e2, s2, e1, s1, e0, s0):
    gx, gy, gz, sy, sz = place()
    nx, ny, nz = f3.shape[0], sy * 6, sz * 6
    coarse_solve(g3, nx, ny, nz, e3, s3, f3, c3, r3, tmp3, f4, r4, w3, sq)
    for ref, n in ((s2, 18), (s1, 36), (s0, 54), (e2, 18), (e1, 36), (e0, 54)):
        zero_ends(ref, n)
    R3 = s3.shape[1]
    pick = lax.broadcasted_iota(jnp.int32, (16, R3), 1) == lax.broadcasted_iota(jnp.int32, (16, R3), 0) + (gy * 6 - 4)
    pick = pick.astype(F32)
    for i in range(9):
        w3[i, 0:16, :] = jnp.dot(pick, s3[i + 1 + gx * 3], precision=HI, preferred_element_type=F32)
    spread = spread_map(lambda l: gz * 6 + jnp.where(l < 64, l // 2, l // 2 - 64))
    add_refined(w3.at[:, 0:16, :], 9, e2i, e2, w2, spread)
    relax(e2, s2, f2, c2, 18, 0.0625, 6)
    relax(s2, e2, f2, c2, 18, 0.0625, 6)
    m = spread_map(lambda l: coarse_lane(l, True))
    add_refined(e2.at[1:19], 18, e1i, e1, w2, m)
    relax(e1, s1, f1, c1, 36, 0.25)
    relax(s1, e1, f1, c1, 36, 0.25)

    def near(i):
        n1[i] = e1[i + 1 + gx * 9, 12:44, :]

    loop(27, near, 3)
    add_refined(n1, 27, e0i, e0, w1, m)
    ok0 = domain(L0, 48, 5, 8, 64, (gx, gy, gz, sy, sz))

    def mask(x):
        e0[x + 1] = jnp.where(ok0, e0[x + 1], 0.0)

    loop(54, mask, 3)
    relax(e0, s0, f0, c0, 54, 1.0)
    relax(s0, e0, f0, c0, 54, 1.0)
    shift = gx * 6

    def last(x, carry):
        u, v = carry
        z = e0[x + shift + 1][8:56, 0:48]
        nb = neighbours(e0, x + shift)[8:56, 0:48]
        az = (6.0 + rea[x]) * z - nb
        f = f0[x + shift][8:56, 0:48]
        z_out[x] = z
        az_out[x] = az
        f_own[x] = f
        return u + f * z, v + z * az

    zero = jnp.zeros((48, 48), F32)
    u, v = lax.fori_loop(0, 24, lambda i, c: last(2 * i + 1, last(2 * i, c)), (zero, zero))

    def total(t):
        return jnp.sum(jnp.sum(t, axis=1, keepdims=True), axis=0, keepdims=True)

    ln = lanes(sums.shape[0])
    sums[...] = jnp.where(ln == 0, total(u), jnp.where(ln == 1, total(v), 0.0))


def k_last(sums, x0, z, az, f, sol, res):
    s = jnp.sum(sums[...], axis=0, keepdims=True)
    ln = lanes(1)
    upper = jnp.sum(jnp.where(ln == 0, s, 0.0), axis=1, keepdims=True)
    lower = jnp.sum(jnp.where(ln == 1, s, 0.0), axis=1, keepdims=True)
    step = upper / lower

    def one(x):
        sol[x] = x0[x] + step * z[x]
        res[x] = f[x] - step * az[x]

    loop(48, one, 4)


def ring(up, dn, axis):
    n = lax.axis_size(axis)
    low = lax.ppermute(up, axis, [(i, (i + 1) % n) for i in range(n)])
    high = lax.ppermute(dn, axis, [(i, (i - 1) % n) for i in range(n)])
    return low, high


def swap(v):
    return lax.ppermute(v, "gx", [(0, 1), (1, 0)])


def body(b, x0, rea):
    ALL = ("gx", "gy", "gz")
    sizes = [lax.axis_size(a) for a in ALL]
    count = sizes[0] * sizes[1] * sizes[2]
    hi, lo = run(k_zpack0, (sds(*L0.zshape),) * 2, (x0, b, rea), [(3, 48, 48, 128)])
    zl, zh = ring(hi, lo, "gz")
    up, dn = run(k_ypack0, (sds(*L0.yshape),) * 2, (x0, b, rea, zl, zh), [(3, 48, 16, 128)])
    yl, yh = ring(up, dn, "gy")
    xs = run(k_xpack0, sds(*L0.xshape), (x0, b, rea, zl, zh, yl, yh))
    xr = swap(xs)
    p0 = (54, 64, 128)
    q0 = (56, 64, 128)
    f0, c0, e0, f1, r1, z1h, z1l = run(
        k_down0,
        (sds(*p0), sds(*p0), sds(*q0), sds(24, 24, 128), sds(24, 24, 128), sds(*L1.zshape), sds(*L1.zshape)),
        (x0, b, rea, zl, zh, yl, yh, xr),
        [q0, p0, p0, q0, (24, 48, 128)],
        mib=M0,
    )
    zl, zh = ring(z1h, z1l, "gz")
    up, dn = run(k_ypack1, (sds(*L1.yshape),) * 2, (f1, r1, zl, zh))
    yl, yh = ring(up, dn, "gy")
    xs = run(k_xpack1, sds(*L1.xshape), (f1, r1, zl, zh, yl, yh))
    xr = swap(xs)
    p1, q1, p2, q2 = (36, 56, 128), (38, 56, 128), (18, 32, 128), (20, 32, 128)
    f1w, c1w, e1w, f2w, c2w, e2w, g = run(
        k_down1,
        (sds(*p1), sds(*p1), sds(*q1), sds(*p2), sds(*p2), sds(*q2), sds(count, 8, 128)),
        (f1, r1, zl, zh, yl, yh, xr),
        [p1, q1, (18, 64, 128), p2, q2, (9, 32, 128), (2, 9, 16, 128), (128, 128)],
        mib=M1,
    )
    g = lax.all_to_all(g, ALL, 0, 0, tiled=True)
    n3 = [6 * s for s in sizes]
    R3 = (n3[1] + 8) // 8 * 8
    if R3 % 16:
        R3 += 8
    p3, q3, p4 = (n3[0], R3, 128), (n3[0] + 2, R3, 128), (n3[0] // 2, R3 // 2, 128)
    z, az, f, sums = run(
        k_up,
        (sds(48, 48, 48), sds(48, 48, 48), sds(48, 48, 48), sds(count, 128)),
        (g, f2w, c2w, e2w, f1w, c1w, e1w, f0, c0, e0, rea),
        [q3, q3, p3, p3, p3, (n3[0] // 2, R3, 128), p4, p4, (sizes[0] * sizes[1], 128, 128), (9, 16, 128), (18, 32, 128),
         (27, 32, 128), (27, 32, 128), q2, q2, q1, q1, q0, q0],
        mib=M2,
    )
    sums = lax.all_to_all(sums.reshape(count, 1, 128), ALL, 0, 0, tiled=True).reshape(count, 128)
    return run(k_last, (sds(48, 48, 48), sds(48, 48, 48)), (sums, x0, z, az, f))


def solution(mesh):
    spec = P("gx", "gy", "gz")
    return jax.shard_map(body, mesh=mesh, in_specs=(spec, spec, spec), out_specs=(spec, spec), check_vma=False)
```

time: 219 us -> 119 us (0.54)
  Pallas kernels: 128 us -> 39.8 us
  local copies, waits for them, and re-layouts: 19.4 us -> 3.82 us
  blocking collectives: 33.6 us -> 36.3 us
    pallas_call x9, Pallas kernels: 128 us -> 39.8 us  [run(): pl.pallas_call(kernel, out_shape=outs, in_specs=[vmem] * len(args), out_s...]
    reshape x2 -> x0, local copies, waits for them, and re-layouts: 5.79 us -> none  [the longest x1 4.6 us: body(): g = g.reshape(2, *n3)]
    transpose x1 -> x0, local copies, waits for them, and re-layouts: 4.86 us -> none  [body(): g.reshape(sizes[0], sizes[1], sizes[2], 2, 6, 6, 6)]
    all_to_all x2, blocking collectives: 33.6 us -> 36.3 us  [the longest x1 21.8 us: body(): g = lax.all_to_all(g, ALL, 0, 0, tiled=True)]
    unnamed x20 -> x12, local copies, waits for them, and re-layouts: 6.28 us -> 3.82 us
where the time goes in v2:
time: 119 us
  Pallas kernels  39.8 us (33%)
  blocking collectives  36.3 us (31%)
  starting transfers between devices  23.2 us (19%)
  waiting for transfers between devices  14.8 us (12%)
  local copies, waits for them, and re-layouts  3.82 us (3%)
    pallas_call x9, Pallas kernels, run(): pl.pallas_call(kernel, out_shape=outs, in_specs=[vmem] * len(args), out_s...  39.8 us
    all_to_all x1, blocking collectives, body(): g = lax.all_to_all(g, ALL, 0, 0, tiled=True)  21.8 us
    all_to_all x1, blocking collectives, body(): lax.all_to_all(sums.reshape(count, 1, 128), ALL, 0, 0, tiled=True)  14.5 us
    ppermute x4, starting transfers between devices, ring(): high = lax.ppermute(dn, axis, [(i, (i - 1) % n) for i in range(n)])  13 us
    ppermute x4, waiting for transfers between devices, ring(): low = lax.ppermute(up, axis, [(i, (i + 1) % n) for i in range(n)])  11.4 us
    ppermute x2, starting transfers between devices, swap(): return lax.ppermute(v, 'gx', [(0, 1), (1, 0)])  5.42 us
    ppermute x4, starting transfers between devices, ring(): low = lax.ppermute(up, axis, [(i, (i + 1) % n) for i in range(n)])  4.83 us
    unnamed x12, local copies, waits for them, and re-layouts  3.82 us
  transfers between devices with their start and end apart: 10, of which 6 were waited for; matrix products, arithmetic and copies ran while one was open for 0% of the time, Pallas kernels for 0%

profile of v2, /device:TPU:1, one launch (start us, length us, event | category | flops | bytes accessed | tf_op | source)
XLA Modules:
  0.0 118.6 jit_solution(14947311116163303090)
XLA Ops:
  1.9 1.3 %copy-done.2 = f32[48,48,48]{2,1,0:T(8,128)S(1)} copy-done((f32[48,48,48]{2,1,0:T(8,128)S(1)}, f32[48,48,48]{2,1,0:T(8,128)}, u32[]{:S(2)}) %copy-start.2) | copy-done | bytes 442392
  4.4 2.5 %shard_map.50 = (f32[6,48,128]{2,1,0:T(8,128)S(1)}, f32[6,48,128]{2,1,0:T(8,128)S(1)}) custom-call(f32[48,48,48]{2,1,0:T(8,128)S(1)} %copy-done.2, f32[48,48,48]{2,1,0:T(8,128)S(1)} %copy-done.4, f32[48,48,48]{2,1,0:T(8,128)S(1)} %copy-done), custom_call_target="tpu_custom_call" | custom-call | tf_op jit(solution)/shard_map/pallas_call | solution.py:38
  6.9 2.2 %collective-permute-start = (f32[6,48,128]{2,1,0:T(8,128)S(1)}, f32[6,48,128]{2,1,0:T(8,128)S(1)}, u32[]{:S(2)}, u32[]{:S(2)}) collective-permute-start(f32[6,48,128]{2,1,0:T(8,128)S(1)} %get-tuple-element.26), channel_id=1, source_target_pairs={{0,1},{1,2},{2,3},{3,4},{4,5},{5,6},{6,7},{7,8},{8,9},{9,10},{10,1... | collective-permute-start | bytes 442376 | tf_op jit(solution)/shard_map/ppermute | solution.py:543
  9.1 5.0 %collective-permute-start.1 = (f32[6,48,128]{2,1,0:T(8,128)S(1)}, f32[6,48,128]{2,1,0:T(8,128)S(1)}, u32[]{:S(2)}, u32[]{:S(2)}) collective-permute-start(f32[6,48,128]{2,1,0:T(8,128)S(1)} %get-tuple-element.27), channel_id=1, source_target_pairs={{0,15},{1,0},{2,1},{3,2},{4,3},{5,4},{6,5},{7,6},{8,7},{9,8},{10,9... | collective-permute-start | bytes 442376 | tf_op jit(solution)/shard_map/ppermute | solution.py:544
  14.1 3.5 %collective-permute-done.zl = f32[6,48,128]{2,1,0:T(8,128)S(1)} collective-permute-done((f32[6,48,128]{2,1,0:T(8,128)S(1)}, f32[6,48,128]{2,1,0:T(8,128)S(1)}, u32[]{:S(2)}, u32[]{:S(2)}) %collective-permute-start) | collective-permute-done | bytes 147488 | tf_op jit(solution)/shard_map/ppermute | solution.py:543
  17.6 1.3 %shard_map.51 = (f32[24,16,128]{2,1,0:T(8,128)S(1)}, f32[24,16,128]{2,1,0:T(8,128)S(1)}) custom-call(f32[48,48,48]{2,1,0:T(8,128)S(1)} %copy-done.2, f32[48,48,48]{2,1,0:T(8,128)S(1)} %copy-done.4, f32[48,48,48]{2,1,0:T(8,128)S(1)} %copy-done, f32[6,48,128]{2,1,0:T(8,128)S(1)} %collective-permute-done.zl, f32[6,48,128]{2,1,0:T(8,128)S(1)} %collective-permute-done.1.zh), custom_call_target="tpu_custom_call" | custom-call | tf_op jit(solution)/shard_map/pallas_call | solution.py:38
  18.9 1.3 %collective-permute-start.2 = (f32[24,16,128]{2,1,0:T(8,128)S(1)}, f32[24,16,128]{2,1,0:T(8,128)S(1)}, u32[]{:S(2)}, u32[]{:S(2)}) collective-permute-start(f32[24,16,128]{2,1,0:T(8,128)S(1)} %get-tuple-element.28), channel_id=1, source_target_pairs={{0,16},{16,32},{32,48},{48,0},{1,17},{17,33},{33,49},{49,1},{2,18}... | collective-permute-start | bytes 589832 | tf_op jit(solution)/shard_map/ppermute | solution.py:543
  20.2 1.5 %collective-permute-start.3 = (f32[24,16,128]{2,1,0:T(8,128)S(1)}, f32[24,16,128]{2,1,0:T(8,128)S(1)}, u32[]{:S(2)}, u32[]{:S(2)}) collective-permute-start(f32[24,16,128]{2,1,0:T(8,128)S(1)} %get-tuple-element.29), channel_id=1, source_target_pairs={{0,48},{16,0},{32,16},{48,32},{1,49},{17,1},{33,17},{49,33},{2,50}... | collective-permute-start | bytes 589832 | tf_op jit(solution)/shard_map/ppermute | solution.py:544
  21.6 3.4 %collective-permute-done.2.yl = f32[24,16,128]{2,1,0:T(8,128)S(1)} collective-permute-done((f32[24,16,128]{2,1,0:T(8,128)S(1)}, f32[24,16,128]{2,1,0:T(8,128)S(1)}, u32[]{:S(2)}, u32[]{:S(2)}) %collective-permute-start.2) | collective-permute-done | bytes 196640 | tf_op jit(solution)/shard_map/ppermute | solution.py:543
  25.6 2.7 %collective-permute-start.4 = (f32[6,3,64,128]{3,2,1,0:T(8,128)S(1)}, f32[6,3,64,128]{3,2,1,0:T(8,128)S(1)}, u32[]{:S(2)}, u32[]{:S(2)}) collective-permute-start(f32[6,3,64,128]{3,2,1,0:T(8,128)S(1)} %shard_map.52), channel_id=1, source_target_pairs={{0,64},{64,0},{1,65},{65,1},{2,66},{66,2},{3,67},{67,3},{4,68},{68... | collective-permute-start | bytes 1769480 | tf_op jit(solution)/shard_map/ppermute | solution.py:549
  28.3 1.6 %collective-permute-done.4.xr = f32[6,3,64,128]{3,2,1,0:T(8,128)S(1)} collective-permute-done((f32[6,3,64,128]{3,2,1,0:T(8,128)S(1)}, f32[6,3,64,128]{3,2,1,0:T(8,128)S(1)}, u32[]{:S(2)}, u32[]{:S(2)}) %collective-permute-start.4) | collective-permute-done | bytes 589856 | tf_op jit(solution)/shard_map/ppermute | solution.py:549
  29.9 10.1 %shard_map.53 = (f32[54,64,128]{2,1,0:T(8,128)S(1)}, f32[54,64,128]{2,1,0:T(8,128)S(1)}, f32[56,64,128]{2,1,0:T(8,128)S(1)}, f32[24,24,128]{2,1,0:T(8,128)S(1)},...) custom-call(f32[48,48,48]{2,1,0:T(8,128)S(1)} %copy-done.3, ...), custom_call_target="tpu_custom_call" | custom-call | tf_op jit(solution)/shard_map/pallas_call | solution.py:38
  40.2 5.0 %collective-permute-start.6 = (f32[6,24,128]{2,1,0:T(8,128)S(1)}, f32[6,24,128]{2,1,0:T(8,128)S(1)}, u32[]{:S(2)}, u32[]{:S(2)}) collective-permute-start(f32[6,24,128]{2,1,0:T(8,128)S(1)} %get-tuple-element.33), channel_id=1, source_target_pairs={{0,15},{1,0},{2,1},{3,2},{4,3},{5,4},{6,5},{7,6},{8,7},{9,8},{10,9... | collective-permute-start | bytes 221192 | tf_op jit(solution)/shard_map/ppermute | solution.py:544
  45.1 2.0 %collective-permute-done.5.zl = f32[6,24,128]{2,1,0:T(8,128)S(1)} collective-permute-done((f32[6,24,128]{2,1,0:T(8,128)S(1)}, f32[6,24,128]{2,1,0:T(8,128)S(1)}, u32[]{:S(2)}, u32[]{:S(2)}) %collective-permute-start.5) | collective-permute-done | bytes 73760 | tf_op jit(solution)/shard_map/ppermute | solution.py:543
  48.1 1.3 %collective-permute-start.7 = (f32[12,24,128]{2,1,0:T(8,128)S(1)}, f32[12,24,128]{2,1,0:T(8,128)S(1)}, u32[]{:S(2)}, u32[]{:S(2)}) collective-permute-start(f32[12,24,128]{2,1,0:T(8,128)S(1)} %get-tuple-element.34), channel_id=1, source_target_pairs={{0,16},{16,32},{32,48},{48,0},{1,17},{17,33},{33,49},{49,1},{2,18}... | collective-permute-start | bytes 442376 | tf_op jit(solution)/shard_map/ppermute | solution.py:543
  49.4 1.5 %collective-permute-start.8 = (f32[12,24,128]{2,1,0:T(8,128)S(1)}, f32[12,24,128]{2,1,0:T(8,128)S(1)}, u32[]{:S(2)}, u32[]{:S(2)}) collective-permute-start(f32[12,24,128]{2,1,0:T(8,128)S(1)} %get-tuple-element.35), channel_id=1, source_target_pairs={{0,48},{16,0},{32,16},{48,32},{1,49},{17,1},{33,17},{49,33},{2,50}... | collective-permute-start | bytes 442376 | tf_op jit(solution)/shard_map/ppermute | solution.py:544
  50.9 2.5 %collective-permute-done.7.yl = f32[12,24,128]{2,1,0:T(8,128)S(1)} collective-permute-done((f32[12,24,128]{2,1,0:T(8,128)S(1)}, f32[12,24,128]{2,1,0:T(8,128)S(1)}, u32[]{:S(2)}, u32[]{:S(2)}) %collective-permute-start.7) | collective-permute-done | bytes 147488 | tf_op jit(solution)/shard_map/ppermute | solution.py:543
  54.1 2.7 %collective-permute-start.9 = (f32[12,2,56,128]{3,2,1,0:T(8,128)S(1)}, f32[12,2,56,128]{3,2,1,0:T(8,128)S(1)}, u32[]{:S(2)}, u32[]{:S(2)}) collective-permute-start(f32[12,2,56,128]{3,2,1,0:T(8,128)S(1)} %shard_map.55), channel_id=1, source_target_pairs={{0,64},{64,0},{1,65},{65,1},{2,66},{66,2},{3,67},{67,3},{4,68},{68... | collective-permute-start | bytes 2064392 | tf_op jit(solution)/shard_map/ppermute | solution.py:549
  56.9 1.8 %collective-permute-done.9.xr = f32[12,2,56,128]{3,2,1,0:T(8,128)S(1)} collective-permute-done((f32[12,2,56,128]{3,2,1,0:T(8,128)S(1)}, f32[12,2,56,128]{3,2,1,0:T(8,128)S(1)}, u32[]{:S(2)}, u32[]{:S(2)}) %collective-permute-start.9) | collective-permute-done | bytes 688160 | tf_op jit(solution)/shard_map/ppermute | solution.py:549
  58.7 6.1 %shard_map.56 = (f32[36,56,128]{2,1,0:T(8,128)S(1)}, f32[36,56,128]{2,1,0:T(8,128)S(1)}, f32[38,56,128]{2,1,0:T(8,128)S(1)}, f32[18,32,128]{2,1,0:T(8,128)S(1)},...) custom-call(f32[24,24,128]{2,1,0:T(8,128)S(1)} %get-tuple-element.30.f1, ...), custom_call_target="tpu_custom_call" | custom-call | tf_op jit(solution)/shard_map/pallas_call | solution.py:38
  64.7 21.8 %all_to_all.10.g3 = f32[128,8,128]{2,1,0:T(8,128)S(1)} all-to-all(f32[128,8,128]{2,1,0:T(8,128)S(1)} %get-tuple-element.36), channel_id=1, replica_groups=mesh['gx'=2,'gy'=4,'gz'=16] {'gx','gy','gz'}, dimensions={0} | all-to-all | bytes 1048576 | tf_op jit(solution)/shard_map/all_to_all | solution.py:584
  86.5 15.8 %shard_map.57 = (f32[48,48,48]{2,1,0:T(8,128)S(1)}, f32[48,48,48]{2,1,0:T(8,128)S(1)}, f32[48,48,48]{2,1,0:T(8,128)S(1)}, f32[128,128]{1,0:T(8,128)S(1)}) custom-call(f32[128,8,128]{2,1,0:T(8,128)S(1)} %all_to_all.10.g3, f32[18,32,128]{2,1,0:T(8,128)S(1)} %get-tuple-element.37.f2, f32[18,32,128]{2,1,0:T(8,128)S(1)} %get-tuple-element.38.c2, ...), custom_call_target="tpu_custom_call" | custom-call | tf_op jit(solution)/shard_map/pallas_call | solution.py:38
  102.3 14.5 %all_to_all.11 = f32[128,1,128]{2,1,0:T(1,128)S(1)} all-to-all(f32[128,1,128]{2,1,0:T(1,128)S(1)} %bitcast.5), channel_id=1, replica_groups=mesh['gx'=2,'gy'=4,'gz'=16] {'gx','gy','gz'}, dimensions={0} | all-to-all | bytes 131072 | tf_op jit(solution)/shard_map/all_to_all | solution.py:598
  116.8 1.8 %shard_map.58 = (f32[48,48,48]{2,1,0:T(8,128)}, f32[48,48,48]{2,1,0:T(8,128)}) custom-call(f32[128,128]{1,0:T(8,128)S(1)} %bitcast.4, f32[48,48,48]{2,1,0:T(8,128)S(1)} %copy-done.3, f32[48,48,48]{2,1,0:T(8,128)S(1)} %get-tuple-element.47.z, f32[48,48,48]{2,1,0:T(8,128)S(1)} %get-tuple-element.48.az, f32[48,48,48]{2,1,0:T(8,128)S(1)} %get-tuple-element.49.f), custom_call_target="tpu_custom_call" | custom-call | tf_op jit(solution)/shard_map/pallas_call | solution.py:38
  (19 shorter events, 4.9 us)
Async XLA Ops:
  0.6 1.3 %copy-start = (f32[48,48,48]{2,1,0:T(8,128)S(1)}, f32[48,48,48]{2,1,0:T(8,128)}, u32[]{:S(2)}) copy-start(f32[48,48,48]{2,1,0:T(8,128)} %rea.9) | copy-start | bytes 1327108
  1.9 1.3 %copy-start.2 = (f32[48,48,48]{2,1,0:T(8,128)S(1)}, f32[48,48,48]{2,1,0:T(8,128)}, u32[]{:S(2)}) copy-start(f32[48,48,48]{2,1,0:T(8,128)} %x0.9) | copy-start | bytes 1327108
  3.2 1.3 %copy-start.4 = (f32[48,48,48]{2,1,0:T(8,128)S(1)}, f32[48,48,48]{2,1,0:T(8,128)}, u32[]{:S(2)}) copy-start(f32[48,48,48]{2,1,0:T(8,128)} %b.7) | copy-start | bytes 1327108
  6.9 10.7 %collective-permute-start = (f32[6,48,128]{2,1,0:T(8,128)S(1)}, f32[6,48,128]{2,1,0:T(8,128)S(1)}, u32[]{:S(2)}, u32[]{:S(2)}) collective-permute-start(f32[6,48,128]{2,1,0:T(8,128)S(1)} %get-tuple-element.26), channel_id=1, source_target_pairs={{0,1},{1,2},{2,3},{3,4},{4,5},{5,6},{6,7},{7,8},{8,9},{9,10},{10,1... | collective-permute-start | bytes 442376 | tf_op jit(solution)/shard_map/ppermute | solution.py:543
  9.1 8.5 %collective-permute-start.1 = (f32[6,48,128]{2,1,0:T(8,128)S(1)}, f32[6,48,128]{2,1,0:T(8,128)S(1)}, u32[]{:S(2)}, u32[]{:S(2)}) collective-permute-start(f32[6,48,128]{2,1,0:T(8,128)S(1)} %get-tuple-element.27), channel_id=1, source_target_pairs={{0,15},{1,0},{2,1},{3,2},{4,3},{5,4},{6,5},{7,6},{8,7},{9,8},{10,9... | collective-permute-start | bytes 442376 | tf_op jit(solution)/shard_map/ppermute | solution.py:544
  18.9 6.2 %collective-permute-start.2 = (f32[24,16,128]{2,1,0:T(8,128)S(1)}, f32[24,16,128]{2,1,0:T(8,128)S(1)}, u32[]{:S(2)}, u32[]{:S(2)}) collective-permute-start(f32[24,16,128]{2,1,0:T(8,128)S(1)} %get-tuple-element.28), channel_id=1, source_target_pairs={{0,16},{16,32},{32,48},{48,0},{1,17},{17,33},{33,49},{49,1},{2,18}... | collective-permute-start | bytes 589832 | tf_op jit(solution)/shard_map/ppermute | solution.py:543
  20.2 9.7 %copy-start.1 = (f32[48,48,48]{2,1,0:T(8,128)S(1)}, f32[48,48,48]{2,1,0:T(8,128)}, u32[]{:S(2)}) copy-start(f32[48,48,48]{2,1,0:T(8,128)} %rea.9) | copy-start | bytes 1327108
  20.2 9.7 %copy-start.3 = (f32[48,48,48]{2,1,0:T(8,128)S(1)}, f32[48,48,48]{2,1,0:T(8,128)}, u32[]{:S(2)}) copy-start(f32[48,48,48]{2,1,0:T(8,128)} %x0.9) | copy-start | bytes 1327108
  20.2 9.8 %copy-start.5 = (f32[48,48,48]{2,1,0:T(8,128)S(1)}, f32[48,48,48]{2,1,0:T(8,128)}, u32[]{:S(2)}) copy-start(f32[48,48,48]{2,1,0:T(8,128)} %b.7) | copy-start | bytes 1327108
  20.2 4.9 %collective-permute-start.3 = (f32[24,16,128]{2,1,0:T(8,128)S(1)}, f32[24,16,128]{2,1,0:T(8,128)S(1)}, u32[]{:S(2)}, u32[]{:S(2)}) collective-permute-start(f32[24,16,128]{2,1,0:T(8,128)S(1)} %get-tuple-element.29), channel_id=1, source_target_pairs={{0,48},{16,0},{32,16},{48,32},{1,49},{17,1},{33,17},{49,33},{2,50}... | collective-permute-start | bytes 589832 | tf_op jit(solution)/shard_map/ppermute | solution.py:544
  25.6 4.3 %collective-permute-start.4 = (f32[6,3,64,128]{3,2,1,0:T(8,128)S(1)}, f32[6,3,64,128]{3,2,1,0:T(8,128)S(1)}, u32[]{:S(2)}, u32[]{:S(2)}) collective-permute-start(f32[6,3,64,128]{3,2,1,0:T(8,128)S(1)} %shard_map.52), channel_id=1, source_target_pairs={{0,64},{64,0},{1,65},{65,1},{2,66},{66,2},{3,67},{67,3},{4,68},{68... | collective-permute-start | bytes 1769480 | tf_op jit(solution)/shard_map/ppermute | solution.py:549
  40.1 7.1 %collective-permute-start.5 = (f32[6,24,128]{2,1,0:T(8,128)S(1)}, f32[6,24,128]{2,1,0:T(8,128)S(1)}, u32[]{:S(2)}, u32[]{:S(2)}) collective-permute-start(f32[6,24,128]{2,1,0:T(8,128)S(1)} %get-tuple-element.32), channel_id=1, source_target_pairs={{0,1},{1,2},{2,3},{3,4},{4,5},{5,6},{6,7},{7,8},{8,9},{9,10},{10,1... | collective-permute-start | bytes 221192 | tf_op jit(solution)/shard_map/ppermute | solution.py:543
  40.2 7.0 %collective-permute-start.6 = (f32[6,24,128]{2,1,0:T(8,128)S(1)}, f32[6,24,128]{2,1,0:T(8,128)S(1)}, u32[]{:S(2)}, u32[]{:S(2)}) collective-permute-start(f32[6,24,128]{2,1,0:T(8,128)S(1)} %get-tuple-element.33), channel_id=1, source_target_pairs={{0,15},{1,0},{2,1},{3,2},{4,3},{5,4},{6,5},{7,6},{8,7},{9,8},{10,9... | collective-permute-start | bytes 221192 | tf_op jit(solution)/shard_map/ppermute | solution.py:544
  48.1 5.3 %collective-permute-start.7 = (f32[12,24,128]{2,1,0:T(8,128)S(1)}, f32[12,24,128]{2,1,0:T(8,128)S(1)}, u32[]{:S(2)}, u32[]{:S(2)}) collective-permute-start(f32[12,24,128]{2,1,0:T(8,128)S(1)} %get-tuple-element.34), channel_id=1, source_target_pairs={{0,16},{16,32},{32,48},{48,0},{1,17},{17,33},{33,49},{49,1},{2,18}... | collective-permute-start | bytes 442376 | tf_op jit(solution)/shard_map/ppermute | solution.py:543
  49.4 4.0 %collective-permute-start.8 = (f32[12,24,128]{2,1,0:T(8,128)S(1)}, f32[12,24,128]{2,1,0:T(8,128)S(1)}, u32[]{:S(2)}, u32[]{:S(2)}) collective-permute-start(f32[12,24,128]{2,1,0:T(8,128)S(1)} %get-tuple-element.35), channel_id=1, source_target_pairs={{0,48},{16,0},{32,16},{48,32},{1,49},{17,1},{33,17},{49,33},{2,50}... | collective-permute-start | bytes 442376 | tf_op jit(solution)/shard_map/ppermute | solution.py:544
  54.1 4.5 %collective-permute-start.9 = (f32[12,2,56,128]{3,2,1,0:T(8,128)S(1)}, f32[12,2,56,128]{3,2,1,0:T(8,128)S(1)}, u32[]{:S(2)}, u32[]{:S(2)}) collective-permute-start(f32[12,2,56,128]{3,2,1,0:T(8,128)S(1)} %shard_map.55), channel_id=1, source_target_pairs={{0,64},{64,0},{1,65},{65,1},{2,66},{66,2},{3,67},{67,3},{4,68},{68... | collective-permute-start | bytes 2064392 | tf_op jit(solution)/shard_map/ppermute | solution.py:549

commit v3 on v2

--- a/solution.py
+++ b/solution.py
@@ -180,7 +180,7 @@
     ref[n + 1] = jnp.zeros(ref.shape[1:], F32)
 
 
-def relax(src, dst, f, c, n, factor, u=3):
+def relax(src, dst, f, c, n, factor, u=9):
     def one(x):
         dst[x + 1] = (1.0 - W) * src[x + 1] + c[x] * (f[x] + factor * neighbours(src, x))
 
@@ -378,7 +378,7 @@
         ew2[x + 1] = c * f2[x]
 
     loop(18, second, 6)
-    relax(ew2, e2, f2, c2, 18, 0.0625, 6)
+    relax(ew2, e2, f2, c2, 18, 0.0625, 18)
 
     def left2(x):
         return f2[x] - (0.375 + r2[x]) * e2[x + 1] + 0.0625 * neighbours(e2, x)
@@ -392,7 +392,15 @@
             at = a * 36 + x * 6
             sq[at : at + 6, :] = t3[a, x + shift, 4:10, :]
     t = sq[...].T[0:8]
-    out3[...] = jnp.broadcast_to(t[None], out3.shape)
+    ln = lanes(1)
+    rows = []
+    for u in range(2):
+        for a in range(2):
+            parts = [roll(t, 36 * (w - a), 1)[3 * u + w : 3 * u + w + 1] for w in range(3)]
+            rows.append(jnp.where(ln < 36, parts[0], jnp.where(ln < 72, parts[1], parts[2])))
+    tile = jnp.concatenate(rows + rows, axis=0)
+    n8 = out3.shape[0] // 8
+    out3[...] = jnp.broadcast_to(tile[None], (n8, 8, 128)).reshape(n8 * 8, 128)
 
 
 def sum_all(v):
@@ -410,8 +418,12 @@
             k = bx * ky + by
             if kz * 6 < 128:
                 sq[k, kz * 6 :, :] = jnp.zeros((128 - kz * 6, 128), F32)
-            for bz in range(kz):
-                sq[k, bz * 6 : bz * 6 + 6, :] = g3[k * kz + bz, 0:6, :]
+            got = [g3[pl.ds(k * kz * 4 + r, kz, stride=4), :] for r in range(4)]
+            ln = lanes(kz)
+            for u in range(2):
+                for w in range(3):
+                    f, r = roll(got[2 * u], -36 * w, 1), roll(got[2 * u + 1], 36 - 36 * w, 1)
+                    sq[k, pl.ds(3 * u + w, kz, stride=6), :] = jnp.where(ln < 36, f, r)
             t = sq[k].T
             for x in range(6):
                 f3[bx * 6 + x, by * 6 : by * 6 + 6, :] = t[x * 6 : x * 6 + 6]
@@ -481,8 +493,8 @@
         w3[i, 0:16, :] = jnp.dot(pick, s3[i + 1 + gx * 3], precision=HI, preferred_element_type=F32)
     spread = spread_map(lambda l: gz * 6 + jnp.where(l < 64, l // 2, l // 2 - 64))
     add_refined(w3.at[:, 0:16, :], 9, e2i, e2, w2, spread)
-    relax(e2, s2, f2, c2, 18, 0.0625, 6)
-    relax(s2, e2, f2, c2, 18, 0.0625, 6)
+    relax(e2, s2, f2, c2, 18, 0.0625, 18)
+    relax(s2, e2, f2, c2, 18, 0.0625, 18)
     m = spread_map(lambda l: coarse_lane(l, True))
     add_refined(e2.at[1:19], 18, e1i, e1, w2, m)
     relax(e1, s1, f1, c1, 36, 0.25)
@@ -576,7 +588,7 @@
     p1, q1, p2, q2 = (36, 56, 128), (38, 56, 128), (18, 32, 128), (20, 32, 128)
     f1w, c1w, e1w, f2w, c2w, e2w, g = run(
         k_down1,
-        (sds(*p1), sds(*p1), sds(*q1), sds(*p2), sds(*p2), sds(*q2), sds(count, 8, 128)),
+        (sds(*p1), sds(*p1), sds(*q1), sds(*p2), sds(*p2), sds(*q2), sds(count * 4, 128)),
         (f1, r1, zl, zh, yl, yh, xr),
         [p1, q1, (18, 64, 128), p2, q2, (9, 32, 128), (2, 9, 16, 128), (128, 128)],
         mib=M1,

time: 119 us -> 111 us (0.933)
  Pallas kernels: 39.8 us -> 35 us
  blocking collectives: 36.3 us -> 33.7 us
    pallas_call x9, Pallas kernels: 39.8 us -> 35 us  [run(): pl.pallas_call(kernel, out_shape=outs, in_specs=[vmem] * len(args), out_s...]
    all_to_all x1, blocking collectives: 21.8 us -> 19.4 us  [body(): g = lax.all_to_all(g, ALL, 0, 0, tiled=True)]
where the time goes in v3:
time: 111 us
  Pallas kernels  35 us (32%)
  blocking collectives  33.7 us (30%)
  starting transfers between devices  23.2 us (21%)
  waiting for transfers between devices  14.8 us (13%)
  local copies, waits for them, and re-layouts  3.82 us (3%)
    pallas_call x9, Pallas kernels, run(): pl.pallas_call(kernel, out_shape=outs, in_specs=[vmem] * len(args), out_s...  35 us
    all_to_all x1, blocking collectives, body(): g = lax.all_to_all(g, ALL, 0, 0, tiled=True)  19.4 us
    all_to_all x1, blocking collectives, body(): lax.all_to_all(sums.reshape(count, 1, 128), ALL, 0, 0, tiled=True)  14.3 us
    ppermute x4, starting transfers between devices, ring(): high = lax.ppermute(dn, axis, [(i, (i - 1) % n) for i in range(n)])  13 us
    ppermute x4, waiting for transfers between devices, ring(): low = lax.ppermute(up, axis, [(i, (i + 1) % n) for i in range(n)])  11.4 us
    ppermute x2, starting transfers between devices, swap(): return lax.ppermute(v, 'gx', [(0, 1), (1, 0)])  5.42 us
    ppermute x4, starting transfers between devices, ring(): low = lax.ppermute(up, axis, [(i, (i + 1) % n) for i in range(n)])  4.83 us
    unnamed x12, local copies, waits for them, and re-layouts  3.82 us
  transfers between devices with their start and end apart: 10, of which 6 were waited for; matrix products, arithmetic and copies ran while one was open for 0% of the time, Pallas kernels for 0%

profile of v3, /device:TPU:1, one launch (start us, length us, event | category | flops | bytes accessed | tf_op | source)
XLA Modules:
  0.0 111.2 jit_solution(16599292458974066519)
XLA Ops:
  1.9 1.3 %copy-done.2 = f32[48,48,48]{2,1,0:T(8,128)S(1)} copy-done((f32[48,48,48]{2,1,0:T(8,128)S(1)}, f32[48,48,48]{2,1,0:T(8,128)}, u32[]{:S(2)}) %copy-start.2) | copy-done | bytes 442392
  4.4 2.5 %shard_map.50 = (f32[6,48,128]{2,1,0:T(8,128)S(1)}, f32[6,48,128]{2,1,0:T(8,128)S(1)}) custom-call(f32[48,48,48]{2,1,0:T(8,128)S(1)} %copy-done.2, f32[48,48,48]{2,1,0:T(8,128)S(1)} %copy-done.4, f32[48,48,48]{2,1,0:T(8,128)S(1)} %copy-done), custom_call_target="tpu_custom_call" | custom-call | tf_op jit(solution)/shard_map/pallas_call | solution.py:38
  6.9 2.2 %collective-permute-start = (f32[6,48,128]{2,1,0:T(8,128)S(1)}, f32[6,48,128]{2,1,0:T(8,128)S(1)}, u32[]{:S(2)}, u32[]{:S(2)}) collective-permute-start(f32[6,48,128]{2,1,0:T(8,128)S(1)} %get-tuple-element.26), channel_id=1, source_target_pairs={{0,1},{1,2},{2,3},{3,4},{4,5},{5,6},{6,7},{7,8},{8,9},{9,10},{10,1... | collective-permute-start | bytes 442376 | tf_op jit(solution)/shard_map/ppermute | solution.py:555
  9.1 5.0 %collective-permute-start.1 = (f32[6,48,128]{2,1,0:T(8,128)S(1)}, f32[6,48,128]{2,1,0:T(8,128)S(1)}, u32[]{:S(2)}, u32[]{:S(2)}) collective-permute-start(f32[6,48,128]{2,1,0:T(8,128)S(1)} %get-tuple-element.27), channel_id=1, source_target_pairs={{0,15},{1,0},{2,1},{3,2},{4,3},{5,4},{6,5},{7,6},{8,7},{9,8},{10,9... | collective-permute-start | bytes 442376 | tf_op jit(solution)/shard_map/ppermute | solution.py:556
  14.1 3.5 %collective-permute-done.zl = f32[6,48,128]{2,1,0:T(8,128)S(1)} collective-permute-done((f32[6,48,128]{2,1,0:T(8,128)S(1)}, f32[6,48,128]{2,1,0:T(8,128)S(1)}, u32[]{:S(2)}, u32[]{:S(2)}) %collective-permute-start) | collective-permute-done | bytes 147488 | tf_op jit(solution)/shard_map/ppermute | solution.py:555
  17.6 1.3 %shard_map.51 = (f32[24,16,128]{2,1,0:T(8,128)S(1)}, f32[24,16,128]{2,1,0:T(8,128)S(1)}) custom-call(f32[48,48,48]{2,1,0:T(8,128)S(1)} %copy-done.2, f32[48,48,48]{2,1,0:T(8,128)S(1)} %copy-done.4, f32[48,48,48]{2,1,0:T(8,128)S(1)} %copy-done, f32[6,48,128]{2,1,0:T(8,128)S(1)} %collective-permute-done.zl, f32[6,48,128]{2,1,0:T(8,128)S(1)} %collective-permute-done.1.zh), custom_call_target="tpu_custom_call" | custom-call | tf_op jit(solution)/shard_map/pallas_call | solution.py:38
  18.9 1.3 %collective-permute-start.2 = (f32[24,16,128]{2,1,0:T(8,128)S(1)}, f32[24,16,128]{2,1,0:T(8,128)S(1)}, u32[]{:S(2)}, u32[]{:S(2)}) collective-permute-start(f32[24,16,128]{2,1,0:T(8,128)S(1)} %get-tuple-element.28), channel_id=1, source_target_pairs={{0,16},{16,32},{32,48},{48,0},{1,17},{17,33},{33,49},{49,1},{2,18}... | collective-permute-start | bytes 589832 | tf_op jit(solution)/shard_map/ppermute | solution.py:555
  20.2 1.5 %collective-permute-start.3 = (f32[24,16,128]{2,1,0:T(8,128)S(1)}, f32[24,16,128]{2,1,0:T(8,128)S(1)}, u32[]{:S(2)}, u32[]{:S(2)}) collective-permute-start(f32[24,16,128]{2,1,0:T(8,128)S(1)} %get-tuple-element.29), channel_id=1, source_target_pairs={{0,48},{16,0},{32,16},{48,32},{1,49},{17,1},{33,17},{49,33},{2,50}... | collective-permute-start | bytes 589832 | tf_op jit(solution)/shard_map/ppermute | solution.py:556
  21.6 3.4 %collective-permute-done.2.yl = f32[24,16,128]{2,1,0:T(8,128)S(1)} collective-permute-done((f32[24,16,128]{2,1,0:T(8,128)S(1)}, f32[24,16,128]{2,1,0:T(8,128)S(1)}, u32[]{:S(2)}, u32[]{:S(2)}) %collective-permute-start.2) | collective-permute-done | bytes 196640 | tf_op jit(solution)/shard_map/ppermute | solution.py:555
  25.6 2.7 %collective-permute-start.4 = (f32[6,3,64,128]{3,2,1,0:T(8,128)S(1)}, f32[6,3,64,128]{3,2,1,0:T(8,128)S(1)}, u32[]{:S(2)}, u32[]{:S(2)}) collective-permute-start(f32[6,3,64,128]{3,2,1,0:T(8,128)S(1)} %shard_map.52), channel_id=1, source_target_pairs={{0,64},{64,0},{1,65},{65,1},{2,66},{66,2},{3,67},{67,3},{4,68},{68... | collective-permute-start | bytes 1769480 | tf_op jit(solution)/shard_map/ppermute | solution.py:561
  28.3 1.6 %collective-permute-done.4.xr = f32[6,3,64,128]{3,2,1,0:T(8,128)S(1)} collective-permute-done((f32[6,3,64,128]{3,2,1,0:T(8,128)S(1)}, f32[6,3,64,128]{3,2,1,0:T(8,128)S(1)}, u32[]{:S(2)}, u32[]{:S(2)}) %collective-permute-start.4) | collective-permute-done | bytes 589856 | tf_op jit(solution)/shard_map/ppermute | solution.py:561
  29.9 9.3 %shard_map.53 = (f32[54,64,128]{2,1,0:T(8,128)S(1)}, f32[54,64,128]{2,1,0:T(8,128)S(1)}, f32[56,64,128]{2,1,0:T(8,128)S(1)}, f32[24,24,128]{2,1,0:T(8,128)S(1)},...) custom-call(f32[48,48,48]{2,1,0:T(8,128)S(1)} %copy-done.3, ...), custom_call_target="tpu_custom_call" | custom-call | tf_op jit(solution)/shard_map/pallas_call | solution.py:38
  39.3 5.0 %collective-permute-start.6 = (f32[6,24,128]{2,1,0:T(8,128)S(1)}, f32[6,24,128]{2,1,0:T(8,128)S(1)}, u32[]{:S(2)}, u32[]{:S(2)}) collective-permute-start(f32[6,24,128]{2,1,0:T(8,128)S(1)} %get-tuple-element.33), channel_id=1, source_target_pairs={{0,15},{1,0},{2,1},{3,2},{4,3},{5,4},{6,5},{7,6},{8,7},{9,8},{10,9... | collective-permute-start | bytes 221192 | tf_op jit(solution)/shard_map/ppermute | solution.py:556
  44.3 2.0 %collective-permute-done.5.zl = f32[6,24,128]{2,1,0:T(8,128)S(1)} collective-permute-done((f32[6,24,128]{2,1,0:T(8,128)S(1)}, f32[6,24,128]{2,1,0:T(8,128)S(1)}, u32[]{:S(2)}, u32[]{:S(2)}) %collective-permute-start.5) | collective-permute-done | bytes 73760 | tf_op jit(solution)/shard_map/ppermute | solution.py:555
  47.2 1.3 %collective-permute-start.7 = (f32[12,24,128]{2,1,0:T(8,128)S(1)}, f32[12,24,128]{2,1,0:T(8,128)S(1)}, u32[]{:S(2)}, u32[]{:S(2)}) collective-permute-start(f32[12,24,128]{2,1,0:T(8,128)S(1)} %get-tuple-element.34), channel_id=1, source_target_pairs={{0,16},{16,32},{32,48},{48,0},{1,17},{17,33},{33,49},{49,1},{2,18}... | collective-permute-start | bytes 442376 | tf_op jit(solution)/shard_map/ppermute | solution.py:555
  48.5 1.5 %collective-permute-start.8 = (f32[12,24,128]{2,1,0:T(8,128)S(1)}, f32[12,24,128]{2,1,0:T(8,128)S(1)}, u32[]{:S(2)}, u32[]{:S(2)}) collective-permute-start(f32[12,24,128]{2,1,0:T(8,128)S(1)} %get-tuple-element.35), channel_id=1, source_target_pairs={{0,48},{16,0},{32,16},{48,32},{1,49},{17,1},{33,17},{49,33},{2,50}... | collective-permute-start | bytes 442376 | tf_op jit(solution)/shard_map/ppermute | solution.py:556
  50.1 2.5 %collective-permute-done.7.yl = f32[12,24,128]{2,1,0:T(8,128)S(1)} collective-permute-done((f32[12,24,128]{2,1,0:T(8,128)S(1)}, f32[12,24,128]{2,1,0:T(8,128)S(1)}, u32[]{:S(2)}, u32[]{:S(2)}) %collective-permute-start.7) | collective-permute-done | bytes 147488 | tf_op jit(solution)/shard_map/ppermute | solution.py:555
  53.3 2.7 %collective-permute-start.9 = (f32[12,2,56,128]{3,2,1,0:T(8,128)S(1)}, f32[12,2,56,128]{3,2,1,0:T(8,128)S(1)}, u32[]{:S(2)}, u32[]{:S(2)}) collective-permute-start(f32[12,2,56,128]{3,2,1,0:T(8,128)S(1)} %shard_map.55), channel_id=1, source_target_pairs={{0,64},{64,0},{1,65},{65,1},{2,66},{66,2},{3,67},{67,3},{4,68},{68... | collective-permute-start | bytes 2064392 | tf_op jit(solution)/shard_map/ppermute | solution.py:561
  56.0 1.8 %collective-permute-done.9.xr = f32[12,2,56,128]{3,2,1,0:T(8,128)S(1)} collective-permute-done((f32[12,2,56,128]{3,2,1,0:T(8,128)S(1)}, f32[12,2,56,128]{3,2,1,0:T(8,128)S(1)}, u32[]{:S(2)}, u32[]{:S(2)}) %collective-permute-start.9) | collective-permute-done | bytes 688160 | tf_op jit(solution)/shard_map/ppermute | solution.py:561
  57.8 5.4 %shard_map.56 = (f32[36,56,128]{2,1,0:T(8,128)S(1)}, f32[36,56,128]{2,1,0:T(8,128)S(1)}, f32[38,56,128]{2,1,0:T(8,128)S(1)}, f32[18,32,128]{2,1,0:T(8,128)S(1)},...) custom-call(f32[24,24,128]{2,1,0:T(8,128)S(1)} %get-tuple-element.30.f1, ...), custom_call_target="tpu_custom_call" | custom-call | tf_op jit(solution)/shard_map/pallas_call | solution.py:38
  63.2 19.4 %all_to_all.16 = f32[128,4,128]{2,1,0:T(4,128)S(1)} all-to-all(f32[128,4,128]{2,1,0:T(4,128)S(1)} %bitcast.8), channel_id=1, replica_groups=mesh['gx'=2,'gy'=4,'gz'=16] {'gx','gy','gz'}, dimensions={0} | all-to-all | bytes 524288 | tf_op jit(solution)/shard_map/all_to_all | solution.py:596
  82.6 12.5 %shard_map.57 = (f32[48,48,48]{2,1,0:T(8,128)S(1)}, f32[48,48,48]{2,1,0:T(8,128)S(1)}, f32[48,48,48]{2,1,0:T(8,128)S(1)}, f32[128,128]{1,0:T(8,128)S(1)}) custom-call(f32[512,128]{1,0:T(8,128)S(1)} %bitcast.6, f32[18,32,128]{2,1,0:T(8,128)S(1)} %get-tuple-element.37.f2, f32[18,32,128]{2,1,0:T(8,128)S(1)} %get-tuple-element.38.c2, ...), custom_call_target="tpu_custom_call" | custom-call | tf_op jit(solution)/shard_map/pallas_call | solution.py:38
  95.1 14.3 %all_to_all.17 = f32[128,1,128]{2,1,0:T(1,128)S(1)} all-to-all(f32[128,1,128]{2,1,0:T(1,128)S(1)} %bitcast.9), channel_id=1, replica_groups=mesh['gx'=2,'gy'=4,'gz'=16] {'gx','gy','gz'}, dimensions={0} | all-to-all | bytes 131072 | tf_op jit(solution)/shard_map/all_to_all | solution.py:610
  109.4 1.8 %shard_map.58 = (f32[48,48,48]{2,1,0:T(8,128)}, f32[48,48,48]{2,1,0:T(8,128)}) custom-call(f32[128,128]{1,0:T(8,128)S(1)} %bitcast.7, f32[48,48,48]{2,1,0:T(8,128)S(1)} %copy-done.3, f32[48,48,48]{2,1,0:T(8,128)S(1)} %get-tuple-element.47.z, f32[48,48,48]{2,1,0:T(8,128)S(1)} %get-tuple-element.48.az, f32[48,48,48]{2,1,0:T(8,128)S(1)} %get-tuple-element.49.f), custom_call_target="tpu_custom_call" | custom-call | tf_op jit(solution)/shard_map/pallas_call | solution.py:38
  (19 shorter events, 4.9 us)
Async XLA Ops:
  0.6 1.3 %copy-start = (f32[48,48,48]{2,1,0:T(8,128)S(1)}, f32[48,48,48]{2,1,0:T(8,128)}, u32[]{:S(2)}) copy-start(f32[48,48,48]{2,1,0:T(8,128)} %rea.9) | copy-start | bytes 1327108
  1.9 1.3 %copy-start.2 = (f32[48,48,48]{2,1,0:T(8,128)S(1)}, f32[48,48,48]{2,1,0:T(8,128)}, u32[]{:S(2)}) copy-start(f32[48,48,48]{2,1,0:T(8,128)} %x0.9) | copy-start | bytes 1327108
  3.2 1.3 %copy-start.4 = (f32[48,48,48]{2,1,0:T(8,128)S(1)}, f32[48,48,48]{2,1,0:T(8,128)}, u32[]{:S(2)}) copy-start(f32[48,48,48]{2,1,0:T(8,128)} %b.7) | copy-start | bytes 1327108
  6.9 10.7 %collective-permute-start = (f32[6,48,128]{2,1,0:T(8,128)S(1)}, f32[6,48,128]{2,1,0:T(8,128)S(1)}, u32[]{:S(2)}, u32[]{:S(2)}) collective-permute-start(f32[6,48,128]{2,1,0:T(8,128)S(1)} %get-tuple-element.26), channel_id=1, source_target_pairs={{0,1},{1,2},{2,3},{3,4},{4,5},{5,6},{6,7},{7,8},{8,9},{9,10},{10,1... | collective-permute-start | bytes 442376 | tf_op jit(solution)/shard_map/ppermute | solution.py:555
  9.1 8.5 %collective-permute-start.1 = (f32[6,48,128]{2,1,0:T(8,128)S(1)}, f32[6,48,128]{2,1,0:T(8,128)S(1)}, u32[]{:S(2)}, u32[]{:S(2)}) collective-permute-start(f32[6,48,128]{2,1,0:T(8,128)S(1)} %get-tuple-element.27), channel_id=1, source_target_pairs={{0,15},{1,0},{2,1},{3,2},{4,3},{5,4},{6,5},{7,6},{8,7},{9,8},{10,9... | collective-permute-start | bytes 442376 | tf_op jit(solution)/shard_map/ppermute | solution.py:556
  18.9 6.2 %collective-permute-start.2 = (f32[24,16,128]{2,1,0:T(8,128)S(1)}, f32[24,16,128]{2,1,0:T(8,128)S(1)}, u32[]{:S(2)}, u32[]{:S(2)}) collective-permute-start(f32[24,16,128]{2,1,0:T(8,128)S(1)} %get-tuple-element.28), channel_id=1, source_target_pairs={{0,16},{16,32},{32,48},{48,0},{1,17},{17,33},{33,49},{49,1},{2,18}... | collective-permute-start | bytes 589832 | tf_op jit(solution)/shard_map/ppermute | solution.py:555
  20.2 9.7 %copy-start.1 = (f32[48,48,48]{2,1,0:T(8,128)S(1)}, f32[48,48,48]{2,1,0:T(8,128)}, u32[]{:S(2)}) copy-start(f32[48,48,48]{2,1,0:T(8,128)} %rea.9) | copy-start | bytes 1327108
  20.2 9.7 %copy-start.3 = (f32[48,48,48]{2,1,0:T(8,128)S(1)}, f32[48,48,48]{2,1,0:T(8,128)}, u32[]{:S(2)}) copy-start(f32[48,48,48]{2,1,0:T(8,128)} %x0.9) | copy-start | bytes 1327108
  20.2 9.8 %copy-start.5 = (f32[48,48,48]{2,1,0:T(8,128)S(1)}, f32[48,48,48]{2,1,0:T(8,128)}, u32[]{:S(2)}) copy-start(f32[48,48,48]{2,1,0:T(8,128)} %b.7) | copy-start | bytes 1327108
  20.2 4.9 %collective-permute-start.3 = (f32[24,16,128]{2,1,0:T(8,128)S(1)}, f32[24,16,128]{2,1,0:T(8,128)S(1)}, u32[]{:S(2)}, u32[]{:S(2)}) collective-permute-start(f32[24,16,128]{2,1,0:T(8,128)S(1)} %get-tuple-element.29), channel_id=1, source_target_pairs={{0,48},{16,0},{32,16},{48,32},{1,49},{17,1},{33,17},{49,33},{2,50}... | collective-permute-start | bytes 589832 | tf_op jit(solution)/shard_map/ppermute | solution.py:556
  25.6 4.3 %collective-permute-start.4 = (f32[6,3,64,128]{3,2,1,0:T(8,128)S(1)}, f32[6,3,64,128]{3,2,1,0:T(8,128)S(1)}, u32[]{:S(2)}, u32[]{:S(2)}) collective-permute-start(f32[6,3,64,128]{3,2,1,0:T(8,128)S(1)} %shard_map.52), channel_id=1, source_target_pairs={{0,64},{64,0},{1,65},{65,1},{2,66},{66,2},{3,67},{67,3},{4,68},{68... | collective-permute-start | bytes 1769480 | tf_op jit(solution)/shard_map/ppermute | solution.py:561
  39.2 7.1 %collective-permute-start.5 = (f32[6,24,128]{2,1,0:T(8,128)S(1)}, f32[6,24,128]{2,1,0:T(8,128)S(1)}, u32[]{:S(2)}, u32[]{:S(2)}) collective-permute-start(f32[6,24,128]{2,1,0:T(8,128)S(1)} %get-tuple-element.32), channel_id=1, source_target_pairs={{0,1},{1,2},{2,3},{3,4},{4,5},{5,6},{6,7},{7,8},{8,9},{9,10},{10,1... | collective-permute-start | bytes 221192 | tf_op jit(solution)/shard_map/ppermute | solution.py:555
  39.3 7.0 %collective-permute-start.6 = (f32[6,24,128]{2,1,0:T(8,128)S(1)}, f32[6,24,128]{2,1,0:T(8,128)S(1)}, u32[]{:S(2)}, u32[]{:S(2)}) collective-permute-start(f32[6,24,128]{2,1,0:T(8,128)S(1)} %get-tuple-element.33), channel_id=1, source_target_pairs={{0,15},{1,0},{2,1},{3,2},{4,3},{5,4},{6,5},{7,6},{8,7},{9,8},{10,9... | collective-permute-start | bytes 221192 | tf_op jit(solution)/shard_map/ppermute | solution.py:556
  47.2 5.3 %collective-permute-start.7 = (f32[12,24,128]{2,1,0:T(8,128)S(1)}, f32[12,24,128]{2,1,0:T(8,128)S(1)}, u32[]{:S(2)}, u32[]{:S(2)}) collective-permute-start(f32[12,24,128]{2,1,0:T(8,128)S(1)} %get-tuple-element.34), channel_id=1, source_target_pairs={{0,16},{16,32},{32,48},{48,0},{1,17},{17,33},{33,49},{49,1},{2,18}... | collective-permute-start | bytes 442376 | tf_op jit(solution)/shard_map/ppermute | solution.py:555
  48.5 4.0 %collective-permute-start.8 = (f32[12,24,128]{2,1,0:T(8,128)S(1)}, f32[12,24,128]{2,1,0:T(8,128)S(1)}, u32[]{:S(2)}, u32[]{:S(2)}) collective-permute-start(f32[12,24,128]{2,1,0:T(8,128)S(1)} %get-tuple-element.35), channel_id=1, source_target_pairs={{0,48},{16,0},{32,16},{48,32},{1,49},{17,1},{33,17},{49,33},{2,50}... | collective-permute-start | bytes 442376 | tf_op jit(solution)/shard_map/ppermute | solution.py:556
  53.3 4.5 %collective-permute-start.9 = (f32[12,2,56,128]{3,2,1,0:T(8,128)S(1)}, f32[12,2,56,128]{3,2,1,0:T(8,128)S(1)}, u32[]{:S(2)}, u32[]{:S(2)}) collective-permute-start(f32[12,2,56,128]{3,2,1,0:T(8,128)S(1)} %shard_map.55), channel_id=1, source_target_pairs={{0,64},{64,0},{1,65},{65,1},{2,66},{66,2},{3,67},{67,3},{4,68},{68... | collective-permute-start | bytes 2064392 | tf_op jit(solution)/shard_map/ppermute | solution.py:561

commit v4 on v3

v4 whole, which is shorter than its diff:
```python
import functools
import jax
import jax.numpy as jnp
from jax import lax
from jax.experimental import pallas as pl
from jax.experimental.pallas import tpu as pltpu
from jax.sharding import PartitionSpec as P

W = 6.0 / 7.0
BOTTOM_ITERS = 6
N0 = 48
F32 = jnp.float32
HI = lax.Precision.HIGHEST
M0, M1, M2 = 10, 8, 12


class Spec:
    def __init__(self, n, h, na, R, o, hx, cut, kp, st):
        self.n, self.h, self.na, self.R, self.o, self.hx, self.cut, self.kp, self.st = n, h, na, R, o, hx, cut, kp, st
        self.half = n // 2
        self.zshape = (n // (kp * st), self.half * st, 128)
        self.yrows = -(-na * h // 8) * 8
        self.yshape = (self.half, self.yrows, 128)
        self.xshape = (hx, na, R, 128)
        self.nx = n + hx


L0 = Spec(48, 5, 3, 32, 8, 6, 56, 4, 1)
L1 = Spec(24, 12, 2, 24, 12, 12, 44, 2, 2)


def sds(*shape):
    return jax.ShapeDtypeStruct(shape, F32)


def run(kernel, outs, args, scratch=(), mib=12):
    vmem = pl.BlockSpec(memory_space=pltpu.VMEM)
    return pl.pallas_call(
        kernel,
        out_shape=outs,
        in_specs=[vmem] * len(args),
        out_specs=jax.tree.map(lambda _: vmem, outs),
        scratch_shapes=[pltpu.VMEM(s, F32) for s in scratch],
        compiler_params=pltpu.CompilerParams(vmem_limit_bytes=mib * 1024 * 1024),
    )(*args)


def place():
    return [lax.axis_index(a) for a in ("gx", "gy", "gz")] + [lax.axis_size(a) for a in ("gy", "gz")]


def lanes(rows):
    return lax.broadcasted_iota(jnp.int32, (rows, 128), 1)


def roll(v, shift, axis):
    if isinstance(shift, int):
        shift = shift % v.shape[axis]
        if shift == 0:
            return v
    return pltpu.roll(v, shift, axis)


def loop(n, f, u=1):
    u = max(d for d in range(1, u + 1) if n % d == 0)

    def some(i, c):
        for k in range(u):
            f(i * u + k)
        return c

    lax.fori_loop(0, n // u, some, 0)


def upper(sp, rows):
    l = lanes(rows)
    return (l >= sp.cut) & (l < sp.cut + 64)


def edge(sp, ids):
    _, gy, gz, ny, nz = ids
    high = jnp.where(gz < nz - 1, sp.n + sp.h, sp.n)
    low = jnp.where(gz > 0, 64 - sp.h, 64)
    return high, low, jnp.where(gy > 0, 1.0, 0.0), jnp.where(gy < ny - 1, 1.0, 0.0)


def zpack(sp, own, hi_ref, lo_ref):
    q = lanes(sp.half) % 64

    def tile(g):
        for t in range(sp.st):
            hi = jnp.zeros((sp.half, 128), F32)
            lo = hi
            for k in range(sp.kp):
                for a in range(sp.na):
                    v = own(t * (sp.n // sp.st) + g * sp.kp + k, a)
                    at = sp.h * (k * sp.na + a)
                    here = (q >= at) & (q < at + sp.h)
                    hi = jnp.where(here, roll(v, at - (sp.n - sp.h), 1), hi)
                    lo = jnp.where(here, roll(v, at, 1), lo)
            hi_ref[g, t * sp.half : (t + 1) * sp.half, :] = hi
            lo_ref[g, t * sp.half : (t + 1) * sp.half, :] = lo

    loop(sp.zshape[0], tile, 2)


def merged(sp, own, zl, zh, x, a, b, e, top, bottom):
    per = sp.n // sp.st
    t, y = lax.div(x, per), lax.rem(x, per)
    g, k = lax.div(y, sp.kp), lax.rem(y, sp.kp)
    at = sp.h * (k * sp.na + a)
    if sp.st == 1:
        high, low = zh[g, b:e, :], zl[g, b:e, :]
    else:
        high = jnp.where(t == 0, zh[g, b:e, :], zh[g, sp.half + b : sp.half + e, :])
        low = jnp.where(t == 0, zl[g, b:e, :], zl[g, sp.half + b : sp.half + e, :])
    high = roll(high, lax.rem(sp.n + 128 - at, 128), 1)
    low = roll(low, lax.rem(256 - sp.h - at, 128), 1)
    q = lanes(e - b) % 64
    return jnp.where(q < sp.n, own(x, a)[b:e], jnp.where(q < top, high, jnp.where(q >= bottom, low, 0.0)))


def ypack(sp, own, zl, zh, up_ref, dn_ref):
    h, half = sp.h, sp.half
    up0 = (half - h) // 8 * 8
    dn1 = min(half, -(-h // 8) * 8)
    top, bottom, _, _ = edge(sp, place())

    def pair(p):
        for a in range(sp.na):
            for ref, b, e, s, t, swap in ((up_ref, up0, half, half - h - up0, half - up0, False), (dn_ref, 0, dn1, 0, h, True)):
                even = merged(sp, own, zl, zh, 2 * p, a, b, e, top, bottom)
                odd = roll(merged(sp, own, zl, zh, 2 * p + 1, a, b, e, top, bottom), 64, 1)
                first, second = (odd, even) if swap else (even, odd)
                ref[p, a * h : (a + 1) * h, :] = jnp.where(upper(sp, e - b), first, second)[s:t]
        if sp.yrows > sp.na * h:
            pad = jnp.zeros((sp.yrows - sp.na * h, 128), F32)
            up_ref[p, sp.na * h :, :] = pad
            dn_ref[p, sp.na * h :, :] = pad

    loop(half, pair, 3)


def plane(sp, own, zl, zh, yl, yh, x, a, dst, xw, ends, spare):
    top, bottom, below, above = ends
    h, half = sp.h, sp.half
    m = merged(sp, own, zl, zh, x, a, 0, half, top, bottom)
    p = lax.div(x, 2)
    turn = 64 * (1 - lax.rem(x, 2))
    if sp.o == 8:
        low = roll(roll(yl[p], 8 - h - a * h, 0)[0:8], turn, 1) * below
        high = roll(roll(yh[p], -a * h, 0)[0:8], turn, 1) * above
        lower = jnp.concatenate([low, m], axis=0)
        higher = jnp.concatenate([m, high], axis=0)
        dst[xw] = jnp.where(upper(sp, sp.R), higher, lower)
    else:
        spare[0, 0:h, :] = roll(yl[p, a * h : (a + 1) * h, :], turn, 1) * below
        spare[0, h:, :] = m
        spare[1, 0:half, :] = m
        spare[1, half:, :] = roll(yh[p, a * h : (a + 1) * h, :], turn, 1) * above
        dst[xw] = jnp.where(upper(sp, sp.R), spare[1], spare[0])


def lane_z(sp, l):
    return jnp.where(l < sp.cut, l, jnp.where(l < sp.cut + 64, l - 64, l - 128))


def inside(sp, ids):
    _, gy, gz, ny, nz = ids
    n, h = sp.n, sp.h
    y = lax.broadcasted_iota(jnp.int32, (sp.R, 128), 0) - sp.o + jnp.where(upper(sp, sp.R), sp.R, 0)
    z = lane_z(sp, lanes(sp.R))
    ok = (y >= -h) & (y < n + h) & (z >= -h) & (z < n + h)
    y, z = y + gy * n, z + gz * n
    return ok & (y >= 0) & (y < ny * n) & (z >= 0) & (z < nz * n)


def paired(ref, x):
    c = ref[x + 1]
    R = c.shape[0]
    s = ref[x] + ref[x + 2]
    sub = lax.broadcasted_iota(jnp.int32, (8, 128), 0)
    seam = roll(jnp.where(sub == 0, c[0:8], c[R - 8 : R]), 64, 1)
    up, down = roll(c, R - 1, 0), roll(c, 1, 0)
    up = jnp.concatenate([up[: R - 8], jnp.where(sub == 7, roll(seam, 7, 0), up[R - 8 :])], axis=0)
    down = jnp.concatenate([jnp.where(sub == 0, roll(seam, 1, 0), down[0:8]), down[8:]], axis=0)
    s = s + (up + down)
    return s + (roll(c, 1, 1) + roll(c, 127, 1))


def domain(sp, n, h, r0, R, ids):
    row = lax.broadcasted_iota(jnp.int32, (R, 128), 0) - r0
    ln = lanes(R)
    z = jnp.where(ln < 64, ln, ln - 128)
    gy, gz, ny, nz = ids[1], ids[2], ids[3], ids[4]
    y_at, z_at = row + gy * n, z + gz * n
    ok = (row >= -h) & (row < n + h) & (z >= -h) & (z < n + h)
    return ok & (y_at >= 0) & (y_at < ny * n) & (z_at >= 0) & (z_at < nz * n)


def neighbours(ref, x):
    c = ref[x + 1]
    R = c.shape[0]
    s = ref[x] + ref[x + 2]
    s = s + (roll(c, 1, 0) + roll(c, R - 1, 0))
    return s + (roll(c, 1, 1) + roll(c, 127, 1))


def zero_ends(ref, n):
    ref[0] = jnp.zeros(ref.shape[1:], F32)
    ref[n + 1] = jnp.zeros(ref.shape[1:], F32)


def relax(src, dst, f, c, n, factor, u=9, near=None):
    near = near or neighbours

    def one(x):
        dst[x + 1] = (1.0 - W) * src[x + 1] + c[x] * (f[x] + factor * near(src, x))

    loop(n, one, u)


def lane_map(pick, value, cols=128):
    l = lax.broadcasted_iota(jnp.int32, (256, cols), 0) % 128
    m = lax.broadcasted_iota(jnp.int32, (256, cols), 1)
    return jnp.where(pick(l, m) == m, value, 0.0).astype(jnp.bfloat16)


def spread_map(pick):
    m = lax.broadcasted_iota(jnp.int32, (256, 128), 0) % 128
    l = lax.broadcasted_iota(jnp.int32, (256, 128), 1)
    return jnp.where(pick(l) == m, 1.0, 0.0).astype(jnp.bfloat16)


def floor_half(z):
    return lax.shift_right_arithmetic(z, 1)


def times(v, m):
    big = v.astype(jnp.bfloat16)
    rest = (v - big.astype(F32)).astype(jnp.bfloat16)
    return jnp.dot(jnp.concatenate([big, rest], axis=1), m, preferred_element_type=F32)


def coarsen_planes(pair, n, tmp, acc, rows, u=2):
    half = rows // 2

    def one(x):
        tmp[x, 0:rows, :] = pair(x)
        acc[x, 0:half, :] = tmp[x, pl.ds(0, half, stride=2), :] + tmp[x, pl.ds(1, half, stride=2), :]

    loop(n, one, u)


def flat(ref):
    n, rows, _ = ref.shape
    return ref[...].reshape(n * rows, 128)


def add_refined(wide, n, src, dst, u=3):
    R = dst.shape[1]

    def one(i):
        v = wide[i, 0 : R // 2, :]
        for k in range(2):
            dst[2 * i + 1, pl.ds(k, R // 2, stride=2), :] = v
        t = dst[2 * i + 1]
        dst[2 * i + 1] = src[2 * i + 1] + t
        dst[2 * i + 2] = src[2 * i + 2] + t

    loop(n, one, u)


def k_zpack0(x0, b, rea, hi, lo, own):
    def one(x):
        for a, ref in enumerate((x0, b, rea)):
            own[a, x, :, 0:48] = ref[x, 0:24, :]
            own[a, x, :, 64:112] = ref[x, 24:48, :]

    loop(48, one, 4)
    zpack(L0, lambda x, a: own[a, x], hi, lo)


def k_ypack0(own, zl, zh, up, dn):
    ypack(L0, lambda x, a: own[a, x], zl, zh, up, dn)


def xpack(sp, own, zl, zh, yl, yh, out, spare):
    ids = place()
    ends = edge(sp, ids)
    start = (1 - ids[0]) * (sp.n - sp.hx)

    def one(i):
        for a in range(sp.na):
            plane(sp, own, zl, zh, yl, yh, start + i, a, out.at[i], a, ends, None if spare is None else spare.at[a])

    loop(sp.hx, one, 2)


def k_xpack0(own, zl, zh, yl, yh, out):
    xpack(L0, lambda x, a: own[a, x], zl, zh, yl, yh, out, None)


def assemble(sp, ids, own, zl, zh, yl, yh, xr, dsts, spare, u):
    shift = ids[0] * sp.hx
    ends = edge(sp, ids)

    def some(i):
        for k in range(u):
            x = i * u + k
            for a, (dst, off) in enumerate(dsts):
                plane(sp, own, zl, zh, yl, yh, x, a, dst, x + shift + off, ends, None if spare is None else spare.at[k * sp.na + a])

    loop(sp.n // u, some)
    other = (1 - ids[0]) * sp.n

    def take(i):
        for a, (dst, off) in enumerate(dsts):
            dst[other + i + off] = xr[i, a]

    loop(sp.hx, take, 2)


def own_rows(sp, v):
    return jnp.where(upper(sp, sp.half), v[0 : sp.half], v[sp.o :])


def k_down0(own, zl, zh, yl, yh, xr, f_out, c_out, d_out, e_out, f1, r1, z1h, z1l, xw, bw, rw, ew, tmp, acc):
    ids = place()
    assemble(L0, ids, lambda x, a: own[a, x], zl, zh, yl, yh, xr, ((xw, 1), (bw, 0), (rw, 0)), None, 4)
    n = L0.nx
    ok = inside(L0, ids)
    zero_ends(xw, n)
    zero_ends(ew, n)
    zero_ends(e_out, n)

    def first(x):
        d = 6.0 + rw[x]
        c = jnp.where(ok, W / d, 0.0)
        f = bw[x] - d * xw[x + 1] + paired(xw, x)
        d_out[x] = d
        f_out[x] = f
        c_out[x] = c
        ew[x + 1] = c * f

    loop(n, first, 6)
    relax(ew, e_out, f_out, c_out, n, 1.0, 9, paired)
    shift = ids[0] * L0.hx

    def left(x):
        return own_rows(L0, f_out[x] - d_out[x] * e_out[x + 1] + paired(e_out, x))

    mine = lanes(24) % 64 < 48
    m = lane_map(lambda l, m: jnp.where(l < 64, l // 2, 32 + l // 2), 0.125)
    for ref, pair in (
        (f1, lambda x: left(2 * x + shift) + left(2 * x + shift + 1)),
        (r1, lambda x: own_rows(L0, rw[2 * x + shift] + rw[2 * x + shift + 1])),
    ):
        coarsen_planes(lambda x, pair=pair: jnp.where(mine, pair(x), 0.0), 24, tmp, acc, 24, 4)
        acc[...] = times(flat(acc), m).reshape(24, 16, 128)

        def keep(x, ref=ref):
            ref[x] = acc[x, 0:12, :]

        loop(24, keep, 6)
    both = (f1, r1)
    zpack(L1, lambda x, a: both[a][x], z1h, z1l)


def k_ypack1(f1, r1, zl, zh, up, dn):
    both = (f1, r1)
    ypack(L1, lambda x, a: both[a][x], zl, zh, up, dn)


def k_xpack1(f1, r1, zl, zh, yl, yh, out, spare):
    both = (f1, r1)
    xpack(L1, lambda x, a: both[a][x], zl, zh, yl, yh, out, spare)


def k_down1(f1, r1, zl, zh, yl, yh, xr, fw, cw, e_out, f2, c2, e2, out3, rw, ew, tmp, acc, r2, ew2, tmp2, t3, sq, spare):
    ids = place()
    both = (f1, r1)
    assemble(L1, ids, lambda x, a: both[a][x], zl, zh, yl, yh, xr, ((fw, 0), (rw, 0)), spare, 4)
    n = L1.nx
    ok = inside(L1, ids)
    zero_ends(ew, n)
    zero_ends(e_out, n)

    def first(x):
        c = jnp.where(ok, W / (1.5 + rw[x]), 0.0)
        cw[x] = c
        ew[x + 1] = c * fw[x]

    loop(n, first, 6)
    relax(ew, e_out, fw, cw, n, 0.25, 12, paired)

    def left(x):
        return fw[x] - (1.5 + rw[x]) * e_out[x + 1] + 0.25 * paired(e_out, x)

    def pick(l, m):
        z = lane_z(L1, l)
        up = (l >= L1.cut) & (l < L1.cut + 64)
        good = (z >= -12) & (z < 36) & (up == (m >= 128))
        return jnp.where(good, floor_half(z) + jnp.where(z < 0, 128, 0) + jnp.where(up, 128, 0), -1)

    m = lane_map(pick, 0.125, 256)
    for ref, pair in ((f2, lambda x: left(2 * x) + left(2 * x + 1)), (r2, lambda x: rw[2 * x] + rw[2 * x + 1])):
        coarsen_planes(pair, 18, tmp, acc.at[0], 24, 6)
        v = times(flat(acc.at[0]), m)
        acc[0] = v[:, 0:128].reshape(18, 16, 128)
        acc[1] = v[:, 128:256].reshape(18, 16, 128)

        def keep(x, ref=ref):
            ref[x] = jnp.zeros((32, 128), F32)
            ref[x, 2:14, :] = acc[0, x, 0:12, :]
            ref[x, 14:26, :] = acc[1, x, 0:12, :]

        loop(18, keep, 6)
    ok2 = domain(None, 12, 6, 8, 32, ids)
    zero_ends(ew2, 18)
    zero_ends(e2, 18)

    def second(x):
        c = jnp.where(ok2, W / (0.375 + r2[x]), 0.0)
        c2[x] = c
        ew2[x + 1] = c * f2[x]

    loop(18, second, 6)
    relax(ew2, e2, f2, c2, 18, 0.0625, 18)

    def left2(x):
        return f2[x] - (0.375 + r2[x]) * e2[x + 1] + 0.0625 * neighbours(e2, x)

    m = lane_map(lambda l, m: jnp.where(l < 64, l // 2, l // 2 + 64), 0.125)
    for a, pair in enumerate((lambda x: left2(2 * x) + left2(2 * x + 1), lambda x: r2[2 * x] + r2[2 * x + 1])):
        coarsen_planes(pair, 9, tmp2, t3.at[a], 32, 9)
        t3[a] = times(flat(t3.at[a]), m).reshape(9, 16, 128)
    shift = ids[0] * 3
    sq[...] = jnp.zeros((128, 128), F32)
    for a in range(2):
        for x in range(6):
            at = a * 36 + x * 6
            sq[at : at + 6, :] = t3[a, x + shift, 4:10, :]
    t = sq[...].T[0:8]
    ln = lanes(1)
    rows = []
    for u in range(2):
        for a in range(2):
            parts = [roll(t, 36 * (w - a), 1)[3 * u + w : 3 * u + w + 1] for w in range(3)]
            rows.append(jnp.where(ln < 36, parts[0], jnp.where(ln < 72, parts[1], parts[2])))
    tile = jnp.concatenate(rows + rows, axis=0)
    n8 = out3.shape[0] // 8
    out3[...] = jnp.broadcast_to(tile[None], (n8, 8, 128)).reshape(n8 * 8, 128)


def sum_all(v):
    s = jnp.sum(v, axis=0)
    return jnp.sum(jnp.sum(s, axis=1, keepdims=True), axis=0, keepdims=True)


def coarse_solve(g3, nx, ny, nz, e3, s3, f3, c3, r3, tmp, f4, r4, sq):
    R = f3.shape[1]
    for ref in (f3, r3):
        ref[...] = jnp.zeros(ref.shape, F32)
    kx, ky, kz = nx // 6, ny // 6, nz // 6
    for bx in range(kx):
        for by in range(ky):
            k = bx * ky + by
            if kz * 6 < 128:
                sq[k, kz * 6 :, :] = jnp.zeros((128 - kz * 6, 128), F32)
            got = [g3[pl.ds(k * kz * 4 + r, kz, stride=4), :] for r in range(4)]
            ln = lanes(kz)
            for u in range(2):
                for w in range(3):
                    f, r = roll(got[2 * u], -36 * w, 1), roll(got[2 * u + 1], 36 - 36 * w, 1)
                    sq[k, pl.ds(3 * u + w, kz, stride=6), :] = jnp.where(ln < 36, f, r)
            t = sq[k].T
            for x in range(6):
                f3[bx * 6 + x, by * 6 : by * 6 + 6, :] = t[x * 6 : x * 6 + 6]
                r3[bx * 6 + x, by * 6 : by * 6 + 6, :] = t[36 + x * 6 : 42 + x * 6]
    factor = 0.25**3
    ok = (lax.broadcasted_iota(jnp.int32, (R, 128), 0) < ny) & (lanes(R) < nz)
    for ref in (e3, s3):
        zero_ends(ref, nx)

    def first(x):
        c = jnp.where(ok, W / (6.0 * factor + r3[x]), 0.0)
        c3[x] = c
        s3[x + 1] = c * f3[x]

    loop(nx, first, 6)
    relax(s3, e3, f3, c3, nx, factor, 6)

    def left(x):
        v = f3[x] - (6.0 * factor + r3[x]) * e3[x + 1] + factor * neighbours(e3, x)
        return jnp.where(ok, v, 0.0)

    m = lane_map(lambda l, m: l // 2, 0.125)
    for ref, pair in ((f4, lambda x: left(2 * x) + left(2 * x + 1)), (r4, lambda x: r3[2 * x] + r3[2 * x + 1])):
        coarsen_planes(pair, nx // 2, tmp, ref, R, 6)
        ref[...] = times(flat(ref), m).reshape(ref.shape)
    f4k = 0.25**4
    H = R // 2
    row = lax.broadcasted_iota(jnp.int32, (nx // 2, H, 128), 1)
    lane = lax.broadcasted_iota(jnp.int32, (nx // 2, H, 128), 2)
    within = (row < ny // 2) & (lane < nz // 2)
    diag = 6.0 * f4k + r4[...]
    zero = jnp.zeros((1, H, 128), F32)

    def apply(p):
        s = jnp.concatenate([zero, p[:-1]], axis=0) + jnp.concatenate([p[1:], zero], axis=0)
        s = s + roll(p, 1, 1) + roll(p, H - 1, 1) + roll(p, 1, 2) + roll(p, 127, 2)
        return jnp.where(within, diag * p - f4k * s, 0.0)

    r = jnp.where(within, f4[...], 0.0)
    p = r
    e = jnp.zeros_like(r)
    rr = sum_all(r * r)
    for i in range(BOTTOM_ITERS):
        q = apply(p)
        a = rr / sum_all(p * q)
        e = e + a * p
        if i + 1 < BOTTOM_ITERS:
            r = r - a * q
            new = sum_all(r * r)
            p = r + (new / rr) * p
            rr = new
    f4[...] = times(e.reshape(nx // 2 * H, 128), spread_map(lambda l: l // 2)).reshape(e.shape)
    add_refined(f4, nx // 2, e3, s3, 6)
    relax(s3, e3, f3, c3, nx, factor, 6)
    relax(e3, s3, f3, c3, nx, factor, 6)


def k_up(g3, f2, c2, e2i, f1, c1, e1i, f0, c0, d0, e0i, z_out, az_out, sums,
         e3, s3, f3, c3, r3, tmp3, f4, r4, sq, w3, w2, na, nb, n1, e2, s2, e1, s1, e0, s0):
    gx, gy, gz, sy, sz = place()
    nx, ny, nz = f3.shape[0], sy * 6, sz * 6
    coarse_solve(g3, nx, ny, nz, e3, s3, f3, c3, r3, tmp3, f4, r4, sq)
    for ref, n in ((s2, 18), (s1, 36), (s0, 54), (e2, 18), (e1, 36), (e0, 54)):
        zero_ends(ref, n)
    R3 = s3.shape[1]
    pick = lax.broadcasted_iota(jnp.int32, (16, R3), 1) == lax.broadcasted_iota(jnp.int32, (16, R3), 0) + (gy * 6 - 4)
    pick = pick.astype(F32)
    for i in range(9):
        w3[i] = jnp.dot(pick, s3[i + 1 + gx * 3], precision=HI, preferred_element_type=F32)
    spread = spread_map(lambda l: gz * 6 + jnp.where(l < 64, l // 2, l // 2 - 64))
    w3[...] = times(flat(w3), spread).reshape(9, 16, 128)
    add_refined(w3, 9, e2i, e2, 9)
    relax(e2, s2, f2, c2, 18, 0.0625, 18)
    relax(s2, e2, f2, c2, 18, 0.0625, 18)

    def halves(i):
        na[i] = e2[i + 1, 2:18, :]
        nb[i] = e2[i + 1, 14:30, :]

    loop(18, halves, 6)

    def down(sp, l, want):
        z = lane_z(sp, l)
        up = (l >= sp.cut) & (l < sp.cut + 64)
        good = (z >= -sp.h) & (z < sp.n + sp.h)
        good = good & (up if want else jnp.logical_not(up))
        return jnp.where(good, floor_half(z) + jnp.where(z < 0, 128, 0), -1)

    w2[...] = (
        times(flat(na), spread_map(lambda l: down(L1, l, False))) + times(flat(nb), spread_map(lambda l: down(L1, l, True)))
    ).reshape(18, 16, 128)
    add_refined(w2, 18, e1i, e1, 6)
    relax(e1, s1, f1, c1, 36, 0.25, 12, paired)
    relax(s1, e1, f1, c1, 36, 0.25, 12, paired)

    def near(i):
        v = e1[i + 1 + gx * 9]
        n1[i] = jnp.where(upper(L1, 16), v[0:16], v[8:24])

    loop(27, near, 9)

    def both(l):
        lower, higher = down(L0, l, False), down(L0, l, True)
        return jnp.where(lower >= 0, lower, jnp.where(higher >= 0, (higher + 64) % 128, -1))

    n1[...] = times(flat(n1), spread_map(both)).reshape(27, 16, 128)
    add_refined(n1, 27, e0i, e0, 9)
    relax(e0, s0, f0, c0, 54, 1.0, 9, paired)
    relax(s0, e0, f0, c0, 54, 1.0, 9, paired)
    shift = gx * 6
    mine = lanes(24) % 64 < 48

    def last(x, carry):
        u, v = carry
        w = x + shift
        z = e0[w + 1]
        az = own_rows(L0, d0[w] * z - paired(e0, w))
        z = own_rows(L0, z)
        f = own_rows(L0, f0[w])
        z_out[x] = z
        az_out[x] = az
        return u + jnp.where(mine, f * z, 0.0), v + jnp.where(mine, z * az, 0.0)

    def some(i, carry):
        for k in range(6):
            carry = last(6 * i + k, carry)
        return carry

    zero = jnp.zeros((24, 128), F32)
    u, v = lax.fori_loop(0, 8, some, (zero, zero))

    def total(t):
        return jnp.sum(jnp.sum(t, axis=1, keepdims=True), axis=0, keepdims=True)

    ln = lanes(sums.shape[0])
    sums[...] = jnp.where(ln == 0, total(u), jnp.where(ln == 1, total(v), 0.0))


def k_last(sums, own, z, az, f, sol, res):
    s = jnp.sum(sums[...], axis=0, keepdims=True)
    ln = lanes(1)
    over = jnp.sum(jnp.where(ln == 0, s, 0.0), axis=1, keepdims=True)
    under = jnp.sum(jnp.where(ln == 1, s, 0.0), axis=1, keepdims=True)
    step = over / under
    shift = lax.axis_index("gx") * 6

    def one(x):
        for ref, v in ((sol, own[0, x] + step * z[x]), (res, own_rows(L0, f[x + shift]) - step * az[x])):
            ref[x, 0:24, :] = v[:, 0:48]
            ref[x, 24:48, :] = roll(v, 64, 1)[:, 0:48]

    loop(48, one, 4)


def ring(up, dn, axis):
    n = lax.axis_size(axis)
    low = lax.ppermute(up, axis, [(i, (i + 1) % n) for i in range(n)])
    high = lax.ppermute(dn, axis, [(i, (i - 1) % n) for i in range(n)])
    return low, high


def swap(v):
    return lax.ppermute(v, "gx", [(0, 1), (1, 0)])


def body(b, x0, rea):
    ALL = ("gx", "gy", "gz")
    sizes = [lax.axis_size(a) for a in ALL]
    count = sizes[0] * sizes[1] * sizes[2]
    hi, lo, own = run(k_zpack0, (sds(*L0.zshape), sds(*L0.zshape), sds(3, 48, 24, 128)), (x0, b, rea))
    zl, zh = ring(hi, lo, "gz")
    up, dn = run(k_ypack0, (sds(*L0.yshape),) * 2, (own, zl, zh))
    yl, yh = ring(up, dn, "gy")
    xr = swap(run(k_xpack0, sds(*L0.xshape), (own, zl, zh, yl, yh)))
    p0, q0 = (54, 32, 128), (56, 32, 128)
    f0, c0, d0, e0, f1, r1, z1h, z1l = run(
        k_down0,
        (sds(*p0), sds(*p0), sds(*p0), sds(*q0), sds(24, 12, 128), sds(24, 12, 128), sds(*L1.zshape), sds(*L1.zshape)),
        (own, zl, zh, yl, yh, xr),
        [q0, p0, p0, q0, (24, 24, 128), (24, 16, 128)],
        mib=M0,
    )
    zl, zh = ring(z1h, z1l, "gz")
    up, dn = run(k_ypack1, (sds(*L1.yshape),) * 2, (f1, r1, zl, zh))
    yl, yh = ring(up, dn, "gy")
    xr = swap(run(k_xpack1, sds(*L1.xshape), (f1, r1, zl, zh, yl, yh), [(2, 2, 24, 128)]))
    p1, q1, p2, q2 = (36, 24, 128), (38, 24, 128), (18, 32, 128), (20, 32, 128)
    f1w, c1w, e1w, f2w, c2w, e2w, g = run(
        k_down1,
        (sds(*p1), sds(*p1), sds(*q1), sds(*p2), sds(*p2), sds(*q2), sds(count * 4, 128)),
        (f1, r1, zl, zh, yl, yh, xr),
        [p1, q1, (18, 24, 128), (2, 18, 16, 128), p2, q2, (9, 32, 128), (2, 9, 16, 128), (128, 128), (8, 2, 24, 128)],
        mib=M1,
    )
    g = lax.all_to_all(g, ALL, 0, 0, tiled=True)
    n3 = [6 * s for s in sizes]
    R3 = (n3[1] + 8) // 8 * 8
    if R3 % 16:
        R3 += 8
    p3, q3, p4 = (n3[0], R3, 128), (n3[0] + 2, R3, 128), (n3[0] // 2, R3 // 2, 128)
    z, az, sums = run(
        k_up,
        (sds(48, 24, 128), sds(48, 24, 128), sds(count, 128)),
        (g, f2w, c2w, e2w, f1w, c1w, e1w, f0, c0, d0, e0),
        [q3, q3, p3, p3, p3, (n3[0] // 2, R3, 128), p4, p4, (sizes[0] * sizes[1], 128, 128), (9, 16, 128), (18, 16, 128),
         (18, 16, 128), (18, 16, 128), (27, 16, 128), q2, q2, q1, q1, q0, q0],
        mib=M2,
    )
    sums = lax.all_to_all(sums.reshape(count, 1, 128), ALL, 0, 0, tiled=True).reshape(count, 128)
    return run(k_last, (sds(48, 48, 48), sds(48, 48, 48)), (sums, own, z, az, f0))


def solution(mesh):
    spec = P("gx", "gy", "gz")
    return jax.shard_map(body, mesh=mesh, in_specs=(spec, spec, spec), out_specs=(spec, spec), check_vma=False)
```

time: 111 us -> 103 us (0.928)
  Pallas kernels: 35 us -> 27.7 us
    pallas_call x9, Pallas kernels: 35 us -> 27.7 us  [run(): pl.pallas_call(kernel, out_shape=outs, in_specs=[vmem] * len(args), out_s...]
    unnamed x12 -> x6, local copies, waits for them, and re-layouts: 3.82 us -> 3.8 us
where the time goes in v4:
time: 103 us
  blocking collectives  33.6 us (33%)
  Pallas kernels  27.7 us (27%)
  starting transfers between devices  23.2 us (23%)
  waiting for transfers between devices  13.8 us (13%)
  local copies, waits for them, and re-layouts  3.8 us (4%)
    pallas_call x9, Pallas kernels, run(): pl.pallas_call(kernel, out_shape=outs, in_specs=[vmem] * len(args), out_s...  27.7 us
    all_to_all x1, blocking collectives, body(): g = lax.all_to_all(g, ALL, 0, 0, tiled=True)  19.3 us
    all_to_all x1, blocking collectives, body(): lax.all_to_all(sums.reshape(count, 1, 128), ALL, 0, 0, tiled=True)  14.3 us
    ppermute x4, starting transfers between devices, ring(): high = lax.ppermute(dn, axis, [(i, (i - 1) % n) for i in range(n)])  13 us
    ppermute x4, waiting for transfers between devices, ring(): low = lax.ppermute(up, axis, [(i, (i + 1) % n) for i in range(n)])  11.4 us
    ppermute x2, starting transfers between devices, swap(): return lax.ppermute(v, 'gx', [(0, 1), (1, 0)])  5.43 us
    ppermute x4, starting transfers between devices, ring(): low = lax.ppermute(up, axis, [(i, (i + 1) % n) for i in range(n)])  4.83 us
    unnamed x6, local copies, waits for them, and re-layouts  3.8 us
  transfers between devices with their start and end apart: 10, of which 6 were waited for; matrix products, arithmetic and copies ran while one was open for 0% of the time, Pallas kernels for 0%

profile of v4, /device:TPU:1, one launch (start us, length us, event | category | flops | bytes accessed | tf_op | source)
XLA Modules:
  0.0 102.9 jit_solution(11452167628729966288)
XLA Ops:
  0.6 1.3 %copy-done = f32[48,48,48]{2,1,0:T(8,128)S(1)} copy-done((f32[48,48,48]{2,1,0:T(8,128)S(1)}, f32[48,48,48]{2,1,0:T(8,128)}, u32[]{:S(2)}) %copy-start) | copy-done | bytes 442392
  1.9 1.3 %copy-done.1 = f32[48,48,48]{2,1,0:T(8,128)S(1)} copy-done((f32[48,48,48]{2,1,0:T(8,128)S(1)}, f32[48,48,48]{2,1,0:T(8,128)}, u32[]{:S(2)}) %copy-start.1) | copy-done | bytes 442392
  3.2 1.3 %copy-done.2 = f32[48,48,48]{2,1,0:T(8,128)S(1)} copy-done((f32[48,48,48]{2,1,0:T(8,128)S(1)}, f32[48,48,48]{2,1,0:T(8,128)}, u32[]{:S(2)}) %copy-start.2) | copy-done | bytes 442392
  4.4 2.5 %shard_map.50 = (f32[12,24,128]{2,1,0:T(8,128)S(1)}, f32[12,24,128]{2,1,0:T(8,128)S(1)}, f32[3,48,24,128]{3,2,1,0:T(8,128)S(1)}) custom-call(f32[48,48,48]{2,1,0:T(8,128)S(1)} %copy-done, f32[48,48,48]{2,1,0:T(8,128)S(1)} %copy-done.1, f32[48,48,48]{2,1,0:T(8,128)S(1)} %copy-done.2), custom_call_target="tpu_custom_call" | custom-call | tf_op jit(solution)/shard_map/pallas_call | solution.py:38
  7.0 2.2 %collective-permute-start = (f32[12,24,128]{2,1,0:T(8,128)S(1)}, f32[12,24,128]{2,1,0:T(8,128)S(1)}, u32[]{:S(2)}, u32[]{:S(2)}) collective-permute-start(f32[12,24,128]{2,1,0:T(8,128)S(1)} %get-tuple-element.28), channel_id=1, source_target_pairs={{0,1},{1,2},{2,3},{3,4},{4,5},{5,6},{6,7},{7,8},{8,9},{9,10},{10,1... | collective-permute-start | bytes 442376 | tf_op jit(solution)/shard_map/ppermute | solution.py:633
  9.2 5.0 %collective-permute-start.1 = (f32[12,24,128]{2,1,0:T(8,128)S(1)}, f32[12,24,128]{2,1,0:T(8,128)S(1)}, u32[]{:S(2)}, u32[]{:S(2)}) collective-permute-start(f32[12,24,128]{2,1,0:T(8,128)S(1)} %get-tuple-element.29), channel_id=1, source_target_pairs={{0,15},{1,0},{2,1},{3,2},{4,3},{5,4},{6,5},{7,6},{8,7},{9,8},{10,9... | collective-permute-start | bytes 442376 | tf_op jit(solution)/shard_map/ppermute | solution.py:634
  14.2 3.5 %collective-permute-done.zl = f32[12,24,128]{2,1,0:T(8,128)S(1)} collective-permute-done((f32[12,24,128]{2,1,0:T(8,128)S(1)}, f32[12,24,128]{2,1,0:T(8,128)S(1)}, u32[]{:S(2)}, u32[]{:S(2)}) %collective-permute-start) | collective-permute-done | bytes 147488 | tf_op jit(solution)/shard_map/ppermute | solution.py:633
  17.7 1.6 %shard_map.51 = (f32[24,16,128]{2,1,0:T(8,128)S(1)}, f32[24,16,128]{2,1,0:T(8,128)S(1)}) custom-call(f32[3,48,24,128]{3,2,1,0:T(8,128)S(1)} %get-tuple-element.27.own, f32[12,24,128]{2,1,0:T(8,128)S(1)} %collective-permute-done.zl, f32[12,24,128]{2,1,0:T(8,128)S(1)} %collective-permute-done.1.zh), custom_call_target="tpu_custom_call" | custom-call | tf_op jit(solution)/shard_map/pallas_call | solution.py:38
  19.3 1.3 %collective-permute-start.2 = (f32[24,16,128]{2,1,0:T(8,128)S(1)}, f32[24,16,128]{2,1,0:T(8,128)S(1)}, u32[]{:S(2)}, u32[]{:S(2)}) collective-permute-start(f32[24,16,128]{2,1,0:T(8,128)S(1)} %get-tuple-element.30), channel_id=1, source_target_pairs={{0,16},{16,32},{32,48},{48,0},{1,17},{17,33},{33,49},{49,1},{2,18}... | collective-permute-start | bytes 589832 | tf_op jit(solution)/shard_map/ppermute | solution.py:633
  20.6 1.5 %collective-permute-start.3 = (f32[24,16,128]{2,1,0:T(8,128)S(1)}, f32[24,16,128]{2,1,0:T(8,128)S(1)}, u32[]{:S(2)}, u32[]{:S(2)}) collective-permute-start(f32[24,16,128]{2,1,0:T(8,128)S(1)} %get-tuple-element.31), channel_id=1, source_target_pairs={{0,48},{16,0},{32,16},{48,32},{1,49},{17,1},{33,17},{49,33},{2,50}... | collective-permute-start | bytes 589832 | tf_op jit(solution)/shard_map/ppermute | solution.py:634
  22.1 3.4 %collective-permute-done.2.yl = f32[24,16,128]{2,1,0:T(8,128)S(1)} collective-permute-done((f32[24,16,128]{2,1,0:T(8,128)S(1)}, f32[24,16,128]{2,1,0:T(8,128)S(1)}, u32[]{:S(2)}, u32[]{:S(2)}) %collective-permute-start.2) | collective-permute-done | bytes 196640 | tf_op jit(solution)/shard_map/ppermute | solution.py:633
  25.9 2.7 %collective-permute-start.4 = (f32[6,3,32,128]{3,2,1,0:T(8,128)S(1)}, f32[6,3,32,128]{3,2,1,0:T(8,128)S(1)}, u32[]{:S(2)}, u32[]{:S(2)}) collective-permute-start(f32[6,3,32,128]{3,2,1,0:T(8,128)S(1)} %shard_map.52), channel_id=1, source_target_pairs={{0,64},{64,0},{1,65},{65,1},{2,66},{66,2},{3,67},{67,3},{4,68},{68... | collective-permute-start | bytes 884744 | tf_op jit(solution)/shard_map/ppermute | solution.py:639
  29.8 6.3 %shard_map.53 = (f32[54,32,128]{2,1,0:T(8,128)S(1)}, f32[54,32,128]{2,1,0:T(8,128)S(1)}, f32[54,32,128]{2,1,0:T(8,128)S(1)}, f32[56,32,128]{2,1,0:T(8,128)S(1)},...) custom-call(f32[3,48,24,128]{3,2,1,0:T(8,128)S(1)} %get-tuple-elemen, ...), custom_call_target="tpu_custom_call" | custom-call | tf_op jit(solution)/shard_map/pallas_call | solution.py:38
  36.2 5.0 %collective-permute-start.6 = (f32[6,24,128]{2,1,0:T(8,128)S(1)}, f32[6,24,128]{2,1,0:T(8,128)S(1)}, u32[]{:S(2)}, u32[]{:S(2)}) collective-permute-start(f32[6,24,128]{2,1,0:T(8,128)S(1)} %get-tuple-element.35), channel_id=1, source_target_pairs={{0,15},{1,0},{2,1},{3,2},{4,3},{5,4},{6,5},{7,6},{8,7},{9,8},{10,9... | collective-permute-start | bytes 221192 | tf_op jit(solution)/shard_map/ppermute | solution.py:634
  41.2 2.0 %collective-permute-done.5.zl = f32[6,24,128]{2,1,0:T(8,128)S(1)} collective-permute-done((f32[6,24,128]{2,1,0:T(8,128)S(1)}, f32[6,24,128]{2,1,0:T(8,128)S(1)}, u32[]{:S(2)}, u32[]{:S(2)}) %collective-permute-start.5) | collective-permute-done | bytes 73760 | tf_op jit(solution)/shard_map/ppermute | solution.py:633
  44.2 1.3 %collective-permute-start.7 = (f32[12,24,128]{2,1,0:T(8,128)S(1)}, f32[12,24,128]{2,1,0:T(8,128)S(1)}, u32[]{:S(2)}, u32[]{:S(2)}) collective-permute-start(f32[12,24,128]{2,1,0:T(8,128)S(1)} %get-tuple-element.36), channel_id=1, source_target_pairs={{0,16},{16,32},{32,48},{48,0},{1,17},{17,33},{33,49},{49,1},{2,18}... | collective-permute-start | bytes 442376 | tf_op jit(solution)/shard_map/ppermute | solution.py:633
  45.5 1.5 %collective-permute-start.8 = (f32[12,24,128]{2,1,0:T(8,128)S(1)}, f32[12,24,128]{2,1,0:T(8,128)S(1)}, u32[]{:S(2)}, u32[]{:S(2)}) collective-permute-start(f32[12,24,128]{2,1,0:T(8,128)S(1)} %get-tuple-element.37), channel_id=1, source_target_pairs={{0,48},{16,0},{32,16},{48,32},{1,49},{17,1},{33,17},{49,33},{2,50}... | collective-permute-start | bytes 442376 | tf_op jit(solution)/shard_map/ppermute | solution.py:634
  47.0 2.5 %collective-permute-done.7.yl = f32[12,24,128]{2,1,0:T(8,128)S(1)} collective-permute-done((f32[12,24,128]{2,1,0:T(8,128)S(1)}, f32[12,24,128]{2,1,0:T(8,128)S(1)}, u32[]{:S(2)}, u32[]{:S(2)}) %collective-permute-start.7) | collective-permute-done | bytes 147488 | tf_op jit(solution)/shard_map/ppermute | solution.py:633
  50.2 2.8 %collective-permute-start.9 = (f32[12,2,24,128]{3,2,1,0:T(8,128)S(1)}, f32[12,2,24,128]{3,2,1,0:T(8,128)S(1)}, u32[]{:S(2)}, u32[]{:S(2)}) collective-permute-start(f32[12,2,24,128]{3,2,1,0:T(8,128)S(1)} %shard_map.55), channel_id=1, source_target_pairs={{0,64},{64,0},{1,65},{65,1},{2,66},{66,2},{3,67},{67,3},{4,68},{68... | collective-permute-start | bytes 884744 | tf_op jit(solution)/shard_map/ppermute | solution.py:639
  54.2 3.7 %shard_map.56 = (f32[36,24,128]{2,1,0:T(8,128)S(1)}, f32[36,24,128]{2,1,0:T(8,128)S(1)}, f32[38,24,128]{2,1,0:T(8,128)S(1)}, f32[18,32,128]{2,1,0:T(8,128)S(1)},...) custom-call(f32[24,12,128]{2,1,0:T(8,128)S(1)} %get-tuple-element.32.f1, ...), custom_call_target="tpu_custom_call" | custom-call | tf_op jit(solution)/shard_map/pallas_call | solution.py:38
  57.9 19.3 %all_to_all.16 = f32[128,4,128]{2,1,0:T(4,128)S(1)} all-to-all(f32[128,4,128]{2,1,0:T(4,128)S(1)} %bitcast.8), channel_id=1, replica_groups=mesh['gx'=2,'gy'=4,'gz'=16] {'gx','gy','gz'}, dimensions={0} | all-to-all | bytes 524288 | tf_op jit(solution)/shard_map/all_to_all | solution.py:671
  77.2 8.7 %shard_map.57 = (f32[48,24,128]{2,1,0:T(8,128)S(1)}, f32[48,24,128]{2,1,0:T(8,128)S(1)}, f32[128,128]{1,0:T(8,128)S(1)}) custom-call(f32[512,128]{1,0:T(8,128)S(1)} %bitcast.6, f32[18,32,128]{2,1,0:T(8,128)S(1)} %get-tuple-element.39.f2, f32[18,32,128]{2,1,0:T(8,128)S(1)} %get-tuple-element.40.c2, f32[20,32,128]{2,1,0:T(8,128)S(1)} %get-tuple-element.41.e2i, ...), custom_call_target="tpu_custom_call" | custom-call | tf_op jit(solution)/shard_map/pallas_call | solution.py:38
  86.0 14.3 %all_to_all.17 = f32[128,1,128]{2,1,0:T(1,128)S(1)} all-to-all(f32[128,1,128]{2,1,0:T(1,128)S(1)} %bitcast.9), channel_id=1, replica_groups=mesh['gx'=2,'gy'=4,'gz'=16] {'gx','gy','gz'}, dimensions={0} | all-to-all | bytes 131072 | tf_op jit(solution)/shard_map/all_to_all | solution.py:685
  100.3 2.7 %shard_map.58 = (f32[48,48,48]{2,1,0:T(8,128)}, f32[48,48,48]{2,1,0:T(8,128)}) custom-call(f32[128,128]{1,0:T(8,128)S(1)} %bitcast.7, f32[3,48,24,128]{3,2,1,0:T(8,128)S(1)} %get-tuple-element.27.own, f32[48,24,128]{2,1,0:T(8,128)S(1)} %get-tuple-element.50.z, f32[48,24,128]{2,1,0:T(8,128)S(1)} %get-tuple-element.51.az, ...), custom_call_target="tpu_custom_call" | custom-call | tf_op jit(solution)/shard_map/pallas_call | solution.py:38
  (13 shorter events, 4.6 us)
Async XLA Ops:
  0.6 1.3 %copy-start = (f32[48,48,48]{2,1,0:T(8,128)S(1)}, f32[48,48,48]{2,1,0:T(8,128)}, u32[]{:S(2)}) copy-start(f32[48,48,48]{2,1,0:T(8,128)} %x0.1) | copy-start | bytes 1327108
  1.9 1.3 %copy-start.1 = (f32[48,48,48]{2,1,0:T(8,128)S(1)}, f32[48,48,48]{2,1,0:T(8,128)}, u32[]{:S(2)}) copy-start(f32[48,48,48]{2,1,0:T(8,128)} %b.1) | copy-start | bytes 1327108
  3.2 1.3 %copy-start.2 = (f32[48,48,48]{2,1,0:T(8,128)S(1)}, f32[48,48,48]{2,1,0:T(8,128)}, u32[]{:S(2)}) copy-start(f32[48,48,48]{2,1,0:T(8,128)} %rea.1) | copy-start | bytes 1327108
  7.0 10.7 %collective-permute-start = (f32[12,24,128]{2,1,0:T(8,128)S(1)}, f32[12,24,128]{2,1,0:T(8,128)S(1)}, u32[]{:S(2)}, u32[]{:S(2)}) collective-permute-start(f32[12,24,128]{2,1,0:T(8,128)S(1)} %get-tuple-element.28), channel_id=1, source_target_pairs={{0,1},{1,2},{2,3},{3,4},{4,5},{5,6},{6,7},{7,8},{8,9},{9,10},{10,1... | collective-permute-start | bytes 442376 | tf_op jit(solution)/shard_map/ppermute | solution.py:633
  9.2 8.5 %collective-permute-start.1 = (f32[12,24,128]{2,1,0:T(8,128)S(1)}, f32[12,24,128]{2,1,0:T(8,128)S(1)}, u32[]{:S(2)}, u32[]{:S(2)}) collective-permute-start(f32[12,24,128]{2,1,0:T(8,128)S(1)} %get-tuple-element.29), channel_id=1, source_target_pairs={{0,15},{1,0},{2,1},{3,2},{4,3},{5,4},{6,5},{7,6},{8,7},{9,8},{10,9... | collective-permute-start | bytes 442376 | tf_op jit(solution)/shard_map/ppermute | solution.py:634
  19.3 6.2 %collective-permute-start.2 = (f32[24,16,128]{2,1,0:T(8,128)S(1)}, f32[24,16,128]{2,1,0:T(8,128)S(1)}, u32[]{:S(2)}, u32[]{:S(2)}) collective-permute-start(f32[24,16,128]{2,1,0:T(8,128)S(1)} %get-tuple-element.30), channel_id=1, source_target_pairs={{0,16},{16,32},{32,48},{48,0},{1,17},{17,33},{33,49},{49,1},{2,18}... | collective-permute-start | bytes 589832 | tf_op jit(solution)/shard_map/ppermute | solution.py:633
  20.6 4.9 %collective-permute-start.3 = (f32[24,16,128]{2,1,0:T(8,128)S(1)}, f32[24,16,128]{2,1,0:T(8,128)S(1)}, u32[]{:S(2)}, u32[]{:S(2)}) collective-permute-start(f32[24,16,128]{2,1,0:T(8,128)S(1)} %get-tuple-element.31), channel_id=1, source_target_pairs={{0,48},{16,0},{32,16},{48,32},{1,49},{17,1},{33,17},{49,33},{2,50}... | collective-permute-start | bytes 589832 | tf_op jit(solution)/shard_map/ppermute | solution.py:634
  25.9 3.9 %collective-permute-start.4 = (f32[6,3,32,128]{3,2,1,0:T(8,128)S(1)}, f32[6,3,32,128]{3,2,1,0:T(8,128)S(1)}, u32[]{:S(2)}, u32[]{:S(2)}) collective-permute-start(f32[6,3,32,128]{3,2,1,0:T(8,128)S(1)} %shard_map.52), channel_id=1, source_target_pairs={{0,64},{64,0},{1,65},{65,1},{2,66},{66,2},{3,67},{67,3},{4,68},{68... | collective-permute-start | bytes 884744 | tf_op jit(solution)/shard_map/ppermute | solution.py:639
  36.1 7.1 %collective-permute-start.5 = (f32[6,24,128]{2,1,0:T(8,128)S(1)}, f32[6,24,128]{2,1,0:T(8,128)S(1)}, u32[]{:S(2)}, u32[]{:S(2)}) collective-permute-start(f32[6,24,128]{2,1,0:T(8,128)S(1)} %get-tuple-element.34), channel_id=1, source_target_pairs={{0,1},{1,2},{2,3},{3,4},{4,5},{5,6},{6,7},{7,8},{8,9},{9,10},{10,1... | collective-permute-start | bytes 221192 | tf_op jit(solution)/shard_map/ppermute | solution.py:633
  36.2 7.0 %collective-permute-start.6 = (f32[6,24,128]{2,1,0:T(8,128)S(1)}, f32[6,24,128]{2,1,0:T(8,128)S(1)}, u32[]{:S(2)}, u32[]{:S(2)}) collective-permute-start(f32[6,24,128]{2,1,0:T(8,128)S(1)} %get-tuple-element.35), channel_id=1, source_target_pairs={{0,15},{1,0},{2,1},{3,2},{4,3},{5,4},{6,5},{7,6},{8,7},{9,8},{10,9... | collective-permute-start | bytes 221192 | tf_op jit(solution)/shard_map/ppermute | solution.py:634
  44.2 5.3 %collective-permute-start.7 = (f32[12,24,128]{2,1,0:T(8,128)S(1)}, f32[12,24,128]{2,1,0:T(8,128)S(1)}, u32[]{:S(2)}, u32[]{:S(2)}) collective-permute-start(f32[12,24,128]{2,1,0:T(8,128)S(1)} %get-tuple-element.36), channel_id=1, source_target_pairs={{0,16},{16,32},{32,48},{48,0},{1,17},{17,33},{33,49},{49,1},{2,18}... | collective-permute-start | bytes 442376 | tf_op jit(solution)/shard_map/ppermute | solution.py:633
  45.5 4.0 %collective-permute-start.8 = (f32[12,24,128]{2,1,0:T(8,128)S(1)}, f32[12,24,128]{2,1,0:T(8,128)S(1)}, u32[]{:S(2)}, u32[]{:S(2)}) collective-permute-start(f32[12,24,128]{2,1,0:T(8,128)S(1)} %get-tuple-element.37), channel_id=1, source_target_pairs={{0,48},{16,0},{32,16},{48,32},{1,49},{17,1},{33,17},{49,33},{2,50}... | collective-permute-start | bytes 442376 | tf_op jit(solution)/shard_map/ppermute | solution.py:634
  50.2 4.0 %collective-permute-start.9 = (f32[12,2,24,128]{3,2,1,0:T(8,128)S(1)}, f32[12,2,24,128]{3,2,1,0:T(8,128)S(1)}, u32[]{:S(2)}, u32[]{:S(2)}) collective-permute-start(f32[12,2,24,128]{3,2,1,0:T(8,128)S(1)} %shard_map.55), channel_id=1, source_target_pairs={{0,64},{64,0},{1,65},{65,1},{2,66},{66,2},{3,67},{67,3},{4,68},{68... | collective-permute-start | bytes 884744 | tf_op jit(solution)/shard_map/ppermute | solution.py:639

commit v5 on v4

--- a/solution.py
+++ b/solution.py
@@ -33,14 +33,15 @@
     return jax.ShapeDtypeStruct(shape, F32)
 
 
-def run(kernel, outs, args, scratch=(), mib=12):
+def run(kernel, outs, args, scratch=(), mib=12, far_in=False, far_out=False):
     vmem = pl.BlockSpec(memory_space=pltpu.VMEM)
+    hbm = pl.BlockSpec(memory_space=pltpu.HBM)
     return pl.pallas_call(
         kernel,
         out_shape=outs,
-        in_specs=[vmem] * len(args),
-        out_specs=jax.tree.map(lambda _: vmem, outs),
-        scratch_shapes=[pltpu.VMEM(s, F32) for s in scratch],
+        in_specs=[hbm if far_in else vmem] * len(args),
+        out_specs=jax.tree.map(lambda _: hbm if far_out else vmem, outs),
+        scratch_shapes=[pltpu.VMEM(s, F32) if isinstance(s, tuple) else s for s in scratch],
         compiler_params=pltpu.CompilerParams(vmem_limit_bytes=mib * 1024 * 1024),
     )(*args)
 
@@ -84,24 +85,20 @@
     return high, low, jnp.where(gy > 0, 1.0, 0.0), jnp.where(gy < ny - 1, 1.0, 0.0)
 
 
-def zpack(sp, own, hi_ref, lo_ref):
+def ztile(sp, own, hi_ref, lo_ref, g):
     q = lanes(sp.half) % 64
-
-    def tile(g):
-        for t in range(sp.st):
-            hi = jnp.zeros((sp.half, 128), F32)
-            lo = hi
-            for k in range(sp.kp):
-                for a in range(sp.na):
-                    v = own(t * (sp.n // sp.st) + g * sp.kp + k, a)
-                    at = sp.h * (k * sp.na + a)
-                    here = (q >= at) & (q < at + sp.h)
-                    hi = jnp.where(here, roll(v, at - (sp.n - sp.h), 1), hi)
-                    lo = jnp.where(here, roll(v, at, 1), lo)
-            hi_ref[g, t * sp.half : (t + 1) * sp.half, :] = hi
-            lo_ref[g, t * sp.half : (t + 1) * sp.half, :] = lo
-
-    loop(sp.zshape[0], tile, 2)
+    for t in range(sp.st):
+        hi = jnp.zeros((sp.half, 128), F32)
+        lo = hi
+        for k in range(sp.kp):
+            for a in range(sp.na):
+                v = own(t * (sp.n // sp.st) + g * sp.kp + k, a)
+                at = sp.h * (k * sp.na + a)
+                here = (q >= at) & (q < at + sp.h)
+                hi = jnp.where(here, roll(v, at - (sp.n - sp.h), 1), hi)
+                lo = jnp.where(here, roll(v, at, 1), lo)
+        hi_ref[g, t * sp.half : (t + 1) * sp.half, :] = hi
+        lo_ref[g, t * sp.half : (t + 1) * sp.half, :] = lo
 
 
 def merged(sp, own, zl, zh, x, a, b, e, top, bottom):
@@ -271,14 +268,28 @@
     loop(n, one, u)
 
 
-def k_zpack0(x0, b, rea, hi, lo, own):
-    def one(x):
-        for a, ref in enumerate((x0, b, rea)):
-            own[a, x, :, 0:48] = ref[x, 0:24, :]
-            own[a, x, :, 64:112] = ref[x, 24:48, :]
-
-    loop(48, one, 4)
-    zpack(L0, lambda x, a: own[a, x], hi, lo)
+def k_zpack0(x0, b, rea, hi, lo, own, raw, sems):
+    def copy(a, ref, i):
+        part = pl.ds(i * 8, 8)
+        return pltpu.make_async_copy(ref.at[part], raw.at[a, part], sems.at[a, i])
+
+    refs = (x0, b, rea)
+    for i in range(6):
+        for a, ref in enumerate(refs):
+            copy(a, ref, i).start()
+
+    def some(i):
+        for a, ref in enumerate(refs):
+            copy(a, ref, i).wait()
+        for k in range(8):
+            x = i * 8 + k
+            for a in range(3):
+                own[a, x, :, 0:48] = raw[a, x, 0:24, :]
+                own[a, x, :, 64:112] = raw[a, x, 24:48, :]
+        for k in range(2):
+            ztile(L0, lambda x, a: own[a, x], hi, lo, i * 2 + k)
+
+    loop(6, some)
 
 
 def k_ypack0(own, zl, zh, up, dn):
@@ -364,7 +375,7 @@
 
         loop(24, keep, 6)
     both = (f1, r1)
-    zpack(L1, lambda x, a: both[a][x], z1h, z1l)
+    loop(6, lambda g: ztile(L1, lambda x, a: both[a][x], z1h, z1l, g), 3)
 
 
 def k_ypack1(f1, r1, zl, zh, up, dn):
@@ -612,20 +623,32 @@
     sums[...] = jnp.where(ln == 0, total(u), jnp.where(ln == 1, total(v), 0.0))
 
 
-def k_last(sums, own, z, az, f, sol, res):
+def k_last(sums, own, z, az, f, sol, res, sv, rv, sems):
     s = jnp.sum(sums[...], axis=0, keepdims=True)
     ln = lanes(1)
     over = jnp.sum(jnp.where(ln == 0, s, 0.0), axis=1, keepdims=True)
     under = jnp.sum(jnp.where(ln == 1, s, 0.0), axis=1, keepdims=True)
     step = over / under
     shift = lax.axis_index("gx") * 6
-
-    def one(x):
-        for ref, v in ((sol, own[0, x] + step * z[x]), (res, own_rows(L0, f[x + shift]) - step * az[x])):
-            ref[x, 0:24, :] = v[:, 0:48]
-            ref[x, 24:48, :] = roll(v, 64, 1)[:, 0:48]
-
-    loop(48, one, 4)
+    pairs = ((0, sv, sol), (1, rv, res))
+
+    def copy(a, src, dst, i):
+        part = pl.ds(i * 8, 8)
+        return pltpu.make_async_copy(src.at[part], dst.at[part], sems.at[a, i])
+
+    def some(i):
+        for k in range(8):
+            x = i * 8 + k
+            for ref, v in ((sv, own[0, x] + step * z[x]), (rv, own_rows(L0, f[x + shift]) - step * az[x])):
+                ref[x, 0:24, :] = v[:, 0:48]
+                ref[x, 24:48, :] = roll(v, 64, 1)[:, 0:48]
+        for a, src, dst in pairs:
+            copy(a, src, dst, i).start()
+
+    loop(6, some)
+    for i in range(6):
+        for a, src, dst in pairs:
+            copy(a, src, dst, i).wait()
 
 
 def ring(up, dn, axis):
@@ -643,7 +666,13 @@
     ALL = ("gx", "gy", "gz")
     sizes = [lax.axis_size(a) for a in ALL]
     count = sizes[0] * sizes[1] * sizes[2]
-    hi, lo, own = run(k_zpack0, (sds(*L0.zshape), sds(*L0.zshape), sds(3, 48, 24, 128)), (x0, b, rea))
+    hi, lo, own = run(
+        k_zpack0,
+        (sds(*L0.zshape), sds(*L0.zshape), sds(3, 48, 24, 128)),
+        (x0, b, rea),
+        [(3, 48, 48, 48), pltpu.SemaphoreType.DMA((3, 6))],
+        far_in=True,
+    )
     zl, zh = ring(hi, lo, "gz")
     up, dn = run(k_ypack0, (sds(*L0.yshape),) * 2, (own, zl, zh))
     yl, yh = ring(up, dn, "gy")
@@ -683,7 +712,13 @@
         mib=M2,
     )
     sums = lax.all_to_all(sums.reshape(count, 1, 128), ALL, 0, 0, tiled=True).reshape(count, 128)
-    return run(k_last, (sds(48, 48, 48), sds(48, 48, 48)), (sums, own, z, az, f0))
+    return run(
+        k_last,
+        (sds(48, 48, 48), sds(48, 48, 48)),
+        (sums, own, z, az, f0),
+        [(48, 48, 48), (48, 48, 48), pltpu.SemaphoreType.DMA((2, 6))],
+        far_out=True,
+    )
 
 
 def solution(mesh):

time: 103 us -> 106 us (1.029)
  Pallas kernels: 27.7 us -> 30.7 us
    pallas_call x9, Pallas kernels: 27.7 us -> 30.7 us  [run(): pl.pallas_call(kernel, out_shape=outs, in_specs=[hbm if far_in else vmem]...]
where the time goes in v5:
time: 106 us
  blocking collectives  33.6 us (32%)
  Pallas kernels  30.7 us (29%)
  starting transfers between devices  23.2 us (22%)
  waiting for transfers between devices  13.8 us (13%)
  local copies, waits for them, and re-layouts  3.8 us (4%)
    pallas_call x9, Pallas kernels, run(): pl.pallas_call(kernel, out_shape=outs, in_specs=[hbm if far_in else vmem]...  30.7 us
    all_to_all x1, blocking collectives, body(): g = lax.all_to_all(g, ALL, 0, 0, tiled=True)  19.3 us
    all_to_all x1, blocking collectives, body(): lax.all_to_all(sums.reshape(count, 1, 128), ALL, 0, 0, tiled=True)  14.3 us
    ppermute x4, starting transfers between devices, ring(): high = lax.ppermute(dn, axis, [(i, (i - 1) % n) for i in range(n)])  13 us
    ppermute x4, waiting for transfers between devices, ring(): low = lax.ppermute(up, axis, [(i, (i + 1) % n) for i in range(n)])  11.4 us
    ppermute x2, starting transfers between devices, swap(): return lax.ppermute(v, 'gx', [(0, 1), (1, 0)])  5.43 us
    ppermute x4, starting transfers between devices, ring(): low = lax.ppermute(up, axis, [(i, (i + 1) % n) for i in range(n)])  4.83 us
    unnamed x6, local copies, waits for them, and re-layouts  3.8 us
  transfers between devices with their start and end apart: 10, of which 6 were waited for; matrix products, arithmetic and copies ran while one was open for 0% of the time, Pallas kernels for 0%

profile of v5, /device:TPU:1, one launch (start us, length us, event | category | flops | bytes accessed | tf_op | source)
XLA Modules:
  0.0 105.9 jit_solution(225105883140853464)
XLA Ops:
  0.6 1.3 %copy-done = f32[48,48,48]{2,1,0:T(8,128)S(1)} copy-done((f32[48,48,48]{2,1,0:T(8,128)S(1)}, f32[48,48,48]{2,1,0:T(8,128)}, u32[]{:S(2)}) %copy-start) | copy-done | bytes 442392
  1.9 1.3 %copy-done.1 = f32[48,48,48]{2,1,0:T(8,128)S(1)} copy-done((f32[48,48,48]{2,1,0:T(8,128)S(1)}, f32[48,48,48]{2,1,0:T(8,128)}, u32[]{:S(2)}) %copy-start.1) | copy-done | bytes 442392
  3.2 1.3 %copy-done.2 = f32[48,48,48]{2,1,0:T(8,128)S(1)} copy-done((f32[48,48,48]{2,1,0:T(8,128)S(1)}, f32[48,48,48]{2,1,0:T(8,128)}, u32[]{:S(2)}) %copy-start.2) | copy-done | bytes 442392
  4.4 6.5 %shard_map.50 = (f32[12,24,128]{2,1,0:T(8,128)S(1)}, f32[12,24,128]{2,1,0:T(8,128)S(1)}, f32[3,48,24,128]{3,2,1,0:T(8,128)S(1)}) custom-call(f32[48,48,48]{2,1,0:T(8,128)S(1)} %copy-done, f32[48,48,48]{2,1,0:T(8,128)S(1)} %copy-done.1, f32[48,48,48]{2,1,0:T(8,128)S(1)} %copy-done.2), custom_call_target="tpu_custom_call" | custom-call | tf_op jit(solution)/shard_map/pallas_call | solution.py:39
  11.0 2.2 %collective-permute-start = (f32[12,24,128]{2,1,0:T(8,128)S(1)}, f32[12,24,128]{2,1,0:T(8,128)S(1)}, u32[]{:S(2)}, u32[]{:S(2)}) collective-permute-start(f32[12,24,128]{2,1,0:T(8,128)S(1)} %get-tuple-element.28), channel_id=1, source_target_pairs={{0,1},{1,2},{2,3},{3,4},{4,5},{5,6},{6,7},{7,8},{8,9},{9,10},{10,1... | collective-permute-start | bytes 442376 | tf_op jit(solution)/shard_map/ppermute | solution.py:656
  13.2 5.0 %collective-permute-start.1 = (f32[12,24,128]{2,1,0:T(8,128)S(1)}, f32[12,24,128]{2,1,0:T(8,128)S(1)}, u32[]{:S(2)}, u32[]{:S(2)}) collective-permute-start(f32[12,24,128]{2,1,0:T(8,128)S(1)} %get-tuple-element.29), channel_id=1, source_target_pairs={{0,15},{1,0},{2,1},{3,2},{4,3},{5,4},{6,5},{7,6},{8,7},{9,8},{10,9... | collective-permute-start | bytes 442376 | tf_op jit(solution)/shard_map/ppermute | solution.py:657
  18.2 3.5 %collective-permute-done.zl = f32[12,24,128]{2,1,0:T(8,128)S(1)} collective-permute-done((f32[12,24,128]{2,1,0:T(8,128)S(1)}, f32[12,24,128]{2,1,0:T(8,128)S(1)}, u32[]{:S(2)}, u32[]{:S(2)}) %collective-permute-start) | collective-permute-done | bytes 147488 | tf_op jit(solution)/shard_map/ppermute | solution.py:656
  21.6 1.6 %shard_map.51 = (f32[24,16,128]{2,1,0:T(8,128)S(1)}, f32[24,16,128]{2,1,0:T(8,128)S(1)}) custom-call(f32[3,48,24,128]{3,2,1,0:T(8,128)S(1)} %get-tuple-element.27.own, f32[12,24,128]{2,1,0:T(8,128)S(1)} %collective-permute-done.zl, f32[12,24,128]{2,1,0:T(8,128)S(1)} %collective-permute-done.1.zh), custom_call_target="tpu_custom_call" | custom-call | tf_op jit(solution)/shard_map/pallas_call | solution.py:39
  23.3 1.3 %collective-permute-start.2 = (f32[24,16,128]{2,1,0:T(8,128)S(1)}, f32[24,16,128]{2,1,0:T(8,128)S(1)}, u32[]{:S(2)}, u32[]{:S(2)}) collective-permute-start(f32[24,16,128]{2,1,0:T(8,128)S(1)} %get-tuple-element.30), channel_id=1, source_target_pairs={{0,16},{16,32},{32,48},{48,0},{1,17},{17,33},{33,49},{49,1},{2,18}... | collective-permute-start | bytes 589832 | tf_op jit(solution)/shard_map/ppermute | solution.py:656
  24.6 1.5 %collective-permute-start.3 = (f32[24,16,128]{2,1,0:T(8,128)S(1)}, f32[24,16,128]{2,1,0:T(8,128)S(1)}, u32[]{:S(2)}, u32[]{:S(2)}) collective-permute-start(f32[24,16,128]{2,1,0:T(8,128)S(1)} %get-tuple-element.31), channel_id=1, source_target_pairs={{0,48},{16,0},{32,16},{48,32},{1,49},{17,1},{33,17},{49,33},{2,50}... | collective-permute-start | bytes 589832 | tf_op jit(solution)/shard_map/ppermute | solution.py:657
  26.0 3.4 %collective-permute-done.2.yl = f32[24,16,128]{2,1,0:T(8,128)S(1)} collective-permute-done((f32[24,16,128]{2,1,0:T(8,128)S(1)}, f32[24,16,128]{2,1,0:T(8,128)S(1)}, u32[]{:S(2)}, u32[]{:S(2)}) %collective-permute-start.2) | collective-permute-done | bytes 196640 | tf_op jit(solution)/shard_map/ppermute | solution.py:656
  29.9 2.7 %collective-permute-start.4 = (f32[6,3,32,128]{3,2,1,0:T(8,128)S(1)}, f32[6,3,32,128]{3,2,1,0:T(8,128)S(1)}, u32[]{:S(2)}, u32[]{:S(2)}) collective-permute-start(f32[6,3,32,128]{3,2,1,0:T(8,128)S(1)} %shard_map.52), channel_id=1, source_target_pairs={{0,64},{64,0},{1,65},{65,1},{2,66},{66,2},{3,67},{67,3},{4,68},{68... | collective-permute-start | bytes 884744 | tf_op jit(solution)/shard_map/ppermute | solution.py:662
  33.8 6.3 %shard_map.53 = (f32[54,32,128]{2,1,0:T(8,128)S(1)}, f32[54,32,128]{2,1,0:T(8,128)S(1)}, f32[54,32,128]{2,1,0:T(8,128)S(1)}, f32[56,32,128]{2,1,0:T(8,128)S(1)},...) custom-call(f32[3,48,24,128]{3,2,1,0:T(8,128)S(1)} %get-tuple-elemen, ...), custom_call_target="tpu_custom_call" | custom-call | tf_op jit(solution)/shard_map/pallas_call | solution.py:39
  40.1 5.0 %collective-permute-start.6 = (f32[6,24,128]{2,1,0:T(8,128)S(1)}, f32[6,24,128]{2,1,0:T(8,128)S(1)}, u32[]{:S(2)}, u32[]{:S(2)}) collective-permute-start(f32[6,24,128]{2,1,0:T(8,128)S(1)} %get-tuple-element.35), channel_id=1, source_target_pairs={{0,15},{1,0},{2,1},{3,2},{4,3},{5,4},{6,5},{7,6},{8,7},{9,8},{10,9... | collective-permute-start | bytes 221192 | tf_op jit(solution)/shard_map/ppermute | solution.py:657
  45.1 2.0 %collective-permute-done.5.zl = f32[6,24,128]{2,1,0:T(8,128)S(1)} collective-permute-done((f32[6,24,128]{2,1,0:T(8,128)S(1)}, f32[6,24,128]{2,1,0:T(8,128)S(1)}, u32[]{:S(2)}, u32[]{:S(2)}) %collective-permute-start.5) | collective-permute-done | bytes 73760 | tf_op jit(solution)/shard_map/ppermute | solution.py:656
  48.1 1.3 %collective-permute-start.7 = (f32[12,24,128]{2,1,0:T(8,128)S(1)}, f32[12,24,128]{2,1,0:T(8,128)S(1)}, u32[]{:S(2)}, u32[]{:S(2)}) collective-permute-start(f32[12,24,128]{2,1,0:T(8,128)S(1)} %get-tuple-element.36), channel_id=1, source_target_pairs={{0,16},{16,32},{32,48},{48,0},{1,17},{17,33},{33,49},{49,1},{2,18}... | collective-permute-start | bytes 442376 | tf_op jit(solution)/shard_map/ppermute | solution.py:656
  49.4 1.5 %collective-permute-start.8 = (f32[12,24,128]{2,1,0:T(8,128)S(1)}, f32[12,24,128]{2,1,0:T(8,128)S(1)}, u32[]{:S(2)}, u32[]{:S(2)}) collective-permute-start(f32[12,24,128]{2,1,0:T(8,128)S(1)} %get-tuple-element.37), channel_id=1, source_target_pairs={{0,48},{16,0},{32,16},{48,32},{1,49},{17,1},{33,17},{49,33},{2,50}... | collective-permute-start | bytes 442376 | tf_op jit(solution)/shard_map/ppermute | solution.py:657
  50.9 2.5 %collective-permute-done.7.yl = f32[12,24,128]{2,1,0:T(8,128)S(1)} collective-permute-done((f32[12,24,128]{2,1,0:T(8,128)S(1)}, f32[12,24,128]{2,1,0:T(8,128)S(1)}, u32[]{:S(2)}, u32[]{:S(2)}) %collective-permute-start.7) | collective-permute-done | bytes 147488 | tf_op jit(solution)/shard_map/ppermute | solution.py:656
  54.2 2.8 %collective-permute-start.9 = (f32[12,2,24,128]{3,2,1,0:T(8,128)S(1)}, f32[12,2,24,128]{3,2,1,0:T(8,128)S(1)}, u32[]{:S(2)}, u32[]{:S(2)}) collective-permute-start(f32[12,2,24,128]{3,2,1,0:T(8,128)S(1)} %shard_map.55), channel_id=1, source_target_pairs={{0,64},{64,0},{1,65},{65,1},{2,66},{66,2},{3,67},{67,3},{4,68},{68... | collective-permute-start | bytes 884744 | tf_op jit(solution)/shard_map/ppermute | solution.py:662
  58.1 3.7 %shard_map.56 = (f32[36,24,128]{2,1,0:T(8,128)S(1)}, f32[36,24,128]{2,1,0:T(8,128)S(1)}, f32[38,24,128]{2,1,0:T(8,128)S(1)}, f32[18,32,128]{2,1,0:T(8,128)S(1)},...) custom-call(f32[24,12,128]{2,1,0:T(8,128)S(1)} %get-tuple-element.32.f1, ...), custom_call_target="tpu_custom_call" | custom-call | tf_op jit(solution)/shard_map/pallas_call | solution.py:39
  61.8 19.3 %all_to_all.16 = f32[128,4,128]{2,1,0:T(4,128)S(1)} all-to-all(f32[128,4,128]{2,1,0:T(4,128)S(1)} %bitcast.8), channel_id=1, replica_groups=mesh['gx'=2,'gy'=4,'gz'=16] {'gx','gy','gz'}, dimensions={0} | all-to-all | bytes 524288 | tf_op jit(solution)/shard_map/all_to_all | solution.py:700
  81.1 8.7 %shard_map.57 = (f32[48,24,128]{2,1,0:T(8,128)S(1)}, f32[48,24,128]{2,1,0:T(8,128)S(1)}, f32[128,128]{1,0:T(8,128)S(1)}) custom-call(f32[512,128]{1,0:T(8,128)S(1)} %bitcast.6, f32[18,32,128]{2,1,0:T(8,128)S(1)} %get-tuple-element.39.f2, f32[18,32,128]{2,1,0:T(8,128)S(1)} %get-tuple-element.40.c2, f32[20,32,128]{2,1,0:T(8,128)S(1)} %get-tuple-element.41.e2i, ...), custom_call_target="tpu_custom_call" | custom-call | tf_op jit(solution)/shard_map/pallas_call | solution.py:39
  89.9 14.3 %all_to_all.17 = f32[128,1,128]{2,1,0:T(1,128)S(1)} all-to-all(f32[128,1,128]{2,1,0:T(1,128)S(1)} %bitcast.9), channel_id=1, replica_groups=mesh['gx'=2,'gy'=4,'gz'=16] {'gx','gy','gz'}, dimensions={0} | all-to-all | bytes 131072 | tf_op jit(solution)/shard_map/all_to_all | solution.py:714
  104.2 1.7 %shard_map.58 = (f32[48,48,48]{2,1,0:T(8,128)}, f32[48,48,48]{2,1,0:T(8,128)}) custom-call(f32[128,128]{1,0:T(8,128)S(1)} %bitcast.7, f32[3,48,24,128]{3,2,1,0:T(8,128)S(1)} %get-tuple-element.27.own, f32[48,24,128]{2,1,0:T(8,128)S(1)} %get-tuple-element.50.z, f32[48,24,128]{2,1,0:T(8,128)S(1)} %get-tuple-element.51.az, ...), custom_call_target="tpu_custom_call" | custom-call | tf_op jit(solution)/shard_map/pallas_call | solution.py:39
  (13 shorter events, 4.6 us)
Async XLA Ops:
  0.6 1.3 %copy-start = (f32[48,48,48]{2,1,0:T(8,128)S(1)}, f32[48,48,48]{2,1,0:T(8,128)}, u32[]{:S(2)}) copy-start(f32[48,48,48]{2,1,0:T(8,128)} %x0.1) | copy-start | bytes 1327108
  1.9 1.3 %copy-start.1 = (f32[48,48,48]{2,1,0:T(8,128)S(1)}, f32[48,48,48]{2,1,0:T(8,128)}, u32[]{:S(2)}) copy-start(f32[48,48,48]{2,1,0:T(8,128)} %b.1) | copy-start | bytes 1327108
  3.2 1.3 %copy-start.2 = (f32[48,48,48]{2,1,0:T(8,128)S(1)}, f32[48,48,48]{2,1,0:T(8,128)}, u32[]{:S(2)}) copy-start(f32[48,48,48]{2,1,0:T(8,128)} %rea.1) | copy-start | bytes 1327108
  11.0 10.7 %collective-permute-start = (f32[12,24,128]{2,1,0:T(8,128)S(1)}, f32[12,24,128]{2,1,0:T(8,128)S(1)}, u32[]{:S(2)}, u32[]{:S(2)}) collective-permute-start(f32[12,24,128]{2,1,0:T(8,128)S(1)} %get-tuple-element.28), channel_id=1, source_target_pairs={{0,1},{1,2},{2,3},{3,4},{4,5},{5,6},{6,7},{7,8},{8,9},{9,10},{10,1... | collective-permute-start | bytes 442376 | tf_op jit(solution)/shard_map/ppermute | solution.py:656
  13.2 8.5 %collective-permute-start.1 = (f32[12,24,128]{2,1,0:T(8,128)S(1)}, f32[12,24,128]{2,1,0:T(8,128)S(1)}, u32[]{:S(2)}, u32[]{:S(2)}) collective-permute-start(f32[12,24,128]{2,1,0:T(8,128)S(1)} %get-tuple-element.29), channel_id=1, source_target_pairs={{0,15},{1,0},{2,1},{3,2},{4,3},{5,4},{6,5},{7,6},{8,7},{9,8},{10,9... | collective-permute-start | bytes 442376 | tf_op jit(solution)/shard_map/ppermute | solution.py:657
  23.3 6.2 %collective-permute-start.2 = (f32[24,16,128]{2,1,0:T(8,128)S(1)}, f32[24,16,128]{2,1,0:T(8,128)S(1)}, u32[]{:S(2)}, u32[]{:S(2)}) collective-permute-start(f32[24,16,128]{2,1,0:T(8,128)S(1)} %get-tuple-element.30), channel_id=1, source_target_pairs={{0,16},{16,32},{32,48},{48,0},{1,17},{17,33},{33,49},{49,1},{2,18}... | collective-permute-start | bytes 589832 | tf_op jit(solution)/shard_map/ppermute | solution.py:656
  24.6 4.9 %collective-permute-start.3 = (f32[24,16,128]{2,1,0:T(8,128)S(1)}, f32[24,16,128]{2,1,0:T(8,128)S(1)}, u32[]{:S(2)}, u32[]{:S(2)}) collective-permute-start(f32[24,16,128]{2,1,0:T(8,128)S(1)} %get-tuple-element.31), channel_id=1, source_target_pairs={{0,48},{16,0},{32,16},{48,32},{1,49},{17,1},{33,17},{49,33},{2,50}... | collective-permute-start | bytes 589832 | tf_op jit(solution)/shard_map/ppermute | solution.py:657
  29.9 3.9 %collective-permute-start.4 = (f32[6,3,32,128]{3,2,1,0:T(8,128)S(1)}, f32[6,3,32,128]{3,2,1,0:T(8,128)S(1)}, u32[]{:S(2)}, u32[]{:S(2)}) collective-permute-start(f32[6,3,32,128]{3,2,1,0:T(8,128)S(1)} %shard_map.52), channel_id=1, source_target_pairs={{0,64},{64,0},{1,65},{65,1},{2,66},{66,2},{3,67},{67,3},{4,68},{68... | collective-permute-start | bytes 884744 | tf_op jit(solution)/shard_map/ppermute | solution.py:662
  40.0 7.1 %collective-permute-start.5 = (f32[6,24,128]{2,1,0:T(8,128)S(1)}, f32[6,24,128]{2,1,0:T(8,128)S(1)}, u32[]{:S(2)}, u32[]{:S(2)}) collective-permute-start(f32[6,24,128]{2,1,0:T(8,128)S(1)} %get-tuple-element.34), channel_id=1, source_target_pairs={{0,1},{1,2},{2,3},{3,4},{4,5},{5,6},{6,7},{7,8},{8,9},{9,10},{10,1... | collective-permute-start | bytes 221192 | tf_op jit(solution)/shard_map/ppermute | solution.py:656
  40.1 7.0 %collective-permute-start.6 = (f32[6,24,128]{2,1,0:T(8,128)S(1)}, f32[6,24,128]{2,1,0:T(8,128)S(1)}, u32[]{:S(2)}, u32[]{:S(2)}) collective-permute-start(f32[6,24,128]{2,1,0:T(8,128)S(1)} %get-tuple-element.35), channel_id=1, source_target_pairs={{0,15},{1,0},{2,1},{3,2},{4,3},{5,4},{6,5},{7,6},{8,7},{9,8},{10,9... | collective-permute-start | bytes 221192 | tf_op jit(solution)/shard_map/ppermute | solution.py:657
  48.1 5.3 %collective-permute-start.7 = (f32[12,24,128]{2,1,0:T(8,128)S(1)}, f32[12,24,128]{2,1,0:T(8,128)S(1)}, u32[]{:S(2)}, u32[]{:S(2)}) collective-permute-start(f32[12,24,128]{2,1,0:T(8,128)S(1)} %get-tuple-element.36), channel_id=1, source_target_pairs={{0,16},{16,32},{32,48},{48,0},{1,17},{17,33},{33,49},{49,1},{2,18}... | collective-permute-start | bytes 442376 | tf_op jit(solution)/shard_map/ppermute | solution.py:656
  49.4 4.0 %collective-permute-start.8 = (f32[12,24,128]{2,1,0:T(8,128)S(1)}, f32[12,24,128]{2,1,0:T(8,128)S(1)}, u32[]{:S(2)}, u32[]{:S(2)}) collective-permute-start(f32[12,24,128]{2,1,0:T(8,128)S(1)} %get-tuple-element.37), channel_id=1, source_target_pairs={{0,48},{16,0},{32,16},{48,32},{1,49},{17,1},{33,17},{49,33},{2,50}... | collective-permute-start | bytes 442376 | tf_op jit(solution)/shard_map/ppermute | solution.py:657
  54.2 4.0 %collective-permute-start.9 = (f32[12,2,24,128]{3,2,1,0:T(8,128)S(1)}, f32[12,2,24,128]{3,2,1,0:T(8,128)S(1)}, u32[]{:S(2)}, u32[]{:S(2)}) collective-permute-start(f32[12,2,24,128]{3,2,1,0:T(8,128)S(1)} %shard_map.55), channel_id=1, source_target_pairs={{0,64},{64,0},{1,65},{65,1},{2,66},{66,2},{3,67},{67,3},{4,68},{68... | collective-permute-start | bytes 884744 | tf_op jit(solution)/shard_map/ppermute | solution.py:662

commit v6 on v5

--- a/solution.py
+++ b/solution.py
@@ -35,7 +35,7 @@
 
 def run(kernel, outs, args, scratch=(), mib=12, far_in=False, far_out=False):
     vmem = pl.BlockSpec(memory_space=pltpu.VMEM)
-    hbm = pl.BlockSpec(memory_space=pltpu.HBM)
+    hbm = pl.BlockSpec(memory_space=pl.ANY)
     return pl.pallas_call(
         kernel,
         out_shape=outs,
@@ -666,6 +666,7 @@
     ALL = ("gx", "gy", "gz")
     sizes = [lax.axis_size(a) for a in ALL]
     count = sizes[0] * sizes[1] * sizes[2]
+    b, x0, rea = (pltpu.with_memory_space_constraint(v, pltpu.HBM) for v in (b, x0, rea))
     hi, lo, own = run(
         k_zpack0,
         (sds(*L0.zshape), sds(*L0.zshape), sds(3, 48, 24, 128)),

time: 106 us -> 98.8 us (0.932)
  local copies, waits for them, and re-layouts: 3.8 us -> 0 us
  Pallas kernels: 30.7 us -> 27.3 us
    unnamed x6 -> x0, local copies, waits for them, and re-layouts: 3.8 us -> none
    pallas_call x9, Pallas kernels: 30.7 us -> 27.3 us  [run(): pl.pallas_call(kernel, out_shape=outs, in_specs=[hbm if far_in else vmem]...]
where the time goes in v6:
time: 98.8 us; the launch traced here: 98.6 us
  blocking collectives  33.6 us (34%)
  Pallas kernels  27.3 us (28%)
  starting transfers between devices  23.2 us (23%)
  waiting for transfers between devices  13.8 us (14%)
    pallas_call x9, Pallas kernels, run(): pl.pallas_call(kernel, out_shape=outs, in_specs=[hbm if far_in else vmem]...  27.3 us
    all_to_all x1, blocking collectives, body(): g = lax.all_to_all(g, ALL, 0, 0, tiled=True)  19.3 us
    all_to_all x1, blocking collectives, body(): lax.all_to_all(sums.reshape(count, 1, 128), ALL, 0, 0, tiled=True)  14.3 us
    ppermute x4, starting transfers between devices, ring(): high = lax.ppermute(dn, axis, [(i, (i - 1) % n) for i in range(n)])  13 us
    ppermute x4, waiting for transfers between devices, ring(): low = lax.ppermute(up, axis, [(i, (i + 1) % n) for i in range(n)])  11.4 us
    ppermute x2, starting transfers between devices, swap(): return lax.ppermute(v, 'gx', [(0, 1), (1, 0)])  5.43 us
    ppermute x4, starting transfers between devices, ring(): low = lax.ppermute(up, axis, [(i, (i + 1) % n) for i in range(n)])  4.83 us
    ppermute x2, waiting for transfers between devices, swap(): return lax.ppermute(v, 'gx', [(0, 1), (1, 0)])  2.42 us
  transfers between devices with their start and end apart: 10, of which 6 were waited for; matrix products, arithmetic and copies ran while one was open for 0% of the time, Pallas kernels for 0%

profile of v6, /device:TPU:1, one launch (start us, length us, event | category | flops | bytes accessed | tf_op | source)
XLA Modules:
  0.0 98.6 jit_solution(15753059867295977895)
XLA Ops:
  0.6 3.1 %shard_map.50 = (f32[12,24,128]{2,1,0:T(8,128)S(1)}, f32[12,24,128]{2,1,0:T(8,128)S(1)}, f32[3,48,24,128]{3,2,1,0:T(8,128)S(1)}) custom-call(f32[48,48,48]{2,1,0:T(8,128)} %x0.1, f32[48,48,48]{2,1,0:T(8,128)} %b.1, f32[48,48,48]{2,1,0:T(8,128)} %rea.1), custom_call_target="tpu_custom_call" | custom-call | tf_op jit(solution)/shard_map/pallas_call | solution.py:39
  3.8 2.2 %collective-permute-start = (f32[12,24,128]{2,1,0:T(8,128)S(1)}, f32[12,24,128]{2,1,0:T(8,128)S(1)}, u32[]{:S(2)}, u32[]{:S(2)}) collective-permute-start(f32[12,24,128]{2,1,0:T(8,128)S(1)} %get-tuple-element.28), channel_id=1, source_target_pairs={{0,1},{1,2},{2,3},{3,4},{4,5},{5,6},{6,7},{7,8},{8,9},{9,10},{10,1... | collective-permute-start | bytes 442376 | tf_op jit(solution)/shard_map/ppermute | solution.py:656
  6.0 5.0 %collective-permute-start.1 = (f32[12,24,128]{2,1,0:T(8,128)S(1)}, f32[12,24,128]{2,1,0:T(8,128)S(1)}, u32[]{:S(2)}, u32[]{:S(2)}) collective-permute-start(f32[12,24,128]{2,1,0:T(8,128)S(1)} %get-tuple-element.29), channel_id=1, source_target_pairs={{0,15},{1,0},{2,1},{3,2},{4,3},{5,4},{6,5},{7,6},{8,7},{9,8},{10,9... | collective-permute-start | bytes 442376 | tf_op jit(solution)/shard_map/ppermute | solution.py:657
  10.9 3.5 %collective-permute-done.zl = f32[12,24,128]{2,1,0:T(8,128)S(1)} collective-permute-done((f32[12,24,128]{2,1,0:T(8,128)S(1)}, f32[12,24,128]{2,1,0:T(8,128)S(1)}, u32[]{:S(2)}, u32[]{:S(2)}) %collective-permute-start) | collective-permute-done | bytes 147488 | tf_op jit(solution)/shard_map/ppermute | solution.py:656
  14.4 1.6 %shard_map.51 = (f32[24,16,128]{2,1,0:T(8,128)S(1)}, f32[24,16,128]{2,1,0:T(8,128)S(1)}) custom-call(f32[3,48,24,128]{3,2,1,0:T(8,128)S(1)} %get-tuple-element.27.own, f32[12,24,128]{2,1,0:T(8,128)S(1)} %collective-permute-done.zl, f32[12,24,128]{2,1,0:T(8,128)S(1)} %collective-permute-done.1.zh), custom_call_target="tpu_custom_call" | custom-call | tf_op jit(solution)/shard_map/pallas_call | solution.py:39
  16.1 1.3 %collective-permute-start.2 = (f32[24,16,128]{2,1,0:T(8,128)S(1)}, f32[24,16,128]{2,1,0:T(8,128)S(1)}, u32[]{:S(2)}, u32[]{:S(2)}) collective-permute-start(f32[24,16,128]{2,1,0:T(8,128)S(1)} %get-tuple-element.30), channel_id=1, source_target_pairs={{0,16},{16,32},{32,48},{48,0},{1,17},{17,33},{33,49},{49,1},{2,18}... | collective-permute-start | bytes 589832 | tf_op jit(solution)/shard_map/ppermute | solution.py:656
  17.4 1.5 %collective-permute-start.3 = (f32[24,16,128]{2,1,0:T(8,128)S(1)}, f32[24,16,128]{2,1,0:T(8,128)S(1)}, u32[]{:S(2)}, u32[]{:S(2)}) collective-permute-start(f32[24,16,128]{2,1,0:T(8,128)S(1)} %get-tuple-element.31), channel_id=1, source_target_pairs={{0,48},{16,0},{32,16},{48,32},{1,49},{17,1},{33,17},{49,33},{2,50}... | collective-permute-start | bytes 589832 | tf_op jit(solution)/shard_map/ppermute | solution.py:657
  18.8 3.4 %collective-permute-done.2.yl = f32[24,16,128]{2,1,0:T(8,128)S(1)} collective-permute-done((f32[24,16,128]{2,1,0:T(8,128)S(1)}, f32[24,16,128]{2,1,0:T(8,128)S(1)}, u32[]{:S(2)}, u32[]{:S(2)}) %collective-permute-start.2) | collective-permute-done | bytes 196640 | tf_op jit(solution)/shard_map/ppermute | solution.py:656
  22.7 2.7 %collective-permute-start.4 = (f32[6,3,32,128]{3,2,1,0:T(8,128)S(1)}, f32[6,3,32,128]{3,2,1,0:T(8,128)S(1)}, u32[]{:S(2)}, u32[]{:S(2)}) collective-permute-start(f32[6,3,32,128]{3,2,1,0:T(8,128)S(1)} %shard_map.52), channel_id=1, source_target_pairs={{0,64},{64,0},{1,65},{65,1},{2,66},{66,2},{3,67},{67,3},{4,68},{68... | collective-permute-start | bytes 884744 | tf_op jit(solution)/shard_map/ppermute | solution.py:662
  25.3 1.2 %collective-permute-done.4.xr = f32[6,3,32,128]{3,2,1,0:T(8,128)S(1)} collective-permute-done((f32[6,3,32,128]{3,2,1,0:T(8,128)S(1)}, f32[6,3,32,128]{3,2,1,0:T(8,128)S(1)}, u32[]{:S(2)}, u32[]{:S(2)}) %collective-permute-start.4) | collective-permute-done | bytes 294944 | tf_op jit(solution)/shard_map/ppermute | solution.py:662
  26.5 6.3 %shard_map.53 = (f32[54,32,128]{2,1,0:T(8,128)S(1)}, f32[54,32,128]{2,1,0:T(8,128)S(1)}, f32[54,32,128]{2,1,0:T(8,128)S(1)}, f32[56,32,128]{2,1,0:T(8,128)S(1)},...) custom-call(f32[3,48,24,128]{3,2,1,0:T(8,128)S(1)} %get-tuple-elemen, ...), custom_call_target="tpu_custom_call" | custom-call | tf_op jit(solution)/shard_map/pallas_call | solution.py:39
  32.9 5.0 %collective-permute-start.6 = (f32[6,24,128]{2,1,0:T(8,128)S(1)}, f32[6,24,128]{2,1,0:T(8,128)S(1)}, u32[]{:S(2)}, u32[]{:S(2)}) collective-permute-start(f32[6,24,128]{2,1,0:T(8,128)S(1)} %get-tuple-element.35), channel_id=1, source_target_pairs={{0,15},{1,0},{2,1},{3,2},{4,3},{5,4},{6,5},{7,6},{8,7},{9,8},{10,9... | collective-permute-start | bytes 221192 | tf_op jit(solution)/shard_map/ppermute | solution.py:657
  37.9 2.0 %collective-permute-done.5.zl = f32[6,24,128]{2,1,0:T(8,128)S(1)} collective-permute-done((f32[6,24,128]{2,1,0:T(8,128)S(1)}, f32[6,24,128]{2,1,0:T(8,128)S(1)}, u32[]{:S(2)}, u32[]{:S(2)}) %collective-permute-start.5) | collective-permute-done | bytes 73760 | tf_op jit(solution)/shard_map/ppermute | solution.py:656
  39.9 1.0 shard_map.54
  40.9 1.3 %collective-permute-start.7 = (f32[12,24,128]{2,1,0:T(8,128)S(1)}, f32[12,24,128]{2,1,0:T(8,128)S(1)}, u32[]{:S(2)}, u32[]{:S(2)}) collective-permute-start(f32[12,24,128]{2,1,0:T(8,128)S(1)} %get-tuple-element.36), channel_id=1, source_target_pairs={{0,16},{16,32},{32,48},{48,0},{1,17},{17,33},{33,49},{49,1},{2,18}... | collective-permute-start | bytes 442376 | tf_op jit(solution)/shard_map/ppermute | solution.py:656
  42.2 1.5 %collective-permute-start.8 = (f32[12,24,128]{2,1,0:T(8,128)S(1)}, f32[12,24,128]{2,1,0:T(8,128)S(1)}, u32[]{:S(2)}, u32[]{:S(2)}) collective-permute-start(f32[12,24,128]{2,1,0:T(8,128)S(1)} %get-tuple-element.37), channel_id=1, source_target_pairs={{0,48},{16,0},{32,16},{48,32},{1,49},{17,1},{33,17},{49,33},{2,50}... | collective-permute-start | bytes 442376 | tf_op jit(solution)/shard_map/ppermute | solution.py:657
  43.7 2.5 %collective-permute-done.7.yl = f32[12,24,128]{2,1,0:T(8,128)S(1)} collective-permute-done((f32[12,24,128]{2,1,0:T(8,128)S(1)}, f32[12,24,128]{2,1,0:T(8,128)S(1)}, u32[]{:S(2)}, u32[]{:S(2)}) %collective-permute-start.7) | collective-permute-done | bytes 147488 | tf_op jit(solution)/shard_map/ppermute | solution.py:656
  46.9 2.7 %collective-permute-start.9 = (f32[12,2,24,128]{3,2,1,0:T(8,128)S(1)}, f32[12,2,24,128]{3,2,1,0:T(8,128)S(1)}, u32[]{:S(2)}, u32[]{:S(2)}) collective-permute-start(f32[12,2,24,128]{3,2,1,0:T(8,128)S(1)} %shard_map.55), channel_id=1, source_target_pairs={{0,64},{64,0},{1,65},{65,1},{2,66},{66,2},{3,67},{67,3},{4,68},{68... | collective-permute-start | bytes 884744 | tf_op jit(solution)/shard_map/ppermute | solution.py:662
  49.7 1.2 %collective-permute-done.9.xr = f32[12,2,24,128]{3,2,1,0:T(8,128)S(1)} collective-permute-done((f32[12,2,24,128]{3,2,1,0:T(8,128)S(1)}, f32[12,2,24,128]{3,2,1,0:T(8,128)S(1)}, u32[]{:S(2)}, u32[]{:S(2)}) %collective-permute-start.9) | collective-permute-done | bytes 294944 | tf_op jit(solution)/shard_map/ppermute | solution.py:662
  50.9 3.7 %shard_map.56 = (f32[36,24,128]{2,1,0:T(8,128)S(1)}, f32[36,24,128]{2,1,0:T(8,128)S(1)}, f32[38,24,128]{2,1,0:T(8,128)S(1)}, f32[18,32,128]{2,1,0:T(8,128)S(1)},...) custom-call(f32[24,12,128]{2,1,0:T(8,128)S(1)} %get-tuple-element.32.f1, ...), custom_call_target="tpu_custom_call" | custom-call | tf_op jit(solution)/shard_map/pallas_call | solution.py:39
  54.6 19.3 %all_to_all.16 = f32[128,4,128]{2,1,0:T(4,128)S(1)} all-to-all(f32[128,4,128]{2,1,0:T(4,128)S(1)} %bitcast.8), channel_id=1, replica_groups=mesh['gx'=2,'gy'=4,'gz'=16] {'gx','gy','gz'}, dimensions={0} | all-to-all | bytes 524288 | tf_op jit(solution)/shard_map/all_to_all | solution.py:701
  73.9 8.7 %shard_map.57 = (f32[48,24,128]{2,1,0:T(8,128)S(1)}, f32[48,24,128]{2,1,0:T(8,128)S(1)}, f32[128,128]{1,0:T(8,128)S(1)}) custom-call(f32[512,128]{1,0:T(8,128)S(1)} %bitcast.6, f32[18,32,128]{2,1,0:T(8,128)S(1)} %get-tuple-element.39.f2, f32[18,32,128]{2,1,0:T(8,128)S(1)} %get-tuple-element.40.c2, f32[20,32,128]{2,1,0:T(8,128)S(1)} %get-tuple-element.41.e2i, ...), custom_call_target="tpu_custom_call" | custom-call | tf_op jit(solution)/shard_map/pallas_call | solution.py:39
  82.7 14.3 %all_to_all.17 = f32[128,1,128]{2,1,0:T(1,128)S(1)} all-to-all(f32[128,1,128]{2,1,0:T(1,128)S(1)} %bitcast.9), channel_id=1, replica_groups=mesh['gx'=2,'gy'=4,'gz'=16] {'gx','gy','gz'}, dimensions={0} | all-to-all | bytes 131072 | tf_op jit(solution)/shard_map/all_to_all | solution.py:715
  96.9 1.7 %shard_map.58 = (f32[48,48,48]{2,1,0:T(8,128)}, f32[48,48,48]{2,1,0:T(8,128)}) custom-call(f32[128,128]{1,0:T(8,128)S(1)} %bitcast.7, f32[3,48,24,128]{3,2,1,0:T(8,128)S(1)} %get-tuple-element.27.own, f32[48,24,128]{2,1,0:T(8,128)S(1)} %get-tuple-element.50.z, f32[48,24,128]{2,1,0:T(8,128)S(1)} %get-tuple-element.51.az, ...), custom_call_target="tpu_custom_call" | custom-call | tf_op jit(solution)/shard_map/pallas_call | solution.py:39
  (7 shorter events, 1.2 us)
Async XLA Ops:
  3.8 10.7 %collective-permute-start = (f32[12,24,128]{2,1,0:T(8,128)S(1)}, f32[12,24,128]{2,1,0:T(8,128)S(1)}, u32[]{:S(2)}, u32[]{:S(2)}) collective-permute-start(f32[12,24,128]{2,1,0:T(8,128)S(1)} %get-tuple-element.28), channel_id=1, source_target_pairs={{0,1},{1,2},{2,3},{3,4},{4,5},{5,6},{6,7},{7,8},{8,9},{9,10},{10,1... | collective-permute-start | bytes 442376 | tf_op jit(solution)/shard_map/ppermute | solution.py:656
  6.0 8.5 %collective-permute-start.1 = (f32[12,24,128]{2,1,0:T(8,128)S(1)}, f32[12,24,128]{2,1,0:T(8,128)S(1)}, u32[]{:S(2)}, u32[]{:S(2)}) collective-permute-start(f32[12,24,128]{2,1,0:T(8,128)S(1)} %get-tuple-element.29), channel_id=1, source_target_pairs={{0,15},{1,0},{2,1},{3,2},{4,3},{5,4},{6,5},{7,6},{8,7},{9,8},{10,9... | collective-permute-start | bytes 442376 | tf_op jit(solution)/shard_map/ppermute | solution.py:657
  16.1 6.2 %collective-permute-start.2 = (f32[24,16,128]{2,1,0:T(8,128)S(1)}, f32[24,16,128]{2,1,0:T(8,128)S(1)}, u32[]{:S(2)}, u32[]{:S(2)}) collective-permute-start(f32[24,16,128]{2,1,0:T(8,128)S(1)} %get-tuple-element.30), channel_id=1, source_target_pairs={{0,16},{16,32},{32,48},{48,0},{1,17},{17,33},{33,49},{49,1},{2,18}... | collective-permute-start | bytes 589832 | tf_op jit(solution)/shard_map/ppermute | solution.py:656
  17.4 4.9 %collective-permute-start.3 = (f32[24,16,128]{2,1,0:T(8,128)S(1)}, f32[24,16,128]{2,1,0:T(8,128)S(1)}, u32[]{:S(2)}, u32[]{:S(2)}) collective-permute-start(f32[24,16,128]{2,1,0:T(8,128)S(1)} %get-tuple-element.31), channel_id=1, source_target_pairs={{0,48},{16,0},{32,16},{48,32},{1,49},{17,1},{33,17},{49,33},{2,50}... | collective-permute-start | bytes 589832 | tf_op jit(solution)/shard_map/ppermute | solution.py:657
  22.7 3.9 %collective-permute-start.4 = (f32[6,3,32,128]{3,2,1,0:T(8,128)S(1)}, f32[6,3,32,128]{3,2,1,0:T(8,128)S(1)}, u32[]{:S(2)}, u32[]{:S(2)}) collective-permute-start(f32[6,3,32,128]{3,2,1,0:T(8,128)S(1)} %shard_map.52), channel_id=1, source_target_pairs={{0,64},{64,0},{1,65},{65,1},{2,66},{66,2},{3,67},{67,3},{4,68},{68... | collective-permute-start | bytes 884744 | tf_op jit(solution)/shard_map/ppermute | solution.py:662
  32.8 7.1 %collective-permute-start.5 = (f32[6,24,128]{2,1,0:T(8,128)S(1)}, f32[6,24,128]{2,1,0:T(8,128)S(1)}, u32[]{:S(2)}, u32[]{:S(2)}) collective-permute-start(f32[6,24,128]{2,1,0:T(8,128)S(1)} %get-tuple-element.34), channel_id=1, source_target_pairs={{0,1},{1,2},{2,3},{3,4},{4,5},{5,6},{6,7},{7,8},{8,9},{9,10},{10,1... | collective-permute-start | bytes 221192 | tf_op jit(solution)/shard_map/ppermute | solution.py:656
  32.9 7.0 %collective-permute-start.6 = (f32[6,24,128]{2,1,0:T(8,128)S(1)}, f32[6,24,128]{2,1,0:T(8,128)S(1)}, u32[]{:S(2)}, u32[]{:S(2)}) collective-permute-start(f32[6,24,128]{2,1,0:T(8,128)S(1)} %get-tuple-element.35), channel_id=1, source_target_pairs={{0,15},{1,0},{2,1},{3,2},{4,3},{5,4},{6,5},{7,6},{8,7},{9,8},{10,9... | collective-permute-start | bytes 221192 | tf_op jit(solution)/shard_map/ppermute | solution.py:657
  40.9 5.3 %collective-permute-start.7 = (f32[12,24,128]{2,1,0:T(8,128)S(1)}, f32[12,24,128]{2,1,0:T(8,128)S(1)}, u32[]{:S(2)}, u32[]{:S(2)}) collective-permute-start(f32[12,24,128]{2,1,0:T(8,128)S(1)} %get-tuple-element.36), channel_id=1, source_target_pairs={{0,16},{16,32},{32,48},{48,0},{1,17},{17,33},{33,49},{49,1},{2,18}... | collective-permute-start | bytes 442376 | tf_op jit(solution)/shard_map/ppermute | solution.py:656
  42.2 4.0 %collective-permute-start.8 = (f32[12,24,128]{2,1,0:T(8,128)S(1)}, f32[12,24,128]{2,1,0:T(8,128)S(1)}, u32[]{:S(2)}, u32[]{:S(2)}) collective-permute-start(f32[12,24,128]{2,1,0:T(8,128)S(1)} %get-tuple-element.37), channel_id=1, source_target_pairs={{0,48},{16,0},{32,16},{48,32},{1,49},{17,1},{33,17},{49,33},{2,50}... | collective-permute-start | bytes 442376 | tf_op jit(solution)/shard_map/ppermute | solution.py:657
  46.9 4.0 %collective-permute-start.9 = (f32[12,2,24,128]{3,2,1,0:T(8,128)S(1)}, f32[12,2,24,128]{3,2,1,0:T(8,128)S(1)}, u32[]{:S(2)}, u32[]{:S(2)}) collective-permute-start(f32[12,2,24,128]{3,2,1,0:T(8,128)S(1)} %shard_map.55), channel_id=1, source_target_pairs={{0,64},{64,0},{1,65},{65,1},{2,66},{66,2},{3,67},{67,3},{4,68},{68... | collective-permute-start | bytes 884744 | tf_op jit(solution)/shard_map/ppermute | solution.py:662

commit v7 on v6

--- a/solution.py
+++ b/solution.py
@@ -12,6 +12,7 @@
 F32 = jnp.float32
 HI = lax.Precision.HIGHEST
 M0, M1, M2 = 10, 8, 12
+UA, UF, UR, UM, UZ, UY, UL = 8, 9, 18, 18, 12, 4, 6
 
 
 class Spec:
@@ -86,7 +87,7 @@
 
 
 def ztile(sp, own, hi_ref, lo_ref, g):
-    q = lanes(sp.half) % 64
+    l = lanes(sp.half)
     for t in range(sp.st):
         hi = jnp.zeros((sp.half, 128), F32)
         lo = hi
@@ -94,9 +95,9 @@
             for a in range(sp.na):
                 v = own(t * (sp.n // sp.st) + g * sp.kp + k, a)
                 at = sp.h * (k * sp.na + a)
-                here = (q >= at) & (q < at + sp.h)
-                hi = jnp.where(here, roll(v, at - (sp.n - sp.h), 1), hi)
-                lo = jnp.where(here, roll(v, at, 1), lo)
+                far = (at - sp.n - sp.h) % 64
+                hi = jnp.where((l - far) % 64 < sp.h, roll(v, at - 2 * sp.n, 1), hi)
+                lo = jnp.where((l - at) % 64 < sp.h, roll(v, at, 1), lo)
         hi_ref[g, t * sp.half : (t + 1) * sp.half, :] = hi
         lo_ref[g, t * sp.half : (t + 1) * sp.half, :] = lo
 
@@ -111,10 +112,11 @@
     else:
         high = jnp.where(t == 0, zh[g, b:e, :], zh[g, sp.half + b : sp.half + e, :])
         low = jnp.where(t == 0, zl[g, b:e, :], zl[g, sp.half + b : sp.half + e, :])
-    high = roll(high, lax.rem(sp.n + 128 - at, 128), 1)
-    low = roll(low, lax.rem(256 - sp.h - at, 128), 1)
-    q = lanes(e - b) % 64
-    return jnp.where(q < sp.n, own(x, a)[b:e], jnp.where(q < top, high, jnp.where(q >= bottom, low, 0.0)))
+    l = lanes(e - b)
+    beside = jnp.where(((l + (64 - at)) & 63) < sp.h, high, low)
+    beside = roll(beside, (sp.n + 128 - at) & 127, 1)
+    q = l & 63
+    return jnp.where(q < sp.n, own(x, a)[b:e], jnp.where((q < top) | (q >= bottom), beside, 0.0))
 
 
 def ypack(sp, own, zl, zh, up_ref, dn_ref):
@@ -135,7 +137,7 @@
             up_ref[p, sp.na * h :, :] = pad
             dn_ref[p, sp.na * h :, :] = pad
 
-    loop(half, pair, 3)
+    loop(half, pair, UY)
 
 
 def plane(sp, own, zl, zh, yl, yh, x, a, dst, xw, ends, spare):
@@ -336,9 +338,25 @@
     return jnp.where(upper(sp, sp.half), v[0 : sp.half], v[sp.o :])
 
 
-def k_down0(own, zl, zh, yl, yh, xr, f_out, c_out, d_out, e_out, f1, r1, z1h, z1l, xw, bw, rw, ew, tmp, acc):
+def half_own(pair, tmp, acc, out, u):
+    coarsen_planes(pair, 24, tmp, acc, 24, u)
+    m = lane_map(lambda l, m: jnp.where(l < 64, l // 2, 32 + l // 2), 0.125)
+    acc[...] = times(flat(acc), m).reshape(24, 16, 128)
+
+    def keep(x):
+        out[x] = acc[x, 0:12, :]
+
+    loop(24, keep, 6)
+
+
+def k_react(own, r1, tmp, acc):
+    mine = lanes(24) % 64 < 48
+    half_own(lambda x: jnp.where(mine, own[2, 2 * x] + own[2, 2 * x + 1], 0.0), tmp, acc, r1, 4)
+
+
+def k_down0(own, r1, zl, zh, yl, yh, xr, f_out, c_out, d_out, e_out, f1, z1h, z1l, xw, bw, rw, ew, tmp, acc):
     ids = place()
-    assemble(L0, ids, lambda x, a: own[a, x], zl, zh, yl, yh, xr, ((xw, 1), (bw, 0), (rw, 0)), None, 4)
+    assemble(L0, ids, lambda x, a: own[a, x], zl, zh, yl, yh, xr, ((xw, 1), (bw, 0), (rw, 0)), None, UA)
     n = L0.nx
     ok = inside(L0, ids)
     zero_ends(xw, n)
@@ -354,26 +372,16 @@
         c_out[x] = c
         ew[x + 1] = c * f
 
-    loop(n, first, 6)
-    relax(ew, e_out, f_out, c_out, n, 1.0, 9, paired)
+    loop(n, first, UF)
+    relax(ew, e_out, f_out, c_out, n, 1.0, UR, paired)
     shift = ids[0] * L0.hx
 
     def left(x):
         return own_rows(L0, f_out[x] - d_out[x] * e_out[x + 1] + paired(e_out, x))
 
     mine = lanes(24) % 64 < 48
-    m = lane_map(lambda l, m: jnp.where(l < 64, l // 2, 32 + l // 2), 0.125)
-    for ref, pair in (
-        (f1, lambda x: left(2 * x + shift) + left(2 * x + shift + 1)),
-        (r1, lambda x: own_rows(L0, rw[2 * x + shift] + rw[2 * x + shift + 1])),
-    ):
-        coarsen_planes(lambda x, pair=pair: jnp.where(mine, pair(x), 0.0), 24, tmp, acc, 24, 4)
-        acc[...] = times(flat(acc), m).reshape(24, 16, 128)
-
-        def keep(x, ref=ref):
-            ref[x] = acc[x, 0:12, :]
-
-        loop(24, keep, 6)
+    pair = lambda x: jnp.where(mine, left(2 * x + shift) + left(2 * x + shift + 1), 0.0)
+    half_own(pair, tmp, acc, f1, UL)
     both = (f1, r1)
     loop(6, lambda g: ztile(L1, lambda x, a: both[a][x], z1h, z1l, g), 3)
 
@@ -403,7 +411,7 @@
         ew[x + 1] = c * fw[x]
 
     loop(n, first, 6)
-    relax(ew, e_out, fw, cw, n, 0.25, 12, paired)
+    relax(ew, e_out, fw, cw, n, 0.25, UM, paired)
 
     def left(x):
         return fw[x] - (1.5 + rw[x]) * e_out[x + 1] + 0.25 * paired(e_out, x)
@@ -500,7 +508,7 @@
         s3[x + 1] = c * f3[x]
 
     loop(nx, first, 6)
-    relax(s3, e3, f3, c3, nx, factor, 6)
+    relax(s3, e3, f3, c3, nx, factor, 12)
 
     def left(x):
         v = f3[x] - (6.0 * factor + r3[x]) * e3[x + 1] + factor * neighbours(e3, x)
@@ -538,8 +546,8 @@
             rr = new
     f4[...] = times(e.reshape(nx // 2 * H, 128), spread_map(lambda l: l // 2)).reshape(e.shape)
     add_refined(f4, nx // 2, e3, s3, 6)
-    relax(s3, e3, f3, c3, nx, factor, 6)
-    relax(e3, s3, f3, c3, nx, factor, 6)
+    relax(s3, e3, f3, c3, nx, factor, 12)
+    relax(e3, s3, f3, c3, nx, factor, 12)
 
 
 def k_up(g3, f2, c2, e2i, f1, c1, e1i, f0, c0, d0, e0i, z_out, az_out, sums,
@@ -577,8 +585,8 @@
         times(flat(na), spread_map(lambda l: down(L1, l, False))) + times(flat(nb), spread_map(lambda l: down(L1, l, True)))
     ).reshape(18, 16, 128)
     add_refined(w2, 18, e1i, e1, 6)
-    relax(e1, s1, f1, c1, 36, 0.25, 12, paired)
-    relax(s1, e1, f1, c1, 36, 0.25, 12, paired)
+    relax(e1, s1, f1, c1, 36, 0.25, UM, paired)
+    relax(s1, e1, f1, c1, 36, 0.25, UM, paired)
 
     def near(i):
         v = e1[i + 1 + gx * 9]
@@ -592,8 +600,8 @@
 
     n1[...] = times(flat(n1), spread_map(both)).reshape(27, 16, 128)
     add_refined(n1, 27, e0i, e0, 9)
-    relax(e0, s0, f0, c0, 54, 1.0, 9, paired)
-    relax(s0, e0, f0, c0, 54, 1.0, 9, paired)
+    relax(e0, s0, f0, c0, 54, 1.0, UR, paired)
+    relax(s0, e0, f0, c0, 54, 1.0, UR, paired)
     shift = gx * 6
     mine = lanes(24) % 64 < 48
 
@@ -609,12 +617,12 @@
         return u + jnp.where(mine, f * z, 0.0), v + jnp.where(mine, z * az, 0.0)
 
     def some(i, carry):
-        for k in range(6):
-            carry = last(6 * i + k, carry)
+        for k in range(UZ):
+            carry = last(UZ * i + k, carry)
         return carry
 
     zero = jnp.zeros((24, 128), F32)
-    u, v = lax.fori_loop(0, 8, some, (zero, zero))
+    u, v = lax.fori_loop(0, 48 // UZ, some, (zero, zero))
 
     def total(t):
         return jnp.sum(jnp.sum(t, axis=1, keepdims=True), axis=0, keepdims=True)
@@ -675,14 +683,15 @@
         far_in=True,
     )
     zl, zh = ring(hi, lo, "gz")
+    r1 = run(k_react, sds(24, 12, 128), (own,), [(24, 24, 128), (24, 16, 128)])
     up, dn = run(k_ypack0, (sds(*L0.yshape),) * 2, (own, zl, zh))
     yl, yh = ring(up, dn, "gy")
     xr = swap(run(k_xpack0, sds(*L0.xshape), (own, zl, zh, yl, yh)))
     p0, q0 = (54, 32, 128), (56, 32, 128)
-    f0, c0, d0, e0, f1, r1, z1h, z1l = run(
+    f0, c0, d0, e0, f1, z1h, z1l = run(
         k_down0,
-        (sds(*p0), sds(*p0), sds(*p0), sds(*q0), sds(24, 12, 128), sds(24, 12, 128), sds(*L1.zshape), sds(*L1.zshape)),
-        (own, zl, zh, yl, yh, xr),
+        (sds(*p0), sds(*p0), sds(*p0), sds(*q0), sds(24, 12, 128), sds(*L1.zshape), sds(*L1.zshape)),
+        (own, r1, zl, zh, yl, yh, xr),
         [q0, p0, p0, q0, (24, 24, 128), (24, 16, 128)],
         mib=M0,
     )

time: 98.8 us -> 94.7 us (0.959)
  Pallas kernels: 27.3 us -> 23.5 us
    pallas_call x9 -> x10, Pallas kernels: 27.3 us -> 23.5 us  [run(): pl.pallas_call(kernel, out_shape=outs, in_specs=[hbm if far_in else vmem]...]
where the time goes in v7:
time: 94.7 us; the launch traced here: 94.5 us
  blocking collectives  33.6 us (35%)
  Pallas kernels  23.5 us (25%)
  starting transfers between devices  23.2 us (24%)
  waiting for transfers between devices  13.5 us (14%)
    pallas_call x10, Pallas kernels, run(): pl.pallas_call(kernel, out_shape=outs, in_specs=[hbm if far_in else vmem]...  23.5 us
    all_to_all x1, blocking collectives, body(): g = lax.all_to_all(g, ALL, 0, 0, tiled=True)  19.4 us
    all_to_all x1, blocking collectives, body(): lax.all_to_all(sums.reshape(count, 1, 128), ALL, 0, 0, tiled=True)  14.3 us
    ppermute x4, starting transfers between devices, ring(): high = lax.ppermute(dn, axis, [(i, (i - 1) % n) for i in range(n)])  13 us
    ppermute x4, waiting for transfers between devices, ring(): low = lax.ppermute(up, axis, [(i, (i + 1) % n) for i in range(n)])  11.4 us
    ppermute x2, starting transfers between devices, swap(): return lax.ppermute(v, 'gx', [(0, 1), (1, 0)])  5.42 us
    ppermute x4, starting transfers between devices, ring(): low = lax.ppermute(up, axis, [(i, (i + 1) % n) for i in range(n)])  4.82 us
    ppermute x2, waiting for transfers between devices, swap(): return lax.ppermute(v, 'gx', [(0, 1), (1, 0)])  2.08 us
  transfers between devices with their start and end apart: 10, of which 6 were waited for; matrix products, arithmetic and copies ran while one was open for 0% of the time, Pallas kernels for 0%

profile of v7, /device:TPU:1, one launch (start us, length us, event | category | flops | bytes accessed | tf_op | source)
XLA Modules:
  0.0 94.5 jit_solution(8449263144024696750)
XLA Ops:
  0.6 3.1 %shard_map.50 = (f32[12,24,128]{2,1,0:T(8,128)S(1)}, f32[12,24,128]{2,1,0:T(8,128)S(1)}, f32[3,48,24,128]{3,2,1,0:T(8,128)S(1)}) custom-call(f32[48,48,48]{2,1,0:T(8,128)} %x0.1, f32[48,48,48]{2,1,0:T(8,128)} %b.1, f32[48,48,48]{2,1,0:T(8,128)} %rea.1), custom_call_target="tpu_custom_call" | custom-call | tf_op jit(solution)/shard_map/pallas_call | solution.py:40
  3.8 2.2 %collective-permute-start = (f32[12,24,128]{2,1,0:T(8,128)S(1)}, f32[12,24,128]{2,1,0:T(8,128)S(1)}, u32[]{:S(2)}, u32[]{:S(2)}) collective-permute-start(f32[12,24,128]{2,1,0:T(8,128)S(1)} %get-tuple-element.27), channel_id=1, source_target_pairs={{0,1},{1,2},{2,3},{3,4},{4,5},{5,6},{6,7},{7,8},{8,9},{9,10},{10,1... | collective-permute-start | bytes 442376 | tf_op jit(solution)/shard_map/ppermute | solution.py:664
  6.0 5.0 %collective-permute-start.1 = (f32[12,24,128]{2,1,0:T(8,128)S(1)}, f32[12,24,128]{2,1,0:T(8,128)S(1)}, u32[]{:S(2)}, u32[]{:S(2)}) collective-permute-start(f32[12,24,128]{2,1,0:T(8,128)S(1)} %get-tuple-element.28), channel_id=1, source_target_pairs={{0,15},{1,0},{2,1},{3,2},{4,3},{5,4},{6,5},{7,6},{8,7},{9,8},{10,9... | collective-permute-start | bytes 442376 | tf_op jit(solution)/shard_map/ppermute | solution.py:665
  11.0 3.5 %collective-permute-done.zl = f32[12,24,128]{2,1,0:T(8,128)S(1)} collective-permute-done((f32[12,24,128]{2,1,0:T(8,128)S(1)}, f32[12,24,128]{2,1,0:T(8,128)S(1)}, u32[]{:S(2)}, u32[]{:S(2)}) %collective-permute-start) | collective-permute-done | bytes 147488 | tf_op jit(solution)/shard_map/ppermute | solution.py:664
  14.4 1.2 %shard_map.52 = (f32[24,16,128]{2,1,0:T(8,128)S(1)}, f32[24,16,128]{2,1,0:T(8,128)S(1)}) custom-call(f32[3,48,24,128]{3,2,1,0:T(8,128)S(1)} %get-tuple-element.26.own, f32[12,24,128]{2,1,0:T(8,128)S(1)} %collective-permute-done.zl, f32[12,24,128]{2,1,0:T(8,128)S(1)} %collective-permute-done.1.zh), custom_call_target="tpu_custom_call" | custom-call | tf_op jit(solution)/shard_map/pallas_call | solution.py:40
  15.7 1.3 %collective-permute-start.2 = (f32[24,16,128]{2,1,0:T(8,128)S(1)}, f32[24,16,128]{2,1,0:T(8,128)S(1)}, u32[]{:S(2)}, u32[]{:S(2)}) collective-permute-start(f32[24,16,128]{2,1,0:T(8,128)S(1)} %get-tuple-element.29), channel_id=1, source_target_pairs={{0,16},{16,32},{32,48},{48,0},{1,17},{17,33},{33,49},{49,1},{2,18}... | collective-permute-start | bytes 589832 | tf_op jit(solution)/shard_map/ppermute | solution.py:664
  16.9 1.5 %collective-permute-start.3 = (f32[24,16,128]{2,1,0:T(8,128)S(1)}, f32[24,16,128]{2,1,0:T(8,128)S(1)}, u32[]{:S(2)}, u32[]{:S(2)}) collective-permute-start(f32[24,16,128]{2,1,0:T(8,128)S(1)} %get-tuple-element.30), channel_id=1, source_target_pairs={{0,48},{16,0},{32,16},{48,32},{1,49},{17,1},{33,17},{49,33},{2,50}... | collective-permute-start | bytes 589832 | tf_op jit(solution)/shard_map/ppermute | solution.py:665
  18.4 3.4 %collective-permute-done.2.yl = f32[24,16,128]{2,1,0:T(8,128)S(1)} collective-permute-done((f32[24,16,128]{2,1,0:T(8,128)S(1)}, f32[24,16,128]{2,1,0:T(8,128)S(1)}, u32[]{:S(2)}, u32[]{:S(2)}) %collective-permute-start.2) | collective-permute-done | bytes 196640 | tf_op jit(solution)/shard_map/ppermute | solution.py:664
  22.2 2.7 %collective-permute-start.4 = (f32[6,3,32,128]{3,2,1,0:T(8,128)S(1)}, f32[6,3,32,128]{3,2,1,0:T(8,128)S(1)}, u32[]{:S(2)}, u32[]{:S(2)}) collective-permute-start(f32[6,3,32,128]{3,2,1,0:T(8,128)S(1)} %shard_map.53), channel_id=1, source_target_pairs={{0,64},{64,0},{1,65},{65,1},{2,66},{66,2},{3,67},{67,3},{4,68},{68... | collective-permute-start | bytes 884744 | tf_op jit(solution)/shard_map/ppermute | solution.py:670
  25.2 0.9 collective-permute-done.4.xr
  26.1 4.4 %shard_map.54 = (f32[54,32,128]{2,1,0:T(8,128)S(1)}, f32[54,32,128]{2,1,0:T(8,128)S(1)}, f32[54,32,128]{2,1,0:T(8,128)S(1)}, f32[56,32,128]{2,1,0:T(8,128)S(1)},...) custom-call(f32[3,48,24,128]{3,2,1,0:T(8,128)S(1)} %get-tuple-element.26.own, ...), custom_call_target="tpu_custom_call" | custom-call | tf_op jit(solution)/shard_map/pallas_call | solution.py:40
  30.6 5.0 %collective-permute-start.6 = (f32[6,24,128]{2,1,0:T(8,128)S(1)}, f32[6,24,128]{2,1,0:T(8,128)S(1)}, u32[]{:S(2)}, u32[]{:S(2)}) collective-permute-start(f32[6,24,128]{2,1,0:T(8,128)S(1)} %get-tuple-element.33), channel_id=1, source_target_pairs={{0,15},{1,0},{2,1},{3,2},{4,3},{5,4},{6,5},{7,6},{8,7},{9,8},{10,9... | collective-permute-start | bytes 221192 | tf_op jit(solution)/shard_map/ppermute | solution.py:665
  35.5 2.0 %collective-permute-done.5.zl = f32[6,24,128]{2,1,0:T(8,128)S(1)} collective-permute-done((f32[6,24,128]{2,1,0:T(8,128)S(1)}, f32[6,24,128]{2,1,0:T(8,128)S(1)}, u32[]{:S(2)}, u32[]{:S(2)}) %collective-permute-start.5) | collective-permute-done | bytes 73760 | tf_op jit(solution)/shard_map/ppermute | solution.py:664
  38.2 1.3 %collective-permute-start.7 = (f32[12,24,128]{2,1,0:T(8,128)S(1)}, f32[12,24,128]{2,1,0:T(8,128)S(1)}, u32[]{:S(2)}, u32[]{:S(2)}) collective-permute-start(f32[12,24,128]{2,1,0:T(8,128)S(1)} %get-tuple-element.34), channel_id=1, source_target_pairs={{0,16},{16,32},{32,48},{48,0},{1,17},{17,33},{33,49},{49,1},{2,18}... | collective-permute-start | bytes 442376 | tf_op jit(solution)/shard_map/ppermute | solution.py:664
  39.5 1.6 %collective-permute-start.8 = (f32[12,24,128]{2,1,0:T(8,128)S(1)}, f32[12,24,128]{2,1,0:T(8,128)S(1)}, u32[]{:S(2)}, u32[]{:S(2)}) collective-permute-start(f32[12,24,128]{2,1,0:T(8,128)S(1)} %get-tuple-element.35), channel_id=1, source_target_pairs={{0,48},{16,0},{32,16},{48,32},{1,49},{17,1},{33,17},{49,33},{2,50}... | collective-permute-start | bytes 442376 | tf_op jit(solution)/shard_map/ppermute | solution.py:665
  41.0 2.5 %collective-permute-done.7.yl = f32[12,24,128]{2,1,0:T(8,128)S(1)} collective-permute-done((f32[12,24,128]{2,1,0:T(8,128)S(1)}, f32[12,24,128]{2,1,0:T(8,128)S(1)}, u32[]{:S(2)}, u32[]{:S(2)}) %collective-permute-start.7) | collective-permute-done | bytes 147488 | tf_op jit(solution)/shard_map/ppermute | solution.py:664
  43.5 0.7 shard_map.56
  44.2 2.7 %collective-permute-start.9 = (f32[12,2,24,128]{3,2,1,0:T(8,128)S(1)}, f32[12,2,24,128]{3,2,1,0:T(8,128)S(1)}, u32[]{:S(2)}, u32[]{:S(2)}) collective-permute-start(f32[12,2,24,128]{3,2,1,0:T(8,128)S(1)} %shard_map.56), channel_id=1, source_target_pairs={{0,64},{64,0},{1,65},{65,1},{2,66},{66,2},{3,67},{67,3},{4,68},{68... | collective-permute-start | bytes 884744 | tf_op jit(solution)/shard_map/ppermute | solution.py:670
  46.9 1.2 %collective-permute-done.9.xr = f32[12,2,24,128]{3,2,1,0:T(8,128)S(1)} collective-permute-done((f32[12,2,24,128]{3,2,1,0:T(8,128)S(1)}, f32[12,2,24,128]{3,2,1,0:T(8,128)S(1)}, u32[]{:S(2)}, u32[]{:S(2)}) %collective-permute-start.9) | collective-permute-done | bytes 294944 | tf_op jit(solution)/shard_map/ppermute | solution.py:670
  48.1 3.5 %shard_map.57 = (f32[36,24,128]{2,1,0:T(8,128)S(1)}, f32[36,24,128]{2,1,0:T(8,128)S(1)}, f32[38,24,128]{2,1,0:T(8,128)S(1)}, f32[18,32,128]{2,1,0:T(8,128)S(1)},...) custom-call(f32[24,12,128]{2,1,0:T(8,128)S(1)} %get-tuple-element.31.f1, ...), custom_call_target="tpu_custom_call" | custom-call | tf_op jit(solution)/shard_map/pallas_call | solution.py:40
  51.6 19.4 %all_to_all.16 = f32[128,4,128]{2,1,0:T(4,128)S(1)} all-to-all(f32[128,4,128]{2,1,0:T(4,128)S(1)} %bitcast.8), channel_id=1, replica_groups=mesh['gx'=2,'gy'=4,'gz'=16] {'gx','gy','gz'}, dimensions={0} | all-to-all | bytes 524288 | tf_op jit(solution)/shard_map/all_to_all | solution.py:710
  71.0 7.6 %shard_map.58 = (f32[48,24,128]{2,1,0:T(8,128)S(1)}, f32[48,24,128]{2,1,0:T(8,128)S(1)}, f32[128,128]{1,0:T(8,128)S(1)}) custom-call(f32[512,128]{1,0:T(8,128)S(1)} %bitcast.6, f32[18,32,128]{2,1,0:T(8,128)S(1)} %get-tuple-element.37.f2, f32[18,32,128]{2,1,0:T(8,128)S(1)} %get-tuple-element.38.c2, f32[20,32,128]{2,1,0:T(8,128)S(1)} %get-tuple-element.39.e2i, ...), custom_call_target="tpu_custom_call" | custom-call | tf_op jit(solution)/shard_map/pallas_call | solution.py:40
  78.6 14.3 %all_to_all.17 = f32[128,1,128]{2,1,0:T(1,128)S(1)} all-to-all(f32[128,1,128]{2,1,0:T(1,128)S(1)} %bitcast.9), channel_id=1, replica_groups=mesh['gx'=2,'gy'=4,'gz'=16] {'gx','gy','gz'}, dimensions={0} | all-to-all | bytes 131072 | tf_op jit(solution)/shard_map/all_to_all | solution.py:724
  92.8 1.7 %shard_map.59 = (f32[48,48,48]{2,1,0:T(8,128)}, f32[48,48,48]{2,1,0:T(8,128)}) custom-call(f32[128,128]{1,0:T(8,128)S(1)} %bitcast.7, f32[3,48,24,128]{3,2,1,0:T(8,128)S(1)} %get-tuple-element.26.own, f32[48,24,128]{2,1,0:T(8,128)S(1)} %get-tuple-element.48.z, f32[48,24,128]{2,1,0:T(8,128)S(1)} %get-tuple-element.49.az, ...), custom_call_target="tpu_custom_call" | custom-call | tf_op jit(solution)/shard_map/pallas_call | solution.py:40
  (8 shorter events, 1.4 us)
Async XLA Ops:
  3.8 10.7 %collective-permute-start = (f32[12,24,128]{2,1,0:T(8,128)S(1)}, f32[12,24,128]{2,1,0:T(8,128)S(1)}, u32[]{:S(2)}, u32[]{:S(2)}) collective-permute-start(f32[12,24,128]{2,1,0:T(8,128)S(1)} %get-tuple-element.27), channel_id=1, source_target_pairs={{0,1},{1,2},{2,3},{3,4},{4,5},{5,6},{6,7},{7,8},{8,9},{9,10},{10,1... | collective-permute-start | bytes 442376 | tf_op jit(solution)/shard_map/ppermute | solution.py:664
  6.0 8.5 %collective-permute-start.1 = (f32[12,24,128]{2,1,0:T(8,128)S(1)}, f32[12,24,128]{2,1,0:T(8,128)S(1)}, u32[]{:S(2)}, u32[]{:S(2)}) collective-permute-start(f32[12,24,128]{2,1,0:T(8,128)S(1)} %get-tuple-element.28), channel_id=1, source_target_pairs={{0,15},{1,0},{2,1},{3,2},{4,3},{5,4},{6,5},{7,6},{8,7},{9,8},{10,9... | collective-permute-start | bytes 442376 | tf_op jit(solution)/shard_map/ppermute | solution.py:665
  15.7 6.2 %collective-permute-start.2 = (f32[24,16,128]{2,1,0:T(8,128)S(1)}, f32[24,16,128]{2,1,0:T(8,128)S(1)}, u32[]{:S(2)}, u32[]{:S(2)}) collective-permute-start(f32[24,16,128]{2,1,0:T(8,128)S(1)} %get-tuple-element.29), channel_id=1, source_target_pairs={{0,16},{16,32},{32,48},{48,0},{1,17},{17,33},{33,49},{49,1},{2,18}... | collective-permute-start | bytes 589832 | tf_op jit(solution)/shard_map/ppermute | solution.py:664
  16.9 4.9 %collective-permute-start.3 = (f32[24,16,128]{2,1,0:T(8,128)S(1)}, f32[24,16,128]{2,1,0:T(8,128)S(1)}, u32[]{:S(2)}, u32[]{:S(2)}) collective-permute-start(f32[24,16,128]{2,1,0:T(8,128)S(1)} %get-tuple-element.30), channel_id=1, source_target_pairs={{0,48},{16,0},{32,16},{48,32},{1,49},{17,1},{33,17},{49,33},{2,50}... | collective-permute-start | bytes 589832 | tf_op jit(solution)/shard_map/ppermute | solution.py:665
  22.2 3.9 %collective-permute-start.4 = (f32[6,3,32,128]{3,2,1,0:T(8,128)S(1)}, f32[6,3,32,128]{3,2,1,0:T(8,128)S(1)}, u32[]{:S(2)}, u32[]{:S(2)}) collective-permute-start(f32[6,3,32,128]{3,2,1,0:T(8,128)S(1)} %shard_map.53), channel_id=1, source_target_pairs={{0,64},{64,0},{1,65},{65,1},{2,66},{66,2},{3,67},{67,3},{4,68},{68... | collective-permute-start | bytes 884744 | tf_op jit(solution)/shard_map/ppermute | solution.py:670
  30.5 7.1 %collective-permute-start.5 = (f32[6,24,128]{2,1,0:T(8,128)S(1)}, f32[6,24,128]{2,1,0:T(8,128)S(1)}, u32[]{:S(2)}, u32[]{:S(2)}) collective-permute-start(f32[6,24,128]{2,1,0:T(8,128)S(1)} %get-tuple-element.32), channel_id=1, source_target_pairs={{0,1},{1,2},{2,3},{3,4},{4,5},{5,6},{6,7},{7,8},{8,9},{9,10},{10,1... | collective-permute-start | bytes 221192 | tf_op jit(solution)/shard_map/ppermute | solution.py:664
  30.6 7.0 %collective-permute-start.6 = (f32[6,24,128]{2,1,0:T(8,128)S(1)}, f32[6,24,128]{2,1,0:T(8,128)S(1)}, u32[]{:S(2)}, u32[]{:S(2)}) collective-permute-start(f32[6,24,128]{2,1,0:T(8,128)S(1)} %get-tuple-element.33), channel_id=1, source_target_pairs={{0,15},{1,0},{2,1},{3,2},{4,3},{5,4},{6,5},{7,6},{8,7},{9,8},{10,9... | collective-permute-start | bytes 221192 | tf_op jit(solution)/shard_map/ppermute | solution.py:665
  38.2 5.3 %collective-permute-start.7 = (f32[12,24,128]{2,1,0:T(8,128)S(1)}, f32[12,24,128]{2,1,0:T(8,128)S(1)}, u32[]{:S(2)}, u32[]{:S(2)}) collective-permute-start(f32[12,24,128]{2,1,0:T(8,128)S(1)} %get-tuple-element.34), channel_id=1, source_target_pairs={{0,16},{16,32},{32,48},{48,0},{1,17},{17,33},{33,49},{49,1},{2,18}... | collective-permute-start | bytes 442376 | tf_op jit(solution)/shard_map/ppermute | solution.py:664
  39.5 4.0 %collective-permute-start.8 = (f32[12,24,128]{2,1,0:T(8,128)S(1)}, f32[12,24,128]{2,1,0:T(8,128)S(1)}, u32[]{:S(2)}, u32[]{:S(2)}) collective-permute-start(f32[12,24,128]{2,1,0:T(8,128)S(1)} %get-tuple-element.35), channel_id=1, source_target_pairs={{0,48},{16,0},{32,16},{48,32},{1,49},{17,1},{33,17},{49,33},{2,50}... | collective-permute-start | bytes 442376 | tf_op jit(solution)/shard_map/ppermute | solution.py:665
  44.2 3.9 %collective-permute-start.9 = (f32[12,2,24,128]{3,2,1,0:T(8,128)S(1)}, f32[12,2,24,128]{3,2,1,0:T(8,128)S(1)}, u32[]{:S(2)}, u32[]{:S(2)}) collective-permute-start(f32[12,2,24,128]{3,2,1,0:T(8,128)S(1)} %shard_map.56), channel_id=1, source_target_pairs={{0,64},{64,0},{1,65},{65,1},{2,66},{66,2},{3,67},{67,3},{4,68},{68... | collective-permute-start | bytes 884744 | tf_op jit(solution)/shard_map/ppermute | solution.py:670

commit v8 on v7

--- a/solution.py
+++ b/solution.py
@@ -12,7 +12,7 @@
 F32 = jnp.float32
 HI = lax.Precision.HIGHEST
 M0, M1, M2 = 10, 8, 12
-UA, UF, UR, UM, UZ, UY, UL = 8, 9, 18, 18, 12, 4, 6
+UA, UF, UR, UM, UZ, UY, UL = 8, 12, 18, 18, 12, 8, 6
 
 
 class Spec:
@@ -30,8 +30,8 @@
 L1 = Spec(24, 12, 2, 24, 12, 12, 44, 2, 2)
 
 
-def sds(*shape):
-    return jax.ShapeDtypeStruct(shape, F32)
+def sds(*shape, dtype=F32):
+    return jax.ShapeDtypeStruct(shape, dtype)
 
 
 def run(kernel, outs, args, scratch=(), mib=12, far_in=False, far_out=False):
@@ -219,20 +219,50 @@
     loop(n, one, u)
 
 
-def lane_map(pick, value, cols=128):
-    l = lax.broadcasted_iota(jnp.int32, (256, cols), 0) % 128
-    m = lax.broadcasted_iota(jnp.int32, (256, cols), 1)
-    return jnp.where(pick(l, m) == m, value, 0.0).astype(jnp.bfloat16)
+def lane_map(pick, value):
+    l = lax.broadcasted_iota(jnp.int32, (256, 128), 0) & 127
+    m = lax.broadcasted_iota(jnp.int32, (256, 128), 1)
+    return jnp.where(pick(l) == m, value, 0.0).astype(jnp.bfloat16)
 
 
 def spread_map(pick):
-    m = lax.broadcasted_iota(jnp.int32, (256, 128), 0) % 128
+    m = lax.broadcasted_iota(jnp.int32, (256, 128), 0) & 127
     l = lax.broadcasted_iota(jnp.int32, (256, 128), 1)
     return jnp.where(pick(l) == m, 1.0, 0.0).astype(jnp.bfloat16)
 
 
 def floor_half(z):
     return lax.shift_right_arithmetic(z, 1)
+
+
+def coarse_lane(sp, l, want):
+    z = lane_z(sp, l)
+    up = (l >= sp.cut) & (l < sp.cut + 64)
+    good = (z >= -sp.h) & (z < sp.n + sp.h)
+    good = good & (up if want else jnp.logical_not(up))
+    return jnp.where(good, floor_half(z) + jnp.where(z < 0, 128, 0), -1)
+
+
+def both_lanes(l):
+    lower, higher = coarse_lane(L0, l, False), coarse_lane(L0, l, True)
+    return jnp.where(lower >= 0, lower, jnp.where(higher >= 0, (higher + 64) & 127, -1))
+
+
+OWN, DOWN1A, DOWN1B, DOWN2, DOWN3, UP3, UP2, UP1A, UP1B, UP0 = range(10)
+
+
+def all_maps(maps, gz):
+    half = floor_half
+    maps[OWN] = lane_map(lambda l: jnp.where(l < 64, half(l), 32 + half(l)), 0.125)
+    maps[DOWN1A] = lane_map(lambda l: coarse_lane(L1, l, False), 0.125)
+    maps[DOWN1B] = lane_map(lambda l: coarse_lane(L1, l, True), 0.125)
+    maps[DOWN2] = lane_map(lambda l: jnp.where(l < 64, half(l), half(l) + 64), 0.125)
+    maps[DOWN3] = lane_map(half, 0.125)
+    maps[UP3] = spread_map(half)
+    maps[UP2] = spread_map(lambda l: gz * 6 + jnp.where(l < 64, half(l), half(l) - 64))
+    maps[UP1A] = spread_map(lambda l: coarse_lane(L1, l, False))
+    maps[UP1B] = spread_map(lambda l: coarse_lane(L1, l, True))
+    maps[UP0] = spread_map(both_lanes)
 
 
 def times(v, m):
@@ -294,7 +324,7 @@
     loop(6, some)
 
 
-def k_ypack0(own, zl, zh, up, dn):
+def k_ypack0(own, zl, zh, r1, up, dn):
     ypack(L0, lambda x, a: own[a, x], zl, zh, up, dn)
 
 
@@ -314,33 +344,24 @@
     xpack(L0, lambda x, a: own[a, x], zl, zh, yl, yh, out, None)
 
 
-def assemble(sp, ids, own, zl, zh, yl, yh, xr, dsts, spare, u):
-    shift = ids[0] * sp.hx
-    ends = edge(sp, ids)
+def windows(sp, own, zl, zh, yl, yh, out, spare, u):
+    ends = edge(sp, place())
 
     def some(i):
         for k in range(u):
             x = i * u + k
-            for a, (dst, off) in enumerate(dsts):
-                plane(sp, own, zl, zh, yl, yh, x, a, dst, x + shift + off, ends, None if spare is None else spare.at[k * sp.na + a])
+            for a in range(sp.na):
+                plane(sp, own, zl, zh, yl, yh, x, a, out.at[a], x, ends, None if spare is None else spare.at[k * sp.na + a])
 
     loop(sp.n // u, some)
-    other = (1 - ids[0]) * sp.n
-
-    def take(i):
-        for a, (dst, off) in enumerate(dsts):
-            dst[other + i + off] = xr[i, a]
-
-    loop(sp.hx, take, 2)
 
 
 def own_rows(sp, v):
     return jnp.where(upper(sp, sp.half), v[0 : sp.half], v[sp.o :])
 
 
-def half_own(pair, tmp, acc, out, u):
+def half_own(pair, tmp, acc, out, u, m):
     coarsen_planes(pair, 24, tmp, acc, 24, u)
-    m = lane_map(lambda l, m: jnp.where(l < 64, l // 2, 32 + l // 2), 0.125)
     acc[...] = times(flat(acc), m).reshape(24, 16, 128)
 
     def keep(x):
@@ -349,39 +370,54 @@
     loop(24, keep, 6)
 
 
-def k_react(own, r1, tmp, acc):
+def k_early(own, r1, maps, tmp, acc):
+    all_maps(maps, lax.axis_index("gz"))
     mine = lanes(24) % 64 < 48
-    half_own(lambda x: jnp.where(mine, own[2, 2 * x] + own[2, 2 * x + 1], 0.0), tmp, acc, r1, 4)
-
-
-def k_down0(own, r1, zl, zh, yl, yh, xr, f_out, c_out, d_out, e_out, f1, z1h, z1l, xw, bw, rw, ew, tmp, acc):
+    half_own(lambda x: jnp.where(mine, own[2, 2 * x] + own[2, 2 * x + 1], 0.0), tmp, acc, r1, 4, maps[OWN])
+
+
+def k_windows0(own, zl, zh, yl, yh, out):
+    windows(L0, lambda x, a: own[a, x], zl, zh, yl, yh, out, None, UA)
+
+
+def k_down0(win, r1, maps, xr, f_out, c_out, d_out, e_out, f1, z1h, z1l, xw, ew, tmp, acc):
     ids = place()
-    assemble(L0, ids, lambda x, a: own[a, x], zl, zh, yl, yh, xr, ((xw, 1), (bw, 0), (rw, 0)), None, UA)
     n = L0.nx
+    shift = ids[0] * L0.hx
+    other = (1 - ids[0]) * L0.n
     ok = inside(L0, ids)
     zero_ends(xw, n)
     zero_ends(ew, n)
     zero_ends(e_out, n)
 
-    def first(x):
-        d = 6.0 + rw[x]
+    def put(x):
+        xw[x + shift + 1] = win[0, x]
+
+    def take(x):
+        xw[x + other + 1] = xr[x, 0]
+
+    loop(48, put, 12)
+    loop(6, take, 6)
+
+    def first(w, b, rea):
+        d = 6.0 + rea
         c = jnp.where(ok, W / d, 0.0)
-        f = bw[x] - d * xw[x + 1] + paired(xw, x)
-        d_out[x] = d
-        f_out[x] = f
-        c_out[x] = c
-        ew[x + 1] = c * f
-
-    loop(n, first, UF)
+        f = b - d * xw[w + 1] + paired(xw, w)
+        d_out[w] = d
+        f_out[w] = f
+        c_out[w] = c
+        ew[w + 1] = c * f
+
+    loop(48, lambda x: first(x + shift, win[1, x], win[2, x]), UF)
+    loop(6, lambda x: first(x + other, xr[x, 1], xr[x, 2]), 6)
     relax(ew, e_out, f_out, c_out, n, 1.0, UR, paired)
-    shift = ids[0] * L0.hx
 
     def left(x):
         return own_rows(L0, f_out[x] - d_out[x] * e_out[x + 1] + paired(e_out, x))
 
     mine = lanes(24) % 64 < 48
     pair = lambda x: jnp.where(mine, left(2 * x + shift) + left(2 * x + shift + 1), 0.0)
-    half_own(pair, tmp, acc, f1, UL)
+    half_own(pair, tmp, acc, f1, UL, maps[OWN])
     both = (f1, r1)
     loop(6, lambda g: ztile(L1, lambda x, a: both[a][x], z1h, z1l, g), 3)
 
@@ -396,11 +432,27 @@
     xpack(L1, lambda x, a: both[a][x], zl, zh, yl, yh, out, spare)
 
 
-def k_down1(f1, r1, zl, zh, yl, yh, xr, fw, cw, e_out, f2, c2, e2, out3, rw, ew, tmp, acc, r2, ew2, tmp2, t3, sq, spare):
+def k_windows1(f1, r1, zl, zh, yl, yh, out, spare):
+    both = (f1, r1)
+    windows(L1, lambda x, a: both[a][x], zl, zh, yl, yh, out, spare, 4)
+
+
+def k_down1(win, maps, xr, fw, cw, e_out, f2, c2, e2, out3, rw, ew, tmp, acc, r2, ew2, tmp2, t3, sq):
     ids = place()
-    both = (f1, r1)
-    assemble(L1, ids, lambda x, a: both[a][x], zl, zh, yl, yh, xr, ((fw, 0), (rw, 0)), spare, 4)
     n = L1.nx
+    shift = ids[0] * L1.hx
+    other = (1 - ids[0]) * L1.n
+
+    def put(x):
+        fw[x + shift] = win[0, x]
+        rw[x + shift] = win[1, x]
+
+    def take(x):
+        fw[x + other] = xr[x, 0]
+        rw[x + other] = xr[x, 1]
+
+    loop(24, put, 8)
+    loop(12, take, 6)
     ok = inside(L1, ids)
     zero_ends(ew, n)
     zero_ends(e_out, n)
@@ -416,18 +468,11 @@
     def left(x):
         return fw[x] - (1.5 + rw[x]) * e_out[x + 1] + 0.25 * paired(e_out, x)
 
-    def pick(l, m):
-        z = lane_z(L1, l)
-        up = (l >= L1.cut) & (l < L1.cut + 64)
-        good = (z >= -12) & (z < 36) & (up == (m >= 128))
-        return jnp.where(good, floor_half(z) + jnp.where(z < 0, 128, 0) + jnp.where(up, 128, 0), -1)
-
-    m = lane_map(pick, 0.125, 256)
     for ref, pair in ((f2, lambda x: left(2 * x) + left(2 * x + 1)), (r2, lambda x: rw[2 * x] + rw[2 * x + 1])):
-        coarsen_planes(pair, 18, tmp, acc.at[0], 24, 6)
-        v = times(flat(acc.at[0]), m)
-        acc[0] = v[:, 0:128].reshape(18, 16, 128)
-        acc[1] = v[:, 128:256].reshape(18, 16, 128)
+        coarsen_planes(pair, 18, tmp, acc.at[0], 24, 9)
+        v = flat(acc.at[0])
+        acc[0] = times(v, maps[DOWN1A]).reshape(18, 16, 128)
+        acc[1] = times(v, maps[DOWN1B]).reshape(18, 16, 128)
 
         def keep(x, ref=ref):
             ref[x] = jnp.zeros((32, 128), F32)
@@ -450,10 +495,9 @@
     def left2(x):
         return f2[x] - (0.375 + r2[x]) * e2[x + 1] + 0.0625 * neighbours(e2, x)
 
-    m = lane_map(lambda l, m: jnp.where(l < 64, l // 2, l // 2 + 64), 0.125)
     for a, pair in enumerate((lambda x: left2(2 * x) + left2(2 * x + 1), lambda x: r2[2 * x] + r2[2 * x + 1])):
         coarsen_planes(pair, 9, tmp2, t3.at[a], 32, 9)
-        t3[a] = times(flat(t3.at[a]), m).reshape(9, 16, 128)
+        t3[a] = times(flat(t3.at[a]), maps[DOWN2]).reshape(9, 16, 128)
     shift = ids[0] * 3
     sq[...] = jnp.zeros((128, 128), F32)
     for a in range(2):
@@ -477,7 +521,7 @@
     return jnp.sum(jnp.sum(s, axis=1, keepdims=True), axis=0, keepdims=True)
 
 
-def coarse_solve(g3, nx, ny, nz, e3, s3, f3, c3, r3, tmp, f4, r4, sq):
+def coarse_solve(g3, maps, nx, ny, nz, e3, s3, f3, c3, r3, tmp, f4, r4, sq):
     R = f3.shape[1]
     for ref in (f3, r3):
         ref[...] = jnp.zeros(ref.shape, F32)
@@ -514,10 +558,9 @@
         v = f3[x] - (6.0 * factor + r3[x]) * e3[x + 1] + factor * neighbours(e3, x)
         return jnp.where(ok, v, 0.0)
 
-    m = lane_map(lambda l, m: l // 2, 0.125)
     for ref, pair in ((f4, lambda x: left(2 * x) + left(2 * x + 1)), (r4, lambda x: r3[2 * x] + r3[2 * x + 1])):
         coarsen_planes(pair, nx // 2, tmp, ref, R, 6)
-        ref[...] = times(flat(ref), m).reshape(ref.shape)
+        ref[...] = times(flat(ref), maps[DOWN3]).reshape(ref.shape)
     f4k = 0.25**4
     H = R // 2
     row = lax.broadcasted_iota(jnp.int32, (nx // 2, H, 128), 1)
@@ -533,28 +576,32 @@
 
     r = jnp.where(within, f4[...], 0.0)
     p = r
-    e = jnp.zeros_like(r)
+    q = apply(r)
     rr = sum_all(r * r)
-    for i in range(BOTTOM_ITERS):
-        q = apply(p)
-        a = rr / sum_all(p * q)
+    a = rr / sum_all(r * q)
+    e = a * p
+    for i in range(1, BOTTOM_ITERS):
+        r = r - a * q
+        w = apply(r)
+        new = sum_all(r * r)
+        rw = sum_all(r * w)
+        b = new / rr
+        a = new / (rw - b * new / a)
+        p = r + b * p
+        q = w + b * q
         e = e + a * p
-        if i + 1 < BOTTOM_ITERS:
-            r = r - a * q
-            new = sum_all(r * r)
-            p = r + (new / rr) * p
-            rr = new
-    f4[...] = times(e.reshape(nx // 2 * H, 128), spread_map(lambda l: l // 2)).reshape(e.shape)
+        rr = new
+    f4[...] = times(e.reshape(nx // 2 * H, 128), maps[UP3]).reshape(e.shape)
     add_refined(f4, nx // 2, e3, s3, 6)
     relax(s3, e3, f3, c3, nx, factor, 12)
     relax(e3, s3, f3, c3, nx, factor, 12)
 
 
-def k_up(g3, f2, c2, e2i, f1, c1, e1i, f0, c0, d0, e0i, z_out, az_out, sums,
+def k_up(g3, maps, f2, c2, e2i, f1, c1, e1i, f0, c0, d0, e0i, z_out, az_out, sums,
          e3, s3, f3, c3, r3, tmp3, f4, r4, sq, w3, w2, na, nb, n1, e2, s2, e1, s1, e0, s0):
     gx, gy, gz, sy, sz = place()
     nx, ny, nz = f3.shape[0], sy * 6, sz * 6
-    coarse_solve(g3, nx, ny, nz, e3, s3, f3, c3, r3, tmp3, f4, r4, sq)
+    coarse_solve(g3, maps, nx, ny, nz, e3, s3, f3, c3, r3, tmp3, f4, r4, sq)
     for ref, n in ((s2, 18), (s1, 36), (s0, 54), (e2, 18), (e1, 36), (e0, 54)):
         zero_ends(ref, n)
     R3 = s3.shape[1]
@@ -562,8 +609,7 @@
     pick = pick.astype(F32)
     for i in range(9):
         w3[i] = jnp.dot(pick, s3[i + 1 + gx * 3], precision=HI, preferred_element_type=F32)
-    spread = spread_map(lambda l: gz * 6 + jnp.where(l < 64, l // 2, l // 2 - 64))
-    w3[...] = times(flat(w3), spread).reshape(9, 16, 128)
+    w3[...] = times(flat(w3), maps[UP2]).reshape(9, 16, 128)
     add_refined(w3, 9, e2i, e2, 9)
     relax(e2, s2, f2, c2, 18, 0.0625, 18)
     relax(s2, e2, f2, c2, 18, 0.0625, 18)
@@ -574,16 +620,7 @@
 
     loop(18, halves, 6)
 
-    def down(sp, l, want):
-        z = lane_z(sp, l)
-        up = (l >= sp.cut) & (l < sp.cut + 64)
-        good = (z >= -sp.h) & (z < sp.n + sp.h)
-        good = good & (up if want else jnp.logical_not(up))
-        return jnp.where(good, floor_half(z) + jnp.where(z < 0, 128, 0), -1)
-
-    w2[...] = (
-        times(flat(na), spread_map(lambda l: down(L1, l, False))) + times(flat(nb), spread_map(lambda l: down(L1, l, True)))
-    ).reshape(18, 16, 128)
+    w2[...] = (times(flat(na), maps[UP1A]) + times(flat(nb), maps[UP1B])).reshape(18, 16, 128)
     add_refined(w2, 18, e1i, e1, 6)
     relax(e1, s1, f1, c1, 36, 0.25, UM, paired)
     relax(s1, e1, f1, c1, 36, 0.25, UM, paired)
@@ -594,11 +631,7 @@
 
     loop(27, near, 9)
 
-    def both(l):
-        lower, higher = down(L0, l, False), down(L0, l, True)
-        return jnp.where(lower >= 0, lower, jnp.where(higher >= 0, (higher + 64) % 128, -1))
-
-    n1[...] = times(flat(n1), spread_map(both)).reshape(27, 16, 128)
+    n1[...] = times(flat(n1), maps[UP0]).reshape(27, 16, 128)
     add_refined(n1, 27, e0i, e0, 9)
     relax(e0, s0, f0, c0, 54, 1.0, UR, paired)
     relax(s0, e0, f0, c0, 54, 1.0, UR, paired)
@@ -683,16 +716,19 @@
         far_in=True,
     )
     zl, zh = ring(hi, lo, "gz")
-    r1 = run(k_react, sds(24, 12, 128), (own,), [(24, 24, 128), (24, 16, 128)])
-    up, dn = run(k_ypack0, (sds(*L0.yshape),) * 2, (own, zl, zh))
+    r1, maps = run(
+        k_early, (sds(24, 12, 128), sds(10, 256, 128, dtype=jnp.bfloat16)), (own,), [(24, 24, 128), (24, 16, 128)]
+    )
+    up, dn = run(k_ypack0, (sds(*L0.yshape),) * 2, (own, zl, zh, r1))
     yl, yh = ring(up, dn, "gy")
     xr = swap(run(k_xpack0, sds(*L0.xshape), (own, zl, zh, yl, yh)))
+    win = run(k_windows0, sds(3, 48, 32, 128), (own, zl, zh, yl, yh))
     p0, q0 = (54, 32, 128), (56, 32, 128)
     f0, c0, d0, e0, f1, z1h, z1l = run(
         k_down0,
         (sds(*p0), sds(*p0), sds(*p0), sds(*q0), sds(24, 12, 128), sds(*L1.zshape), sds(*L1.zshape)),
-        (own, r1, zl, zh, yl, yh, xr),
-        [q0, p0, p0, q0, (24, 24, 128), (24, 16, 128)],
+        (win, r1, maps, xr),
+        [q0, q0, (24, 24, 128), (24, 16, 128)],
         mib=M0,
     )
     zl, zh = ring(z1h, z1l, "gz")
@@ -700,11 +736,12 @@
     yl, yh = ring(up, dn, "gy")
     xr = swap(run(k_xpack1, sds(*L1.xshape), (f1, r1, zl, zh, yl, yh), [(2, 2, 24, 128)]))
     p1, q1, p2, q2 = (36, 24, 128), (38, 24, 128), (18, 32, 128), (20, 32, 128)
+    win = run(k_windows1, sds(2, 24, 24, 128), (f1, r1, zl, zh, yl, yh), [(8, 2, 24, 128)])
     f1w, c1w, e1w, f2w, c2w, e2w, g = run(
         k_down1,
         (sds(*p1), sds(*p1), sds(*q1), sds(*p2), sds(*p2), sds(*q2), sds(count * 4, 128)),
-        (f1, r1, zl, zh, yl, yh, xr),
-        [p1, q1, (18, 24, 128), (2, 18, 16, 128), p2, q2, (9, 32, 128), (2, 9, 16, 128), (128, 128), (8, 2, 24, 128)],
+        (win, maps, xr),
+        [p1, q1, (18, 24, 128), (2, 18, 16, 128), p2, q2, (9, 32, 128), (2, 9, 16, 128), (128, 128)],
         mib=M1,
     )
     g = lax.all_to_all(g, ALL, 0, 0, tiled=True)
@@ -716,7 +753,7 @@
     z, az, sums = run(
         k_up,
         (sds(48, 24, 128), sds(48, 24, 128), sds(count, 128)),
-        (g, f2w, c2w, e2w, f1w, c1w, e1w, f0, c0, d0, e0),
+        (g, maps, f2w, c2w, e2w, f1w, c1w, e1w, f0, c0, d0, e0),
         [q3, q3, p3, p3, p3, (n3[0] // 2, R3, 128), p4, p4, (sizes[0] * sizes[1], 128, 128), (9, 16, 128), (18, 16, 128),
          (18, 16, 128), (18, 16, 128), (27, 16, 128), q2, q2, q1, q1, q0, q0],
         mib=M2,

time: 94.7 us -> 91.7 us (0.968)
  waiting for transfers between devices: 13.5 us -> 11.2 us
    ppermute x2, waiting for transfers between devices: 2.08 us -> 0.27 us  [swap(): return lax.ppermute(v, 'gx', [(0, 1), (1, 0)])]
    pallas_call x10 -> x12, Pallas kernels: 23.5 us -> 22.8 us  [run(): pl.pallas_call(kernel, out_shape=outs, in_specs=[hbm if far_in else vmem]...]
  transfers between devices with their start and end apart: 10 -> 10, of which waited for: 6 -> 5; matrix products, arithmetic and copies ran while one was open for 0% -> 0% of each run, Pallas kernels for 0% -> 3%
where the time goes in v8:
time: 91.7 us; the launch traced here: 91.5 us
  blocking collectives  33.5 us (37%)
  starting transfers between devices  23.3 us (25%)
  Pallas kernels  22.8 us (25%)
  waiting for transfers between devices  11.2 us (12%)
    pallas_call x12, Pallas kernels, run(): pl.pallas_call(kernel, out_shape=outs, in_specs=[hbm if far_in else vmem]...  22.8 us
    all_to_all x1, blocking collectives, body(): g = lax.all_to_all(g, ALL, 0, 0, tiled=True)  19.2 us
    all_to_all x1, blocking collectives, body(): lax.all_to_all(sums.reshape(count, 1, 128), ALL, 0, 0, tiled=True)  14.3 us
    ppermute x4, starting transfers between devices, ring(): high = lax.ppermute(dn, axis, [(i, (i - 1) % n) for i in range(n)])  13 us
    ppermute x4, waiting for transfers between devices, ring(): low = lax.ppermute(up, axis, [(i, (i + 1) % n) for i in range(n)])  11 us
    ppermute x2, starting transfers between devices, swap(): return lax.ppermute(v, 'gx', [(0, 1), (1, 0)])  5.45 us
    ppermute x4, starting transfers between devices, ring(): low = lax.ppermute(up, axis, [(i, (i + 1) % n) for i in range(n)])  4.83 us
  transfers between devices with their start and end apart: 10, of which 5 were waited for; matrix products, arithmetic and copies ran while one was open for 0% of the time, Pallas kernels for 3%

profile of v8, /device:TPU:1, one launch (start us, length us, event | category | flops | bytes accessed | tf_op | source)
XLA Modules:
  0.0 91.5 jit_solution(8237451576599430686)
XLA Ops:
  0.6 3.1 %shard_map.50 = (f32[12,24,128]{2,1,0:T(8,128)S(1)}, f32[12,24,128]{2,1,0:T(8,128)S(1)}, f32[3,48,24,128]{3,2,1,0:T(8,128)S(1)}) custom-call(f32[48,48,48]{2,1,0:T(8,128)} %x0.1, f32[48,48,48]{2,1,0:T(8,128)} %b.1, f32[48,48,48]{2,1,0:T(8,128)} %rea.1), custom_call_target="tpu_custom_call" | custom-call | tf_op jit(solution)/shard_map/pallas_call | solution.py:40
  3.8 2.2 %collective-permute-start = (f32[12,24,128]{2,1,0:T(8,128)S(1)}, f32[12,24,128]{2,1,0:T(8,128)S(1)}, u32[]{:S(2)}, u32[]{:S(2)}) collective-permute-start(f32[12,24,128]{2,1,0:T(8,128)S(1)} %get-tuple-element.29), channel_id=1, source_target_pairs={{0,1},{1,2},{2,3},{3,4},{4,5},{5,6},{6,7},{7,8},{8,9},{9,10},{10,1... | collective-permute-start | bytes 442376 | tf_op jit(solution)/shard_map/ppermute | solution.py:697
  6.0 5.0 %collective-permute-start.1 = (f32[12,24,128]{2,1,0:T(8,128)S(1)}, f32[12,24,128]{2,1,0:T(8,128)S(1)}, u32[]{:S(2)}, u32[]{:S(2)}) collective-permute-start(f32[12,24,128]{2,1,0:T(8,128)S(1)} %get-tuple-element.30), channel_id=1, source_target_pairs={{0,15},{1,0},{2,1},{3,2},{4,3},{5,4},{6,5},{7,6},{8,7},{9,8},{10,9... | collective-permute-start | bytes 442376 | tf_op jit(solution)/shard_map/ppermute | solution.py:698
  11.4 3.0 %collective-permute-done.zl = f32[12,24,128]{2,1,0:T(8,128)S(1)} collective-permute-done((f32[12,24,128]{2,1,0:T(8,128)S(1)}, f32[12,24,128]{2,1,0:T(8,128)S(1)}, u32[]{:S(2)}, u32[]{:S(2)}) %collective-permute-start) | collective-permute-done | bytes 147488 | tf_op jit(solution)/shard_map/ppermute | solution.py:697
  14.4 1.0 %shard_map.52 = (f32[24,16,128]{2,1,0:T(8,128)S(1)}, f32[24,16,128]{2,1,0:T(8,128)S(1)}) custom-call(f32[3,48,24,128]{3,2,1,0:T(8,128)S(1)} %get-tuple-element.28.own, f32[12,24,128]{2,1,0:T(8,128)S(1)} %collective-permute-done.zl, f32[12,24,128]{2,1,0:T(8,128)S(1)} %collective-permute-done.1.zh, f32[24,12,128]{2,1,0:T(8,128)S(1)} %get-tuple-element.31.r1), custom_call_target="tpu_custom_call" | custom-call | tf_op jit(solution)/shard_map/pallas_call | solution.py:40
  15.4 1.3 %collective-permute-start.2 = (f32[24,16,128]{2,1,0:T(8,128)S(1)}, f32[24,16,128]{2,1,0:T(8,128)S(1)}, u32[]{:S(2)}, u32[]{:S(2)}) collective-permute-start(f32[24,16,128]{2,1,0:T(8,128)S(1)} %get-tuple-element.32), channel_id=1, source_target_pairs={{0,16},{16,32},{32,48},{48,0},{1,17},{17,33},{33,49},{49,1},{2,18}... | collective-permute-start | bytes 589832 | tf_op jit(solution)/shard_map/ppermute | solution.py:697
  16.7 1.5 %collective-permute-start.3 = (f32[24,16,128]{2,1,0:T(8,128)S(1)}, f32[24,16,128]{2,1,0:T(8,128)S(1)}, u32[]{:S(2)}, u32[]{:S(2)}) collective-permute-start(f32[24,16,128]{2,1,0:T(8,128)S(1)} %get-tuple-element.33), channel_id=1, source_target_pairs={{0,48},{16,0},{32,16},{48,32},{1,49},{17,1},{33,17},{49,33},{2,50}... | collective-permute-start | bytes 589832 | tf_op jit(solution)/shard_map/ppermute | solution.py:698
  18.2 3.4 %collective-permute-done.2.yl = f32[24,16,128]{2,1,0:T(8,128)S(1)} collective-permute-done((f32[24,16,128]{2,1,0:T(8,128)S(1)}, f32[24,16,128]{2,1,0:T(8,128)S(1)}, u32[]{:S(2)}, u32[]{:S(2)}) %collective-permute-start.2) | collective-permute-done | bytes 196640 | tf_op jit(solution)/shard_map/ppermute | solution.py:697
  21.9 2.7 %collective-permute-start.4 = (f32[6,3,32,128]{3,2,1,0:T(8,128)S(1)}, f32[6,3,32,128]{3,2,1,0:T(8,128)S(1)}, u32[]{:S(2)}, u32[]{:S(2)}) collective-permute-start(f32[6,3,32,128]{3,2,1,0:T(8,128)S(1)} %shard_map.54), channel_id=1, source_target_pairs={{0,64},{64,0},{1,65},{65,1},{2,66},{66,2},{3,67},{67,3},{4,68},{68... | collective-permute-start | bytes 884744 | tf_op jit(solution)/shard_map/ppermute | solution.py:703
  24.6 1.2 %shard_map.53.win = f32[3,48,32,128]{3,2,1,0:T(8,128)S(1)} custom-call(f32[3,48,24,128]{3,2,1,0:T(8,128)S(1)} %get-tuple-element.28.own, f32[12,24,128]{2,1,0:T(8,128)S(1)} %collective-permute-done.zl, f32[12,24,128]{2,1,0:T(8,128)S(1)} %collective-permute-done.1.zh, f32[24,16,128]{2,1,0:T(8,128)S(1)} %collective-permute-done.2.yl, ...), custom_call_target="tpu_custom_call" | custom-call | tf_op jit(solution)/shard_map/pallas_call | solution.py:40
  25.9 3.1 %shard_map.55 = (f32[54,32,128]{2,1,0:T(8,128)S(1)}, f32[54,32,128]{2,1,0:T(8,128)S(1)}, f32[54,32,128]{2,1,0:T(8,128)S(1)}, f32[56,32,128]{2,1,0:T(8,128)S(1)},...) custom-call(f32[3,48,32,128]{3,2,1,0:T(8,128)S(1)} %shard_map.53.win, ...), custom_call_target="tpu_custom_call" | custom-call | tf_op jit(solution)/shard_map/pallas_call | solution.py:40
  29.1 5.0 %collective-permute-start.6 = (f32[6,24,128]{2,1,0:T(8,128)S(1)}, f32[6,24,128]{2,1,0:T(8,128)S(1)}, u32[]{:S(2)}, u32[]{:S(2)}) collective-permute-start(f32[6,24,128]{2,1,0:T(8,128)S(1)} %get-tuple-element.37), channel_id=1, source_target_pairs={{0,15},{1,0},{2,1},{3,2},{4,3},{5,4},{6,5},{7,6},{8,7},{9,8},{10,9... | collective-permute-start | bytes 221192 | tf_op jit(solution)/shard_map/ppermute | solution.py:698
  34.0 2.1 %collective-permute-done.5.zl = f32[6,24,128]{2,1,0:T(8,128)S(1)} collective-permute-done((f32[6,24,128]{2,1,0:T(8,128)S(1)}, f32[6,24,128]{2,1,0:T(8,128)S(1)}, u32[]{:S(2)}, u32[]{:S(2)}) %collective-permute-start.5) | collective-permute-done | bytes 73760 | tf_op jit(solution)/shard_map/ppermute | solution.py:697
  36.7 1.3 %collective-permute-start.7 = (f32[12,24,128]{2,1,0:T(8,128)S(1)}, f32[12,24,128]{2,1,0:T(8,128)S(1)}, u32[]{:S(2)}, u32[]{:S(2)}) collective-permute-start(f32[12,24,128]{2,1,0:T(8,128)S(1)} %get-tuple-element.38), channel_id=1, source_target_pairs={{0,16},{16,32},{32,48},{48,0},{1,17},{17,33},{33,49},{49,1},{2,18}... | collective-permute-start | bytes 442376 | tf_op jit(solution)/shard_map/ppermute | solution.py:697
  38.0 1.5 %collective-permute-start.8 = (f32[12,24,128]{2,1,0:T(8,128)S(1)}, f32[12,24,128]{2,1,0:T(8,128)S(1)}, u32[]{:S(2)}, u32[]{:S(2)}) collective-permute-start(f32[12,24,128]{2,1,0:T(8,128)S(1)} %get-tuple-element.39), channel_id=1, source_target_pairs={{0,48},{16,0},{32,16},{48,32},{1,49},{17,1},{33,17},{49,33},{2,50}... | collective-permute-start | bytes 442376 | tf_op jit(solution)/shard_map/ppermute | solution.py:698
  39.5 2.5 %collective-permute-done.7.yl = f32[12,24,128]{2,1,0:T(8,128)S(1)} collective-permute-done((f32[12,24,128]{2,1,0:T(8,128)S(1)}, f32[12,24,128]{2,1,0:T(8,128)S(1)}, u32[]{:S(2)}, u32[]{:S(2)}) %collective-permute-start.7) | collective-permute-done | bytes 147488 | tf_op jit(solution)/shard_map/ppermute | solution.py:697
  42.0 0.7 shard_map.58
  42.7 2.8 %collective-permute-start.9 = (f32[12,2,24,128]{3,2,1,0:T(8,128)S(1)}, f32[12,2,24,128]{3,2,1,0:T(8,128)S(1)}, u32[]{:S(2)}, u32[]{:S(2)}) collective-permute-start(f32[12,2,24,128]{3,2,1,0:T(8,128)S(1)} %shard_map.58), channel_id=1, source_target_pairs={{0,64},{64,0},{1,65},{65,1},{2,66},{66,2},{3,67},{67,3},{4,68},{68... | collective-permute-start | bytes 884744 | tf_op jit(solution)/shard_map/ppermute | solution.py:703
  45.5 0.9 %shard_map.57.win = f32[2,24,24,128]{3,2,1,0:T(8,128)S(1)} custom-call(f32[24,12,128]{2,1,0:T(8,128)S(1)} %get-tuple-element.35.f1, f32[24,12,128]{2,1,0:T(8,128)S(1)} %get-tuple-element.31.r1, f32[6,24,128]{2,1,0:T(8,128)S(1)} %collective-permute-done.5.zl, f32[6,24,128]{2,1,0:T(8,128)S(1)} %collective-permute-done.6.zh, ...), custom_call_target="tpu_custom_call" | custom-call | tf_op jit(solution)/shard_map/pallas_call | solution.py:40
  46.7 2.5 %shard_map.59 = (f32[36,24,128]{2,1,0:T(8,128)S(1)}, f32[36,24,128]{2,1,0:T(8,128)S(1)}, f32[38,24,128]{2,1,0:T(8,128)S(1)}, f32[18,32,128]{2,1,0:T(8,128)S(1)},...) custom-call(f32[2,24,24,128]{3,2,1,0:T(8,128)S(1)} %shard_map.57.win, ...), custom_call_target="tpu_custom_call" | custom-call | tf_op jit(solution)/shard_map/pallas_call | solution.py:40
  49.2 19.2 %all_to_all.16 = f32[128,4,128]{2,1,0:T(4,128)S(1)} all-to-all(f32[128,4,128]{2,1,0:T(4,128)S(1)} %bitcast.8), channel_id=1, replica_groups=mesh['gx'=2,'gy'=4,'gz'=16] {'gx','gy','gz'}, dimensions={0} | all-to-all | bytes 524288 | tf_op jit(solution)/shard_map/all_to_all | solution.py:747
  68.4 7.1 %shard_map.60 = (f32[48,24,128]{2,1,0:T(8,128)S(1)}, f32[48,24,128]{2,1,0:T(8,128)S(1)}, f32[128,128]{1,0:T(8,128)S(1)}) custom-call(f32[512,128]{1,0:T(8,128)S(1)} %bitcast.6, bf16[10,256,128]{2,1,0:T(8,128)(2,1)S(1)} %get-tuple-element.34.maps, f32[18,32,128]{2,1,0:T(8,128)S(1)} %get-tuple-element.41.f2, f32[18,32,128]{2,1,0:T(8,128)S(1)} %get-tuple-element.42.c2, ...), custom_call_target="tpu_custom_call" | custom-call | tf_op jit(solution)/shard_map/pallas_call | solution.py:40
  75.5 14.3 %all_to_all.17 = f32[128,1,128]{2,1,0:T(1,128)S(1)} all-to-all(f32[128,1,128]{2,1,0:T(1,128)S(1)} %bitcast.9), channel_id=1, replica_groups=mesh['gx'=2,'gy'=4,'gz'=16] {'gx','gy','gz'}, dimensions={0} | all-to-all | bytes 131072 | tf_op jit(solution)/shard_map/all_to_all | solution.py:761
  89.8 1.7 %shard_map.61 = (f32[48,48,48]{2,1,0:T(8,128)}, f32[48,48,48]{2,1,0:T(8,128)}) custom-call(f32[128,128]{1,0:T(8,128)S(1)} %bitcast.7, f32[3,48,24,128]{3,2,1,0:T(8,128)S(1)} %get-tuple-element.28.own, f32[48,24,128]{2,1,0:T(8,128)S(1)} %get-tuple-element.52.z, f32[48,24,128]{2,1,0:T(8,128)S(1)} %get-tuple-element.53.az, ...), custom_call_target="tpu_custom_call" | custom-call | tf_op jit(solution)/shard_map/pallas_call | solution.py:40
  (10 shorter events, 1.8 us)
Async XLA Ops:
  3.8 10.7 %collective-permute-start = (f32[12,24,128]{2,1,0:T(8,128)S(1)}, f32[12,24,128]{2,1,0:T(8,128)S(1)}, u32[]{:S(2)}, u32[]{:S(2)}) collective-permute-start(f32[12,24,128]{2,1,0:T(8,128)S(1)} %get-tuple-element.29), channel_id=1, source_target_pairs={{0,1},{1,2},{2,3},{3,4},{4,5},{5,6},{6,7},{7,8},{8,9},{9,10},{10,1... | collective-permute-start | bytes 442376 | tf_op jit(solution)/shard_map/ppermute | solution.py:697
  6.0 8.5 %collective-permute-start.1 = (f32[12,24,128]{2,1,0:T(8,128)S(1)}, f32[12,24,128]{2,1,0:T(8,128)S(1)}, u32[]{:S(2)}, u32[]{:S(2)}) collective-permute-start(f32[12,24,128]{2,1,0:T(8,128)S(1)} %get-tuple-element.30), channel_id=1, source_target_pairs={{0,15},{1,0},{2,1},{3,2},{4,3},{5,4},{6,5},{7,6},{8,7},{9,8},{10,9... | collective-permute-start | bytes 442376 | tf_op jit(solution)/shard_map/ppermute | solution.py:698
  15.4 6.2 %collective-permute-start.2 = (f32[24,16,128]{2,1,0:T(8,128)S(1)}, f32[24,16,128]{2,1,0:T(8,128)S(1)}, u32[]{:S(2)}, u32[]{:S(2)}) collective-permute-start(f32[24,16,128]{2,1,0:T(8,128)S(1)} %get-tuple-element.32), channel_id=1, source_target_pairs={{0,16},{16,32},{32,48},{48,0},{1,17},{17,33},{33,49},{49,1},{2,18}... | collective-permute-start | bytes 589832 | tf_op jit(solution)/shard_map/ppermute | solution.py:697
  16.7 4.9 %collective-permute-start.3 = (f32[24,16,128]{2,1,0:T(8,128)S(1)}, f32[24,16,128]{2,1,0:T(8,128)S(1)}, u32[]{:S(2)}, u32[]{:S(2)}) collective-permute-start(f32[24,16,128]{2,1,0:T(8,128)S(1)} %get-tuple-element.33), channel_id=1, source_target_pairs={{0,48},{16,0},{32,16},{48,32},{1,49},{17,1},{33,17},{49,33},{2,50}... | collective-permute-start | bytes 589832 | tf_op jit(solution)/shard_map/ppermute | solution.py:698
  21.9 3.9 %collective-permute-start.4 = (f32[6,3,32,128]{3,2,1,0:T(8,128)S(1)}, f32[6,3,32,128]{3,2,1,0:T(8,128)S(1)}, u32[]{:S(2)}, u32[]{:S(2)}) collective-permute-start(f32[6,3,32,128]{3,2,1,0:T(8,128)S(1)} %shard_map.54), channel_id=1, source_target_pairs={{0,64},{64,0},{1,65},{65,1},{2,66},{66,2},{3,67},{67,3},{4,68},{68... | collective-permute-start | bytes 884744 | tf_op jit(solution)/shard_map/ppermute | solution.py:703
  29.0 7.1 %collective-permute-start.5 = (f32[6,24,128]{2,1,0:T(8,128)S(1)}, f32[6,24,128]{2,1,0:T(8,128)S(1)}, u32[]{:S(2)}, u32[]{:S(2)}) collective-permute-start(f32[6,24,128]{2,1,0:T(8,128)S(1)} %get-tuple-element.36), channel_id=1, source_target_pairs={{0,1},{1,2},{2,3},{3,4},{4,5},{5,6},{6,7},{7,8},{8,9},{9,10},{10,1... | collective-permute-start | bytes 221192 | tf_op jit(solution)/shard_map/ppermute | solution.py:697
  29.1 7.0 %collective-permute-start.6 = (f32[6,24,128]{2,1,0:T(8,128)S(1)}, f32[6,24,128]{2,1,0:T(8,128)S(1)}, u32[]{:S(2)}, u32[]{:S(2)}) collective-permute-start(f32[6,24,128]{2,1,0:T(8,128)S(1)} %get-tuple-element.37), channel_id=1, source_target_pairs={{0,15},{1,0},{2,1},{3,2},{4,3},{5,4},{6,5},{7,6},{8,7},{9,8},{10,9... | collective-permute-start | bytes 221192 | tf_op jit(solution)/shard_map/ppermute | solution.py:698
  36.7 5.3 %collective-permute-start.7 = (f32[12,24,128]{2,1,0:T(8,128)S(1)}, f32[12,24,128]{2,1,0:T(8,128)S(1)}, u32[]{:S(2)}, u32[]{:S(2)}) collective-permute-start(f32[12,24,128]{2,1,0:T(8,128)S(1)} %get-tuple-element.38), channel_id=1, source_target_pairs={{0,16},{16,32},{32,48},{48,0},{1,17},{17,33},{33,49},{49,1},{2,18}... | collective-permute-start | bytes 442376 | tf_op jit(solution)/shard_map/ppermute | solution.py:697
  38.0 4.0 %collective-permute-start.8 = (f32[12,24,128]{2,1,0:T(8,128)S(1)}, f32[12,24,128]{2,1,0:T(8,128)S(1)}, u32[]{:S(2)}, u32[]{:S(2)}) collective-permute-start(f32[12,24,128]{2,1,0:T(8,128)S(1)} %get-tuple-element.39), channel_id=1, source_target_pairs={{0,48},{16,0},{32,16},{48,32},{1,49},{17,1},{33,17},{49,33},{2,50}... | collective-permute-start | bytes 442376 | tf_op jit(solution)/shard_map/ppermute | solution.py:698
  42.7 4.0 %collective-permute-start.9 = (f32[12,2,24,128]{3,2,1,0:T(8,128)S(1)}, f32[12,2,24,128]{3,2,1,0:T(8,128)S(1)}, u32[]{:S(2)}, u32[]{:S(2)}) collective-permute-start(f32[12,2,24,128]{3,2,1,0:T(8,128)S(1)} %shard_map.58), channel_id=1, source_target_pairs={{0,64},{64,0},{1,65},{65,1},{2,66},{66,2},{3,67},{67,3},{4,68},{68... | collective-permute-start | bytes 884744 | tf_op jit(solution)/shard_map/ppermute | solution.py:703

commit v9 on v8

--- a/solution.py
+++ b/solution.py
@@ -12,7 +12,7 @@
 F32 = jnp.float32
 HI = lax.Precision.HIGHEST
 M0, M1, M2 = 10, 8, 12
-UA, UF, UR, UM, UZ, UY, UL = 8, 12, 18, 18, 12, 8, 6
+UF, UR, UM, UZ, UL = 12, 27, 18, 12, 6
 
 
 class Spec:
@@ -20,14 +20,28 @@
         self.n, self.h, self.na, self.R, self.o, self.hx, self.cut, self.kp, self.st = n, h, na, R, o, hx, cut, kp, st
         self.half = n // 2
         self.zshape = (n // (kp * st), self.half * st, 128)
-        self.yrows = -(-na * h // 8) * 8
-        self.yshape = (self.half, self.yrows, 128)
+        self.yshape = (self.half, na * h, 128)
+        self.hs = (h,) * na
         self.xshape = (hx, na, R, 128)
         self.nx = n + hx
 
+    def slot(self, x, a):
+        if self.st == 1:
+            h = self.hs[a]
+            many = 64 // h
+            return ZBASE[a] + lax.div(x, many), 0, h * lax.rem(x, many)
+        per = self.n // self.st
+        t, y = lax.div(x, per), lax.rem(x, per)
+        return lax.div(y, self.kp), t, self.h * (lax.rem(y, self.kp) * self.na + a)
+
 
 L0 = Spec(48, 5, 3, 32, 8, 6, 56, 4, 1)
 L1 = Spec(24, 12, 2, 24, 12, 12, 44, 2, 2)
+L0.hs = (5, 4, 4)
+ZBASE = (0, 4, 7)
+YBASE = (0, 40, 72)
+L0.zshape = (10, 24, 128)
+L0.yshape = (3, 104, 128)
 
 
 def sds(*shape, dtype=F32):
@@ -86,78 +100,94 @@
     return high, low, jnp.where(gy > 0, 1.0, 0.0), jnp.where(gy < ny - 1, 1.0, 0.0)
 
 
-def ztile(sp, own, hi_ref, lo_ref, g):
+def zslot(sp, v, at, h, hi, lo):
     l = lanes(sp.half)
+    hi = jnp.where((l - (at - sp.n - h)) % 64 < h, roll(v, at - 2 * sp.n, 1), hi)
+    lo = jnp.where((l - at) % 64 < h, roll(v, at, 1), lo)
+    return hi, lo
+
+
+def ztile1(own, hi_ref, lo_ref, g):
+    sp = L1
     for t in range(sp.st):
-        hi = jnp.zeros((sp.half, 128), F32)
-        lo = hi
+        hi = lo = jnp.zeros((sp.half, 128), F32)
         for k in range(sp.kp):
             for a in range(sp.na):
                 v = own(t * (sp.n // sp.st) + g * sp.kp + k, a)
-                at = sp.h * (k * sp.na + a)
-                far = (at - sp.n - sp.h) % 64
-                hi = jnp.where((l - far) % 64 < sp.h, roll(v, at - 2 * sp.n, 1), hi)
-                lo = jnp.where((l - at) % 64 < sp.h, roll(v, at, 1), lo)
+                hi, lo = zslot(sp, v, sp.h * (k * sp.na + a), sp.h, hi, lo)
         hi_ref[g, t * sp.half : (t + 1) * sp.half, :] = hi
         lo_ref[g, t * sp.half : (t + 1) * sp.half, :] = lo
 
 
 def merged(sp, own, zl, zh, x, a, b, e, top, bottom):
-    per = sp.n // sp.st
-    t, y = lax.div(x, per), lax.rem(x, per)
-    g, k = lax.div(y, sp.kp), lax.rem(y, sp.kp)
-    at = sp.h * (k * sp.na + a)
+    g, t, at = sp.slot(x, a)
     if sp.st == 1:
         high, low = zh[g, b:e, :], zl[g, b:e, :]
     else:
         high = jnp.where(t == 0, zh[g, b:e, :], zh[g, sp.half + b : sp.half + e, :])
         low = jnp.where(t == 0, zl[g, b:e, :], zl[g, sp.half + b : sp.half + e, :])
     l = lanes(e - b)
-    beside = jnp.where(((l + (64 - at)) & 63) < sp.h, high, low)
+    beside = jnp.where(((l + (64 - at)) & 63) < sp.hs[a], high, low)
     beside = roll(beside, (sp.n + 128 - at) & 127, 1)
     q = l & 63
     return jnp.where(q < sp.n, own(x, a)[b:e], jnp.where((q < top) | (q >= bottom), beside, 0.0))
 
 
-def ypack(sp, own, zl, zh, up_ref, dn_ref):
-    h, half = sp.h, sp.half
-    up0 = (half - h) // 8 * 8
-    dn1 = min(half, -(-h // 8) * 8)
+def ypack(sp, own, zl, zh, up_ref, dn_ref, u):
+    half = sp.half
     top, bottom, _, _ = edge(sp, place())
 
-    def pair(p):
-        for a in range(sp.na):
-            for ref, b, e, s, t, swap in ((up_ref, up0, half, half - h - up0, half - up0, False), (dn_ref, 0, dn1, 0, h, True)):
-                even = merged(sp, own, zl, zh, 2 * p, a, b, e, top, bottom)
-                odd = roll(merged(sp, own, zl, zh, 2 * p + 1, a, b, e, top, bottom), 64, 1)
-                first, second = (odd, even) if swap else (even, odd)
-                ref[p, a * h : (a + 1) * h, :] = jnp.where(upper(sp, e - b), first, second)[s:t]
-        if sp.yrows > sp.na * h:
-            pad = jnp.zeros((sp.yrows - sp.na * h, 128), F32)
-            up_ref[p, sp.na * h :, :] = pad
-            dn_ref[p, sp.na * h :, :] = pad
-
-    loop(half, pair, UY)
-
-
-def plane(sp, own, zl, zh, yl, yh, x, a, dst, xw, ends, spare):
+    def some(i):
+        for k in range(u):
+            p = i * u + k
+            for a in range(sp.na):
+                h = sp.hs[a]
+                up0 = (half - h) // 8 * 8
+                dn1 = min(half, -(-h // 8) * 8)
+                for ref, b, e, s, t, swap in ((up_ref, up0, half, half - h - up0, half - up0, False), (dn_ref, 0, dn1, 0, h, True)):
+                    even = merged(sp, own, zl, zh, 2 * p, a, b, e, top, bottom)
+                    odd = roll(merged(sp, own, zl, zh, 2 * p + 1, a, b, e, top, bottom), 64, 1)
+                    first, second = (odd, even) if swap else (even, odd)
+                    v = jnp.where(upper(sp, e - b), first, second)[s:t]
+                    if sp is L0:
+                        ref[i, pl.ds(YBASE[a] + k, h, stride=8), :] = v
+                    else:
+                        ref[p, a * h : (a + 1) * h, :] = v
+
+    loop(half // u, some)
+
+
+def y_tiles0(yl, yh, g, t, a):
+    def rows(ref, start):
+        return ref[g, pl.ds(start + t, 8, stride=8), :]
+
+    if a == 0:
+        return roll(rows(yl, 0), 3, 0), rows(yh, 0)
+    return rows(yl, YBASE[a] - 32), rows(yh, 40) if a == 1 else roll(rows(yh, 40), 4, 0)
+
+
+def plane0(own, zl, zh, tiles, x, a, dst, xw, ends, turn):
     top, bottom, below, above = ends
+    sp = L0
+    m = merged(sp, own, zl, zh, x, a, 0, sp.half, top, bottom)
+    low, high = tiles
+    lower = jnp.concatenate([roll(low, turn, 1) * below, m], axis=0)
+    higher = jnp.concatenate([m, roll(high, turn, 1) * above], axis=0)
+    dst[xw] = jnp.where(upper(sp, sp.R), higher, lower)
+
+
+def plane1(own, zl, zh, yl, yh, x, a, dst, xw, ends, spare):
+    top, bottom, below, above = ends
+    sp = L1
     h, half = sp.h, sp.half
     m = merged(sp, own, zl, zh, x, a, 0, half, top, bottom)
     p = lax.div(x, 2)
     turn = 64 * (1 - lax.rem(x, 2))
-    if sp.o == 8:
-        low = roll(roll(yl[p], 8 - h - a * h, 0)[0:8], turn, 1) * below
-        high = roll(roll(yh[p], -a * h, 0)[0:8], turn, 1) * above
-        lower = jnp.concatenate([low, m], axis=0)
-        higher = jnp.concatenate([m, high], axis=0)
-        dst[xw] = jnp.where(upper(sp, sp.R), higher, lower)
-    else:
-        spare[0, 0:h, :] = roll(yl[p, a * h : (a + 1) * h, :], turn, 1) * below
-        spare[0, h:, :] = m
-        spare[1, 0:half, :] = m
-        spare[1, half:, :] = roll(yh[p, a * h : (a + 1) * h, :], turn, 1) * above
-        dst[xw] = jnp.where(upper(sp, sp.R), spare[1], spare[0])
+    spare[0, 0:h, :] = roll(yl[p, a * h : (a + 1) * h, :], turn, 1) * below
+    spare[0, h:, :] = m
+    spare[1, 0:half, :] = m
+    spare[1, half:, :] = roll(yh[p, a * h : (a + 1) * h, :], turn, 1) * above
+    dst[xw] = jnp.where(upper(sp, sp.R), spare[1], spare[0])
 
 
 def lane_z(sp, l):
@@ -166,7 +196,7 @@
 
 def inside(sp, ids):
     _, gy, gz, ny, nz = ids
-    n, h = sp.n, sp.h
+    n, h = sp.n, min(sp.hs)
     y = lax.broadcasted_iota(jnp.int32, (sp.R, 128), 0) - sp.o + jnp.where(upper(sp, sp.R), sp.R, 0)
     z = lane_z(sp, lanes(sp.R))
     ok = (y >= -h) & (y < n + h) & (z >= -h) & (z < n + h)
@@ -302,58 +332,73 @@
 
 def k_zpack0(x0, b, rea, hi, lo, own, raw, sems):
     def copy(a, ref, i):
-        part = pl.ds(i * 8, 8)
+        many = 64 // L0.hs[a]
+        part = pl.ds(i * many, many)
         return pltpu.make_async_copy(ref.at[part], raw.at[a, part], sems.at[a, i])
 
     refs = (x0, b, rea)
-    for i in range(6):
-        for a, ref in enumerate(refs):
+    parts = [48 * h // (64 // h * h) for h in L0.hs]
+    for a, ref in enumerate(refs):
+        for i in range(parts[a]):
             copy(a, ref, i).start()
 
-    def some(i):
-        for a, ref in enumerate(refs):
+    for a, ref in enumerate(refs):
+        h = L0.hs[a]
+        many = 64 // h
+
+        def some(i, a=a, ref=ref, h=h, many=many):
             copy(a, ref, i).wait()
-        for k in range(8):
-            x = i * 8 + k
-            for a in range(3):
+            hi_tile = lo_tile = jnp.zeros((24, 128), F32)
+            for k in range(many):
+                x = i * many + k
                 own[a, x, :, 0:48] = raw[a, x, 0:24, :]
                 own[a, x, :, 64:112] = raw[a, x, 24:48, :]
-        for k in range(2):
-            ztile(L0, lambda x, a: own[a, x], hi, lo, i * 2 + k)
-
-    loop(6, some)
+            for k in range(many):
+                hi_tile, lo_tile = zslot(L0, own[a, i * many + k], h * k, h, hi_tile, lo_tile)
+            hi[ZBASE[a] + i] = hi_tile
+            lo[ZBASE[a] + i] = lo_tile
+
+        loop(parts[a], some)
 
 
 def k_ypack0(own, zl, zh, r1, up, dn):
-    ypack(L0, lambda x, a: own[a, x], zl, zh, up, dn)
-
-
-def xpack(sp, own, zl, zh, yl, yh, out, spare):
+    ypack(L0, lambda x, a: own[a, x], zl, zh, up, dn, 8)
+
+
+def k_xpack0(own, zl, zh, yl, yh, out):
     ids = place()
-    ends = edge(sp, ids)
-    start = (1 - ids[0]) * (sp.n - sp.hx)
+    ends = edge(L0, ids)
+    first = ids[0] == 0
+    for i in range(6):
+        x = jnp.where(first, 42, 0) + i
+        for a in range(3):
+            there, here = y_tiles0(yl, yh, 2, 5 + i // 2, a), y_tiles0(yl, yh, 0, i // 2, a)
+            tiles = [jnp.where(first, v, w) for v, w in zip(there, here)]
+            plane0(lambda x, a: own[a, x], zl, zh, tiles, x, a, out.at[i], a, ends, 64 * (1 - i % 2))
+
+
+def k_xpack1(f1, r1, zl, zh, yl, yh, out, spare):
+    both = (f1, r1)
+    ids = place()
+    ends = edge(L1, ids)
 
     def one(i):
-        for a in range(sp.na):
-            plane(sp, own, zl, zh, yl, yh, start + i, a, out.at[i], a, ends, None if spare is None else spare.at[a])
-
-    loop(sp.hx, one, 2)
-
-
-def k_xpack0(own, zl, zh, yl, yh, out):
-    xpack(L0, lambda x, a: own[a, x], zl, zh, yl, yh, out, None)
-
-
-def windows(sp, own, zl, zh, yl, yh, out, spare, u):
-    ends = edge(sp, place())
+        for a in range(2):
+            plane1(lambda x, a: both[a][x], zl, zh, yl, yh, (1 - ids[0]) * 12 + i, a, out.at[i], a, ends, spare.at[a])
+
+    loop(12, one, 2)
+
+
+def k_windows0(own, zl, zh, yl, yh, out):
+    ends = edge(L0, place())
 
     def some(i):
-        for k in range(u):
-            x = i * u + k
-            for a in range(sp.na):
-                plane(sp, own, zl, zh, yl, yh, x, a, out.at[a], x, ends, None if spare is None else spare.at[k * sp.na + a])
-
-    loop(sp.n // u, some)
+        for k in range(16):
+            for a in range(3):
+                tiles = y_tiles0(yl, yh, i, k // 2, a)
+                plane0(lambda x, a: own[a, x], zl, zh, tiles, 16 * i + k, a, out.at[a], 16 * i + k, ends, 64 * (1 - k % 2))
+
+    loop(3, some)
 
 
 def own_rows(sp, v):
@@ -374,10 +419,6 @@
     all_maps(maps, lax.axis_index("gz"))
     mine = lanes(24) % 64 < 48
     half_own(lambda x: jnp.where(mine, own[2, 2 * x] + own[2, 2 * x + 1], 0.0), tmp, acc, r1, 4, maps[OWN])
-
-
-def k_windows0(own, zl, zh, yl, yh, out):
-    windows(L0, lambda x, a: own[a, x], zl, zh, yl, yh, out, None, UA)
 
 
 def k_down0(win, r1, maps, xr, f_out, c_out, d_out, e_out, f1, z1h, z1l, xw, ew, tmp, acc):
@@ -419,22 +460,24 @@
     pair = lambda x: jnp.where(mine, left(2 * x + shift) + left(2 * x + shift + 1), 0.0)
     half_own(pair, tmp, acc, f1, UL, maps[OWN])
     both = (f1, r1)
-    loop(6, lambda g: ztile(L1, lambda x, a: both[a][x], z1h, z1l, g), 3)
+    loop(6, lambda g: ztile1(lambda x, a: both[a][x], z1h, z1l, g), 3)
 
 
 def k_ypack1(f1, r1, zl, zh, up, dn):
     both = (f1, r1)
-    ypack(L1, lambda x, a: both[a][x], zl, zh, up, dn)
-
-
-def k_xpack1(f1, r1, zl, zh, yl, yh, out, spare):
-    both = (f1, r1)
-    xpack(L1, lambda x, a: both[a][x], zl, zh, yl, yh, out, spare)
+    ypack(L1, lambda x, a: both[a][x], zl, zh, up, dn, 6)
 
 
 def k_windows1(f1, r1, zl, zh, yl, yh, out, spare):
     both = (f1, r1)
-    windows(L1, lambda x, a: both[a][x], zl, zh, yl, yh, out, spare, 4)
+    ends = edge(L1, place())
+
+    def some(i):
+        for k in range(4):
+            for a in range(2):
+                plane1(lambda x, a: both[a][x], zl, zh, yl, yh, 4 * i + k, a, out.at[a], 4 * i + k, ends, spare.at[2 * k + a])
+
+    loop(6, some)
 
 
 def k_down1(win, maps, xr, fw, cw, e_out, f2, c2, e2, out3, rw, ew, tmp, acc, r2, ew2, tmp2, t3, sq):
@@ -604,11 +647,13 @@
     coarse_solve(g3, maps, nx, ny, nz, e3, s3, f3, c3, r3, tmp3, f4, r4, sq)
     for ref, n in ((s2, 18), (s1, 36), (s0, 54), (e2, 18), (e1, 36), (e0, 54)):
         zero_ends(ref, n)
-    R3 = s3.shape[1]
-    pick = lax.broadcasted_iota(jnp.int32, (16, R3), 1) == lax.broadcasted_iota(jnp.int32, (16, R3), 0) + (gy * 6 - 4)
-    pick = pick.astype(F32)
     for i in range(9):
-        w3[i] = jnp.dot(pick, s3[i + 1 + gx * 3], precision=HI, preferred_element_type=F32)
+        e = s3[i + 1 + gx * 3]
+        e = jnp.concatenate([jnp.zeros((8, 128), F32), e, jnp.zeros((8, 128), F32)], axis=0)
+        v = e[4:20]
+        for k in range(1, sy):
+            v = jnp.where(gy == k, e[6 * k + 4 : 6 * k + 20], v)
+        w3[i] = v
     w3[...] = times(flat(w3), maps[UP2]).reshape(9, 16, 128)
     add_refined(w3, 9, e2i, e2, 9)
     relax(e2, s2, f2, c2, 18, 0.0625, 18)
@@ -712,7 +757,7 @@
         k_zpack0,
         (sds(*L0.zshape), sds(*L0.zshape), sds(3, 48, 24, 128)),
         (x0, b, rea),
-        [(3, 48, 48, 48), pltpu.SemaphoreType.DMA((3, 6))],
+        [(3, 48, 48, 48), pltpu.SemaphoreType.DMA((3, 4))],
         far_in=True,
     )
     zl, zh = ring(hi, lo, "gz")

time: 91.7 us -> 90.8 us (level)
  waiting for transfers between devices: 11.2 us -> 10.2 us
    ppermute x4, waiting for transfers between devices: 11 us -> 9.55 us  [ring(): low = lax.ppermute(up, axis, [(i, (i + 1) % n) for i in range(n)])]
  transfers between devices with their start and end apart: 10 -> 10, of which waited for: 5 -> 6; matrix products, arithmetic and copies ran while one was open for 0% -> 0% of each run, Pallas kernels for 3% -> 3%
where the time goes in v9:
time: 90.8 us; the launch traced here: 90.7 us
  blocking collectives  33.8 us (37%)
  starting transfers between devices  23.5 us (26%)
  Pallas kernels  22.3 us (25%)
  waiting for transfers between devices  10.2 us (11%)
    pallas_call x12, Pallas kernels, run(): pl.pallas_call(kernel, out_shape=outs, in_specs=[hbm if far_in else vmem]...  22.3 us
    all_to_all x1, blocking collectives, body(): g = lax.all_to_all(g, ALL, 0, 0, tiled=True)  19.5 us
    all_to_all x1, blocking collectives, body(): lax.all_to_all(sums.reshape(count, 1, 128), ALL, 0, 0, tiled=True)  14.3 us
    ppermute x4, starting transfers between devices, ring(): high = lax.ppermute(dn, axis, [(i, (i - 1) % n) for i in range(n)])  12.9 us
    ppermute x4, waiting for transfers between devices, ring(): low = lax.ppermute(up, axis, [(i, (i + 1) % n) for i in range(n)])  9.55 us
    ppermute x2, starting transfers between devices, swap(): return lax.ppermute(v, 'gx', [(0, 1), (1, 0)])  5.79 us
    ppermute x4, starting transfers between devices, ring(): low = lax.ppermute(up, axis, [(i, (i + 1) % n) for i in range(n)])  4.83 us
  transfers between devices with their start and end apart: 10, of which 6 were waited for; matrix products, arithmetic and copies ran while one was open for 0% of the time, Pallas kernels for 3%

profile of v9, /device:TPU:1, one launch (start us, length us, event | category | flops | bytes accessed | tf_op | source)
XLA Modules:
  0.0 90.7 jit_solution(9877623075204762463)
XLA Ops:
  0.6 3.5 %shard_map.50 = (f32[10,24,128]{2,1,0:T(8,128)S(1)}, f32[10,24,128]{2,1,0:T(8,128)S(1)}, f32[3,48,24,128]{3,2,1,0:T(8,128)S(1)}) custom-call(f32[48,48,48]{2,1,0:T(8,128)} %x0.1, f32[48,48,48]{2,1,0:T(8,128)} %b.1, f32[48,48,48]{2,1,0:T(8,128)} %rea.1), custom_call_target="tpu_custom_call" | custom-call | tf_op jit(solution)/shard_map/pallas_call | solution.py:54
  4.2 2.2 %collective-permute-start = (f32[10,24,128]{2,1,0:T(8,128)S(1)}, f32[10,24,128]{2,1,0:T(8,128)S(1)}, u32[]{:S(2)}, u32[]{:S(2)}) collective-permute-start(f32[10,24,128]{2,1,0:T(8,128)S(1)} %get-tuple-element.29), channel_id=1, source_target_pairs={{0,1},{1,2},{2,3},{3,4},{4,5},{5,6},{6,7},{7,8},{8,9},{9,10},{10,1... | collective-permute-start | bytes 368648 | tf_op jit(solution)/shard_map/ppermute | solution.py:742
  6.3 5.0 %collective-permute-start.1 = (f32[10,24,128]{2,1,0:T(8,128)S(1)}, f32[10,24,128]{2,1,0:T(8,128)S(1)}, u32[]{:S(2)}, u32[]{:S(2)}) collective-permute-start(f32[10,24,128]{2,1,0:T(8,128)S(1)} %get-tuple-element.30), channel_id=1, source_target_pairs={{0,15},{1,0},{2,1},{3,2},{4,3},{5,4},{6,5},{7,6},{8,7},{9,8},{10,9... | collective-permute-start | bytes 368648 | tf_op jit(solution)/shard_map/ppermute | solution.py:743
  11.8 2.5 %collective-permute-done.zl = f32[10,24,128]{2,1,0:T(8,128)S(1)} collective-permute-done((f32[10,24,128]{2,1,0:T(8,128)S(1)}, f32[10,24,128]{2,1,0:T(8,128)S(1)}, u32[]{:S(2)}, u32[]{:S(2)}) %collective-permute-start) | collective-permute-done | bytes 122912 | tf_op jit(solution)/shard_map/ppermute | solution.py:742
  14.3 1.0 %shard_map.52 = (f32[3,104,128]{2,1,0:T(8,128)S(1)}, f32[3,104,128]{2,1,0:T(8,128)S(1)}) custom-call(f32[3,48,24,128]{3,2,1,0:T(8,128)S(1)} %get-tuple-element.28.own, f32[10,24,128]{2,1,0:T(8,128)S(1)} %collective-permute-done.zl, f32[10,24,128]{2,1,0:T(8,128)S(1)} %collective-permute-done.1.zh, f32[24,12,128]{2,1,0:T(8,128)S(1)} %get-tuple-element.31.r1), custom_call_target="tpu_custom_call" | custom-call | tf_op jit(solution)/shard_map/pallas_call | solution.py:54
  15.3 1.3 %collective-permute-start.2 = (f32[3,104,128]{2,1,0:T(8,128)S(1)}, f32[3,104,128]{2,1,0:T(8,128)S(1)}, u32[]{:S(2)}, u32[]{:S(2)}) collective-permute-start(f32[3,104,128]{2,1,0:T(8,128)S(1)} %get-tuple-element.32), channel_id=1, source_target_pairs={{0,16},{16,32},{32,48},{48,0},{1,17},{17,33},{33,49},{49,1},{2,18}... | collective-permute-start | bytes 479240 | tf_op jit(solution)/shard_map/ppermute | solution.py:742
  16.6 1.5 %collective-permute-start.3 = (f32[3,104,128]{2,1,0:T(8,128)S(1)}, f32[3,104,128]{2,1,0:T(8,128)S(1)}, u32[]{:S(2)}, u32[]{:S(2)}) collective-permute-start(f32[3,104,128]{2,1,0:T(8,128)S(1)} %get-tuple-element.33), channel_id=1, source_target_pairs={{0,48},{16,0},{32,16},{48,32},{1,49},{17,1},{33,17},{49,33},{2,50}... | collective-permute-start | bytes 479240 | tf_op jit(solution)/shard_map/ppermute | solution.py:743
  18.1 2.7 %collective-permute-done.2.yl = f32[3,104,128]{2,1,0:T(8,128)S(1)} collective-permute-done((f32[3,104,128]{2,1,0:T(8,128)S(1)}, f32[3,104,128]{2,1,0:T(8,128)S(1)}, u32[]{:S(2)}, u32[]{:S(2)}) %collective-permute-start.2) | collective-permute-done | bytes 159776 | tf_op jit(solution)/shard_map/ppermute | solution.py:742
  20.9 3.1 %collective-permute-start.4 = (f32[6,3,32,128]{3,2,1,0:T(8,128)S(1)}, f32[6,3,32,128]{3,2,1,0:T(8,128)S(1)}, u32[]{:S(2)}, u32[]{:S(2)}) collective-permute-start(f32[6,3,32,128]{3,2,1,0:T(8,128)S(1)} %shard_map.54), channel_id=1, source_target_pairs={{0,64},{64,0},{1,65},{65,1},{2,66},{66,2},{3,67},{67,3},{4,68},{68... | collective-permute-start | bytes 884744 | tf_op jit(solution)/shard_map/ppermute | solution.py:748
  24.0 0.9 shard_map.53.win
  25.2 3.0 %shard_map.55 = (f32[54,32,128]{2,1,0:T(8,128)S(1)}, f32[54,32,128]{2,1,0:T(8,128)S(1)}, f32[54,32,128]{2,1,0:T(8,128)S(1)}, f32[56,32,128]{2,1,0:T(8,128)S(1)},...) custom-call(f32[3,48,32,128]{3,2,1,0:T(8,128)S(1)} %shard_map.53.win, ...), custom_call_target="tpu_custom_call" | custom-call | tf_op jit(solution)/shard_map/pallas_call | solution.py:54
  28.3 4.9 %collective-permute-start.6 = (f32[6,24,128]{2,1,0:T(8,128)S(1)}, f32[6,24,128]{2,1,0:T(8,128)S(1)}, u32[]{:S(2)}, u32[]{:S(2)}) collective-permute-start(f32[6,24,128]{2,1,0:T(8,128)S(1)} %get-tuple-element.37), channel_id=1, source_target_pairs={{0,15},{1,0},{2,1},{3,2},{4,3},{5,4},{6,5},{7,6},{8,7},{9,8},{10,9... | collective-permute-start | bytes 221192 | tf_op jit(solution)/shard_map/ppermute | solution.py:743
  33.2 2.0 %collective-permute-done.5.zl = f32[6,24,128]{2,1,0:T(8,128)S(1)} collective-permute-done((f32[6,24,128]{2,1,0:T(8,128)S(1)}, f32[6,24,128]{2,1,0:T(8,128)S(1)}, u32[]{:S(2)}, u32[]{:S(2)}) %collective-permute-start.5) | collective-permute-done | bytes 73760 | tf_op jit(solution)/shard_map/ppermute | solution.py:742
  35.8 1.3 %collective-permute-start.7 = (f32[12,24,128]{2,1,0:T(8,128)S(1)}, f32[12,24,128]{2,1,0:T(8,128)S(1)}, u32[]{:S(2)}, u32[]{:S(2)}) collective-permute-start(f32[12,24,128]{2,1,0:T(8,128)S(1)} %get-tuple-element.38), channel_id=1, source_target_pairs={{0,16},{16,32},{32,48},{48,0},{1,17},{17,33},{33,49},{49,1},{2,18}... | collective-permute-start | bytes 442376 | tf_op jit(solution)/shard_map/ppermute | solution.py:742
  37.1 1.5 %collective-permute-start.8 = (f32[12,24,128]{2,1,0:T(8,128)S(1)}, f32[12,24,128]{2,1,0:T(8,128)S(1)}, u32[]{:S(2)}, u32[]{:S(2)}) collective-permute-start(f32[12,24,128]{2,1,0:T(8,128)S(1)} %get-tuple-element.39), channel_id=1, source_target_pairs={{0,48},{16,0},{32,16},{48,32},{1,49},{17,1},{33,17},{49,33},{2,50}... | collective-permute-start | bytes 442376 | tf_op jit(solution)/shard_map/ppermute | solution.py:743
  38.6 2.5 %collective-permute-done.7.yl = f32[12,24,128]{2,1,0:T(8,128)S(1)} collective-permute-done((f32[12,24,128]{2,1,0:T(8,128)S(1)}, f32[12,24,128]{2,1,0:T(8,128)S(1)}, u32[]{:S(2)}, u32[]{:S(2)}) %collective-permute-start.7) | collective-permute-done | bytes 147488 | tf_op jit(solution)/shard_map/ppermute | solution.py:742
  41.1 0.7 shard_map.58
  41.8 2.7 %collective-permute-start.9 = (f32[12,2,24,128]{3,2,1,0:T(8,128)S(1)}, f32[12,2,24,128]{3,2,1,0:T(8,128)S(1)}, u32[]{:S(2)}, u32[]{:S(2)}) collective-permute-start(f32[12,2,24,128]{3,2,1,0:T(8,128)S(1)} %shard_map.58), channel_id=1, source_target_pairs={{0,64},{64,0},{1,65},{65,1},{2,66},{66,2},{3,67},{67,3},{4,68},{68... | collective-permute-start | bytes 884744 | tf_op jit(solution)/shard_map/ppermute | solution.py:748
  44.5 0.9 %shard_map.57.win = f32[2,24,24,128]{3,2,1,0:T(8,128)S(1)} custom-call(f32[24,12,128]{2,1,0:T(8,128)S(1)} %get-tuple-element.35.f1, f32[24,12,128]{2,1,0:T(8,128)S(1)} %get-tuple-element.31.r1, f32[6,24,128]{2,1,0:T(8,128)S(1)} %collective-permute-done.5.zl, f32[6,24,128]{2,1,0:T(8,128)S(1)} %collective-permute-done.6.zh, ...), custom_call_target="tpu_custom_call" | custom-call | tf_op jit(solution)/shard_map/pallas_call | solution.py:54
  45.7 2.5 %shard_map.59 = (f32[36,24,128]{2,1,0:T(8,128)S(1)}, f32[36,24,128]{2,1,0:T(8,128)S(1)}, f32[38,24,128]{2,1,0:T(8,128)S(1)}, f32[18,32,128]{2,1,0:T(8,128)S(1)},...) custom-call(f32[2,24,24,128]{3,2,1,0:T(8,128)S(1)} %shard_map.57.win, ...), custom_call_target="tpu_custom_call" | custom-call | tf_op jit(solution)/shard_map/pallas_call | solution.py:54
  48.2 19.5 %all_to_all.16 = f32[128,4,128]{2,1,0:T(4,128)S(1)} all-to-all(f32[128,4,128]{2,1,0:T(4,128)S(1)} %bitcast.8), channel_id=1, replica_groups=mesh['gx'=2,'gy'=4,'gz'=16] {'gx','gy','gz'}, dimensions={0} | all-to-all | bytes 524288 | tf_op jit(solution)/shard_map/all_to_all | solution.py:792
  67.7 6.8 %shard_map.60 = (f32[48,24,128]{2,1,0:T(8,128)S(1)}, f32[48,24,128]{2,1,0:T(8,128)S(1)}, f32[128,128]{1,0:T(8,128)S(1)}) custom-call(f32[512,128]{1,0:T(8,128)S(1)} %bitcast.6, bf16[10,256,128]{2,1,0:T(8,128)(2,1)S(1)} %get-tuple-element.34.maps, f32[18,32,128]{2,1,0:T(8,128)S(1)} %get-tuple-element.41.f2, f32[18,32,128]{2,1,0:T(8,128)S(1)} %get-tuple-element.42.c2, ...), custom_call_target="tpu_custom_call" | custom-call | tf_op jit(solution)/shard_map/pallas_call | solution.py:54
  74.5 14.3 %all_to_all.17 = f32[128,1,128]{2,1,0:T(1,128)S(1)} all-to-all(f32[128,1,128]{2,1,0:T(1,128)S(1)} %bitcast.9), channel_id=1, replica_groups=mesh['gx'=2,'gy'=4,'gz'=16] {'gx','gy','gz'}, dimensions={0} | all-to-all | bytes 131072 | tf_op jit(solution)/shard_map/all_to_all | solution.py:806
  88.8 1.7 %shard_map.61 = (f32[48,48,48]{2,1,0:T(8,128)}, f32[48,48,48]{2,1,0:T(8,128)}) custom-call(f32[128,128]{1,0:T(8,128)S(1)} %bitcast.7, f32[3,48,24,128]{3,2,1,0:T(8,128)S(1)} %get-tuple-element.28.own, f32[48,24,128]{2,1,0:T(8,128)S(1)} %get-tuple-element.52.z, f32[48,24,128]{2,1,0:T(8,128)S(1)} %get-tuple-element.53.az, ...), custom_call_target="tpu_custom_call" | custom-call | tf_op jit(solution)/shard_map/pallas_call | solution.py:54
  (10 shorter events, 1.9 us)
Async XLA Ops:
  4.2 10.1 %collective-permute-start = (f32[10,24,128]{2,1,0:T(8,128)S(1)}, f32[10,24,128]{2,1,0:T(8,128)S(1)}, u32[]{:S(2)}, u32[]{:S(2)}) collective-permute-start(f32[10,24,128]{2,1,0:T(8,128)S(1)} %get-tuple-element.29), channel_id=1, source_target_pairs={{0,1},{1,2},{2,3},{3,4},{4,5},{5,6},{6,7},{7,8},{8,9},{9,10},{10,1... | collective-permute-start | bytes 368648 | tf_op jit(solution)/shard_map/ppermute | solution.py:742
  6.3 7.9 %collective-permute-start.1 = (f32[10,24,128]{2,1,0:T(8,128)S(1)}, f32[10,24,128]{2,1,0:T(8,128)S(1)}, u32[]{:S(2)}, u32[]{:S(2)}) collective-permute-start(f32[10,24,128]{2,1,0:T(8,128)S(1)} %get-tuple-element.30), channel_id=1, source_target_pairs={{0,15},{1,0},{2,1},{3,2},{4,3},{5,4},{6,5},{7,6},{8,7},{9,8},{10,9... | collective-permute-start | bytes 368648 | tf_op jit(solution)/shard_map/ppermute | solution.py:743
  15.3 5.4 %collective-permute-start.2 = (f32[3,104,128]{2,1,0:T(8,128)S(1)}, f32[3,104,128]{2,1,0:T(8,128)S(1)}, u32[]{:S(2)}, u32[]{:S(2)}) collective-permute-start(f32[3,104,128]{2,1,0:T(8,128)S(1)} %get-tuple-element.32), channel_id=1, source_target_pairs={{0,16},{16,32},{32,48},{48,0},{1,17},{17,33},{33,49},{49,1},{2,18}... | collective-permute-start | bytes 479240 | tf_op jit(solution)/shard_map/ppermute | solution.py:742
  16.6 4.1 %collective-permute-start.3 = (f32[3,104,128]{2,1,0:T(8,128)S(1)}, f32[3,104,128]{2,1,0:T(8,128)S(1)}, u32[]{:S(2)}, u32[]{:S(2)}) collective-permute-start(f32[3,104,128]{2,1,0:T(8,128)S(1)} %get-tuple-element.33), channel_id=1, source_target_pairs={{0,48},{16,0},{32,16},{48,32},{1,49},{17,1},{33,17},{49,33},{2,50}... | collective-permute-start | bytes 479240 | tf_op jit(solution)/shard_map/ppermute | solution.py:743
  20.9 4.3 %collective-permute-start.4 = (f32[6,3,32,128]{3,2,1,0:T(8,128)S(1)}, f32[6,3,32,128]{3,2,1,0:T(8,128)S(1)}, u32[]{:S(2)}, u32[]{:S(2)}) collective-permute-start(f32[6,3,32,128]{3,2,1,0:T(8,128)S(1)} %shard_map.54), channel_id=1, source_target_pairs={{0,64},{64,0},{1,65},{65,1},{2,66},{66,2},{3,67},{67,3},{4,68},{68... | collective-permute-start | bytes 884744 | tf_op jit(solution)/shard_map/ppermute | solution.py:748
  28.2 7.0 %collective-permute-start.5 = (f32[6,24,128]{2,1,0:T(8,128)S(1)}, f32[6,24,128]{2,1,0:T(8,128)S(1)}, u32[]{:S(2)}, u32[]{:S(2)}) collective-permute-start(f32[6,24,128]{2,1,0:T(8,128)S(1)} %get-tuple-element.36), channel_id=1, source_target_pairs={{0,1},{1,2},{2,3},{3,4},{4,5},{5,6},{6,7},{7,8},{8,9},{9,10},{10,1... | collective-permute-start | bytes 221192 | tf_op jit(solution)/shard_map/ppermute | solution.py:742
  28.3 6.9 %collective-permute-start.6 = (f32[6,24,128]{2,1,0:T(8,128)S(1)}, f32[6,24,128]{2,1,0:T(8,128)S(1)}, u32[]{:S(2)}, u32[]{:S(2)}) collective-permute-start(f32[6,24,128]{2,1,0:T(8,128)S(1)} %get-tuple-element.37), channel_id=1, source_target_pairs={{0,15},{1,0},{2,1},{3,2},{4,3},{5,4},{6,5},{7,6},{8,7},{9,8},{10,9... | collective-permute-start | bytes 221192 | tf_op jit(solution)/shard_map/ppermute | solution.py:743
  35.8 5.3 %collective-permute-start.7 = (f32[12,24,128]{2,1,0:T(8,128)S(1)}, f32[12,24,128]{2,1,0:T(8,128)S(1)}, u32[]{:S(2)}, u32[]{:S(2)}) collective-permute-start(f32[12,24,128]{2,1,0:T(8,128)S(1)} %get-tuple-element.38), channel_id=1, source_target_pairs={{0,16},{16,32},{32,48},{48,0},{1,17},{17,33},{33,49},{49,1},{2,18}... | collective-permute-start | bytes 442376 | tf_op jit(solution)/shard_map/ppermute | solution.py:742
  37.1 4.0 %collective-permute-start.8 = (f32[12,24,128]{2,1,0:T(8,128)S(1)}, f32[12,24,128]{2,1,0:T(8,128)S(1)}, u32[]{:S(2)}, u32[]{:S(2)}) collective-permute-start(f32[12,24,128]{2,1,0:T(8,128)S(1)} %get-tuple-element.39), channel_id=1, source_target_pairs={{0,48},{16,0},{32,16},{48,32},{1,49},{17,1},{33,17},{49,33},{2,50}... | collective-permute-start | bytes 442376 | tf_op jit(solution)/shard_map/ppermute | solution.py:743
  41.8 3.9 %collective-permute-start.9 = (f32[12,2,24,128]{3,2,1,0:T(8,128)S(1)}, f32[12,2,24,128]{3,2,1,0:T(8,128)S(1)}, u32[]{:S(2)}, u32[]{:S(2)}) collective-permute-start(f32[12,2,24,128]{3,2,1,0:T(8,128)S(1)} %shard_map.58), channel_id=1, source_target_pairs={{0,64},{64,0},{1,65},{65,1},{2,66},{66,2},{3,67},{67,3},{4,68},{68... | collective-permute-start | bytes 884744 | tf_op jit(solution)/shard_map/ppermute | solution.py:748

commit v10 on v9

--- a/solution.py
+++ b/solution.py
@@ -100,21 +100,26 @@
     return high, low, jnp.where(gy > 0, 1.0, 0.0), jnp.where(gy < ny - 1, 1.0, 0.0)
 
 
-def zslot(sp, v, at, h, hi, lo):
+def ztile(sp, items):
     l = lanes(sp.half)
-    hi = jnp.where((l - (at - sp.n - h)) % 64 < h, roll(v, at - 2 * sp.n, 1), hi)
-    lo = jnp.where((l - at) % 64 < h, roll(v, at, 1), lo)
-    return hi, lo
+    hi = [jnp.zeros((sp.half, 128), F32)] * 2
+    lo = list(hi)
+    for k, (v, at, h) in enumerate(items):
+        r = roll(v, at, 1)
+        hi[k % 2] = jnp.where(((l + (64 - (at + sp.n - h) % 64)) & 63) < h, r, hi[k % 2])
+        lo[k % 2] = jnp.where(((l + (64 - at)) & 63) < h, r, lo[k % 2])
+    return roll(hi[0] + hi[1], -2 * sp.n, 1), lo[0] + lo[1]
 
 
 def ztile1(own, hi_ref, lo_ref, g):
     sp = L1
     for t in range(sp.st):
-        hi = lo = jnp.zeros((sp.half, 128), F32)
-        for k in range(sp.kp):
-            for a in range(sp.na):
-                v = own(t * (sp.n // sp.st) + g * sp.kp + k, a)
-                hi, lo = zslot(sp, v, sp.h * (k * sp.na + a), sp.h, hi, lo)
+        items = [
+            (own(t * (sp.n // sp.st) + g * sp.kp + k, a), sp.h * (k * sp.na + a), sp.h)
+            for k in range(sp.kp)
+            for a in range(sp.na)
+        ]
+        hi, lo = ztile(sp, items)
         hi_ref[g, t * sp.half : (t + 1) * sp.half, :] = hi
         lo_ref[g, t * sp.half : (t + 1) * sp.half, :] = lo
 
@@ -133,28 +138,46 @@
     return jnp.where(q < sp.n, own(x, a)[b:e], jnp.where((q < top) | (q >= bottom), beside, 0.0))
 
 
-def ypack(sp, own, zl, zh, up_ref, dn_ref, u):
+def ypack0(own, turned, zl, zh, up_ref, dn_ref):
+    top, bottom, _, _ = edge(L0, place())
+    l = lanes(8)
+    q = l & 63
+    up = upper(L0, 8)
+
+    def beside(x, a, b, turn):
+        g, _, at = L0.slot(x, a)
+        v = jnp.where(((l + (64 - at)) & 63) < L0.hs[a], zh[g, b : b + 8, :], zl[g, b : b + 8, :])
+        v = roll(v, (L0.n + turn + 128 - at) & 127, 1)
+        return jnp.where((q < top) | (q >= bottom), v, 0.0)
+
+    def some(i):
+        for k in range(8):
+            p = 8 * i + k
+            for a in range(3):
+                h = L0.hs[a]
+                for ref, b, s in ((up_ref, 16, 8 - h), (dn_ref, 0, 0)):
+                    even = jnp.where(q < L0.n, own[a, 2 * p, b : b + 8, :], beside(2 * p, a, b, 0))
+                    odd = jnp.where(q < L0.n, turned[a, p, b // 2 : b // 2 + 8, :], beside(2 * p + 1, a, b, 64))
+                    v = jnp.where(up, even, odd) if b else jnp.where(up, odd, even)
+                    ref[i, pl.ds(YBASE[a] + k, h, stride=8), :] = v[s : s + h]
+
+    loop(3, some)
+
+
+def ypack1(own, zl, zh, up_ref, dn_ref, u):
+    sp = L1
     half = sp.half
     top, bottom, _, _ = edge(sp, place())
 
-    def some(i):
-        for k in range(u):
-            p = i * u + k
-            for a in range(sp.na):
-                h = sp.hs[a]
-                up0 = (half - h) // 8 * 8
-                dn1 = min(half, -(-h // 8) * 8)
-                for ref, b, e, s, t, swap in ((up_ref, up0, half, half - h - up0, half - up0, False), (dn_ref, 0, dn1, 0, h, True)):
-                    even = merged(sp, own, zl, zh, 2 * p, a, b, e, top, bottom)
-                    odd = roll(merged(sp, own, zl, zh, 2 * p + 1, a, b, e, top, bottom), 64, 1)
-                    first, second = (odd, even) if swap else (even, odd)
-                    v = jnp.where(upper(sp, e - b), first, second)[s:t]
-                    if sp is L0:
-                        ref[i, pl.ds(YBASE[a] + k, h, stride=8), :] = v
-                    else:
-                        ref[p, a * h : (a + 1) * h, :] = v
-
-    loop(half // u, some)
+    def pair(p):
+        for a in range(sp.na):
+            even = merged(sp, own, zl, zh, 2 * p, a, 0, half, top, bottom)
+            odd = roll(merged(sp, own, zl, zh, 2 * p + 1, a, 0, half, top, bottom), 64, 1)
+            up = upper(sp, half)
+            up_ref[p, a * half : (a + 1) * half, :] = jnp.where(up, even, odd)
+            dn_ref[p, a * half : (a + 1) * half, :] = jnp.where(up, odd, even)
+
+    loop(half, pair, u)
 
 
 def y_tiles0(yl, yh, g, t, a):
@@ -210,9 +233,10 @@
     s = ref[x] + ref[x + 2]
     sub = lax.broadcasted_iota(jnp.int32, (8, 128), 0)
     seam = roll(jnp.where(sub == 0, c[0:8], c[R - 8 : R]), 64, 1)
-    up, down = roll(c, R - 1, 0), roll(c, 1, 0)
-    up = jnp.concatenate([up[: R - 8], jnp.where(sub == 7, roll(seam, 7, 0), up[R - 8 :])], axis=0)
-    down = jnp.concatenate([jnp.where(sub == 0, roll(seam, 1, 0), down[0:8]), down[8:]], axis=0)
+    last = jnp.where(sub == 7, roll(seam, 7, 0), roll(c[R - 8 :], 7, 0))
+    first = jnp.where(sub == 0, roll(seam, 1, 0), roll(c[0:8], 1, 0))
+    up = jnp.concatenate([ref[x + 1, 1 : R - 7, :], last], axis=0)
+    down = jnp.concatenate([first, ref[x + 1, 7 : R - 1, :]], axis=0)
     s = s + (up + down)
     return s + (roll(c, 1, 1) + roll(c, 127, 1))
 
@@ -342,27 +366,25 @@
         for i in range(parts[a]):
             copy(a, ref, i).start()
 
-    for a, ref in enumerate(refs):
+    def pack(a, i):
         h = L0.hs[a]
         many = 64 // h
-
-        def some(i, a=a, ref=ref, h=h, many=many):
-            copy(a, ref, i).wait()
-            hi_tile = lo_tile = jnp.zeros((24, 128), F32)
-            for k in range(many):
-                x = i * many + k
-                own[a, x, :, 0:48] = raw[a, x, 0:24, :]
-                own[a, x, :, 64:112] = raw[a, x, 24:48, :]
-            for k in range(many):
-                hi_tile, lo_tile = zslot(L0, own[a, i * many + k], h * k, h, hi_tile, lo_tile)
-            hi[ZBASE[a] + i] = hi_tile
-            lo[ZBASE[a] + i] = lo_tile
-
-        loop(parts[a], some)
-
-
-def k_ypack0(own, zl, zh, r1, up, dn):
-    ypack(L0, lambda x, a: own[a, x], zl, zh, up, dn, 8)
+        hi[ZBASE[a] + i], lo[ZBASE[a] + i] = ztile(L0, [(own[a, i * many + k], h * k, h) for k in range(many)])
+
+    steps = [(a, ref, i) for a, ref in enumerate(refs) for i in range(parts[a])]
+    for n, (a, ref, i) in enumerate(steps):
+        copy(a, ref, i).wait()
+        if n:
+            pack(steps[n - 1][0], steps[n - 1][2])
+        many = 64 // L0.hs[a]
+        for x in range(i * many, i * many + many):
+            own[a, x, :, 0:48] = raw[a, x, 0:24, :]
+            own[a, x, :, 64:112] = raw[a, x, 24:48, :]
+    pack(steps[-1][0], steps[-1][2])
+
+
+def k_ypack0(own, turned, zl, zh, up, dn):
+    ypack0(own, turned, zl, zh, up, dn)
 
 
 def k_xpack0(own, zl, zh, yl, yh, out):
@@ -415,7 +437,14 @@
     loop(24, keep, 6)
 
 
-def k_early(own, r1, maps, tmp, acc):
+def k_early(own, turned, r1, maps, tmp, acc):
+    def turn(p):
+        for a in range(3):
+            v = own[a, 2 * p + 1]
+            turned[a, p, 0:8, :] = roll(v[0:8], 64, 1)
+            turned[a, p, 8:16, :] = roll(v[16:24], 64, 1)
+
+    loop(24, turn, 4)
     all_maps(maps, lax.axis_index("gz"))
     mine = lanes(24) % 64 < 48
     half_own(lambda x: jnp.where(mine, own[2, 2 * x] + own[2, 2 * x + 1], 0.0), tmp, acc, r1, 4, maps[OWN])
@@ -465,7 +494,7 @@
 
 def k_ypack1(f1, r1, zl, zh, up, dn):
     both = (f1, r1)
-    ypack(L1, lambda x, a: both[a][x], zl, zh, up, dn, 6)
+    ypack1(lambda x, a: both[a][x], zl, zh, up, dn, 6)
 
 
 def k_windows1(f1, r1, zl, zh, yl, yh, out, spare):
@@ -761,10 +790,13 @@
         far_in=True,
     )
     zl, zh = ring(hi, lo, "gz")
-    r1, maps = run(
-        k_early, (sds(24, 12, 128), sds(10, 256, 128, dtype=jnp.bfloat16)), (own,), [(24, 24, 128), (24, 16, 128)]
+    turned, r1, maps = run(
+        k_early,
+        (sds(3, 24, 16, 128), sds(24, 12, 128), sds(10, 256, 128, dtype=jnp.bfloat16)),
+        (own,),
+        [(24, 24, 128), (24, 16, 128)],
     )
-    up, dn = run(k_ypack0, (sds(*L0.yshape),) * 2, (own, zl, zh, r1))
+    up, dn = run(k_ypack0, (sds(*L0.yshape),) * 2, (own, turned, zl, zh))
     yl, yh = ring(up, dn, "gy")
     xr = swap(run(k_xpack0, sds(*L0.xshape), (own, zl, zh, yl, yh)))
     win = run(k_windows0, sds(3, 48, 32, 128), (own, zl, zh, yl, yh))

time: 90.8 us -> 89.9 us (0.990)
  no operation moved by 1% of the time
where the time goes in v10:
time: 89.9 us; the launch traced here: 89.7 us
  blocking collectives  33.8 us (38%)
  starting transfers between devices  23.5 us (26%)
  Pallas kernels  21.9 us (24%)
  waiting for transfers between devices  9.63 us (11%)
    pallas_call x12, Pallas kernels, run(): pl.pallas_call(kernel, out_shape=outs, in_specs=[hbm if far_in else vmem]...  21.9 us
    all_to_all x1, blocking collectives, body(): g = lax.all_to_all(g, ALL, 0, 0, tiled=True)  19.5 us
    all_to_all x1, blocking collectives, body(): lax.all_to_all(sums.reshape(count, 1, 128), ALL, 0, 0, tiled=True)  14.3 us
    ppermute x4, starting transfers between devices, ring(): high = lax.ppermute(dn, axis, [(i, (i - 1) % n) for i in range(n)])  12.9 us
    ppermute x4, waiting for transfers between devices, ring(): low = lax.ppermute(up, axis, [(i, (i + 1) % n) for i in range(n)])  9.03 us
    ppermute x2, starting transfers between devices, swap(): return lax.ppermute(v, 'gx', [(0, 1), (1, 0)])  5.79 us
    ppermute x4, starting transfers between devices, ring(): low = lax.ppermute(up, axis, [(i, (i + 1) % n) for i in range(n)])  4.81 us
  transfers between devices with their start and end apart: 10, of which 6 were waited for; matrix products, arithmetic and copies ran while one was open for 0% of the time, Pallas kernels for 3%

profile of v10, /device:TPU:1, one launch (start us, length us, event | category | flops | bytes accessed | tf_op | source)
XLA Modules:
  0.0 89.7 jit_solution(6000836589227755859)
XLA Ops:
  0.6 3.1 %shard_map.50 = (f32[10,24,128]{2,1,0:T(8,128)S(1)}, f32[10,24,128]{2,1,0:T(8,128)S(1)}, f32[3,48,24,128]{3,2,1,0:T(8,128)S(1)}) custom-call(f32[48,48,48]{2,1,0:T(8,128)} %x0.1, f32[48,48,48]{2,1,0:T(8,128)} %b.1, f32[48,48,48]{2,1,0:T(8,128)} %rea.1), custom_call_target="tpu_custom_call" | custom-call | tf_op jit(solution)/shard_map/pallas_call | solution.py:54
  3.7 2.2 %collective-permute-start = (f32[10,24,128]{2,1,0:T(8,128)S(1)}, f32[10,24,128]{2,1,0:T(8,128)S(1)}, u32[]{:S(2)}, u32[]{:S(2)}) collective-permute-start(f32[10,24,128]{2,1,0:T(8,128)S(1)} %get-tuple-element.30), channel_id=1, source_target_pairs={{0,1},{1,2},{2,3},{3,4},{4,5},{5,6},{6,7},{7,8},{8,9},{9,10},{10,1... | collective-permute-start | bytes 368648 | tf_op jit(solution)/shard_map/ppermute | solution.py:771
  5.9 5.0 %collective-permute-start.1 = (f32[10,24,128]{2,1,0:T(8,128)S(1)}, f32[10,24,128]{2,1,0:T(8,128)S(1)}, u32[]{:S(2)}, u32[]{:S(2)}) collective-permute-start(f32[10,24,128]{2,1,0:T(8,128)S(1)} %get-tuple-element.31), channel_id=1, source_target_pairs={{0,15},{1,0},{2,1},{3,2},{4,3},{5,4},{6,5},{7,6},{8,7},{9,8},{10,9... | collective-permute-start | bytes 368648 | tf_op jit(solution)/shard_map/ppermute | solution.py:772
  10.9 1.0 %shard_map.51 = (f32[3,24,16,128]{3,2,1,0:T(8,128)S(1)}, f32[24,12,128]{2,1,0:T(8,128)S(1)}, bf16[10,256,128]{2,1,0:T(8,128)(2,1)S(1)}) custom-call(f32[3,48,24,128]{3,2,1,0:T(8,128)S(1)} %get-tuple-element.29.own), custom_call_target="tpu_custom_call" | custom-call | tf_op jit(solution)/shard_map/pallas_call | solution.py:54
  11.9 1.9 %collective-permute-done.zl = f32[10,24,128]{2,1,0:T(8,128)S(1)} collective-permute-done((f32[10,24,128]{2,1,0:T(8,128)S(1)}, f32[10,24,128]{2,1,0:T(8,128)S(1)}, u32[]{:S(2)}, u32[]{:S(2)}) %collective-permute-start) | collective-permute-done | bytes 122912 | tf_op jit(solution)/shard_map/ppermute | solution.py:771
  13.8 0.7 shard_map.52
  14.5 1.3 %collective-permute-start.2 = (f32[3,104,128]{2,1,0:T(8,128)S(1)}, f32[3,104,128]{2,1,0:T(8,128)S(1)}, u32[]{:S(2)}, u32[]{:S(2)}) collective-permute-start(f32[3,104,128]{2,1,0:T(8,128)S(1)} %get-tuple-element.33), channel_id=1, source_target_pairs={{0,16},{16,32},{32,48},{48,0},{1,17},{17,33},{33,49},{49,1},{2,18}... | collective-permute-start | bytes 479240 | tf_op jit(solution)/shard_map/ppermute | solution.py:771
  15.8 1.5 %collective-permute-start.3 = (f32[3,104,128]{2,1,0:T(8,128)S(1)}, f32[3,104,128]{2,1,0:T(8,128)S(1)}, u32[]{:S(2)}, u32[]{:S(2)}) collective-permute-start(f32[3,104,128]{2,1,0:T(8,128)S(1)} %get-tuple-element.34), channel_id=1, source_target_pairs={{0,48},{16,0},{32,16},{48,32},{1,49},{17,1},{33,17},{49,33},{2,50}... | collective-permute-start | bytes 479240 | tf_op jit(solution)/shard_map/ppermute | solution.py:772
  17.3 2.7 %collective-permute-done.2.yl = f32[3,104,128]{2,1,0:T(8,128)S(1)} collective-permute-done((f32[3,104,128]{2,1,0:T(8,128)S(1)}, f32[3,104,128]{2,1,0:T(8,128)S(1)}, u32[]{:S(2)}, u32[]{:S(2)}) %collective-permute-start.2) | collective-permute-done | bytes 159776 | tf_op jit(solution)/shard_map/ppermute | solution.py:771
  20.1 3.1 %collective-permute-start.4 = (f32[6,3,32,128]{3,2,1,0:T(8,128)S(1)}, f32[6,3,32,128]{3,2,1,0:T(8,128)S(1)}, u32[]{:S(2)}, u32[]{:S(2)}) collective-permute-start(f32[6,3,32,128]{3,2,1,0:T(8,128)S(1)} %shard_map.54), channel_id=1, source_target_pairs={{0,64},{64,0},{1,65},{65,1},{2,66},{66,2},{3,67},{67,3},{4,68},{68... | collective-permute-start | bytes 884744 | tf_op jit(solution)/shard_map/ppermute | solution.py:777
  23.2 0.9 shard_map.53.win
  24.4 3.1 %shard_map.55 = (f32[54,32,128]{2,1,0:T(8,128)S(1)}, f32[54,32,128]{2,1,0:T(8,128)S(1)}, f32[54,32,128]{2,1,0:T(8,128)S(1)}, f32[56,32,128]{2,1,0:T(8,128)S(1)},...) custom-call(f32[3,48,32,128]{3,2,1,0:T(8,128)S(1)} %shard_map.53.win, ...), custom_call_target="tpu_custom_call" | custom-call | tf_op jit(solution)/shard_map/pallas_call | solution.py:54
  27.6 4.9 %collective-permute-start.6 = (f32[6,24,128]{2,1,0:T(8,128)S(1)}, f32[6,24,128]{2,1,0:T(8,128)S(1)}, u32[]{:S(2)}, u32[]{:S(2)}) collective-permute-start(f32[6,24,128]{2,1,0:T(8,128)S(1)} %get-tuple-element.39), channel_id=1, source_target_pairs={{0,15},{1,0},{2,1},{3,2},{4,3},{5,4},{6,5},{7,6},{8,7},{9,8},{10,9... | collective-permute-start | bytes 221192 | tf_op jit(solution)/shard_map/ppermute | solution.py:772
  32.5 2.0 %collective-permute-done.5.zl = f32[6,24,128]{2,1,0:T(8,128)S(1)} collective-permute-done((f32[6,24,128]{2,1,0:T(8,128)S(1)}, f32[6,24,128]{2,1,0:T(8,128)S(1)}, u32[]{:S(2)}, u32[]{:S(2)}) %collective-permute-start.5) | collective-permute-done | bytes 73760 | tf_op jit(solution)/shard_map/ppermute | solution.py:771
  34.9 1.3 %collective-permute-start.7 = (f32[12,24,128]{2,1,0:T(8,128)S(1)}, f32[12,24,128]{2,1,0:T(8,128)S(1)}, u32[]{:S(2)}, u32[]{:S(2)}) collective-permute-start(f32[12,24,128]{2,1,0:T(8,128)S(1)} %get-tuple-element.40), channel_id=1, source_target_pairs={{0,16},{16,32},{32,48},{48,0},{1,17},{17,33},{33,49},{49,1},{2,18}... | collective-permute-start | bytes 442376 | tf_op jit(solution)/shard_map/ppermute | solution.py:771
  36.2 1.5 %collective-permute-start.8 = (f32[12,24,128]{2,1,0:T(8,128)S(1)}, f32[12,24,128]{2,1,0:T(8,128)S(1)}, u32[]{:S(2)}, u32[]{:S(2)}) collective-permute-start(f32[12,24,128]{2,1,0:T(8,128)S(1)} %get-tuple-element.41), channel_id=1, source_target_pairs={{0,48},{16,0},{32,16},{48,32},{1,49},{17,1},{33,17},{49,33},{2,50}... | collective-permute-start | bytes 442376 | tf_op jit(solution)/shard_map/ppermute | solution.py:772
  37.7 2.5 %collective-permute-done.7.yl = f32[12,24,128]{2,1,0:T(8,128)S(1)} collective-permute-done((f32[12,24,128]{2,1,0:T(8,128)S(1)}, f32[12,24,128]{2,1,0:T(8,128)S(1)}, u32[]{:S(2)}, u32[]{:S(2)}) %collective-permute-start.7) | collective-permute-done | bytes 147488 | tf_op jit(solution)/shard_map/ppermute | solution.py:771
  40.9 2.7 %collective-permute-start.9 = (f32[12,2,24,128]{3,2,1,0:T(8,128)S(1)}, f32[12,2,24,128]{3,2,1,0:T(8,128)S(1)}, u32[]{:S(2)}, u32[]{:S(2)}) collective-permute-start(f32[12,2,24,128]{3,2,1,0:T(8,128)S(1)} %shard_map.58), channel_id=1, source_target_pairs={{0,64},{64,0},{1,65},{65,1},{2,66},{66,2},{3,67},{67,3},{4,68},{68... | collective-permute-start | bytes 884744 | tf_op jit(solution)/shard_map/ppermute | solution.py:777
  43.6 0.9 %shard_map.57.win = f32[2,24,24,128]{3,2,1,0:T(8,128)S(1)} custom-call(f32[24,12,128]{2,1,0:T(8,128)S(1)} %get-tuple-element.37.f1, f32[24,12,128]{2,1,0:T(8,128)S(1)} %get-tuple-element.35.r1, f32[6,24,128]{2,1,0:T(8,128)S(1)} %collective-permute-done.5.zl, f32[6,24,128]{2,1,0:T(8,128)S(1)} %collective-permute-done.6.zh, ...), custom_call_target="tpu_custom_call" | custom-call | tf_op jit(solution)/shard_map/pallas_call | solution.py:54
  44.8 2.5 %shard_map.59 = (f32[36,24,128]{2,1,0:T(8,128)S(1)}, f32[36,24,128]{2,1,0:T(8,128)S(1)}, f32[38,24,128]{2,1,0:T(8,128)S(1)}, f32[18,32,128]{2,1,0:T(8,128)S(1)},...) custom-call(f32[2,24,24,128]{3,2,1,0:T(8,128)S(1)} %shard_map.57.win, ...), custom_call_target="tpu_custom_call" | custom-call | tf_op jit(solution)/shard_map/pallas_call | solution.py:54
  47.3 19.5 %all_to_all.16 = f32[128,4,128]{2,1,0:T(4,128)S(1)} all-to-all(f32[128,4,128]{2,1,0:T(4,128)S(1)} %bitcast.8), channel_id=1, replica_groups=mesh['gx'=2,'gy'=4,'gz'=16] {'gx','gy','gz'}, dimensions={0} | all-to-all | bytes 524288 | tf_op jit(solution)/shard_map/all_to_all | solution.py:824
  66.8 6.8 %shard_map.60 = (f32[48,24,128]{2,1,0:T(8,128)S(1)}, f32[48,24,128]{2,1,0:T(8,128)S(1)}, f32[128,128]{1,0:T(8,128)S(1)}) custom-call(f32[512,128]{1,0:T(8,128)S(1)} %bitcast.6, bf16[10,256,128]{2,1,0:T(8,128)(2,1)S(1)} %get-tuple-element.36.maps, f32[18,32,128]{2,1,0:T(8,128)S(1)} %get-tuple-element.43.f2, f32[18,32,128]{2,1,0:T(8,128)S(1)} %get-tuple-element.44.c2, ...), custom_call_target="tpu_custom_call" | custom-call | tf_op jit(solution)/shard_map/pallas_call | solution.py:54
  73.6 14.3 %all_to_all.17 = f32[128,1,128]{2,1,0:T(1,128)S(1)} all-to-all(f32[128,1,128]{2,1,0:T(1,128)S(1)} %bitcast.9), channel_id=1, replica_groups=mesh['gx'=2,'gy'=4,'gz'=16] {'gx','gy','gz'}, dimensions={0} | all-to-all | bytes 131072 | tf_op jit(solution)/shard_map/all_to_all | solution.py:838
  87.9 1.7 %shard_map.61 = (f32[48,48,48]{2,1,0:T(8,128)}, f32[48,48,48]{2,1,0:T(8,128)}) custom-call(f32[128,128]{1,0:T(8,128)S(1)} %bitcast.7, f32[3,48,24,128]{3,2,1,0:T(8,128)S(1)} %get-tuple-element.29.own, f32[48,24,128]{2,1,0:T(8,128)S(1)} %get-tuple-element.54.z, f32[48,24,128]{2,1,0:T(8,128)S(1)} %get-tuple-element.55.az, ...), custom_call_target="tpu_custom_call" | custom-call | tf_op jit(solution)/shard_map/pallas_call | solution.py:54
  (10 shorter events, 1.9 us)
Async XLA Ops:
  3.7 10.1 %collective-permute-start = (f32[10,24,128]{2,1,0:T(8,128)S(1)}, f32[10,24,128]{2,1,0:T(8,128)S(1)}, u32[]{:S(2)}, u32[]{:S(2)}) collective-permute-start(f32[10,24,128]{2,1,0:T(8,128)S(1)} %get-tuple-element.30), channel_id=1, source_target_pairs={{0,1},{1,2},{2,3},{3,4},{4,5},{5,6},{6,7},{7,8},{8,9},{9,10},{10,1... | collective-permute-start | bytes 368648 | tf_op jit(solution)/shard_map/ppermute | solution.py:771
  5.9 7.9 %collective-permute-start.1 = (f32[10,24,128]{2,1,0:T(8,128)S(1)}, f32[10,24,128]{2,1,0:T(8,128)S(1)}, u32[]{:S(2)}, u32[]{:S(2)}) collective-permute-start(f32[10,24,128]{2,1,0:T(8,128)S(1)} %get-tuple-element.31), channel_id=1, source_target_pairs={{0,15},{1,0},{2,1},{3,2},{4,3},{5,4},{6,5},{7,6},{8,7},{9,8},{10,9... | collective-permute-start | bytes 368648 | tf_op jit(solution)/shard_map/ppermute | solution.py:772
  14.5 5.4 %collective-permute-start.2 = (f32[3,104,128]{2,1,0:T(8,128)S(1)}, f32[3,104,128]{2,1,0:T(8,128)S(1)}, u32[]{:S(2)}, u32[]{:S(2)}) collective-permute-start(f32[3,104,128]{2,1,0:T(8,128)S(1)} %get-tuple-element.33), channel_id=1, source_target_pairs={{0,16},{16,32},{32,48},{48,0},{1,17},{17,33},{33,49},{49,1},{2,18}... | collective-permute-start | bytes 479240 | tf_op jit(solution)/shard_map/ppermute | solution.py:771
  15.8 4.1 %collective-permute-start.3 = (f32[3,104,128]{2,1,0:T(8,128)S(1)}, f32[3,104,128]{2,1,0:T(8,128)S(1)}, u32[]{:S(2)}, u32[]{:S(2)}) collective-permute-start(f32[3,104,128]{2,1,0:T(8,128)S(1)} %get-tuple-element.34), channel_id=1, source_target_pairs={{0,48},{16,0},{32,16},{48,32},{1,49},{17,1},{33,17},{49,33},{2,50}... | collective-permute-start | bytes 479240 | tf_op jit(solution)/shard_map/ppermute | solution.py:772
  20.1 4.3 %collective-permute-start.4 = (f32[6,3,32,128]{3,2,1,0:T(8,128)S(1)}, f32[6,3,32,128]{3,2,1,0:T(8,128)S(1)}, u32[]{:S(2)}, u32[]{:S(2)}) collective-permute-start(f32[6,3,32,128]{3,2,1,0:T(8,128)S(1)} %shard_map.54), channel_id=1, source_target_pairs={{0,64},{64,0},{1,65},{65,1},{2,66},{66,2},{3,67},{67,3},{4,68},{68... | collective-permute-start | bytes 884744 | tf_op jit(solution)/shard_map/ppermute | solution.py:777
  27.5 7.0 %collective-permute-start.5 = (f32[6,24,128]{2,1,0:T(8,128)S(1)}, f32[6,24,128]{2,1,0:T(8,128)S(1)}, u32[]{:S(2)}, u32[]{:S(2)}) collective-permute-start(f32[6,24,128]{2,1,0:T(8,128)S(1)} %get-tuple-element.38), channel_id=1, source_target_pairs={{0,1},{1,2},{2,3},{3,4},{4,5},{5,6},{6,7},{7,8},{8,9},{9,10},{10,1... | collective-permute-start | bytes 221192 | tf_op jit(solution)/shard_map/ppermute | solution.py:771
  27.6 6.9 %collective-permute-start.6 = (f32[6,24,128]{2,1,0:T(8,128)S(1)}, f32[6,24,128]{2,1,0:T(8,128)S(1)}, u32[]{:S(2)}, u32[]{:S(2)}) collective-permute-start(f32[6,24,128]{2,1,0:T(8,128)S(1)} %get-tuple-element.39), channel_id=1, source_target_pairs={{0,15},{1,0},{2,1},{3,2},{4,3},{5,4},{6,5},{7,6},{8,7},{9,8},{10,9... | collective-permute-start | bytes 221192 | tf_op jit(solution)/shard_map/ppermute | solution.py:772
  34.9 5.3 %collective-permute-start.7 = (f32[12,24,128]{2,1,0:T(8,128)S(1)}, f32[12,24,128]{2,1,0:T(8,128)S(1)}, u32[]{:S(2)}, u32[]{:S(2)}) collective-permute-start(f32[12,24,128]{2,1,0:T(8,128)S(1)} %get-tuple-element.40), channel_id=1, source_target_pairs={{0,16},{16,32},{32,48},{48,0},{1,17},{17,33},{33,49},{49,1},{2,18}... | collective-permute-start | bytes 442376 | tf_op jit(solution)/shard_map/ppermute | solution.py:771
  36.2 4.0 %collective-permute-start.8 = (f32[12,24,128]{2,1,0:T(8,128)S(1)}, f32[12,24,128]{2,1,0:T(8,128)S(1)}, u32[]{:S(2)}, u32[]{:S(2)}) collective-permute-start(f32[12,24,128]{2,1,0:T(8,128)S(1)} %get-tuple-element.41), channel_id=1, source_target_pairs={{0,48},{16,0},{32,16},{48,32},{1,49},{17,1},{33,17},{49,33},{2,50}... | collective-permute-start | bytes 442376 | tf_op jit(solution)/shard_map/ppermute | solution.py:772
  40.9 3.9 %collective-permute-start.9 = (f32[12,2,24,128]{3,2,1,0:T(8,128)S(1)}, f32[12,2,24,128]{3,2,1,0:T(8,128)S(1)}, u32[]{:S(2)}, u32[]{:S(2)}) collective-permute-start(f32[12,2,24,128]{3,2,1,0:T(8,128)S(1)} %shard_map.58), channel_id=1, source_target_pairs={{0,64},{64,0},{1,65},{65,1},{2,66},{66,2},{3,67},{67,3},{4,68},{68... | collective-permute-start | bytes 884744 | tf_op jit(solution)/shard_map/ppermute | solution.py:777

commit v11 on v10

--- a/solution.py
+++ b/solution.py
@@ -189,14 +189,12 @@
     return rows(yl, YBASE[a] - 32), rows(yh, 40) if a == 1 else roll(rows(yh, 40), 4, 0)
 
 
-def plane0(own, zl, zh, tiles, x, a, dst, xw, ends, turn):
-    top, bottom, below, above = ends
-    sp = L0
-    m = merged(sp, own, zl, zh, x, a, 0, sp.half, top, bottom)
+def plane0(m, tiles, ends, turn):
+    _, _, below, above = ends
     low, high = tiles
     lower = jnp.concatenate([roll(low, turn, 1) * below, m], axis=0)
     higher = jnp.concatenate([m, roll(high, turn, 1) * above], axis=0)
-    dst[xw] = jnp.where(upper(sp, sp.R), higher, lower)
+    return jnp.where(upper(L0, L0.R), higher, lower)
 
 
 def plane1(own, zl, zh, yl, yh, x, a, dst, xw, ends, spare):
@@ -387,7 +385,7 @@
     ypack0(own, turned, zl, zh, up, dn)
 
 
-def k_xpack0(own, zl, zh, yl, yh, out):
+def k_xpack0(mid, yl, yh, out):
     ids = place()
     ends = edge(L0, ids)
     first = ids[0] == 0
@@ -396,7 +394,7 @@
         for a in range(3):
             there, here = y_tiles0(yl, yh, 2, 5 + i // 2, a), y_tiles0(yl, yh, 0, i // 2, a)
             tiles = [jnp.where(first, v, w) for v, w in zip(there, here)]
-            plane0(lambda x, a: own[a, x], zl, zh, tiles, x, a, out.at[i], a, ends, 64 * (1 - i % 2))
+            out[i, a] = plane0(mid[a, x], tiles, ends, 64 * (1 - i % 2))
 
 
 def k_xpack1(f1, r1, zl, zh, yl, yh, out, spare):
@@ -411,14 +409,30 @@
     loop(12, one, 2)
 
 
-def k_windows0(own, zl, zh, yl, yh, out):
-    ends = edge(L0, place())
+def beside0(c):
+    R = L0.R
+    sub = lax.broadcasted_iota(jnp.int32, (8, 128), 0)
+    seam = roll(jnp.where(sub == 0, c[0:8], c[R - 8 : R]), 64, 1)
+    up, down = roll(c, R - 1, 0), roll(c, 1, 0)
+    up = jnp.concatenate([up[: R - 8], jnp.where(sub == 7, roll(seam, 7, 0), up[R - 8 :])], axis=0)
+    down = jnp.concatenate([jnp.where(sub == 0, roll(seam, 1, 0), down[0:8]), down[8:]], axis=0)
+    return (up + down) + (roll(c, 1, 1) + roll(c, 127, 1))
+
+
+def k_windows0(mid, yl, yh, xw, part, d_out, c_out):
+    ids = place()
+    ends = edge(L0, ids)
+    ok = inside(L0, ids)
 
     def some(i):
         for k in range(16):
-            for a in range(3):
-                tiles = y_tiles0(yl, yh, i, k // 2, a)
-                plane0(lambda x, a: own[a, x], zl, zh, tiles, 16 * i + k, a, out.at[a], 16 * i + k, ends, 64 * (1 - k % 2))
+            x = 16 * i + k
+            v, b, rea = (plane0(mid[a, x], y_tiles0(yl, yh, i, k // 2, a), ends, 64 * (1 - k % 2)) for a in range(3))
+            d = 6.0 + rea
+            xw[x] = v
+            part[x] = b - d * v + beside0(v)
+            d_out[x] = d
+            c_out[x] = jnp.where(ok, W / d, 0.0)
 
     loop(3, some)
 
@@ -435,6 +449,16 @@
         out[x] = acc[x, 0:12, :]
 
     loop(24, keep, 6)
+
+
+def k_zmerge(own, zl, zh, up, out):
+    top, bottom, _, _ = edge(L0, place())
+
+    def one(x):
+        for a in range(3):
+            out[a, x] = merged(L0, lambda x, a: own[a, x], zl, zh, x, a, 0, 24, top, bottom)
+
+    loop(48, one, 8)
 
 
 def k_early(own, turned, r1, maps, tmp, acc):
@@ -450,43 +474,47 @@
     half_own(lambda x: jnp.where(mine, own[2, 2 * x] + own[2, 2 * x + 1], 0.0), tmp, acc, r1, 4, maps[OWN])
 
 
-def k_down0(win, r1, maps, xr, f_out, c_out, d_out, e_out, f1, z1h, z1l, xw, ew, tmp, acc):
+def k_down0(xw, part, d, cw, r1, maps, xr, f_out, c_out, e_out, f1, z1h, z1l, xb, ew, tmp, acc):
     ids = place()
     n = L0.nx
     shift = ids[0] * L0.hx
     other = (1 - ids[0]) * L0.n
+    low_side = ids[0] == 0
     ok = inside(L0, ids)
-    zero_ends(xw, n)
     zero_ends(ew, n)
     zero_ends(e_out, n)
-
-    def put(x):
-        xw[x + shift + 1] = win[0, x]
-
-    def take(x):
-        xw[x + other + 1] = xr[x, 0]
-
-    loop(48, put, 12)
-    loop(6, take, 6)
-
-    def first(w, b, rea):
-        d = 6.0 + rea
-        c = jnp.where(ok, W / d, 0.0)
-        f = b - d * xw[w + 1] + paired(xw, w)
-        d_out[w] = d
+    zero = jnp.zeros((L0.R, 128), F32)
+    xb[0] = jnp.where(low_side, xw[47], zero)
+    xb[7] = jnp.where(low_side, zero, xw[0])
+    for i in range(6):
+        xb[i + 1] = xr[i, 0]
+
+    def put(w, f, c):
         f_out[w] = f
         c_out[w] = c
         ew[w + 1] = c * f
 
-    loop(48, lambda x: first(x + shift, win[1, x], win[2, x]), UF)
-    loop(6, lambda x: first(x + other, xr[x, 1], xr[x, 2]), 6)
+    def mine(x):
+        put(x + shift, part[x] + (xw[x - 1] + xw[x + 1]), cw[x])
+
+    loop(46, lambda i: mine(i + 1), 23)
+    put(shift, part[0] + (jnp.where(low_side, zero, xr[5, 0]) + xw[1]), cw[0])
+    put(47 + shift, part[47] + (xw[46] + jnp.where(low_side, xr[0, 0], zero)), cw[47])
+
+    def theirs(i):
+        v = xb[i + 1]
+        dd = 6.0 + xr[i, 2]
+        f = xr[i, 1] - dd * v + beside0(v) + (xb[i] + xb[i + 2])
+        put(i + other, f, jnp.where(ok, W / dd, 0.0))
+
+    loop(6, theirs, 6)
     relax(ew, e_out, f_out, c_out, n, 1.0, UR, paired)
 
     def left(x):
-        return own_rows(L0, f_out[x] - d_out[x] * e_out[x + 1] + paired(e_out, x))
-
-    mine = lanes(24) % 64 < 48
-    pair = lambda x: jnp.where(mine, left(2 * x + shift) + left(2 * x + shift + 1), 0.0)
+        return own_rows(L0, f_out[x + shift] - d[x] * e_out[x + shift + 1] + paired(e_out, x + shift))
+
+    within = lanes(24) % 64 < 48
+    pair = lambda x: jnp.where(within, left(2 * x) + left(2 * x + 1), 0.0)
     half_own(pair, tmp, acc, f1, UL, maps[OWN])
     both = (f1, r1)
     loop(6, lambda g: ztile1(lambda x, a: both[a][x], z1h, z1l, g), 3)
@@ -590,6 +618,7 @@
 
 def sum_all(v):
     s = jnp.sum(v, axis=0)
+    s = sum(s[k : k + 8] for k in range(0, s.shape[0], 8))
     return jnp.sum(jnp.sum(s, axis=1, keepdims=True), axis=0, keepdims=True)
 
 
@@ -650,19 +679,22 @@
     p = r
     q = apply(r)
     rr = sum_all(r * r)
-    a = rr / sum_all(r * q)
+    den = sum_all(r * q)
+    a = rr / den
+    one_over_rr, one_over_a = 1.0 / rr, den / rr
     e = a * p
     for i in range(1, BOTTOM_ITERS):
         r = r - a * q
         w = apply(r)
         new = sum_all(r * r)
         rw = sum_all(r * w)
-        b = new / rr
-        a = new / (rw - b * new / a)
+        b = new * one_over_rr
+        den = rw - b * new * one_over_a
+        a = new / den
+        one_over_rr, one_over_a = 1.0 / new, den / new
         p = r + b * p
         q = w + b * q
         e = e + a * p
-        rr = new
     f4[...] = times(e.reshape(nx // 2 * H, 128), maps[UP3]).reshape(e.shape)
     add_refined(f4, nx // 2, e3, s3, 6)
     relax(s3, e3, f3, c3, nx, factor, 12)
@@ -716,7 +748,7 @@
         u, v = carry
         w = x + shift
         z = e0[w + 1]
-        az = own_rows(L0, d0[w] * z - paired(e0, w))
+        az = own_rows(L0, d0[x] * z - paired(e0, w))
         z = own_rows(L0, z)
         f = own_rows(L0, f0[w])
         z_out[x] = z
@@ -798,14 +830,15 @@
     )
     up, dn = run(k_ypack0, (sds(*L0.yshape),) * 2, (own, turned, zl, zh))
     yl, yh = ring(up, dn, "gy")
-    xr = swap(run(k_xpack0, sds(*L0.xshape), (own, zl, zh, yl, yh)))
-    win = run(k_windows0, sds(3, 48, 32, 128), (own, zl, zh, yl, yh))
-    p0, q0 = (54, 32, 128), (56, 32, 128)
-    f0, c0, d0, e0, f1, z1h, z1l = run(
+    mid = run(k_zmerge, sds(3, 48, 24, 128), (own, zl, zh, up))
+    xr = swap(run(k_xpack0, sds(*L0.xshape), (mid, yl, yh)))
+    p0, q0, o0 = (54, 32, 128), (56, 32, 128), (48, 32, 128)
+    xw, part, d0, cw = run(k_windows0, (sds(*o0),) * 4, (mid, yl, yh))
+    f0, c0, e0, f1, z1h, z1l = run(
         k_down0,
-        (sds(*p0), sds(*p0), sds(*p0), sds(*q0), sds(24, 12, 128), sds(*L1.zshape), sds(*L1.zshape)),
-        (win, r1, maps, xr),
-        [q0, q0, (24, 24, 128), (24, 16, 128)],
+        (sds(*p0), sds(*p0), sds(*q0), sds(24, 12, 128), sds(*L1.zshape), sds(*L1.zshape)),
+        (xw, part, d0, cw, r1, maps, xr),
+        [(8, 32, 128), q0, (24, 24, 128), (24, 16, 128)],
         mib=M0,
     )
     zl, zh = ring(z1h, z1l, "gz")

time: 89.9 us -> 92.1 us (1.024)
  waiting for transfers between devices: 9.63 us -> 11.8 us
    ppermute x4, starting transfers between devices: 4.81 us -> 2.33 us  [ring(): low = lax.ppermute(up, axis, [(i, (i + 1) % n) for i in range(n)])]
    ppermute x4, starting transfers between devices: 12.9 us -> 15.1 us  [ring(): high = lax.ppermute(dn, axis, [(i, (i - 1) % n) for i in range(n)])]
    ppermute x4, waiting for transfers between devices: 0.01 us -> 1.3 us  [ring(): high = lax.ppermute(dn, axis, [(i, (i - 1) % n) for i in range(n)])]
    ppermute x4, waiting for transfers between devices: 9.03 us -> 10.2 us  [ring(): low = lax.ppermute(up, axis, [(i, (i + 1) % n) for i in range(n)])]
    pallas_call x12 -> x13, Pallas kernels: 21.9 us -> 22.8 us  [run(): pl.pallas_call(kernel, out_shape=outs, in_specs=[hbm if far_in else vmem]...]
  transfers between devices with their start and end apart: 10 -> 10, of which waited for: 6 -> 6; matrix products, arithmetic and copies ran while one was open for 0% -> 0% of each run, Pallas kernels for 3% -> 5%
where the time goes in v11:
time: 92.1 us; the launch traced here: 91.9 us
  blocking collectives  33.9 us (37%)
  Pallas kernels  22.8 us (25%)
  starting transfers between devices  22.6 us (25%)
  waiting for transfers between devices  11.8 us (13%)
    pallas_call x13, Pallas kernels, run(): pl.pallas_call(kernel, out_shape=outs, in_specs=[hbm if far_in else vmem]...  22.8 us
    all_to_all x1, blocking collectives, body(): g = lax.all_to_all(g, ALL, 0, 0, tiled=True)  19.6 us
    ppermute x4, starting transfers between devices, ring(): high = lax.ppermute(dn, axis, [(i, (i - 1) % n) for i in range(n)])  15.1 us
    all_to_all x1, blocking collectives, body(): lax.all_to_all(sums.reshape(count, 1, 128), ALL, 0, 0, tiled=True)  14.3 us
    ppermute x4, waiting for transfers between devices, ring(): low = lax.ppermute(up, axis, [(i, (i + 1) % n) for i in range(n)])  10.2 us
    ppermute x2, starting transfers between devices, swap(): return lax.ppermute(v, 'gx', [(0, 1), (1, 0)])  5.14 us
    ppermute x4, starting transfers between devices, ring(): low = lax.ppermute(up, axis, [(i, (i + 1) % n) for i in range(n)])  2.33 us
  transfers between devices with their start and end apart: 10, of which 6 were waited for; matrix products, arithmetic and copies ran while one was open for 0% of the time, Pallas kernels for 5%

profile of v11, /device:TPU:1, one launch (start us, length us, event | category | flops | bytes accessed | tf_op | source)
XLA Modules:
  0.0 91.9 jit_solution(8783163659674344745)
XLA Ops:
  0.6 3.1 %shard_map.50 = (f32[10,24,128]{2,1,0:T(8,128)S(1)}, f32[10,24,128]{2,1,0:T(8,128)S(1)}, f32[3,48,24,128]{3,2,1,0:T(8,128)S(1)}) custom-call(f32[48,48,48]{2,1,0:T(8,128)} %x0.1, f32[48,48,48]{2,1,0:T(8,128)} %b.1, f32[48,48,48]{2,1,0:T(8,128)} %rea.1), custom_call_target="tpu_custom_call" | custom-call | tf_op jit(solution)/shard_map/pallas_call | solution.py:54
  3.7 2.2 %collective-permute-start = (f32[10,24,128]{2,1,0:T(8,128)S(1)}, f32[10,24,128]{2,1,0:T(8,128)S(1)}, u32[]{:S(2)}, u32[]{:S(2)}) collective-permute-start(f32[10,24,128]{2,1,0:T(8,128)S(1)} %get-tuple-element.33), channel_id=1, source_target_pairs={{0,1},{1,2},{2,3},{3,4},{4,5},{5,6},{6,7},{7,8},{8,9},{9,10},{10,1... | collective-permute-start | bytes 368648 | tf_op jit(solution)/shard_map/ppermute | solution.py:803
  5.9 5.0 %collective-permute-start.1 = (f32[10,24,128]{2,1,0:T(8,128)S(1)}, f32[10,24,128]{2,1,0:T(8,128)S(1)}, u32[]{:S(2)}, u32[]{:S(2)}) collective-permute-start(f32[10,24,128]{2,1,0:T(8,128)S(1)} %get-tuple-element.34), channel_id=1, source_target_pairs={{0,15},{1,0},{2,1},{3,2},{4,3},{5,4},{6,5},{7,6},{8,7},{9,8},{10,9... | collective-permute-start | bytes 368648 | tf_op jit(solution)/shard_map/ppermute | solution.py:804
  10.9 1.0 %shard_map.51 = (f32[3,24,16,128]{3,2,1,0:T(8,128)S(1)}, f32[24,12,128]{2,1,0:T(8,128)S(1)}, bf16[10,256,128]{2,1,0:T(8,128)(2,1)S(1)}) custom-call(f32[3,48,24,128]{3,2,1,0:T(8,128)S(1)} %get-tuple-element.32.own), custom_call_target="tpu_custom_call" | custom-call | tf_op jit(solution)/shard_map/pallas_call | solution.py:54
  11.9 1.9 %collective-permute-done.zl = f32[10,24,128]{2,1,0:T(8,128)S(1)} collective-permute-done((f32[10,24,128]{2,1,0:T(8,128)S(1)}, f32[10,24,128]{2,1,0:T(8,128)S(1)}, u32[]{:S(2)}, u32[]{:S(2)}) %collective-permute-start) | collective-permute-done | bytes 122912 | tf_op jit(solution)/shard_map/ppermute | solution.py:803
  13.8 0.7 shard_map.52
  14.6 2.5 %collective-permute-start.3 = (f32[3,104,128]{2,1,0:T(8,128)S(1)}, f32[3,104,128]{2,1,0:T(8,128)S(1)}, u32[]{:S(2)}, u32[]{:S(2)}) collective-permute-start(f32[3,104,128]{2,1,0:T(8,128)S(1)} %get-tuple-element.37), channel_id=1, source_target_pairs={{0,48},{16,0},{32,16},{48,32},{1,49},{17,1},{33,17},{49,33},{2,50}... | collective-permute-start | bytes 479240 | tf_op jit(solution)/shard_map/ppermute | solution.py:804
  17.1 0.9 shard_map.53.mid
  18.0 1.3 %collective-permute-done.3.yh = f32[3,104,128]{2,1,0:T(8,128)S(1)} collective-permute-done((f32[3,104,128]{2,1,0:T(8,128)S(1)}, f32[3,104,128]{2,1,0:T(8,128)S(1)}, u32[]{:S(2)}, u32[]{:S(2)}) %collective-permute-start.3) | collective-permute-done | bytes 159776 | tf_op jit(solution)/shard_map/ppermute | solution.py:804
  19.3 3.1 %collective-permute-done.2.yl = f32[3,104,128]{2,1,0:T(8,128)S(1)} collective-permute-done((f32[3,104,128]{2,1,0:T(8,128)S(1)}, f32[3,104,128]{2,1,0:T(8,128)S(1)}, u32[]{:S(2)}, u32[]{:S(2)}) %collective-permute-start.2) | collective-permute-done | bytes 159776 | tf_op jit(solution)/shard_map/ppermute | solution.py:803
  22.5 3.1 %collective-permute-start.4 = (f32[6,3,32,128]{3,2,1,0:T(8,128)S(1)}, f32[6,3,32,128]{3,2,1,0:T(8,128)S(1)}, u32[]{:S(2)}, u32[]{:S(2)}) collective-permute-start(f32[6,3,32,128]{3,2,1,0:T(8,128)S(1)} %shard_map.55), channel_id=1, source_target_pairs={{0,64},{64,0},{1,65},{65,1},{2,66},{66,2},{3,67},{67,3},{4,68},{68... | collective-permute-start | bytes 884744 | tf_op jit(solution)/shard_map/ppermute | solution.py:809
  25.6 1.5 %shard_map.54 = (f32[48,32,128]{2,1,0:T(8,128)S(1)}, f32[48,32,128]{2,1,0:T(8,128)S(1)}, f32[48,32,128]{2,1,0:T(8,128)S(1)}, f32[48,32,128]{2,1,0:T(8,128)S(1)}) custom-call(f32[3,48,24,128]{3,2,1,0:T(8,128)S(1)} %shard_map.53.mid, f32[3,104,128]{2,1,0:T(8,128)S(1)} %collective-permute-done.2.yl, f32[3,104,128]{2,1,0:T(8,128)S(1)} %collective-permute-done.3.yh), custom_call_target="tpu_custom_call" | custom-call | tf_op jit(solution)/shard_map/pallas_call | solution.py:54
  27.2 2.4 %shard_map.56 = (f32[54,32,128]{2,1,0:T(8,128)S(1)}, f32[54,32,128]{2,1,0:T(8,128)S(1)}, f32[56,32,128]{2,1,0:T(8,128)S(1)}, f32[24,12,128]{2,1,0:T(8,128)S(1)},...) custom-call(f32[48,32,128]{2,1,0:T(8,128)S(1)} %get-tuple-element.38.xw, ...), custom_call_target="tpu_custom_call" | custom-call | tf_op jit(solution)/shard_map/pallas_call | solution.py:54
  29.7 4.9 %collective-permute-start.6 = (f32[6,24,128]{2,1,0:T(8,128)S(1)}, f32[6,24,128]{2,1,0:T(8,128)S(1)}, u32[]{:S(2)}, u32[]{:S(2)}) collective-permute-start(f32[6,24,128]{2,1,0:T(8,128)S(1)} %get-tuple-element.46), channel_id=1, source_target_pairs={{0,15},{1,0},{2,1},{3,2},{4,3},{5,4},{6,5},{7,6},{8,7},{9,8},{10,9... | collective-permute-start | bytes 221192 | tf_op jit(solution)/shard_map/ppermute | solution.py:804
  34.6 2.3 %collective-permute-done.5.zl = f32[6,24,128]{2,1,0:T(8,128)S(1)} collective-permute-done((f32[6,24,128]{2,1,0:T(8,128)S(1)}, f32[6,24,128]{2,1,0:T(8,128)S(1)}, u32[]{:S(2)}, u32[]{:S(2)}) %collective-permute-start.5) | collective-permute-done | bytes 73760 | tf_op jit(solution)/shard_map/ppermute | solution.py:803
  37.4 2.7 %collective-permute-start.8 = (f32[12,24,128]{2,1,0:T(8,128)S(1)}, f32[12,24,128]{2,1,0:T(8,128)S(1)}, u32[]{:S(2)}, u32[]{:S(2)}) collective-permute-start(f32[12,24,128]{2,1,0:T(8,128)S(1)} %get-tuple-element.48), channel_id=1, source_target_pairs={{0,48},{16,0},{32,16},{48,32},{1,49},{17,1},{33,17},{49,33},{2,50}... | collective-permute-start | bytes 442376 | tf_op jit(solution)/shard_map/ppermute | solution.py:804
  40.1 2.8 %collective-permute-done.7.yl = f32[12,24,128]{2,1,0:T(8,128)S(1)} collective-permute-done((f32[12,24,128]{2,1,0:T(8,128)S(1)}, f32[12,24,128]{2,1,0:T(8,128)S(1)}, u32[]{:S(2)}, u32[]{:S(2)}) %collective-permute-start.7) | collective-permute-done | bytes 147488 | tf_op jit(solution)/shard_map/ppermute | solution.py:803
  43.6 2.1 %collective-permute-start.9 = (f32[12,2,24,128]{3,2,1,0:T(8,128)S(1)}, f32[12,2,24,128]{3,2,1,0:T(8,128)S(1)}, u32[]{:S(2)}, u32[]{:S(2)}) collective-permute-start(f32[12,2,24,128]{3,2,1,0:T(8,128)S(1)} %shard_map.59), channel_id=1, source_target_pairs={{0,64},{64,0},{1,65},{65,1},{2,66},{66,2},{3,67},{67,3},{4,68},{68... | collective-permute-start | bytes 884744 | tf_op jit(solution)/shard_map/ppermute | solution.py:809
  45.7 0.9 %shard_map.58.win = f32[2,24,24,128]{3,2,1,0:T(8,128)S(1)} custom-call(f32[24,12,128]{2,1,0:T(8,128)S(1)} %get-tuple-element.44.f1, f32[24,12,128]{2,1,0:T(8,128)S(1)} %get-tuple-element.42.r1, f32[6,24,128]{2,1,0:T(8,128)S(1)} %collective-permute-done.5.zl, f32[6,24,128]{2,1,0:T(8,128)S(1)} %collective-permute-done.6.zh, ...), custom_call_target="tpu_custom_call" | custom-call | tf_op jit(solution)/shard_map/pallas_call | solution.py:54
  46.9 2.5 %shard_map.60 = (f32[36,24,128]{2,1,0:T(8,128)S(1)}, f32[36,24,128]{2,1,0:T(8,128)S(1)}, f32[38,24,128]{2,1,0:T(8,128)S(1)}, f32[18,32,128]{2,1,0:T(8,128)S(1)},...) custom-call(f32[2,24,24,128]{3,2,1,0:T(8,128)S(1)} %shard_map.58.win, ...), custom_call_target="tpu_custom_call" | custom-call | tf_op jit(solution)/shard_map/pallas_call | solution.py:54
  49.4 19.6 %all_to_all.16 = f32[128,4,128]{2,1,0:T(4,128)S(1)} all-to-all(f32[128,4,128]{2,1,0:T(4,128)S(1)} %bitcast.8), channel_id=1, replica_groups=mesh['gx'=2,'gy'=4,'gz'=16] {'gx','gy','gz'}, dimensions={0} | all-to-all | bytes 524288 | tf_op jit(solution)/shard_map/all_to_all | solution.py:857
  69.0 6.8 %shard_map.61 = (f32[48,24,128]{2,1,0:T(8,128)S(1)}, f32[48,24,128]{2,1,0:T(8,128)S(1)}, f32[128,128]{1,0:T(8,128)S(1)}) custom-call(f32[512,128]{1,0:T(8,128)S(1)} %bitcast.6, bf16[10,256,128]{2,1,0:T(8,128)(2,1)S(1)} %get-tuple-element.43.maps, f32[18,32,128]{2,1,0:T(8,128)S(1)} %get-tuple-element.50.f2, f32[18,32,128]{2,1,0:T(8,128)S(1)} %get-tuple-element.51.c2, ...), custom_call_target="tpu_custom_call" | custom-call | tf_op jit(solution)/shard_map/pallas_call | solution.py:54
  75.8 14.3 %all_to_all.17 = f32[128,1,128]{2,1,0:T(1,128)S(1)} all-to-all(f32[128,1,128]{2,1,0:T(1,128)S(1)} %bitcast.9), channel_id=1, replica_groups=mesh['gx'=2,'gy'=4,'gz'=16] {'gx','gy','gz'}, dimensions={0} | all-to-all | bytes 131072 | tf_op jit(solution)/shard_map/all_to_all | solution.py:871
  90.1 1.7 %shard_map.62 = (f32[48,48,48]{2,1,0:T(8,128)}, f32[48,48,48]{2,1,0:T(8,128)}) custom-call(f32[128,128]{1,0:T(8,128)S(1)} %bitcast.7, f32[3,48,24,128]{3,2,1,0:T(8,128)S(1)} %get-tuple-element.32.own, f32[48,24,128]{2,1,0:T(8,128)S(1)} %get-tuple-element.60.z, f32[48,24,128]{2,1,0:T(8,128)S(1)} %get-tuple-element.61.az, ...), custom_call_target="tpu_custom_call" | custom-call | tf_op jit(solution)/shard_map/pallas_call | solution.py:54
  (11 shorter events, 1.6 us)
Async XLA Ops:
  3.7 10.1 %collective-permute-start = (f32[10,24,128]{2,1,0:T(8,128)S(1)}, f32[10,24,128]{2,1,0:T(8,128)S(1)}, u32[]{:S(2)}, u32[]{:S(2)}) collective-permute-start(f32[10,24,128]{2,1,0:T(8,128)S(1)} %get-tuple-element.33), channel_id=1, source_target_pairs={{0,1},{1,2},{2,3},{3,4},{4,5},{5,6},{6,7},{7,8},{8,9},{9,10},{10,1... | collective-permute-start | bytes 368648 | tf_op jit(solution)/shard_map/ppermute | solution.py:803
  5.9 7.9 %collective-permute-start.1 = (f32[10,24,128]{2,1,0:T(8,128)S(1)}, f32[10,24,128]{2,1,0:T(8,128)S(1)}, u32[]{:S(2)}, u32[]{:S(2)}) collective-permute-start(f32[10,24,128]{2,1,0:T(8,128)S(1)} %get-tuple-element.34), channel_id=1, source_target_pairs={{0,15},{1,0},{2,1},{3,2},{4,3},{5,4},{6,5},{7,6},{8,7},{9,8},{10,9... | collective-permute-start | bytes 368648 | tf_op jit(solution)/shard_map/ppermute | solution.py:804
  14.6 4.8 %collective-permute-start.3 = (f32[3,104,128]{2,1,0:T(8,128)S(1)}, f32[3,104,128]{2,1,0:T(8,128)S(1)}, u32[]{:S(2)}, u32[]{:S(2)}) collective-permute-start(f32[3,104,128]{2,1,0:T(8,128)S(1)} %get-tuple-element.37), channel_id=1, source_target_pairs={{0,48},{16,0},{32,16},{48,32},{1,49},{17,1},{33,17},{49,33},{2,50}... | collective-permute-start | bytes 479240 | tf_op jit(solution)/shard_map/ppermute | solution.py:804
  17.1 5.3 %collective-permute-start.2 = (f32[3,104,128]{2,1,0:T(8,128)S(1)}, f32[3,104,128]{2,1,0:T(8,128)S(1)}, u32[]{:S(2)}, u32[]{:S(2)}) collective-permute-start(f32[3,104,128]{2,1,0:T(8,128)S(1)} %get-tuple-element.36.up), channel_id=1, source_target_pairs={{0,16},{16,32},{32,48},{48,0},{1,17},{17,33},{33,49},{49,1},{2,18}... | collective-permute-start | bytes 479240 | tf_op jit(solution)/shard_map/ppermute | solution.py:803
  22.5 4.6 %collective-permute-start.4 = (f32[6,3,32,128]{3,2,1,0:T(8,128)S(1)}, f32[6,3,32,128]{3,2,1,0:T(8,128)S(1)}, u32[]{:S(2)}, u32[]{:S(2)}) collective-permute-start(f32[6,3,32,128]{3,2,1,0:T(8,128)S(1)} %shard_map.55), channel_id=1, source_target_pairs={{0,64},{64,0},{1,65},{65,1},{2,66},{66,2},{3,67},{67,3},{4,68},{68... | collective-permute-start | bytes 884744 | tf_op jit(solution)/shard_map/ppermute | solution.py:809
  29.6 7.3 %collective-permute-start.5 = (f32[6,24,128]{2,1,0:T(8,128)S(1)}, f32[6,24,128]{2,1,0:T(8,128)S(1)}, u32[]{:S(2)}, u32[]{:S(2)}) collective-permute-start(f32[6,24,128]{2,1,0:T(8,128)S(1)} %get-tuple-element.45), channel_id=1, source_target_pairs={{0,1},{1,2},{2,3},{3,4},{4,5},{5,6},{6,7},{7,8},{8,9},{9,10},{10,1... | collective-permute-start | bytes 221192 | tf_op jit(solution)/shard_map/ppermute | solution.py:803
  29.7 7.2 %collective-permute-start.6 = (f32[6,24,128]{2,1,0:T(8,128)S(1)}, f32[6,24,128]{2,1,0:T(8,128)S(1)}, u32[]{:S(2)}, u32[]{:S(2)}) collective-permute-start(f32[6,24,128]{2,1,0:T(8,128)S(1)} %get-tuple-element.46), channel_id=1, source_target_pairs={{0,15},{1,0},{2,1},{3,2},{4,3},{5,4},{6,5},{7,6},{8,7},{9,8},{10,9... | collective-permute-start | bytes 221192 | tf_op jit(solution)/shard_map/ppermute | solution.py:804
  37.4 5.6 %collective-permute-start.7 = (f32[12,24,128]{2,1,0:T(8,128)S(1)}, f32[12,24,128]{2,1,0:T(8,128)S(1)}, u32[]{:S(2)}, u32[]{:S(2)}) collective-permute-start(f32[12,24,128]{2,1,0:T(8,128)S(1)} %get-tuple-element.47), channel_id=1, source_target_pairs={{0,16},{16,32},{32,48},{48,0},{1,17},{17,33},{33,49},{49,1},{2,18}... | collective-permute-start | bytes 442376 | tf_op jit(solution)/shard_map/ppermute | solution.py:803
  37.4 5.5 %collective-permute-start.8 = (f32[12,24,128]{2,1,0:T(8,128)S(1)}, f32[12,24,128]{2,1,0:T(8,128)S(1)}, u32[]{:S(2)}, u32[]{:S(2)}) collective-permute-start(f32[12,24,128]{2,1,0:T(8,128)S(1)} %get-tuple-element.48), channel_id=1, source_target_pairs={{0,48},{16,0},{32,16},{48,32},{1,49},{17,1},{33,17},{49,33},{2,50}... | collective-permute-start | bytes 442376 | tf_op jit(solution)/shard_map/ppermute | solution.py:804
  43.6 3.3 %collective-permute-start.9 = (f32[12,2,24,128]{3,2,1,0:T(8,128)S(1)}, f32[12,2,24,128]{3,2,1,0:T(8,128)S(1)}, u32[]{:S(2)}, u32[]{:S(2)}) collective-permute-start(f32[12,2,24,128]{3,2,1,0:T(8,128)S(1)} %shard_map.59), channel_id=1, source_target_pairs={{0,64},{64,0},{1,65},{65,1},{2,66},{66,2},{3,67},{67,3},{4,68},{68... | collective-permute-start | bytes 884744 | tf_op jit(solution)/shard_map/ppermute | solution.py:809

commit v12 on v11

--- a/solution.py
+++ b/solution.py
@@ -451,7 +451,7 @@
     loop(24, keep, 6)
 
 
-def k_zmerge(own, zl, zh, up, out):
+def k_zmerge(own, zl, zh, dn, out):
     top, bottom, _, _ = edge(L0, place())
 
     def one(x):
@@ -798,10 +798,16 @@
             copy(a, src, dst, i).wait()
 
 
-def ring(up, dn, axis):
+def ring(up, dn, axis, low_first=True):
     n = lax.axis_size(axis)
-    low = lax.ppermute(up, axis, [(i, (i + 1) % n) for i in range(n)])
-    high = lax.ppermute(dn, axis, [(i, (i - 1) % n) for i in range(n)])
+    rise = [(i, (i + 1) % n) for i in range(n)]
+    fall = [(i, (i - 1) % n) for i in range(n)]
+    if low_first:
+        low = lax.ppermute(up, axis, rise)
+        high = lax.ppermute(dn, axis, fall)
+    else:
+        high = lax.ppermute(dn, axis, fall)
+        low = lax.ppermute(up, axis, rise)
     return low, high
 
 
@@ -830,7 +836,7 @@
     )
     up, dn = run(k_ypack0, (sds(*L0.yshape),) * 2, (own, turned, zl, zh))
     yl, yh = ring(up, dn, "gy")
-    mid = run(k_zmerge, sds(3, 48, 24, 128), (own, zl, zh, up))
+    mid = run(k_zmerge, sds(3, 48, 24, 128), (own, zl, zh, dn))
     xr = swap(run(k_xpack0, sds(*L0.xshape), (mid, yl, yh)))
     p0, q0, o0 = (54, 32, 128), (56, 32, 128), (48, 32, 128)
     xw, part, d0, cw = run(k_windows0, (sds(*o0),) * 4, (mid, yl, yh))

time: 92.1 us -> 89.6 us (0.973)
  waiting for transfers between devices: 11.8 us -> 9.05 us
    ppermute x8, waiting for transfers between devices: 11.5 us -> 8.78 us  [the longest x4 8.77 us: ring(): low = lax.ppermute(up, axis, rise)]
  transfers between devices with their start and end apart: 10 -> 10, of which waited for: 6 -> 5; matrix products, arithmetic and copies ran while one was open for 0% -> 0% of each run, Pallas kernels for 5% -> 5%
where the time goes in v12:
time: 89.6 us; the launch traced here: 89.5 us
  blocking collectives  33.6 us (38%)
  starting transfers between devices  23.1 us (26%)
  Pallas kernels  22.8 us (25%)
  waiting for transfers between devices  9.05 us (10%)
    pallas_call x13, Pallas kernels, run(): pl.pallas_call(kernel, out_shape=outs, in_specs=[hbm if far_in else vmem]...  22.8 us
    all_to_all x1, blocking collectives, body(): g = lax.all_to_all(g, ALL, 0, 0, tiled=True)  19.3 us
    all_to_all x1, blocking collectives, body(): lax.all_to_all(sums.reshape(count, 1, 128), ALL, 0, 0, tiled=True)  14.3 us
    ppermute x4, starting transfers between devices, ring(): high = lax.ppermute(dn, axis, fall)  12.9 us
    ppermute x4, waiting for transfers between devices, ring(): low = lax.ppermute(up, axis, rise)  8.77 us
    ppermute x2, starting transfers between devices, swap(): return lax.ppermute(v, 'gx', [(0, 1), (1, 0)])  5.39 us
    ppermute x4, starting transfers between devices, ring(): low = lax.ppermute(up, axis, rise)  4.82 us
  transfers between devices with their start and end apart: 10, of which 5 were waited for; matrix products, arithmetic and copies ran while one was open for 0% of the time, Pallas kernels for 5%

profile of v12, /device:TPU:1, one launch (start us, length us, event | category | flops | bytes accessed | tf_op | source)
XLA Modules:
  0.0 89.5 jit_solution(5231106936832874703)
XLA Ops:
  0.6 3.1 %shard_map.50 = (f32[10,24,128]{2,1,0:T(8,128)S(1)}, f32[10,24,128]{2,1,0:T(8,128)S(1)}, f32[3,48,24,128]{3,2,1,0:T(8,128)S(1)}) custom-call(f32[48,48,48]{2,1,0:T(8,128)} %x0.1, f32[48,48,48]{2,1,0:T(8,128)} %b.1, f32[48,48,48]{2,1,0:T(8,128)} %rea.1), custom_call_target="tpu_custom_call" | custom-call | tf_op jit(solution)/shard_map/pallas_call | solution.py:54
  3.7 2.2 %collective-permute-start = (f32[10,24,128]{2,1,0:T(8,128)S(1)}, f32[10,24,128]{2,1,0:T(8,128)S(1)}, u32[]{:S(2)}, u32[]{:S(2)}) collective-permute-start(f32[10,24,128]{2,1,0:T(8,128)S(1)} %get-tuple-element.33), channel_id=1, source_target_pairs={{0,1},{1,2},{2,3},{3,4},{4,5},{5,6},{6,7},{7,8},{8,9},{9,10},{10,1... | collective-permute-start | bytes 368648 | tf_op jit(solution)/shard_map/ppermute | solution.py:806
  5.9 5.0 %collective-permute-start.1 = (f32[10,24,128]{2,1,0:T(8,128)S(1)}, f32[10,24,128]{2,1,0:T(8,128)S(1)}, u32[]{:S(2)}, u32[]{:S(2)}) collective-permute-start(f32[10,24,128]{2,1,0:T(8,128)S(1)} %get-tuple-element.34), channel_id=1, source_target_pairs={{0,15},{1,0},{2,1},{3,2},{4,3},{5,4},{6,5},{7,6},{8,7},{9,8},{10,9... | collective-permute-start | bytes 368648 | tf_op jit(solution)/shard_map/ppermute | solution.py:807
  10.9 1.0 %shard_map.51 = (f32[3,24,16,128]{3,2,1,0:T(8,128)S(1)}, f32[24,12,128]{2,1,0:T(8,128)S(1)}, bf16[10,256,128]{2,1,0:T(8,128)(2,1)S(1)}) custom-call(f32[3,48,24,128]{3,2,1,0:T(8,128)S(1)} %get-tuple-element.32.own), custom_call_target="tpu_custom_call" | custom-call | tf_op jit(solution)/shard_map/pallas_call | solution.py:54
  11.9 1.9 %collective-permute-done.zl = f32[10,24,128]{2,1,0:T(8,128)S(1)} collective-permute-done((f32[10,24,128]{2,1,0:T(8,128)S(1)}, f32[10,24,128]{2,1,0:T(8,128)S(1)}, u32[]{:S(2)}, u32[]{:S(2)}) %collective-permute-start) | collective-permute-done | bytes 122912 | tf_op jit(solution)/shard_map/ppermute | solution.py:806
  14.6 1.3 %collective-permute-start.2 = (f32[3,104,128]{2,1,0:T(8,128)S(1)}, f32[3,104,128]{2,1,0:T(8,128)S(1)}, u32[]{:S(2)}, u32[]{:S(2)}) collective-permute-start(f32[3,104,128]{2,1,0:T(8,128)S(1)} %get-tuple-element.37), channel_id=1, source_target_pairs={{0,16},{16,32},{32,48},{48,0},{1,17},{17,33},{33,49},{49,1},{2,18}... | collective-permute-start | bytes 479240 | tf_op jit(solution)/shard_map/ppermute | solution.py:806
  15.8 1.5 %collective-permute-start.3 = (f32[3,104,128]{2,1,0:T(8,128)S(1)}, f32[3,104,128]{2,1,0:T(8,128)S(1)}, u32[]{:S(2)}, u32[]{:S(2)}) collective-permute-start(f32[3,104,128]{2,1,0:T(8,128)S(1)} %get-tuple-element.36.dn), channel_id=1, source_target_pairs={{0,48},{16,0},{32,16},{48,32},{1,49},{17,1},{33,17},{49,33},{2,50}... | collective-permute-start | bytes 479240 | tf_op jit(solution)/shard_map/ppermute | solution.py:807
  17.3 0.9 %shard_map.53.mid = f32[3,48,24,128]{3,2,1,0:T(8,128)S(1)} custom-call(f32[3,48,24,128]{3,2,1,0:T(8,128)S(1)} %get-tuple-element.32.own, f32[10,24,128]{2,1,0:T(8,128)S(1)} %collective-permute-done.zl, f32[10,24,128]{2,1,0:T(8,128)S(1)} %collective-permute-done.1.zh, f32[3,104,128]{2,1,0:T(8,128)S(1)} %get-tuple-element.36.dn), custom_call_target="tpu_custom_call" | custom-call | tf_op jit(solution)/shard_map/pallas_call | solution.py:54
  18.2 1.7 %collective-permute-done.2.yl = f32[3,104,128]{2,1,0:T(8,128)S(1)} collective-permute-done((f32[3,104,128]{2,1,0:T(8,128)S(1)}, f32[3,104,128]{2,1,0:T(8,128)S(1)}, u32[]{:S(2)}, u32[]{:S(2)}) %collective-permute-start.2) | collective-permute-done | bytes 159776 | tf_op jit(solution)/shard_map/ppermute | solution.py:806
  20.1 3.1 %collective-permute-start.4 = (f32[6,3,32,128]{3,2,1,0:T(8,128)S(1)}, f32[6,3,32,128]{3,2,1,0:T(8,128)S(1)}, u32[]{:S(2)}, u32[]{:S(2)}) collective-permute-start(f32[6,3,32,128]{3,2,1,0:T(8,128)S(1)} %shard_map.55), channel_id=1, source_target_pairs={{0,64},{64,0},{1,65},{65,1},{2,66},{66,2},{3,67},{67,3},{4,68},{68... | collective-permute-start | bytes 884744 | tf_op jit(solution)/shard_map/ppermute | solution.py:815
  23.2 1.5 %shard_map.54 = (f32[48,32,128]{2,1,0:T(8,128)S(1)}, f32[48,32,128]{2,1,0:T(8,128)S(1)}, f32[48,32,128]{2,1,0:T(8,128)S(1)}, f32[48,32,128]{2,1,0:T(8,128)S(1)}) custom-call(f32[3,48,24,128]{3,2,1,0:T(8,128)S(1)} %shard_map.53.mid, f32[3,104,128]{2,1,0:T(8,128)S(1)} %collective-permute-done.2.yl, f32[3,104,128]{2,1,0:T(8,128)S(1)} %collective-permute-done.3.yh), custom_call_target="tpu_custom_call" | custom-call | tf_op jit(solution)/shard_map/pallas_call | solution.py:54
  24.7 2.4 %shard_map.56 = (f32[54,32,128]{2,1,0:T(8,128)S(1)}, f32[54,32,128]{2,1,0:T(8,128)S(1)}, f32[56,32,128]{2,1,0:T(8,128)S(1)}, f32[24,12,128]{2,1,0:T(8,128)S(1)},...) custom-call(f32[48,32,128]{2,1,0:T(8,128)S(1)} %get-tuple-element.38.xw, ...), custom_call_target="tpu_custom_call" | custom-call | tf_op jit(solution)/shard_map/pallas_call | solution.py:54
  27.2 4.9 %collective-permute-start.6 = (f32[6,24,128]{2,1,0:T(8,128)S(1)}, f32[6,24,128]{2,1,0:T(8,128)S(1)}, u32[]{:S(2)}, u32[]{:S(2)}) collective-permute-start(f32[6,24,128]{2,1,0:T(8,128)S(1)} %get-tuple-element.46), channel_id=1, source_target_pairs={{0,15},{1,0},{2,1},{3,2},{4,3},{5,4},{6,5},{7,6},{8,7},{9,8},{10,9... | collective-permute-start | bytes 221192 | tf_op jit(solution)/shard_map/ppermute | solution.py:807
  32.1 2.3 %collective-permute-done.5.zl = f32[6,24,128]{2,1,0:T(8,128)S(1)} collective-permute-done((f32[6,24,128]{2,1,0:T(8,128)S(1)}, f32[6,24,128]{2,1,0:T(8,128)S(1)}, u32[]{:S(2)}, u32[]{:S(2)}) %collective-permute-start.5) | collective-permute-done | bytes 73760 | tf_op jit(solution)/shard_map/ppermute | solution.py:806
  34.9 1.3 %collective-permute-start.7 = (f32[12,24,128]{2,1,0:T(8,128)S(1)}, f32[12,24,128]{2,1,0:T(8,128)S(1)}, u32[]{:S(2)}, u32[]{:S(2)}) collective-permute-start(f32[12,24,128]{2,1,0:T(8,128)S(1)} %get-tuple-element.47), channel_id=1, source_target_pairs={{0,16},{16,32},{32,48},{48,0},{1,17},{17,33},{33,49},{49,1},{2,18}... | collective-permute-start | bytes 442376 | tf_op jit(solution)/shard_map/ppermute | solution.py:806
  36.2 1.5 %collective-permute-start.8 = (f32[12,24,128]{2,1,0:T(8,128)S(1)}, f32[12,24,128]{2,1,0:T(8,128)S(1)}, u32[]{:S(2)}, u32[]{:S(2)}) collective-permute-start(f32[12,24,128]{2,1,0:T(8,128)S(1)} %get-tuple-element.48), channel_id=1, source_target_pairs={{0,48},{16,0},{32,16},{48,32},{1,49},{17,1},{33,17},{49,33},{2,50}... | collective-permute-start | bytes 442376 | tf_op jit(solution)/shard_map/ppermute | solution.py:807
  37.7 2.8 %collective-permute-done.7.yl = f32[12,24,128]{2,1,0:T(8,128)S(1)} collective-permute-done((f32[12,24,128]{2,1,0:T(8,128)S(1)}, f32[12,24,128]{2,1,0:T(8,128)S(1)}, u32[]{:S(2)}, u32[]{:S(2)}) %collective-permute-start.7) | collective-permute-done | bytes 147488 | tf_op jit(solution)/shard_map/ppermute | solution.py:806
  41.2 2.3 %collective-permute-start.9 = (f32[12,2,24,128]{3,2,1,0:T(8,128)S(1)}, f32[12,2,24,128]{3,2,1,0:T(8,128)S(1)}, u32[]{:S(2)}, u32[]{:S(2)}) collective-permute-start(f32[12,2,24,128]{3,2,1,0:T(8,128)S(1)} %shard_map.59), channel_id=1, source_target_pairs={{0,64},{64,0},{1,65},{65,1},{2,66},{66,2},{3,67},{67,3},{4,68},{68... | collective-permute-start | bytes 884744 | tf_op jit(solution)/shard_map/ppermute | solution.py:815
  43.5 0.9 %shard_map.58.win = f32[2,24,24,128]{3,2,1,0:T(8,128)S(1)} custom-call(f32[24,12,128]{2,1,0:T(8,128)S(1)} %get-tuple-element.44.f1, f32[24,12,128]{2,1,0:T(8,128)S(1)} %get-tuple-element.42.r1, f32[6,24,128]{2,1,0:T(8,128)S(1)} %collective-permute-done.5.zl, f32[6,24,128]{2,1,0:T(8,128)S(1)} %collective-permute-done.6.zh, ...), custom_call_target="tpu_custom_call" | custom-call | tf_op jit(solution)/shard_map/pallas_call | solution.py:54
  44.7 2.5 %shard_map.60 = (f32[36,24,128]{2,1,0:T(8,128)S(1)}, f32[36,24,128]{2,1,0:T(8,128)S(1)}, f32[38,24,128]{2,1,0:T(8,128)S(1)}, f32[18,32,128]{2,1,0:T(8,128)S(1)},...) custom-call(f32[2,24,24,128]{3,2,1,0:T(8,128)S(1)} %shard_map.58.win, ...), custom_call_target="tpu_custom_call" | custom-call | tf_op jit(solution)/shard_map/pallas_call | solution.py:54
  47.2 19.3 %all_to_all.16 = f32[128,4,128]{2,1,0:T(4,128)S(1)} all-to-all(f32[128,4,128]{2,1,0:T(4,128)S(1)} %bitcast.8), channel_id=1, replica_groups=mesh['gx'=2,'gy'=4,'gz'=16] {'gx','gy','gz'}, dimensions={0} | all-to-all | bytes 524288 | tf_op jit(solution)/shard_map/all_to_all | solution.py:863
  66.5 6.8 %shard_map.61 = (f32[48,24,128]{2,1,0:T(8,128)S(1)}, f32[48,24,128]{2,1,0:T(8,128)S(1)}, f32[128,128]{1,0:T(8,128)S(1)}) custom-call(f32[512,128]{1,0:T(8,128)S(1)} %bitcast.6, bf16[10,256,128]{2,1,0:T(8,128)(2,1)S(1)} %get-tuple-element.43.maps, f32[18,32,128]{2,1,0:T(8,128)S(1)} %get-tuple-element.50.f2, f32[18,32,128]{2,1,0:T(8,128)S(1)} %get-tuple-element.51.c2, ...), custom_call_target="tpu_custom_call" | custom-call | tf_op jit(solution)/shard_map/pallas_call | solution.py:54
  73.3 14.3 %all_to_all.17 = f32[128,1,128]{2,1,0:T(1,128)S(1)} all-to-all(f32[128,1,128]{2,1,0:T(1,128)S(1)} %bitcast.9), channel_id=1, replica_groups=mesh['gx'=2,'gy'=4,'gz'=16] {'gx','gy','gz'}, dimensions={0} | all-to-all | bytes 131072 | tf_op jit(solution)/shard_map/all_to_all | solution.py:877
  87.6 1.7 %shard_map.62 = (f32[48,48,48]{2,1,0:T(8,128)}, f32[48,48,48]{2,1,0:T(8,128)}) custom-call(f32[128,128]{1,0:T(8,128)S(1)} %bitcast.7, f32[3,48,24,128]{3,2,1,0:T(8,128)S(1)} %get-tuple-element.32.own, f32[48,24,128]{2,1,0:T(8,128)S(1)} %get-tuple-element.60.z, f32[48,24,128]{2,1,0:T(8,128)S(1)} %get-tuple-element.61.az, ...), custom_call_target="tpu_custom_call" | custom-call | tf_op jit(solution)/shard_map/pallas_call | solution.py:54
  (11 shorter events, 2.3 us)
Async XLA Ops:
  3.7 10.1 %collective-permute-start = (f32[10,24,128]{2,1,0:T(8,128)S(1)}, f32[10,24,128]{2,1,0:T(8,128)S(1)}, u32[]{:S(2)}, u32[]{:S(2)}) collective-permute-start(f32[10,24,128]{2,1,0:T(8,128)S(1)} %get-tuple-element.33), channel_id=1, source_target_pairs={{0,1},{1,2},{2,3},{3,4},{4,5},{5,6},{6,7},{7,8},{8,9},{9,10},{10,1... | collective-permute-start | bytes 368648 | tf_op jit(solution)/shard_map/ppermute | solution.py:806
  5.9 7.9 %collective-permute-start.1 = (f32[10,24,128]{2,1,0:T(8,128)S(1)}, f32[10,24,128]{2,1,0:T(8,128)S(1)}, u32[]{:S(2)}, u32[]{:S(2)}) collective-permute-start(f32[10,24,128]{2,1,0:T(8,128)S(1)} %get-tuple-element.34), channel_id=1, source_target_pairs={{0,15},{1,0},{2,1},{3,2},{4,3},{5,4},{6,5},{7,6},{8,7},{9,8},{10,9... | collective-permute-start | bytes 368648 | tf_op jit(solution)/shard_map/ppermute | solution.py:807
  14.6 5.4 %collective-permute-start.2 = (f32[3,104,128]{2,1,0:T(8,128)S(1)}, f32[3,104,128]{2,1,0:T(8,128)S(1)}, u32[]{:S(2)}, u32[]{:S(2)}) collective-permute-start(f32[3,104,128]{2,1,0:T(8,128)S(1)} %get-tuple-element.37), channel_id=1, source_target_pairs={{0,16},{16,32},{32,48},{48,0},{1,17},{17,33},{33,49},{49,1},{2,18}... | collective-permute-start | bytes 479240 | tf_op jit(solution)/shard_map/ppermute | solution.py:806
  15.8 4.1 %collective-permute-start.3 = (f32[3,104,128]{2,1,0:T(8,128)S(1)}, f32[3,104,128]{2,1,0:T(8,128)S(1)}, u32[]{:S(2)}, u32[]{:S(2)}) collective-permute-start(f32[3,104,128]{2,1,0:T(8,128)S(1)} %get-tuple-element.36.dn), channel_id=1, source_target_pairs={{0,48},{16,0},{32,16},{48,32},{1,49},{17,1},{33,17},{49,33},{2,50}... | collective-permute-start | bytes 479240 | tf_op jit(solution)/shard_map/ppermute | solution.py:807
  20.1 4.6 %collective-permute-start.4 = (f32[6,3,32,128]{3,2,1,0:T(8,128)S(1)}, f32[6,3,32,128]{3,2,1,0:T(8,128)S(1)}, u32[]{:S(2)}, u32[]{:S(2)}) collective-permute-start(f32[6,3,32,128]{3,2,1,0:T(8,128)S(1)} %shard_map.55), channel_id=1, source_target_pairs={{0,64},{64,0},{1,65},{65,1},{2,66},{66,2},{3,67},{67,3},{4,68},{68... | collective-permute-start | bytes 884744 | tf_op jit(solution)/shard_map/ppermute | solution.py:815
  27.1 7.3 %collective-permute-start.5 = (f32[6,24,128]{2,1,0:T(8,128)S(1)}, f32[6,24,128]{2,1,0:T(8,128)S(1)}, u32[]{:S(2)}, u32[]{:S(2)}) collective-permute-start(f32[6,24,128]{2,1,0:T(8,128)S(1)} %get-tuple-element.45), channel_id=1, source_target_pairs={{0,1},{1,2},{2,3},{3,4},{4,5},{5,6},{6,7},{7,8},{8,9},{9,10},{10,1... | collective-permute-start | bytes 221192 | tf_op jit(solution)/shard_map/ppermute | solution.py:806
  27.2 7.2 %collective-permute-start.6 = (f32[6,24,128]{2,1,0:T(8,128)S(1)}, f32[6,24,128]{2,1,0:T(8,128)S(1)}, u32[]{:S(2)}, u32[]{:S(2)}) collective-permute-start(f32[6,24,128]{2,1,0:T(8,128)S(1)} %get-tuple-element.46), channel_id=1, source_target_pairs={{0,15},{1,0},{2,1},{3,2},{4,3},{5,4},{6,5},{7,6},{8,7},{9,8},{10,9... | collective-permute-start | bytes 221192 | tf_op jit(solution)/shard_map/ppermute | solution.py:807
  34.9 5.6 %collective-permute-start.7 = (f32[12,24,128]{2,1,0:T(8,128)S(1)}, f32[12,24,128]{2,1,0:T(8,128)S(1)}, u32[]{:S(2)}, u32[]{:S(2)}) collective-permute-start(f32[12,24,128]{2,1,0:T(8,128)S(1)} %get-tuple-element.47), channel_id=1, source_target_pairs={{0,16},{16,32},{32,48},{48,0},{1,17},{17,33},{33,49},{49,1},{2,18}... | collective-permute-start | bytes 442376 | tf_op jit(solution)/shard_map/ppermute | solution.py:806
  36.2 4.3 %collective-permute-start.8 = (f32[12,24,128]{2,1,0:T(8,128)S(1)}, f32[12,24,128]{2,1,0:T(8,128)S(1)}, u32[]{:S(2)}, u32[]{:S(2)}) collective-permute-start(f32[12,24,128]{2,1,0:T(8,128)S(1)} %get-tuple-element.48), channel_id=1, source_target_pairs={{0,48},{16,0},{32,16},{48,32},{1,49},{17,1},{33,17},{49,33},{2,50}... | collective-permute-start | bytes 442376 | tf_op jit(solution)/shard_map/ppermute | solution.py:807
  41.2 3.5 %collective-permute-start.9 = (f32[12,2,24,128]{3,2,1,0:T(8,128)S(1)}, f32[12,2,24,128]{3,2,1,0:T(8,128)S(1)}, u32[]{:S(2)}, u32[]{:S(2)}) collective-permute-start(f32[12,2,24,128]{3,2,1,0:T(8,128)S(1)} %shard_map.59), channel_id=1, source_target_pairs={{0,64},{64,0},{1,65},{65,1},{2,66},{66,2},{3,67},{67,3},{4,68},{68... | collective-permute-start | bytes 884744 | tf_op jit(solution)/shard_map/ppermute | solution.py:815

commit v13 on v12

--- a/solution.py
+++ b/solution.py
@@ -12,7 +12,7 @@
 F32 = jnp.float32
 HI = lax.Precision.HIGHEST
 M0, M1, M2 = 10, 8, 12
-UF, UR, UM, UZ, UL = 12, 27, 18, 12, 6
+UF, UR, UM, UZ, UL = 12, 54, 36, 24, 24
 
 
 class Spec:
@@ -569,7 +569,7 @@
         return fw[x] - (1.5 + rw[x]) * e_out[x + 1] + 0.25 * paired(e_out, x)
 
     for ref, pair in ((f2, lambda x: left(2 * x) + left(2 * x + 1)), (r2, lambda x: rw[2 * x] + rw[2 * x + 1])):
-        coarsen_planes(pair, 18, tmp, acc.at[0], 24, 9)
+        coarsen_planes(pair, 18, tmp, acc.at[0], 24, 18)
         v = flat(acc.at[0])
         acc[0] = times(v, maps[DOWN1A]).reshape(18, 16, 128)
         acc[1] = times(v, maps[DOWN1B]).reshape(18, 16, 128)

time: 89.6 us -> 88.3 us (0.985)
  Pallas kernels: 22.8 us -> 21.4 us
    pallas_call x13, Pallas kernels: 22.8 us -> 21.4 us  [run(): pl.pallas_call(kernel, out_shape=outs, in_specs=[hbm if far_in else vmem]...]
where the time goes in v13:
time: 88.3 us; the launch traced here: 88.1 us
  blocking collectives  33.6 us (38%)
  starting transfers between devices  23.1 us (26%)
  Pallas kernels  21.4 us (24%)
  waiting for transfers between devices  9.06 us (10%)
  between operations  0.89 us (1%)
    pallas_call x13, Pallas kernels, run(): pl.pallas_call(kernel, out_shape=outs, in_specs=[hbm if far_in else vmem]...  21.4 us
    all_to_all x1, blocking collectives, body(): g = lax.all_to_all(g, ALL, 0, 0, tiled=True)  19.3 us
    all_to_all x1, blocking collectives, body(): lax.all_to_all(sums.reshape(count, 1, 128), ALL, 0, 0, tiled=True)  14.3 us
    ppermute x4, starting transfers between devices, ring(): high = lax.ppermute(dn, axis, fall)  12.9 us
    ppermute x4, waiting for transfers between devices, ring(): low = lax.ppermute(up, axis, rise)  8.77 us
    ppermute x2, starting transfers between devices, swap(): return lax.ppermute(v, 'gx', [(0, 1), (1, 0)])  5.39 us
    ppermute x4, starting transfers between devices, ring(): low = lax.ppermute(up, axis, rise)  4.81 us
  transfers between devices with their start and end apart: 10, of which 5 were waited for; matrix products, arithmetic and copies ran while one was open for 0% of the time, Pallas kernels for 5%

profile of v13, /device:TPU:1, one launch (start us, length us, event | category | flops | bytes accessed | tf_op | source)
XLA Modules:
  0.0 88.1 jit_solution(13131865628458186314)
XLA Ops:
  0.6 3.1 %shard_map.50 = (f32[10,24,128]{2,1,0:T(8,128)S(1)}, f32[10,24,128]{2,1,0:T(8,128)S(1)}, f32[3,48,24,128]{3,2,1,0:T(8,128)S(1)}) custom-call(f32[48,48,48]{2,1,0:T(8,128)} %x0.1, f32[48,48,48]{2,1,0:T(8,128)} %b.1, f32[48,48,48]{2,1,0:T(8,128)} %rea.1), custom_call_target="tpu_custom_call" | custom-call | tf_op jit(solution)/shard_map/pallas_call | solution.py:54
  3.7 2.2 %collective-permute-start = (f32[10,24,128]{2,1,0:T(8,128)S(1)}, f32[10,24,128]{2,1,0:T(8,128)S(1)}, u32[]{:S(2)}, u32[]{:S(2)}) collective-permute-start(f32[10,24,128]{2,1,0:T(8,128)S(1)} %get-tuple-element.33), channel_id=1, source_target_pairs={{0,1},{1,2},{2,3},{3,4},{4,5},{5,6},{6,7},{7,8},{8,9},{9,10},{10,1... | collective-permute-start | bytes 368648 | tf_op jit(solution)/shard_map/ppermute | solution.py:806
  5.9 5.0 %collective-permute-start.1 = (f32[10,24,128]{2,1,0:T(8,128)S(1)}, f32[10,24,128]{2,1,0:T(8,128)S(1)}, u32[]{:S(2)}, u32[]{:S(2)}) collective-permute-start(f32[10,24,128]{2,1,0:T(8,128)S(1)} %get-tuple-element.34), channel_id=1, source_target_pairs={{0,15},{1,0},{2,1},{3,2},{4,3},{5,4},{6,5},{7,6},{8,7},{9,8},{10,9... | collective-permute-start | bytes 368648 | tf_op jit(solution)/shard_map/ppermute | solution.py:807
  10.9 1.0 %shard_map.51 = (f32[3,24,16,128]{3,2,1,0:T(8,128)S(1)}, f32[24,12,128]{2,1,0:T(8,128)S(1)}, bf16[10,256,128]{2,1,0:T(8,128)(2,1)S(1)}) custom-call(f32[3,48,24,128]{3,2,1,0:T(8,128)S(1)} %get-tuple-element.32.own), custom_call_target="tpu_custom_call" | custom-call | tf_op jit(solution)/shard_map/pallas_call | solution.py:54
  11.9 1.9 %collective-permute-done.zl = f32[10,24,128]{2,1,0:T(8,128)S(1)} collective-permute-done((f32[10,24,128]{2,1,0:T(8,128)S(1)}, f32[10,24,128]{2,1,0:T(8,128)S(1)}, u32[]{:S(2)}, u32[]{:S(2)}) %collective-permute-start) | collective-permute-done | bytes 122912 | tf_op jit(solution)/shard_map/ppermute | solution.py:806
  14.6 1.3 %collective-permute-start.2 = (f32[3,104,128]{2,1,0:T(8,128)S(1)}, f32[3,104,128]{2,1,0:T(8,128)S(1)}, u32[]{:S(2)}, u32[]{:S(2)}) collective-permute-start(f32[3,104,128]{2,1,0:T(8,128)S(1)} %get-tuple-element.37), channel_id=1, source_target_pairs={{0,16},{16,32},{32,48},{48,0},{1,17},{17,33},{33,49},{49,1},{2,18}... | collective-permute-start | bytes 479240 | tf_op jit(solution)/shard_map/ppermute | solution.py:806
  15.8 1.5 %collective-permute-start.3 = (f32[3,104,128]{2,1,0:T(8,128)S(1)}, f32[3,104,128]{2,1,0:T(8,128)S(1)}, u32[]{:S(2)}, u32[]{:S(2)}) collective-permute-start(f32[3,104,128]{2,1,0:T(8,128)S(1)} %get-tuple-element.36.dn), channel_id=1, source_target_pairs={{0,48},{16,0},{32,16},{48,32},{1,49},{17,1},{33,17},{49,33},{2,50}... | collective-permute-start | bytes 479240 | tf_op jit(solution)/shard_map/ppermute | solution.py:807
  17.3 0.9 %shard_map.53.mid = f32[3,48,24,128]{3,2,1,0:T(8,128)S(1)} custom-call(f32[3,48,24,128]{3,2,1,0:T(8,128)S(1)} %get-tuple-element.32.own, f32[10,24,128]{2,1,0:T(8,128)S(1)} %collective-permute-done.zl, f32[10,24,128]{2,1,0:T(8,128)S(1)} %collective-permute-done.1.zh, f32[3,104,128]{2,1,0:T(8,128)S(1)} %get-tuple-element.36.dn), custom_call_target="tpu_custom_call" | custom-call | tf_op jit(solution)/shard_map/pallas_call | solution.py:54
  18.2 1.7 %collective-permute-done.2.yl = f32[3,104,128]{2,1,0:T(8,128)S(1)} collective-permute-done((f32[3,104,128]{2,1,0:T(8,128)S(1)}, f32[3,104,128]{2,1,0:T(8,128)S(1)}, u32[]{:S(2)}, u32[]{:S(2)}) %collective-permute-start.2) | collective-permute-done | bytes 159776 | tf_op jit(solution)/shard_map/ppermute | solution.py:806
  20.1 3.1 %collective-permute-start.4 = (f32[6,3,32,128]{3,2,1,0:T(8,128)S(1)}, f32[6,3,32,128]{3,2,1,0:T(8,128)S(1)}, u32[]{:S(2)}, u32[]{:S(2)}) collective-permute-start(f32[6,3,32,128]{3,2,1,0:T(8,128)S(1)} %shard_map.55), channel_id=1, source_target_pairs={{0,64},{64,0},{1,65},{65,1},{2,66},{66,2},{3,67},{67,3},{4,68},{68... | collective-permute-start | bytes 884744 | tf_op jit(solution)/shard_map/ppermute | solution.py:815
  23.2 1.5 %shard_map.54 = (f32[48,32,128]{2,1,0:T(8,128)S(1)}, f32[48,32,128]{2,1,0:T(8,128)S(1)}, f32[48,32,128]{2,1,0:T(8,128)S(1)}, f32[48,32,128]{2,1,0:T(8,128)S(1)}) custom-call(f32[3,48,24,128]{3,2,1,0:T(8,128)S(1)} %shard_map.53.mid, f32[3,104,128]{2,1,0:T(8,128)S(1)} %collective-permute-done.2.yl, f32[3,104,128]{2,1,0:T(8,128)S(1)} %collective-permute-done.3.yh), custom_call_target="tpu_custom_call" | custom-call | tf_op jit(solution)/shard_map/pallas_call | solution.py:54
  24.7 2.0 %shard_map.56 = (f32[54,32,128]{2,1,0:T(8,128)S(1)}, f32[54,32,128]{2,1,0:T(8,128)S(1)}, f32[56,32,128]{2,1,0:T(8,128)S(1)}, f32[24,12,128]{2,1,0:T(8,128)S(1)},...) custom-call(f32[48,32,128]{2,1,0:T(8,128)S(1)} %get-tuple-element.38.xw, ...), custom_call_target="tpu_custom_call" | custom-call | tf_op jit(solution)/shard_map/pallas_call | solution.py:54
  26.8 4.9 %collective-permute-start.6 = (f32[6,24,128]{2,1,0:T(8,128)S(1)}, f32[6,24,128]{2,1,0:T(8,128)S(1)}, u32[]{:S(2)}, u32[]{:S(2)}) collective-permute-start(f32[6,24,128]{2,1,0:T(8,128)S(1)} %get-tuple-element.46), channel_id=1, source_target_pairs={{0,15},{1,0},{2,1},{3,2},{4,3},{5,4},{6,5},{7,6},{8,7},{9,8},{10,9... | collective-permute-start | bytes 221192 | tf_op jit(solution)/shard_map/ppermute | solution.py:807
  31.7 2.3 %collective-permute-done.5.zl = f32[6,24,128]{2,1,0:T(8,128)S(1)} collective-permute-done((f32[6,24,128]{2,1,0:T(8,128)S(1)}, f32[6,24,128]{2,1,0:T(8,128)S(1)}, u32[]{:S(2)}, u32[]{:S(2)}) %collective-permute-start.5) | collective-permute-done | bytes 73760 | tf_op jit(solution)/shard_map/ppermute | solution.py:806
  34.5 1.3 %collective-permute-start.7 = (f32[12,24,128]{2,1,0:T(8,128)S(1)}, f32[12,24,128]{2,1,0:T(8,128)S(1)}, u32[]{:S(2)}, u32[]{:S(2)}) collective-permute-start(f32[12,24,128]{2,1,0:T(8,128)S(1)} %get-tuple-element.47), channel_id=1, source_target_pairs={{0,16},{16,32},{32,48},{48,0},{1,17},{17,33},{33,49},{49,1},{2,18}... | collective-permute-start | bytes 442376 | tf_op jit(solution)/shard_map/ppermute | solution.py:806
  35.7 1.5 %collective-permute-start.8 = (f32[12,24,128]{2,1,0:T(8,128)S(1)}, f32[12,24,128]{2,1,0:T(8,128)S(1)}, u32[]{:S(2)}, u32[]{:S(2)}) collective-permute-start(f32[12,24,128]{2,1,0:T(8,128)S(1)} %get-tuple-element.48), channel_id=1, source_target_pairs={{0,48},{16,0},{32,16},{48,32},{1,49},{17,1},{33,17},{49,33},{2,50}... | collective-permute-start | bytes 442376 | tf_op jit(solution)/shard_map/ppermute | solution.py:807
  37.3 2.8 %collective-permute-done.7.yl = f32[12,24,128]{2,1,0:T(8,128)S(1)} collective-permute-done((f32[12,24,128]{2,1,0:T(8,128)S(1)}, f32[12,24,128]{2,1,0:T(8,128)S(1)}, u32[]{:S(2)}, u32[]{:S(2)}) %collective-permute-start.7) | collective-permute-done | bytes 147488 | tf_op jit(solution)/shard_map/ppermute | solution.py:806
  40.7 2.3 %collective-permute-start.9 = (f32[12,2,24,128]{3,2,1,0:T(8,128)S(1)}, f32[12,2,24,128]{3,2,1,0:T(8,128)S(1)}, u32[]{:S(2)}, u32[]{:S(2)}) collective-permute-start(f32[12,2,24,128]{3,2,1,0:T(8,128)S(1)} %shard_map.59), channel_id=1, source_target_pairs={{0,64},{64,0},{1,65},{65,1},{2,66},{66,2},{3,67},{67,3},{4,68},{68... | collective-permute-start | bytes 884744 | tf_op jit(solution)/shard_map/ppermute | solution.py:815
  43.0 0.9 %shard_map.58.win = f32[2,24,24,128]{3,2,1,0:T(8,128)S(1)} custom-call(f32[24,12,128]{2,1,0:T(8,128)S(1)} %get-tuple-element.44.f1, f32[24,12,128]{2,1,0:T(8,128)S(1)} %get-tuple-element.42.r1, f32[6,24,128]{2,1,0:T(8,128)S(1)} %collective-permute-done.5.zl, f32[6,24,128]{2,1,0:T(8,128)S(1)} %collective-permute-done.6.zh, ...), custom_call_target="tpu_custom_call" | custom-call | tf_op jit(solution)/shard_map/pallas_call | solution.py:54
  44.2 2.1 %shard_map.60 = (f32[36,24,128]{2,1,0:T(8,128)S(1)}, f32[36,24,128]{2,1,0:T(8,128)S(1)}, f32[38,24,128]{2,1,0:T(8,128)S(1)}, f32[18,32,128]{2,1,0:T(8,128)S(1)},...) custom-call(f32[2,24,24,128]{3,2,1,0:T(8,128)S(1)} %shard_map.58.win, ...), custom_call_target="tpu_custom_call" | custom-call | tf_op jit(solution)/shard_map/pallas_call | solution.py:54
  46.4 19.3 %all_to_all.16 = f32[128,4,128]{2,1,0:T(4,128)S(1)} all-to-all(f32[128,4,128]{2,1,0:T(4,128)S(1)} %bitcast.8), channel_id=1, replica_groups=mesh['gx'=2,'gy'=4,'gz'=16] {'gx','gy','gz'}, dimensions={0} | all-to-all | bytes 524288 | tf_op jit(solution)/shard_map/all_to_all | solution.py:863
  65.7 6.3 %shard_map.61 = (f32[48,24,128]{2,1,0:T(8,128)S(1)}, f32[48,24,128]{2,1,0:T(8,128)S(1)}, f32[128,128]{1,0:T(8,128)S(1)}) custom-call(f32[512,128]{1,0:T(8,128)S(1)} %bitcast.6, bf16[10,256,128]{2,1,0:T(8,128)(2,1)S(1)} %get-tuple-element.43.maps, f32[18,32,128]{2,1,0:T(8,128)S(1)} %get-tuple-element.50.f2, f32[18,32,128]{2,1,0:T(8,128)S(1)} %get-tuple-element.51.c2, ...), custom_call_target="tpu_custom_call" | custom-call | tf_op jit(solution)/shard_map/pallas_call | solution.py:54
  72.0 14.3 %all_to_all.17 = f32[128,1,128]{2,1,0:T(1,128)S(1)} all-to-all(f32[128,1,128]{2,1,0:T(1,128)S(1)} %bitcast.9), channel_id=1, replica_groups=mesh['gx'=2,'gy'=4,'gz'=16] {'gx','gy','gz'}, dimensions={0} | all-to-all | bytes 131072 | tf_op jit(solution)/shard_map/all_to_all | solution.py:877
  86.3 1.7 %shard_map.62 = (f32[48,48,48]{2,1,0:T(8,128)}, f32[48,48,48]{2,1,0:T(8,128)}) custom-call(f32[128,128]{1,0:T(8,128)S(1)} %bitcast.7, f32[3,48,24,128]{3,2,1,0:T(8,128)S(1)} %get-tuple-element.32.own, f32[48,24,128]{2,1,0:T(8,128)S(1)} %get-tuple-element.60.z, f32[48,24,128]{2,1,0:T(8,128)S(1)} %get-tuple-element.61.az, ...), custom_call_target="tpu_custom_call" | custom-call | tf_op jit(solution)/shard_map/pallas_call | solution.py:54
  (11 shorter events, 2.3 us)
Async XLA Ops:
  3.7 10.1 %collective-permute-start = (f32[10,24,128]{2,1,0:T(8,128)S(1)}, f32[10,24,128]{2,1,0:T(8,128)S(1)}, u32[]{:S(2)}, u32[]{:S(2)}) collective-permute-start(f32[10,24,128]{2,1,0:T(8,128)S(1)} %get-tuple-element.33), channel_id=1, source_target_pairs={{0,1},{1,2},{2,3},{3,4},{4,5},{5,6},{6,7},{7,8},{8,9},{9,10},{10,1... | collective-permute-start | bytes 368648 | tf_op jit(solution)/shard_map/ppermute | solution.py:806
  5.9 7.9 %collective-permute-start.1 = (f32[10,24,128]{2,1,0:T(8,128)S(1)}, f32[10,24,128]{2,1,0:T(8,128)S(1)}, u32[]{:S(2)}, u32[]{:S(2)}) collective-permute-start(f32[10,24,128]{2,1,0:T(8,128)S(1)} %get-tuple-element.34), channel_id=1, source_target_pairs={{0,15},{1,0},{2,1},{3,2},{4,3},{5,4},{6,5},{7,6},{8,7},{9,8},{10,9... | collective-permute-start | bytes 368648 | tf_op jit(solution)/shard_map/ppermute | solution.py:807
  14.6 5.4 %collective-permute-start.2 = (f32[3,104,128]{2,1,0:T(8,128)S(1)}, f32[3,104,128]{2,1,0:T(8,128)S(1)}, u32[]{:S(2)}, u32[]{:S(2)}) collective-permute-start(f32[3,104,128]{2,1,0:T(8,128)S(1)} %get-tuple-element.37), channel_id=1, source_target_pairs={{0,16},{16,32},{32,48},{48,0},{1,17},{17,33},{33,49},{49,1},{2,18}... | collective-permute-start | bytes 479240 | tf_op jit(solution)/shard_map/ppermute | solution.py:806
  15.8 4.1 %collective-permute-start.3 = (f32[3,104,128]{2,1,0:T(8,128)S(1)}, f32[3,104,128]{2,1,0:T(8,128)S(1)}, u32[]{:S(2)}, u32[]{:S(2)}) collective-permute-start(f32[3,104,128]{2,1,0:T(8,128)S(1)} %get-tuple-element.36.dn), channel_id=1, source_target_pairs={{0,48},{16,0},{32,16},{48,32},{1,49},{17,1},{33,17},{49,33},{2,50}... | collective-permute-start | bytes 479240 | tf_op jit(solution)/shard_map/ppermute | solution.py:807
  20.1 4.6 %collective-permute-start.4 = (f32[6,3,32,128]{3,2,1,0:T(8,128)S(1)}, f32[6,3,32,128]{3,2,1,0:T(8,128)S(1)}, u32[]{:S(2)}, u32[]{:S(2)}) collective-permute-start(f32[6,3,32,128]{3,2,1,0:T(8,128)S(1)} %shard_map.55), channel_id=1, source_target_pairs={{0,64},{64,0},{1,65},{65,1},{2,66},{66,2},{3,67},{67,3},{4,68},{68... | collective-permute-start | bytes 884744 | tf_op jit(solution)/shard_map/ppermute | solution.py:815
  26.7 7.3 %collective-permute-start.5 = (f32[6,24,128]{2,1,0:T(8,128)S(1)}, f32[6,24,128]{2,1,0:T(8,128)S(1)}, u32[]{:S(2)}, u32[]{:S(2)}) collective-permute-start(f32[6,24,128]{2,1,0:T(8,128)S(1)} %get-tuple-element.45), channel_id=1, source_target_pairs={{0,1},{1,2},{2,3},{3,4},{4,5},{5,6},{6,7},{7,8},{8,9},{9,10},{10,1... | collective-permute-start | bytes 221192 | tf_op jit(solution)/shard_map/ppermute | solution.py:806
  26.8 7.3 %collective-permute-start.6 = (f32[6,24,128]{2,1,0:T(8,128)S(1)}, f32[6,24,128]{2,1,0:T(8,128)S(1)}, u32[]{:S(2)}, u32[]{:S(2)}) collective-permute-start(f32[6,24,128]{2,1,0:T(8,128)S(1)} %get-tuple-element.46), channel_id=1, source_target_pairs={{0,15},{1,0},{2,1},{3,2},{4,3},{5,4},{6,5},{7,6},{8,7},{9,8},{10,9... | collective-permute-start | bytes 221192 | tf_op jit(solution)/shard_map/ppermute | solution.py:807
  34.5 5.6 %collective-permute-start.7 = (f32[12,24,128]{2,1,0:T(8,128)S(1)}, f32[12,24,128]{2,1,0:T(8,128)S(1)}, u32[]{:S(2)}, u32[]{:S(2)}) collective-permute-start(f32[12,24,128]{2,1,0:T(8,128)S(1)} %get-tuple-element.47), channel_id=1, source_target_pairs={{0,16},{16,32},{32,48},{48,0},{1,17},{17,33},{33,49},{49,1},{2,18}... | collective-permute-start | bytes 442376 | tf_op jit(solution)/shard_map/ppermute | solution.py:806
  35.7 4.3 %collective-permute-start.8 = (f32[12,24,128]{2,1,0:T(8,128)S(1)}, f32[12,24,128]{2,1,0:T(8,128)S(1)}, u32[]{:S(2)}, u32[]{:S(2)}) collective-permute-start(f32[12,24,128]{2,1,0:T(8,128)S(1)} %get-tuple-element.48), channel_id=1, source_target_pairs={{0,48},{16,0},{32,16},{48,32},{1,49},{17,1},{33,17},{49,33},{2,50}... | collective-permute-start | bytes 442376 | tf_op jit(solution)/shard_map/ppermute | solution.py:807
  40.7 3.5 %collective-permute-start.9 = (f32[12,2,24,128]{3,2,1,0:T(8,128)S(1)}, f32[12,2,24,128]{3,2,1,0:T(8,128)S(1)}, u32[]{:S(2)}, u32[]{:S(2)}) collective-permute-start(f32[12,2,24,128]{3,2,1,0:T(8,128)S(1)} %shard_map.59), channel_id=1, source_target_pairs={{0,64},{64,0},{1,65},{65,1},{2,66},{66,2},{3,67},{67,3},{4,68},{68... | collective-permute-start | bytes 884744 | tf_op jit(solution)/shard_map/ppermute | solution.py:815

commit v14 on v13

--- a/solution.py
+++ b/solution.py
@@ -161,7 +161,7 @@
                     v = jnp.where(up, even, odd) if b else jnp.where(up, odd, even)
                     ref[i, pl.ds(YBASE[a] + k, h, stride=8), :] = v[s : s + h]
 
-    loop(3, some)
+    loop(3, some, 3)
 
 
 def ypack1(own, zl, zh, up_ref, dn_ref, u):
@@ -404,9 +404,9 @@
 
     def one(i):
         for a in range(2):
-            plane1(lambda x, a: both[a][x], zl, zh, yl, yh, (1 - ids[0]) * 12 + i, a, out.at[i], a, ends, spare.at[a])
-
-    loop(12, one, 2)
+            plane1(lambda x, a: both[a][x], zl, zh, yl, yh, (1 - ids[0]) * 12 + i, a, out.at[i], a, ends, spare.at[i, a])
+
+    loop(12, one, 12)
 
 
 def beside0(c):
@@ -522,7 +522,7 @@
 
 def k_ypack1(f1, r1, zl, zh, up, dn):
     both = (f1, r1)
-    ypack1(lambda x, a: both[a][x], zl, zh, up, dn, 6)
+    ypack1(lambda x, a: both[a][x], zl, zh, up, dn, 12)
 
 
 def k_windows1(f1, r1, zl, zh, yl, yh, out, spare):
@@ -850,7 +850,7 @@
     zl, zh = ring(z1h, z1l, "gz")
     up, dn = run(k_ypack1, (sds(*L1.yshape),) * 2, (f1, r1, zl, zh))
     yl, yh = ring(up, dn, "gy")
-    xr = swap(run(k_xpack1, sds(*L1.xshape), (f1, r1, zl, zh, yl, yh), [(2, 2, 24, 128)]))
+    xr = swap(run(k_xpack1, sds(*L1.xshape), (f1, r1, zl, zh, yl, yh), [(12, 2, 2, 24, 128)]))
     p1, q1, p2, q2 = (36, 24, 128), (38, 24, 128), (18, 32, 128), (20, 32, 128)
     win = run(k_windows1, sds(2, 24, 24, 128), (f1, r1, zl, zh, yl, yh), [(8, 2, 24, 128)])
     f1w, c1w, e1w, f2w, c2w, e2w, g = run(

time: 88.3 us -> 87.3 us (0.989)
  Pallas kernels: 21.4 us -> 20.5 us
    pallas_call x13, Pallas kernels: 21.4 us -> 20.5 us  [run(): pl.pallas_call(kernel, out_shape=outs, in_specs=[hbm if far_in else vmem]...]
where the time goes in v14:
time: 87.3 us; the launch traced here: 87.2 us
  blocking collectives  33.6 us (38%)
  starting transfers between devices  23.1 us (26%)
  Pallas kernels  20.5 us (23%)
  waiting for transfers between devices  9.06 us (10%)
  between operations  0.89 us (1%)
    pallas_call x13, Pallas kernels, run(): pl.pallas_call(kernel, out_shape=outs, in_specs=[hbm if far_in else vmem]...  20.5 us
    all_to_all x1, blocking collectives, body(): g = lax.all_to_all(g, ALL, 0, 0, tiled=True)  19.3 us
    all_to_all x1, blocking collectives, body(): lax.all_to_all(sums.reshape(count, 1, 128), ALL, 0, 0, tiled=True)  14.3 us
    ppermute x4, starting transfers between devices, ring(): high = lax.ppermute(dn, axis, fall)  12.9 us
    ppermute x4, waiting for transfers between devices, ring(): low = lax.ppermute(up, axis, rise)  8.77 us
    ppermute x2, starting transfers between devices, swap(): return lax.ppermute(v, 'gx', [(0, 1), (1, 0)])  5.39 us
    ppermute x4, starting transfers between devices, ring(): low = lax.ppermute(up, axis, rise)  4.81 us
  transfers between devices with their start and end apart: 10, of which 5 were waited for; matrix products, arithmetic and copies ran while one was open for 0% of the time, Pallas kernels for 5%

profile of v14, /device:TPU:1, one launch (start us, length us, event | category | flops | bytes accessed | tf_op | source)
XLA Modules:
  0.0 87.2 jit_solution(2648974676797640508)
XLA Ops:
  0.6 3.1 %shard_map.50 = (f32[10,24,128]{2,1,0:T(8,128)S(1)}, f32[10,24,128]{2,1,0:T(8,128)S(1)}, f32[3,48,24,128]{3,2,1,0:T(8,128)S(1)}) custom-call(f32[48,48,48]{2,1,0:T(8,128)} %x0.1, f32[48,48,48]{2,1,0:T(8,128)} %b.1, f32[48,48,48]{2,1,0:T(8,128)} %rea.1), custom_call_target="tpu_custom_call" | custom-call | tf_op jit(solution)/shard_map/pallas_call | solution.py:54
  3.7 2.2 %collective-permute-start = (f32[10,24,128]{2,1,0:T(8,128)S(1)}, f32[10,24,128]{2,1,0:T(8,128)S(1)}, u32[]{:S(2)}, u32[]{:S(2)}) collective-permute-start(f32[10,24,128]{2,1,0:T(8,128)S(1)} %get-tuple-element.33), channel_id=1, source_target_pairs={{0,1},{1,2},{2,3},{3,4},{4,5},{5,6},{6,7},{7,8},{8,9},{9,10},{10,1... | collective-permute-start | bytes 368648 | tf_op jit(solution)/shard_map/ppermute | solution.py:806
  5.9 5.0 %collective-permute-start.1 = (f32[10,24,128]{2,1,0:T(8,128)S(1)}, f32[10,24,128]{2,1,0:T(8,128)S(1)}, u32[]{:S(2)}, u32[]{:S(2)}) collective-permute-start(f32[10,24,128]{2,1,0:T(8,128)S(1)} %get-tuple-element.34), channel_id=1, source_target_pairs={{0,15},{1,0},{2,1},{3,2},{4,3},{5,4},{6,5},{7,6},{8,7},{9,8},{10,9... | collective-permute-start | bytes 368648 | tf_op jit(solution)/shard_map/ppermute | solution.py:807
  10.9 1.0 %shard_map.51 = (f32[3,24,16,128]{3,2,1,0:T(8,128)S(1)}, f32[24,12,128]{2,1,0:T(8,128)S(1)}, bf16[10,256,128]{2,1,0:T(8,128)(2,1)S(1)}) custom-call(f32[3,48,24,128]{3,2,1,0:T(8,128)S(1)} %get-tuple-element.32.own), custom_call_target="tpu_custom_call" | custom-call | tf_op jit(solution)/shard_map/pallas_call | solution.py:54
  11.9 1.9 %collective-permute-done.zl = f32[10,24,128]{2,1,0:T(8,128)S(1)} collective-permute-done((f32[10,24,128]{2,1,0:T(8,128)S(1)}, f32[10,24,128]{2,1,0:T(8,128)S(1)}, u32[]{:S(2)}, u32[]{:S(2)}) %collective-permute-start) | collective-permute-done | bytes 122912 | tf_op jit(solution)/shard_map/ppermute | solution.py:806
  14.2 1.3 %collective-permute-start.2 = (f32[3,104,128]{2,1,0:T(8,128)S(1)}, f32[3,104,128]{2,1,0:T(8,128)S(1)}, u32[]{:S(2)}, u32[]{:S(2)}) collective-permute-start(f32[3,104,128]{2,1,0:T(8,128)S(1)} %get-tuple-element.37), channel_id=1, source_target_pairs={{0,16},{16,32},{32,48},{48,0},{1,17},{17,33},{33,49},{49,1},{2,18}... | collective-permute-start | bytes 479240 | tf_op jit(solution)/shard_map/ppermute | solution.py:806
  15.5 1.5 %collective-permute-start.3 = (f32[3,104,128]{2,1,0:T(8,128)S(1)}, f32[3,104,128]{2,1,0:T(8,128)S(1)}, u32[]{:S(2)}, u32[]{:S(2)}) collective-permute-start(f32[3,104,128]{2,1,0:T(8,128)S(1)} %get-tuple-element.36.dn), channel_id=1, source_target_pairs={{0,48},{16,0},{32,16},{48,32},{1,49},{17,1},{33,17},{49,33},{2,50}... | collective-permute-start | bytes 479240 | tf_op jit(solution)/shard_map/ppermute | solution.py:807
  16.9 0.9 %shard_map.53.mid = f32[3,48,24,128]{3,2,1,0:T(8,128)S(1)} custom-call(f32[3,48,24,128]{3,2,1,0:T(8,128)S(1)} %get-tuple-element.32.own, f32[10,24,128]{2,1,0:T(8,128)S(1)} %collective-permute-done.zl, f32[10,24,128]{2,1,0:T(8,128)S(1)} %collective-permute-done.1.zh, f32[3,104,128]{2,1,0:T(8,128)S(1)} %get-tuple-element.36.dn), custom_call_target="tpu_custom_call" | custom-call | tf_op jit(solution)/shard_map/pallas_call | solution.py:54
  17.9 1.7 %collective-permute-done.2.yl = f32[3,104,128]{2,1,0:T(8,128)S(1)} collective-permute-done((f32[3,104,128]{2,1,0:T(8,128)S(1)}, f32[3,104,128]{2,1,0:T(8,128)S(1)}, u32[]{:S(2)}, u32[]{:S(2)}) %collective-permute-start.2) | collective-permute-done | bytes 159776 | tf_op jit(solution)/shard_map/ppermute | solution.py:806
  19.7 3.1 %collective-permute-start.4 = (f32[6,3,32,128]{3,2,1,0:T(8,128)S(1)}, f32[6,3,32,128]{3,2,1,0:T(8,128)S(1)}, u32[]{:S(2)}, u32[]{:S(2)}) collective-permute-start(f32[6,3,32,128]{3,2,1,0:T(8,128)S(1)} %shard_map.55), channel_id=1, source_target_pairs={{0,64},{64,0},{1,65},{65,1},{2,66},{66,2},{3,67},{67,3},{4,68},{68... | collective-permute-start | bytes 884744 | tf_op jit(solution)/shard_map/ppermute | solution.py:815
  22.8 1.5 %shard_map.54 = (f32[48,32,128]{2,1,0:T(8,128)S(1)}, f32[48,32,128]{2,1,0:T(8,128)S(1)}, f32[48,32,128]{2,1,0:T(8,128)S(1)}, f32[48,32,128]{2,1,0:T(8,128)S(1)}) custom-call(f32[3,48,24,128]{3,2,1,0:T(8,128)S(1)} %shard_map.53.mid, f32[3,104,128]{2,1,0:T(8,128)S(1)} %collective-permute-done.2.yl, f32[3,104,128]{2,1,0:T(8,128)S(1)} %collective-permute-done.3.yh), custom_call_target="tpu_custom_call" | custom-call | tf_op jit(solution)/shard_map/pallas_call | solution.py:54
  24.4 2.0 %shard_map.56 = (f32[54,32,128]{2,1,0:T(8,128)S(1)}, f32[54,32,128]{2,1,0:T(8,128)S(1)}, f32[56,32,128]{2,1,0:T(8,128)S(1)}, f32[24,12,128]{2,1,0:T(8,128)S(1)},...) custom-call(f32[48,32,128]{2,1,0:T(8,128)S(1)} %get-tuple-element.38.xw, ...), custom_call_target="tpu_custom_call" | custom-call | tf_op jit(solution)/shard_map/pallas_call | solution.py:54
  26.4 4.9 %collective-permute-start.6 = (f32[6,24,128]{2,1,0:T(8,128)S(1)}, f32[6,24,128]{2,1,0:T(8,128)S(1)}, u32[]{:S(2)}, u32[]{:S(2)}) collective-permute-start(f32[6,24,128]{2,1,0:T(8,128)S(1)} %get-tuple-element.46), channel_id=1, source_target_pairs={{0,15},{1,0},{2,1},{3,2},{4,3},{5,4},{6,5},{7,6},{8,7},{9,8},{10,9... | collective-permute-start | bytes 221192 | tf_op jit(solution)/shard_map/ppermute | solution.py:807
  31.3 2.3 %collective-permute-done.5.zl = f32[6,24,128]{2,1,0:T(8,128)S(1)} collective-permute-done((f32[6,24,128]{2,1,0:T(8,128)S(1)}, f32[6,24,128]{2,1,0:T(8,128)S(1)}, u32[]{:S(2)}, u32[]{:S(2)}) %collective-permute-start.5) | collective-permute-done | bytes 73760 | tf_op jit(solution)/shard_map/ppermute | solution.py:806
  33.9 1.3 %collective-permute-start.7 = (f32[12,24,128]{2,1,0:T(8,128)S(1)}, f32[12,24,128]{2,1,0:T(8,128)S(1)}, u32[]{:S(2)}, u32[]{:S(2)}) collective-permute-start(f32[12,24,128]{2,1,0:T(8,128)S(1)} %get-tuple-element.47), channel_id=1, source_target_pairs={{0,16},{16,32},{32,48},{48,0},{1,17},{17,33},{33,49},{49,1},{2,18}... | collective-permute-start | bytes 442376 | tf_op jit(solution)/shard_map/ppermute | solution.py:806
  35.2 1.5 %collective-permute-start.8 = (f32[12,24,128]{2,1,0:T(8,128)S(1)}, f32[12,24,128]{2,1,0:T(8,128)S(1)}, u32[]{:S(2)}, u32[]{:S(2)}) collective-permute-start(f32[12,24,128]{2,1,0:T(8,128)S(1)} %get-tuple-element.48), channel_id=1, source_target_pairs={{0,48},{16,0},{32,16},{48,32},{1,49},{17,1},{33,17},{49,33},{2,50}... | collective-permute-start | bytes 442376 | tf_op jit(solution)/shard_map/ppermute | solution.py:807
  36.7 2.8 %collective-permute-done.7.yl = f32[12,24,128]{2,1,0:T(8,128)S(1)} collective-permute-done((f32[12,24,128]{2,1,0:T(8,128)S(1)}, f32[12,24,128]{2,1,0:T(8,128)S(1)}, u32[]{:S(2)}, u32[]{:S(2)}) %collective-permute-start.7) | collective-permute-done | bytes 147488 | tf_op jit(solution)/shard_map/ppermute | solution.py:806
  39.8 2.3 %collective-permute-start.9 = (f32[12,2,24,128]{3,2,1,0:T(8,128)S(1)}, f32[12,2,24,128]{3,2,1,0:T(8,128)S(1)}, u32[]{:S(2)}, u32[]{:S(2)}) collective-permute-start(f32[12,2,24,128]{3,2,1,0:T(8,128)S(1)} %shard_map.59), channel_id=1, source_target_pairs={{0,64},{64,0},{1,65},{65,1},{2,66},{66,2},{3,67},{67,3},{4,68},{68... | collective-permute-start | bytes 884744 | tf_op jit(solution)/shard_map/ppermute | solution.py:815
  42.1 0.9 %shard_map.58.win = f32[2,24,24,128]{3,2,1,0:T(8,128)S(1)} custom-call(f32[24,12,128]{2,1,0:T(8,128)S(1)} %get-tuple-element.44.f1, f32[24,12,128]{2,1,0:T(8,128)S(1)} %get-tuple-element.42.r1, f32[6,24,128]{2,1,0:T(8,128)S(1)} %collective-permute-done.5.zl, f32[6,24,128]{2,1,0:T(8,128)S(1)} %collective-permute-done.6.zh, ...), custom_call_target="tpu_custom_call" | custom-call | tf_op jit(solution)/shard_map/pallas_call | solution.py:54
  43.3 2.1 %shard_map.60 = (f32[36,24,128]{2,1,0:T(8,128)S(1)}, f32[36,24,128]{2,1,0:T(8,128)S(1)}, f32[38,24,128]{2,1,0:T(8,128)S(1)}, f32[18,32,128]{2,1,0:T(8,128)S(1)},...) custom-call(f32[2,24,24,128]{3,2,1,0:T(8,128)S(1)} %shard_map.58.win, ...), custom_call_target="tpu_custom_call" | custom-call | tf_op jit(solution)/shard_map/pallas_call | solution.py:54
  45.4 19.3 %all_to_all.16 = f32[128,4,128]{2,1,0:T(4,128)S(1)} all-to-all(f32[128,4,128]{2,1,0:T(4,128)S(1)} %bitcast.8), channel_id=1, replica_groups=mesh['gx'=2,'gy'=4,'gz'=16] {'gx','gy','gz'}, dimensions={0} | all-to-all | bytes 524288 | tf_op jit(solution)/shard_map/all_to_all | solution.py:863
  64.8 6.3 %shard_map.61 = (f32[48,24,128]{2,1,0:T(8,128)S(1)}, f32[48,24,128]{2,1,0:T(8,128)S(1)}, f32[128,128]{1,0:T(8,128)S(1)}) custom-call(f32[512,128]{1,0:T(8,128)S(1)} %bitcast.6, bf16[10,256,128]{2,1,0:T(8,128)(2,1)S(1)} %get-tuple-element.43.maps, f32[18,32,128]{2,1,0:T(8,128)S(1)} %get-tuple-element.50.f2, f32[18,32,128]{2,1,0:T(8,128)S(1)} %get-tuple-element.51.c2, ...), custom_call_target="tpu_custom_call" | custom-call | tf_op jit(solution)/shard_map/pallas_call | solution.py:54
  71.0 14.3 %all_to_all.17 = f32[128,1,128]{2,1,0:T(1,128)S(1)} all-to-all(f32[128,1,128]{2,1,0:T(1,128)S(1)} %bitcast.9), channel_id=1, replica_groups=mesh['gx'=2,'gy'=4,'gz'=16] {'gx','gy','gz'}, dimensions={0} | all-to-all | bytes 131072 | tf_op jit(solution)/shard_map/all_to_all | solution.py:877
  85.3 1.7 %shard_map.62 = (f32[48,48,48]{2,1,0:T(8,128)}, f32[48,48,48]{2,1,0:T(8,128)}) custom-call(f32[128,128]{1,0:T(8,128)S(1)} %bitcast.7, f32[3,48,24,128]{3,2,1,0:T(8,128)S(1)} %get-tuple-element.32.own, f32[48,24,128]{2,1,0:T(8,128)S(1)} %get-tuple-element.60.z, f32[48,24,128]{2,1,0:T(8,128)S(1)} %get-tuple-element.61.az, ...), custom_call_target="tpu_custom_call" | custom-call | tf_op jit(solution)/shard_map/pallas_call | solution.py:54
  (11 shorter events, 1.4 us)
Async XLA Ops:
  3.7 10.1 %collective-permute-start = (f32[10,24,128]{2,1,0:T(8,128)S(1)}, f32[10,24,128]{2,1,0:T(8,128)S(1)}, u32[]{:S(2)}, u32[]{:S(2)}) collective-permute-start(f32[10,24,128]{2,1,0:T(8,128)S(1)} %get-tuple-element.33), channel_id=1, source_target_pairs={{0,1},{1,2},{2,3},{3,4},{4,5},{5,6},{6,7},{7,8},{8,9},{9,10},{10,1... | collective-permute-start | bytes 368648 | tf_op jit(solution)/shard_map/ppermute | solution.py:806
  5.9 7.9 %collective-permute-start.1 = (f32[10,24,128]{2,1,0:T(8,128)S(1)}, f32[10,24,128]{2,1,0:T(8,128)S(1)}, u32[]{:S(2)}, u32[]{:S(2)}) collective-permute-start(f32[10,24,128]{2,1,0:T(8,128)S(1)} %get-tuple-element.34), channel_id=1, source_target_pairs={{0,15},{1,0},{2,1},{3,2},{4,3},{5,4},{6,5},{7,6},{8,7},{9,8},{10,9... | collective-permute-start | bytes 368648 | tf_op jit(solution)/shard_map/ppermute | solution.py:807
  14.2 5.4 %collective-permute-start.2 = (f32[3,104,128]{2,1,0:T(8,128)S(1)}, f32[3,104,128]{2,1,0:T(8,128)S(1)}, u32[]{:S(2)}, u32[]{:S(2)}) collective-permute-start(f32[3,104,128]{2,1,0:T(8,128)S(1)} %get-tuple-element.37), channel_id=1, source_target_pairs={{0,16},{16,32},{32,48},{48,0},{1,17},{17,33},{33,49},{49,1},{2,18}... | collective-permute-start | bytes 479240 | tf_op jit(solution)/shard_map/ppermute | solution.py:806
  15.5 4.1 %collective-permute-start.3 = (f32[3,104,128]{2,1,0:T(8,128)S(1)}, f32[3,104,128]{2,1,0:T(8,128)S(1)}, u32[]{:S(2)}, u32[]{:S(2)}) collective-permute-start(f32[3,104,128]{2,1,0:T(8,128)S(1)} %get-tuple-element.36.dn), channel_id=1, source_target_pairs={{0,48},{16,0},{32,16},{48,32},{1,49},{17,1},{33,17},{49,33},{2,50}... | collective-permute-start | bytes 479240 | tf_op jit(solution)/shard_map/ppermute | solution.py:807
  19.7 4.6 %collective-permute-start.4 = (f32[6,3,32,128]{3,2,1,0:T(8,128)S(1)}, f32[6,3,32,128]{3,2,1,0:T(8,128)S(1)}, u32[]{:S(2)}, u32[]{:S(2)}) collective-permute-start(f32[6,3,32,128]{3,2,1,0:T(8,128)S(1)} %shard_map.55), channel_id=1, source_target_pairs={{0,64},{64,0},{1,65},{65,1},{2,66},{66,2},{3,67},{67,3},{4,68},{68... | collective-permute-start | bytes 884744 | tf_op jit(solution)/shard_map/ppermute | solution.py:815
  26.3 7.3 %collective-permute-start.5 = (f32[6,24,128]{2,1,0:T(8,128)S(1)}, f32[6,24,128]{2,1,0:T(8,128)S(1)}, u32[]{:S(2)}, u32[]{:S(2)}) collective-permute-start(f32[6,24,128]{2,1,0:T(8,128)S(1)} %get-tuple-element.45), channel_id=1, source_target_pairs={{0,1},{1,2},{2,3},{3,4},{4,5},{5,6},{6,7},{7,8},{8,9},{9,10},{10,1... | collective-permute-start | bytes 221192 | tf_op jit(solution)/shard_map/ppermute | solution.py:806
  26.4 7.3 %collective-permute-start.6 = (f32[6,24,128]{2,1,0:T(8,128)S(1)}, f32[6,24,128]{2,1,0:T(8,128)S(1)}, u32[]{:S(2)}, u32[]{:S(2)}) collective-permute-start(f32[6,24,128]{2,1,0:T(8,128)S(1)} %get-tuple-element.46), channel_id=1, source_target_pairs={{0,15},{1,0},{2,1},{3,2},{4,3},{5,4},{6,5},{7,6},{8,7},{9,8},{10,9... | collective-permute-start | bytes 221192 | tf_op jit(solution)/shard_map/ppermute | solution.py:807
  33.9 5.6 %collective-permute-start.7 = (f32[12,24,128]{2,1,0:T(8,128)S(1)}, f32[12,24,128]{2,1,0:T(8,128)S(1)}, u32[]{:S(2)}, u32[]{:S(2)}) collective-permute-start(f32[12,24,128]{2,1,0:T(8,128)S(1)} %get-tuple-element.47), channel_id=1, source_target_pairs={{0,16},{16,32},{32,48},{48,0},{1,17},{17,33},{33,49},{49,1},{2,18}... | collective-permute-start | bytes 442376 | tf_op jit(solution)/shard_map/ppermute | solution.py:806
  35.2 4.3 %collective-permute-start.8 = (f32[12,24,128]{2,1,0:T(8,128)S(1)}, f32[12,24,128]{2,1,0:T(8,128)S(1)}, u32[]{:S(2)}, u32[]{:S(2)}) collective-permute-start(f32[12,24,128]{2,1,0:T(8,128)S(1)} %get-tuple-element.48), channel_id=1, source_target_pairs={{0,48},{16,0},{32,16},{48,32},{1,49},{17,1},{33,17},{49,33},{2,50}... | collective-permute-start | bytes 442376 | tf_op jit(solution)/shard_map/ppermute | solution.py:807
  39.8 3.5 %collective-permute-start.9 = (f32[12,2,24,128]{3,2,1,0:T(8,128)S(1)}, f32[12,2,24,128]{3,2,1,0:T(8,128)S(1)}, u32[]{:S(2)}, u32[]{:S(2)}) collective-permute-start(f32[12,2,24,128]{3,2,1,0:T(8,128)S(1)} %shard_map.59), channel_id=1, source_target_pairs={{0,64},{64,0},{1,65},{65,1},{2,66},{66,2},{3,67},{67,3},{4,68},{68... | collective-permute-start | bytes 884744 | tf_op jit(solution)/shard_map/ppermute | solution.py:815

commit v15 on v14

--- a/solution.py
+++ b/solution.py
@@ -434,7 +434,7 @@
             d_out[x] = d
             c_out[x] = jnp.where(ok, W / d, 0.0)
 
-    loop(3, some)
+    loop(3, some, 3)
 
 
 def own_rows(sp, v):
@@ -497,7 +497,7 @@
     def mine(x):
         put(x + shift, part[x] + (xw[x - 1] + xw[x + 1]), cw[x])
 
-    loop(46, lambda i: mine(i + 1), 23)
+    loop(46, lambda i: mine(i + 1), 46)
     put(shift, part[0] + (jnp.where(low_side, zero, xr[5, 0]) + xw[1]), cw[0])
     put(47 + shift, part[47] + (xw[46] + jnp.where(low_side, xr[0, 0], zero)), cw[47])
 
@@ -532,9 +532,9 @@
     def some(i):
         for k in range(4):
             for a in range(2):
-                plane1(lambda x, a: both[a][x], zl, zh, yl, yh, 4 * i + k, a, out.at[a], 4 * i + k, ends, spare.at[2 * k + a])
-
-    loop(6, some)
+                plane1(lambda x, a: both[a][x], zl, zh, yl, yh, 4 * i + k, a, out.at[a], 4 * i + k, ends, spare.at[8 * i + 2 * k + a])
+
+    loop(6, some, 6)
 
 
 def k_down1(win, maps, xr, fw, cw, e_out, f2, c2, e2, out3, rw, ew, tmp, acc, r2, ew2, tmp2, t3, sq):
@@ -852,7 +852,7 @@
     yl, yh = ring(up, dn, "gy")
     xr = swap(run(k_xpack1, sds(*L1.xshape), (f1, r1, zl, zh, yl, yh), [(12, 2, 2, 24, 128)]))
     p1, q1, p2, q2 = (36, 24, 128), (38, 24, 128), (18, 32, 128), (20, 32, 128)
-    win = run(k_windows1, sds(2, 24, 24, 128), (f1, r1, zl, zh, yl, yh), [(8, 2, 24, 128)])
+    win = run(k_windows1, sds(2, 24, 24, 128), (f1, r1, zl, zh, yl, yh), [(48, 2, 24, 128)])
     f1w, c1w, e1w, f2w, c2w, e2w, g = run(
         k_down1,
         (sds(*p1), sds(*p1), sds(*q1), sds(*p2), sds(*p2), sds(*q2), sds(count * 4, 128)),

time: 87.3 us -> 87.7 us (level)
  no operation moved by 1% of the time
where the time goes in v15:
time: 87.7 us; the launch traced here: 87.6 us
  blocking collectives  33.6 us (38%)
  starting transfers between devices  23.1 us (26%)
  Pallas kernels  20.3 us (23%)
  waiting for transfers between devices  9.65 us (11%)
  between operations  0.89 us (1%)
    pallas_call x13, Pallas kernels, run(): pl.pallas_call(kernel, out_shape=outs, in_specs=[hbm if far_in else vmem]...  20.3 us
    all_to_all x1, blocking collectives, body(): g = lax.all_to_all(g, ALL, 0, 0, tiled=True)  19.3 us
    all_to_all x1, blocking collectives, body(): lax.all_to_all(sums.reshape(count, 1, 128), ALL, 0, 0, tiled=True)  14.3 us
    ppermute x4, starting transfers between devices, ring(): high = lax.ppermute(dn, axis, fall)  12.9 us
    ppermute x4, waiting for transfers between devices, ring(): low = lax.ppermute(up, axis, rise)  8.76 us
    ppermute x2, starting transfers between devices, swap(): return lax.ppermute(v, 'gx', [(0, 1), (1, 0)])  5.4 us
    ppermute x4, starting transfers between devices, ring(): low = lax.ppermute(up, axis, rise)  4.81 us
  transfers between devices with their start and end apart: 10, of which 5 were waited for; matrix products, arithmetic and copies ran while one was open for 0% of the time, Pallas kernels for 5%

profile of v15, /device:TPU:1, one launch (start us, length us, event | category | flops | bytes accessed | tf_op | source)
XLA Modules:
  0.0 87.6 jit_solution(16765418027485969844)
XLA Ops:
  0.6 3.1 %shard_map.50 = (f32[10,24,128]{2,1,0:T(8,128)S(1)}, f32[10,24,128]{2,1,0:T(8,128)S(1)}, f32[3,48,24,128]{3,2,1,0:T(8,128)S(1)}) custom-call(f32[48,48,48]{2,1,0:T(8,128)} %x0.1, f32[48,48,48]{2,1,0:T(8,128)} %b.1, f32[48,48,48]{2,1,0:T(8,128)} %rea.1), custom_call_target="tpu_custom_call" | custom-call | tf_op jit(solution)/shard_map/pallas_call | solution.py:54
  3.7 2.2 %collective-permute-start = (f32[10,24,128]{2,1,0:T(8,128)S(1)}, f32[10,24,128]{2,1,0:T(8,128)S(1)}, u32[]{:S(2)}, u32[]{:S(2)}) collective-permute-start(f32[10,24,128]{2,1,0:T(8,128)S(1)} %get-tuple-element.33), channel_id=1, source_target_pairs={{0,1},{1,2},{2,3},{3,4},{4,5},{5,6},{6,7},{7,8},{8,9},{9,10},{10,1... | collective-permute-start | bytes 368648 | tf_op jit(solution)/shard_map/ppermute | solution.py:806
  5.9 5.0 %collective-permute-start.1 = (f32[10,24,128]{2,1,0:T(8,128)S(1)}, f32[10,24,128]{2,1,0:T(8,128)S(1)}, u32[]{:S(2)}, u32[]{:S(2)}) collective-permute-start(f32[10,24,128]{2,1,0:T(8,128)S(1)} %get-tuple-element.34), channel_id=1, source_target_pairs={{0,15},{1,0},{2,1},{3,2},{4,3},{5,4},{6,5},{7,6},{8,7},{9,8},{10,9... | collective-permute-start | bytes 368648 | tf_op jit(solution)/shard_map/ppermute | solution.py:807
  10.9 1.0 %shard_map.51 = (f32[3,24,16,128]{3,2,1,0:T(8,128)S(1)}, f32[24,12,128]{2,1,0:T(8,128)S(1)}, bf16[10,256,128]{2,1,0:T(8,128)(2,1)S(1)}) custom-call(f32[3,48,24,128]{3,2,1,0:T(8,128)S(1)} %get-tuple-element.32.own), custom_call_target="tpu_custom_call" | custom-call | tf_op jit(solution)/shard_map/pallas_call | solution.py:54
  11.9 1.9 %collective-permute-done.zl = f32[10,24,128]{2,1,0:T(8,128)S(1)} collective-permute-done((f32[10,24,128]{2,1,0:T(8,128)S(1)}, f32[10,24,128]{2,1,0:T(8,128)S(1)}, u32[]{:S(2)}, u32[]{:S(2)}) %collective-permute-start) | collective-permute-done | bytes 122912 | tf_op jit(solution)/shard_map/ppermute | solution.py:806
  14.2 1.3 %collective-permute-start.2 = (f32[3,104,128]{2,1,0:T(8,128)S(1)}, f32[3,104,128]{2,1,0:T(8,128)S(1)}, u32[]{:S(2)}, u32[]{:S(2)}) collective-permute-start(f32[3,104,128]{2,1,0:T(8,128)S(1)} %get-tuple-element.37), channel_id=1, source_target_pairs={{0,16},{16,32},{32,48},{48,0},{1,17},{17,33},{33,49},{49,1},{2,18}... | collective-permute-start | bytes 479240 | tf_op jit(solution)/shard_map/ppermute | solution.py:806
  15.5 1.5 %collective-permute-start.3 = (f32[3,104,128]{2,1,0:T(8,128)S(1)}, f32[3,104,128]{2,1,0:T(8,128)S(1)}, u32[]{:S(2)}, u32[]{:S(2)}) collective-permute-start(f32[3,104,128]{2,1,0:T(8,128)S(1)} %get-tuple-element.36.dn), channel_id=1, source_target_pairs={{0,48},{16,0},{32,16},{48,32},{1,49},{17,1},{33,17},{49,33},{2,50}... | collective-permute-start | bytes 479240 | tf_op jit(solution)/shard_map/ppermute | solution.py:807
  16.9 0.9 %shard_map.53.mid = f32[3,48,24,128]{3,2,1,0:T(8,128)S(1)} custom-call(f32[3,48,24,128]{3,2,1,0:T(8,128)S(1)} %get-tuple-element.32.own, f32[10,24,128]{2,1,0:T(8,128)S(1)} %collective-permute-done.zl, f32[10,24,128]{2,1,0:T(8,128)S(1)} %collective-permute-done.1.zh, f32[3,104,128]{2,1,0:T(8,128)S(1)} %get-tuple-element.36.dn), custom_call_target="tpu_custom_call" | custom-call | tf_op jit(solution)/shard_map/pallas_call | solution.py:54
  17.9 1.7 %collective-permute-done.2.yl = f32[3,104,128]{2,1,0:T(8,128)S(1)} collective-permute-done((f32[3,104,128]{2,1,0:T(8,128)S(1)}, f32[3,104,128]{2,1,0:T(8,128)S(1)}, u32[]{:S(2)}, u32[]{:S(2)}) %collective-permute-start.2) | collective-permute-done | bytes 159776 | tf_op jit(solution)/shard_map/ppermute | solution.py:806
  19.7 3.1 %collective-permute-start.4 = (f32[6,3,32,128]{3,2,1,0:T(8,128)S(1)}, f32[6,3,32,128]{3,2,1,0:T(8,128)S(1)}, u32[]{:S(2)}, u32[]{:S(2)}) collective-permute-start(f32[6,3,32,128]{3,2,1,0:T(8,128)S(1)} %shard_map.55), channel_id=1, source_target_pairs={{0,64},{64,0},{1,65},{65,1},{2,66},{66,2},{3,67},{67,3},{4,68},{68... | collective-permute-start | bytes 884744 | tf_op jit(solution)/shard_map/ppermute | solution.py:815
  22.8 1.9 %shard_map.54 = (f32[48,32,128]{2,1,0:T(8,128)S(1)}, f32[48,32,128]{2,1,0:T(8,128)S(1)}, f32[48,32,128]{2,1,0:T(8,128)S(1)}, f32[48,32,128]{2,1,0:T(8,128)S(1)}) custom-call(f32[3,48,24,128]{3,2,1,0:T(8,128)S(1)} %shard_map.53.mid, f32[3,104,128]{2,1,0:T(8,128)S(1)} %collective-permute-done.2.yl, f32[3,104,128]{2,1,0:T(8,128)S(1)} %collective-permute-done.3.yh), custom_call_target="tpu_custom_call" | custom-call | tf_op jit(solution)/shard_map/pallas_call | solution.py:54
  24.7 2.0 %shard_map.56 = (f32[54,32,128]{2,1,0:T(8,128)S(1)}, f32[54,32,128]{2,1,0:T(8,128)S(1)}, f32[56,32,128]{2,1,0:T(8,128)S(1)}, f32[24,12,128]{2,1,0:T(8,128)S(1)},...) custom-call(f32[48,32,128]{2,1,0:T(8,128)S(1)} %get-tuple-element.38.xw, ...), custom_call_target="tpu_custom_call" | custom-call | tf_op jit(solution)/shard_map/pallas_call | solution.py:54
  26.8 4.9 %collective-permute-start.6 = (f32[6,24,128]{2,1,0:T(8,128)S(1)}, f32[6,24,128]{2,1,0:T(8,128)S(1)}, u32[]{:S(2)}, u32[]{:S(2)}) collective-permute-start(f32[6,24,128]{2,1,0:T(8,128)S(1)} %get-tuple-element.46), channel_id=1, source_target_pairs={{0,15},{1,0},{2,1},{3,2},{4,3},{5,4},{6,5},{7,6},{8,7},{9,8},{10,9... | collective-permute-start | bytes 221192 | tf_op jit(solution)/shard_map/ppermute | solution.py:807
  31.7 2.3 %collective-permute-done.5.zl = f32[6,24,128]{2,1,0:T(8,128)S(1)} collective-permute-done((f32[6,24,128]{2,1,0:T(8,128)S(1)}, f32[6,24,128]{2,1,0:T(8,128)S(1)}, u32[]{:S(2)}, u32[]{:S(2)}) %collective-permute-start.5) | collective-permute-done | bytes 73760 | tf_op jit(solution)/shard_map/ppermute | solution.py:806
  34.3 1.3 %collective-permute-start.7 = (f32[12,24,128]{2,1,0:T(8,128)S(1)}, f32[12,24,128]{2,1,0:T(8,128)S(1)}, u32[]{:S(2)}, u32[]{:S(2)}) collective-permute-start(f32[12,24,128]{2,1,0:T(8,128)S(1)} %get-tuple-element.47), channel_id=1, source_target_pairs={{0,16},{16,32},{32,48},{48,0},{1,17},{17,33},{33,49},{49,1},{2,18}... | collective-permute-start | bytes 442376 | tf_op jit(solution)/shard_map/ppermute | solution.py:806
  35.6 1.5 %collective-permute-start.8 = (f32[12,24,128]{2,1,0:T(8,128)S(1)}, f32[12,24,128]{2,1,0:T(8,128)S(1)}, u32[]{:S(2)}, u32[]{:S(2)}) collective-permute-start(f32[12,24,128]{2,1,0:T(8,128)S(1)} %get-tuple-element.48), channel_id=1, source_target_pairs={{0,48},{16,0},{32,16},{48,32},{1,49},{17,1},{33,17},{49,33},{2,50}... | collective-permute-start | bytes 442376 | tf_op jit(solution)/shard_map/ppermute | solution.py:807
  37.1 2.8 %collective-permute-done.7.yl = f32[12,24,128]{2,1,0:T(8,128)S(1)} collective-permute-done((f32[12,24,128]{2,1,0:T(8,128)S(1)}, f32[12,24,128]{2,1,0:T(8,128)S(1)}, u32[]{:S(2)}, u32[]{:S(2)}) %collective-permute-start.7) | collective-permute-done | bytes 147488 | tf_op jit(solution)/shard_map/ppermute | solution.py:806
  40.2 2.3 %collective-permute-start.9 = (f32[12,2,24,128]{3,2,1,0:T(8,128)S(1)}, f32[12,2,24,128]{3,2,1,0:T(8,128)S(1)}, u32[]{:S(2)}, u32[]{:S(2)}) collective-permute-start(f32[12,2,24,128]{3,2,1,0:T(8,128)S(1)} %shard_map.59), channel_id=1, source_target_pairs={{0,64},{64,0},{1,65},{65,1},{2,66},{66,2},{3,67},{67,3},{4,68},{68... | collective-permute-start | bytes 884744 | tf_op jit(solution)/shard_map/ppermute | solution.py:815
  42.8 0.9 collective-permute-done.9.xr
  43.7 2.1 %shard_map.60 = (f32[36,24,128]{2,1,0:T(8,128)S(1)}, f32[36,24,128]{2,1,0:T(8,128)S(1)}, f32[38,24,128]{2,1,0:T(8,128)S(1)}, f32[18,32,128]{2,1,0:T(8,128)S(1)},...) custom-call(f32[2,24,24,128]{3,2,1,0:T(8,128)S(1)} %shard_map.58.win, ...), custom_call_target="tpu_custom_call" | custom-call | tf_op jit(solution)/shard_map/pallas_call | solution.py:54
  45.9 19.3 %all_to_all.16 = f32[128,4,128]{2,1,0:T(4,128)S(1)} all-to-all(f32[128,4,128]{2,1,0:T(4,128)S(1)} %bitcast.8), channel_id=1, replica_groups=mesh['gx'=2,'gy'=4,'gz'=16] {'gx','gy','gz'}, dimensions={0} | all-to-all | bytes 524288 | tf_op jit(solution)/shard_map/all_to_all | solution.py:863
  65.2 6.3 %shard_map.61 = (f32[48,24,128]{2,1,0:T(8,128)S(1)}, f32[48,24,128]{2,1,0:T(8,128)S(1)}, f32[128,128]{1,0:T(8,128)S(1)}) custom-call(f32[512,128]{1,0:T(8,128)S(1)} %bitcast.6, bf16[10,256,128]{2,1,0:T(8,128)(2,1)S(1)} %get-tuple-element.43.maps, f32[18,32,128]{2,1,0:T(8,128)S(1)} %get-tuple-element.50.f2, f32[18,32,128]{2,1,0:T(8,128)S(1)} %get-tuple-element.51.c2, ...), custom_call_target="tpu_custom_call" | custom-call | tf_op jit(solution)/shard_map/pallas_call | solution.py:54
  71.4 14.3 %all_to_all.17 = f32[128,1,128]{2,1,0:T(1,128)S(1)} all-to-all(f32[128,1,128]{2,1,0:T(1,128)S(1)} %bitcast.9), channel_id=1, replica_groups=mesh['gx'=2,'gy'=4,'gz'=16] {'gx','gy','gz'}, dimensions={0} | all-to-all | bytes 131072 | tf_op jit(solution)/shard_map/all_to_all | solution.py:877
  85.7 1.7 %shard_map.62 = (f32[48,48,48]{2,1,0:T(8,128)}, f32[48,48,48]{2,1,0:T(8,128)}) custom-call(f32[128,128]{1,0:T(8,128)S(1)} %bitcast.7, f32[3,48,24,128]{3,2,1,0:T(8,128)S(1)} %get-tuple-element.32.own, f32[48,24,128]{2,1,0:T(8,128)S(1)} %get-tuple-element.60.z, f32[48,24,128]{2,1,0:T(8,128)S(1)} %get-tuple-element.61.az, ...), custom_call_target="tpu_custom_call" | custom-call | tf_op jit(solution)/shard_map/pallas_call | solution.py:54
  (11 shorter events, 1.4 us)
Async XLA Ops:
  3.7 10.1 %collective-permute-start = (f32[10,24,128]{2,1,0:T(8,128)S(1)}, f32[10,24,128]{2,1,0:T(8,128)S(1)}, u32[]{:S(2)}, u32[]{:S(2)}) collective-permute-start(f32[10,24,128]{2,1,0:T(8,128)S(1)} %get-tuple-element.33), channel_id=1, source_target_pairs={{0,1},{1,2},{2,3},{3,4},{4,5},{5,6},{6,7},{7,8},{8,9},{9,10},{10,1... | collective-permute-start | bytes 368648 | tf_op jit(solution)/shard_map/ppermute | solution.py:806
  5.9 7.9 %collective-permute-start.1 = (f32[10,24,128]{2,1,0:T(8,128)S(1)}, f32[10,24,128]{2,1,0:T(8,128)S(1)}, u32[]{:S(2)}, u32[]{:S(2)}) collective-permute-start(f32[10,24,128]{2,1,0:T(8,128)S(1)} %get-tuple-element.34), channel_id=1, source_target_pairs={{0,15},{1,0},{2,1},{3,2},{4,3},{5,4},{6,5},{7,6},{8,7},{9,8},{10,9... | collective-permute-start | bytes 368648 | tf_op jit(solution)/shard_map/ppermute | solution.py:807
  14.2 5.4 %collective-permute-start.2 = (f32[3,104,128]{2,1,0:T(8,128)S(1)}, f32[3,104,128]{2,1,0:T(8,128)S(1)}, u32[]{:S(2)}, u32[]{:S(2)}) collective-permute-start(f32[3,104,128]{2,1,0:T(8,128)S(1)} %get-tuple-element.37), channel_id=1, source_target_pairs={{0,16},{16,32},{32,48},{48,0},{1,17},{17,33},{33,49},{49,1},{2,18}... | collective-permute-start | bytes 479240 | tf_op jit(solution)/shard_map/ppermute | solution.py:806
  15.5 4.1 %collective-permute-start.3 = (f32[3,104,128]{2,1,0:T(8,128)S(1)}, f32[3,104,128]{2,1,0:T(8,128)S(1)}, u32[]{:S(2)}, u32[]{:S(2)}) collective-permute-start(f32[3,104,128]{2,1,0:T(8,128)S(1)} %get-tuple-element.36.dn), channel_id=1, source_target_pairs={{0,48},{16,0},{32,16},{48,32},{1,49},{17,1},{33,17},{49,33},{2,50}... | collective-permute-start | bytes 479240 | tf_op jit(solution)/shard_map/ppermute | solution.py:807
  19.7 5.0 %collective-permute-start.4 = (f32[6,3,32,128]{3,2,1,0:T(8,128)S(1)}, f32[6,3,32,128]{3,2,1,0:T(8,128)S(1)}, u32[]{:S(2)}, u32[]{:S(2)}) collective-permute-start(f32[6,3,32,128]{3,2,1,0:T(8,128)S(1)} %shard_map.55), channel_id=1, source_target_pairs={{0,64},{64,0},{1,65},{65,1},{2,66},{66,2},{3,67},{67,3},{4,68},{68... | collective-permute-start | bytes 884744 | tf_op jit(solution)/shard_map/ppermute | solution.py:815
  26.7 7.3 %collective-permute-start.5 = (f32[6,24,128]{2,1,0:T(8,128)S(1)}, f32[6,24,128]{2,1,0:T(8,128)S(1)}, u32[]{:S(2)}, u32[]{:S(2)}) collective-permute-start(f32[6,24,128]{2,1,0:T(8,128)S(1)} %get-tuple-element.45), channel_id=1, source_target_pairs={{0,1},{1,2},{2,3},{3,4},{4,5},{5,6},{6,7},{7,8},{8,9},{9,10},{10,1... | collective-permute-start | bytes 221192 | tf_op jit(solution)/shard_map/ppermute | solution.py:806
  26.8 7.2 %collective-permute-start.6 = (f32[6,24,128]{2,1,0:T(8,128)S(1)}, f32[6,24,128]{2,1,0:T(8,128)S(1)}, u32[]{:S(2)}, u32[]{:S(2)}) collective-permute-start(f32[6,24,128]{2,1,0:T(8,128)S(1)} %get-tuple-element.46), channel_id=1, source_target_pairs={{0,15},{1,0},{2,1},{3,2},{4,3},{5,4},{6,5},{7,6},{8,7},{9,8},{10,9... | collective-permute-start | bytes 221192 | tf_op jit(solution)/shard_map/ppermute | solution.py:807
  34.3 5.6 %collective-permute-start.7 = (f32[12,24,128]{2,1,0:T(8,128)S(1)}, f32[12,24,128]{2,1,0:T(8,128)S(1)}, u32[]{:S(2)}, u32[]{:S(2)}) collective-permute-start(f32[12,24,128]{2,1,0:T(8,128)S(1)} %get-tuple-element.47), channel_id=1, source_target_pairs={{0,16},{16,32},{32,48},{48,0},{1,17},{17,33},{33,49},{49,1},{2,18}... | collective-permute-start | bytes 442376 | tf_op jit(solution)/shard_map/ppermute | solution.py:806
  35.6 4.3 %collective-permute-start.8 = (f32[12,24,128]{2,1,0:T(8,128)S(1)}, f32[12,24,128]{2,1,0:T(8,128)S(1)}, u32[]{:S(2)}, u32[]{:S(2)}) collective-permute-start(f32[12,24,128]{2,1,0:T(8,128)S(1)} %get-tuple-element.48), channel_id=1, source_target_pairs={{0,48},{16,0},{32,16},{48,32},{1,49},{17,1},{33,17},{49,33},{2,50}... | collective-permute-start | bytes 442376 | tf_op jit(solution)/shard_map/ppermute | solution.py:807
  40.2 3.5 %collective-permute-start.9 = (f32[12,2,24,128]{3,2,1,0:T(8,128)S(1)}, f32[12,2,24,128]{3,2,1,0:T(8,128)S(1)}, u32[]{:S(2)}, u32[]{:S(2)}) collective-permute-start(f32[12,2,24,128]{3,2,1,0:T(8,128)S(1)} %shard_map.59), channel_id=1, source_target_pairs={{0,64},{64,0},{1,65},{65,1},{2,66},{66,2},{3,67},{67,3},{4,68},{68... | collective-permute-start | bytes 884744 | tf_op jit(solution)/shard_map/ppermute | solution.py:815

commit v16 on v14

--- a/solution.py
+++ b/solution.py
@@ -497,7 +497,7 @@
     def mine(x):
         put(x + shift, part[x] + (xw[x - 1] + xw[x + 1]), cw[x])
 
-    loop(46, lambda i: mine(i + 1), 23)
+    loop(46, lambda i: mine(i + 1), 46)
     put(shift, part[0] + (jnp.where(low_side, zero, xr[5, 0]) + xw[1]), cw[0])
     put(47 + shift, part[47] + (xw[46] + jnp.where(low_side, xr[0, 0], zero)), cw[47])
 

time: 87.3 us -> 87.3 us (level)
  no operation moved by 1% of the time
where the time goes in v16:
time: 87.3 us; the launch traced here: 87.2 us
  blocking collectives  33.6 us (38%)
  starting transfers between devices  23.1 us (26%)
  Pallas kernels  20.5 us (23%)
  waiting for transfers between devices  9.04 us (10%)
  between operations  0.89 us (1%)
    pallas_call x13, Pallas kernels, run(): pl.pallas_call(kernel, out_shape=outs, in_specs=[hbm if far_in else vmem]...  20.5 us
    all_to_all x1, blocking collectives, body(): g = lax.all_to_all(g, ALL, 0, 0, tiled=True)  19.3 us
    all_to_all x1, blocking collectives, body(): lax.all_to_all(sums.reshape(count, 1, 128), ALL, 0, 0, tiled=True)  14.3 us
    ppermute x4, starting transfers between devices, ring(): high = lax.ppermute(dn, axis, fall)  12.9 us
    ppermute x4, waiting for transfers between devices, ring(): low = lax.ppermute(up, axis, rise)  8.76 us
    ppermute x2, starting transfers between devices, swap(): return lax.ppermute(v, 'gx', [(0, 1), (1, 0)])  5.4 us
    ppermute x4, starting transfers between devices, ring(): low = lax.ppermute(up, axis, rise)  4.81 us
  transfers between devices with their start and end apart: 10, of which 5 were waited for; matrix products, arithmetic and copies ran while one was open for 0% of the time, Pallas kernels for 5%

profile of v16, /device:TPU:1, one launch (start us, length us, event | category | flops | bytes accessed | tf_op | source)
XLA Modules:
  0.0 87.2 jit_solution(1356241816345581023)
XLA Ops:
  0.6 3.1 %shard_map.50 = (f32[10,24,128]{2,1,0:T(8,128)S(1)}, f32[10,24,128]{2,1,0:T(8,128)S(1)}, f32[3,48,24,128]{3,2,1,0:T(8,128)S(1)}) custom-call(f32[48,48,48]{2,1,0:T(8,128)} %x0.1, f32[48,48,48]{2,1,0:T(8,128)} %b.1, f32[48,48,48]{2,1,0:T(8,128)} %rea.1), custom_call_target="tpu_custom_call" | custom-call | tf_op jit(solution)/shard_map/pallas_call | solution.py:54
  3.7 2.2 %collective-permute-start = (f32[10,24,128]{2,1,0:T(8,128)S(1)}, f32[10,24,128]{2,1,0:T(8,128)S(1)}, u32[]{:S(2)}, u32[]{:S(2)}) collective-permute-start(f32[10,24,128]{2,1,0:T(8,128)S(1)} %get-tuple-element.33), channel_id=1, source_target_pairs={{0,1},{1,2},{2,3},{3,4},{4,5},{5,6},{6,7},{7,8},{8,9},{9,10},{10,1... | collective-permute-start | bytes 368648 | tf_op jit(solution)/shard_map/ppermute | solution.py:806
  5.9 5.0 %collective-permute-start.1 = (f32[10,24,128]{2,1,0:T(8,128)S(1)}, f32[10,24,128]{2,1,0:T(8,128)S(1)}, u32[]{:S(2)}, u32[]{:S(2)}) collective-permute-start(f32[10,24,128]{2,1,0:T(8,128)S(1)} %get-tuple-element.34), channel_id=1, source_target_pairs={{0,15},{1,0},{2,1},{3,2},{4,3},{5,4},{6,5},{7,6},{8,7},{9,8},{10,9... | collective-permute-start | bytes 368648 | tf_op jit(solution)/shard_map/ppermute | solution.py:807
  10.9 1.0 %shard_map.51 = (f32[3,24,16,128]{3,2,1,0:T(8,128)S(1)}, f32[24,12,128]{2,1,0:T(8,128)S(1)}, bf16[10,256,128]{2,1,0:T(8,128)(2,1)S(1)}) custom-call(f32[3,48,24,128]{3,2,1,0:T(8,128)S(1)} %get-tuple-element.32.own), custom_call_target="tpu_custom_call" | custom-call | tf_op jit(solution)/shard_map/pallas_call | solution.py:54
  11.9 1.9 %collective-permute-done.zl = f32[10,24,128]{2,1,0:T(8,128)S(1)} collective-permute-done((f32[10,24,128]{2,1,0:T(8,128)S(1)}, f32[10,24,128]{2,1,0:T(8,128)S(1)}, u32[]{:S(2)}, u32[]{:S(2)}) %collective-permute-start) | collective-permute-done | bytes 122912 | tf_op jit(solution)/shard_map/ppermute | solution.py:806
  14.2 1.3 %collective-permute-start.2 = (f32[3,104,128]{2,1,0:T(8,128)S(1)}, f32[3,104,128]{2,1,0:T(8,128)S(1)}, u32[]{:S(2)}, u32[]{:S(2)}) collective-permute-start(f32[3,104,128]{2,1,0:T(8,128)S(1)} %get-tuple-element.37), channel_id=1, source_target_pairs={{0,16},{16,32},{32,48},{48,0},{1,17},{17,33},{33,49},{49,1},{2,18}... | collective-permute-start | bytes 479240 | tf_op jit(solution)/shard_map/ppermute | solution.py:806
  15.5 1.5 %collective-permute-start.3 = (f32[3,104,128]{2,1,0:T(8,128)S(1)}, f32[3,104,128]{2,1,0:T(8,128)S(1)}, u32[]{:S(2)}, u32[]{:S(2)}) collective-permute-start(f32[3,104,128]{2,1,0:T(8,128)S(1)} %get-tuple-element.36.dn), channel_id=1, source_target_pairs={{0,48},{16,0},{32,16},{48,32},{1,49},{17,1},{33,17},{49,33},{2,50}... | collective-permute-start | bytes 479240 | tf_op jit(solution)/shard_map/ppermute | solution.py:807
  16.9 0.9 %shard_map.53.mid = f32[3,48,24,128]{3,2,1,0:T(8,128)S(1)} custom-call(f32[3,48,24,128]{3,2,1,0:T(8,128)S(1)} %get-tuple-element.32.own, f32[10,24,128]{2,1,0:T(8,128)S(1)} %collective-permute-done.zl, f32[10,24,128]{2,1,0:T(8,128)S(1)} %collective-permute-done.1.zh, f32[3,104,128]{2,1,0:T(8,128)S(1)} %get-tuple-element.36.dn), custom_call_target="tpu_custom_call" | custom-call | tf_op jit(solution)/shard_map/pallas_call | solution.py:54
  17.9 1.7 %collective-permute-done.2.yl = f32[3,104,128]{2,1,0:T(8,128)S(1)} collective-permute-done((f32[3,104,128]{2,1,0:T(8,128)S(1)}, f32[3,104,128]{2,1,0:T(8,128)S(1)}, u32[]{:S(2)}, u32[]{:S(2)}) %collective-permute-start.2) | collective-permute-done | bytes 159776 | tf_op jit(solution)/shard_map/ppermute | solution.py:806
  19.7 3.1 %collective-permute-start.4 = (f32[6,3,32,128]{3,2,1,0:T(8,128)S(1)}, f32[6,3,32,128]{3,2,1,0:T(8,128)S(1)}, u32[]{:S(2)}, u32[]{:S(2)}) collective-permute-start(f32[6,3,32,128]{3,2,1,0:T(8,128)S(1)} %shard_map.55), channel_id=1, source_target_pairs={{0,64},{64,0},{1,65},{65,1},{2,66},{66,2},{3,67},{67,3},{4,68},{68... | collective-permute-start | bytes 884744 | tf_op jit(solution)/shard_map/ppermute | solution.py:815
  22.8 1.5 %shard_map.54 = (f32[48,32,128]{2,1,0:T(8,128)S(1)}, f32[48,32,128]{2,1,0:T(8,128)S(1)}, f32[48,32,128]{2,1,0:T(8,128)S(1)}, f32[48,32,128]{2,1,0:T(8,128)S(1)}) custom-call(f32[3,48,24,128]{3,2,1,0:T(8,128)S(1)} %shard_map.53.mid, f32[3,104,128]{2,1,0:T(8,128)S(1)} %collective-permute-done.2.yl, f32[3,104,128]{2,1,0:T(8,128)S(1)} %collective-permute-done.3.yh), custom_call_target="tpu_custom_call" | custom-call | tf_op jit(solution)/shard_map/pallas_call | solution.py:54
  24.4 2.0 %shard_map.56 = (f32[54,32,128]{2,1,0:T(8,128)S(1)}, f32[54,32,128]{2,1,0:T(8,128)S(1)}, f32[56,32,128]{2,1,0:T(8,128)S(1)}, f32[24,12,128]{2,1,0:T(8,128)S(1)},...) custom-call(f32[48,32,128]{2,1,0:T(8,128)S(1)} %get-tuple-element.38.xw, ...), custom_call_target="tpu_custom_call" | custom-call | tf_op jit(solution)/shard_map/pallas_call | solution.py:54
  26.4 4.9 %collective-permute-start.6 = (f32[6,24,128]{2,1,0:T(8,128)S(1)}, f32[6,24,128]{2,1,0:T(8,128)S(1)}, u32[]{:S(2)}, u32[]{:S(2)}) collective-permute-start(f32[6,24,128]{2,1,0:T(8,128)S(1)} %get-tuple-element.46), channel_id=1, source_target_pairs={{0,15},{1,0},{2,1},{3,2},{4,3},{5,4},{6,5},{7,6},{8,7},{9,8},{10,9... | collective-permute-start | bytes 221192 | tf_op jit(solution)/shard_map/ppermute | solution.py:807
  31.3 2.3 %collective-permute-done.5.zl = f32[6,24,128]{2,1,0:T(8,128)S(1)} collective-permute-done((f32[6,24,128]{2,1,0:T(8,128)S(1)}, f32[6,24,128]{2,1,0:T(8,128)S(1)}, u32[]{:S(2)}, u32[]{:S(2)}) %collective-permute-start.5) | collective-permute-done | bytes 73760 | tf_op jit(solution)/shard_map/ppermute | solution.py:806
  33.9 1.3 %collective-permute-start.7 = (f32[12,24,128]{2,1,0:T(8,128)S(1)}, f32[12,24,128]{2,1,0:T(8,128)S(1)}, u32[]{:S(2)}, u32[]{:S(2)}) collective-permute-start(f32[12,24,128]{2,1,0:T(8,128)S(1)} %get-tuple-element.47), channel_id=1, source_target_pairs={{0,16},{16,32},{32,48},{48,0},{1,17},{17,33},{33,49},{49,1},{2,18}... | collective-permute-start | bytes 442376 | tf_op jit(solution)/shard_map/ppermute | solution.py:806
  35.2 1.5 %collective-permute-start.8 = (f32[12,24,128]{2,1,0:T(8,128)S(1)}, f32[12,24,128]{2,1,0:T(8,128)S(1)}, u32[]{:S(2)}, u32[]{:S(2)}) collective-permute-start(f32[12,24,128]{2,1,0:T(8,128)S(1)} %get-tuple-element.48), channel_id=1, source_target_pairs={{0,48},{16,0},{32,16},{48,32},{1,49},{17,1},{33,17},{49,33},{2,50}... | collective-permute-start | bytes 442376 | tf_op jit(solution)/shard_map/ppermute | solution.py:807
  36.7 2.8 %collective-permute-done.7.yl = f32[12,24,128]{2,1,0:T(8,128)S(1)} collective-permute-done((f32[12,24,128]{2,1,0:T(8,128)S(1)}, f32[12,24,128]{2,1,0:T(8,128)S(1)}, u32[]{:S(2)}, u32[]{:S(2)}) %collective-permute-start.7) | collective-permute-done | bytes 147488 | tf_op jit(solution)/shard_map/ppermute | solution.py:806
  39.8 2.3 %collective-permute-start.9 = (f32[12,2,24,128]{3,2,1,0:T(8,128)S(1)}, f32[12,2,24,128]{3,2,1,0:T(8,128)S(1)}, u32[]{:S(2)}, u32[]{:S(2)}) collective-permute-start(f32[12,2,24,128]{3,2,1,0:T(8,128)S(1)} %shard_map.59), channel_id=1, source_target_pairs={{0,64},{64,0},{1,65},{65,1},{2,66},{66,2},{3,67},{67,3},{4,68},{68... | collective-permute-start | bytes 884744 | tf_op jit(solution)/shard_map/ppermute | solution.py:815
  42.1 0.9 %shard_map.58.win = f32[2,24,24,128]{3,2,1,0:T(8,128)S(1)} custom-call(f32[24,12,128]{2,1,0:T(8,128)S(1)} %get-tuple-element.44.f1, f32[24,12,128]{2,1,0:T(8,128)S(1)} %get-tuple-element.42.r1, f32[6,24,128]{2,1,0:T(8,128)S(1)} %collective-permute-done.5.zl, f32[6,24,128]{2,1,0:T(8,128)S(1)} %collective-permute-done.6.zh, ...), custom_call_target="tpu_custom_call" | custom-call | tf_op jit(solution)/shard_map/pallas_call | solution.py:54
  43.3 2.1 %shard_map.60 = (f32[36,24,128]{2,1,0:T(8,128)S(1)}, f32[36,24,128]{2,1,0:T(8,128)S(1)}, f32[38,24,128]{2,1,0:T(8,128)S(1)}, f32[18,32,128]{2,1,0:T(8,128)S(1)},...) custom-call(f32[2,24,24,128]{3,2,1,0:T(8,128)S(1)} %shard_map.58.win, ...), custom_call_target="tpu_custom_call" | custom-call | tf_op jit(solution)/shard_map/pallas_call | solution.py:54
  45.5 19.3 %all_to_all.16 = f32[128,4,128]{2,1,0:T(4,128)S(1)} all-to-all(f32[128,4,128]{2,1,0:T(4,128)S(1)} %bitcast.8), channel_id=1, replica_groups=mesh['gx'=2,'gy'=4,'gz'=16] {'gx','gy','gz'}, dimensions={0} | all-to-all | bytes 524288 | tf_op jit(solution)/shard_map/all_to_all | solution.py:863
  64.8 6.3 %shard_map.61 = (f32[48,24,128]{2,1,0:T(8,128)S(1)}, f32[48,24,128]{2,1,0:T(8,128)S(1)}, f32[128,128]{1,0:T(8,128)S(1)}) custom-call(f32[512,128]{1,0:T(8,128)S(1)} %bitcast.6, bf16[10,256,128]{2,1,0:T(8,128)(2,1)S(1)} %get-tuple-element.43.maps, f32[18,32,128]{2,1,0:T(8,128)S(1)} %get-tuple-element.50.f2, f32[18,32,128]{2,1,0:T(8,128)S(1)} %get-tuple-element.51.c2, ...), custom_call_target="tpu_custom_call" | custom-call | tf_op jit(solution)/shard_map/pallas_call | solution.py:54
  71.1 14.3 %all_to_all.17 = f32[128,1,128]{2,1,0:T(1,128)S(1)} all-to-all(f32[128,1,128]{2,1,0:T(1,128)S(1)} %bitcast.9), channel_id=1, replica_groups=mesh['gx'=2,'gy'=4,'gz'=16] {'gx','gy','gz'}, dimensions={0} | all-to-all | bytes 131072 | tf_op jit(solution)/shard_map/all_to_all | solution.py:877
  85.3 1.7 %shard_map.62 = (f32[48,48,48]{2,1,0:T(8,128)}, f32[48,48,48]{2,1,0:T(8,128)}) custom-call(f32[128,128]{1,0:T(8,128)S(1)} %bitcast.7, f32[3,48,24,128]{3,2,1,0:T(8,128)S(1)} %get-tuple-element.32.own, f32[48,24,128]{2,1,0:T(8,128)S(1)} %get-tuple-element.60.z, f32[48,24,128]{2,1,0:T(8,128)S(1)} %get-tuple-element.61.az, ...), custom_call_target="tpu_custom_call" | custom-call | tf_op jit(solution)/shard_map/pallas_call | solution.py:54
  (11 shorter events, 1.4 us)
Async XLA Ops:
  3.7 10.1 %collective-permute-start = (f32[10,24,128]{2,1,0:T(8,128)S(1)}, f32[10,24,128]{2,1,0:T(8,128)S(1)}, u32[]{:S(2)}, u32[]{:S(2)}) collective-permute-start(f32[10,24,128]{2,1,0:T(8,128)S(1)} %get-tuple-element.33), channel_id=1, source_target_pairs={{0,1},{1,2},{2,3},{3,4},{4,5},{5,6},{6,7},{7,8},{8,9},{9,10},{10,1... | collective-permute-start | bytes 368648 | tf_op jit(solution)/shard_map/ppermute | solution.py:806
  5.9 7.9 %collective-permute-start.1 = (f32[10,24,128]{2,1,0:T(8,128)S(1)}, f32[10,24,128]{2,1,0:T(8,128)S(1)}, u32[]{:S(2)}, u32[]{:S(2)}) collective-permute-start(f32[10,24,128]{2,1,0:T(8,128)S(1)} %get-tuple-element.34), channel_id=1, source_target_pairs={{0,15},{1,0},{2,1},{3,2},{4,3},{5,4},{6,5},{7,6},{8,7},{9,8},{10,9... | collective-permute-start | bytes 368648 | tf_op jit(solution)/shard_map/ppermute | solution.py:807
  14.2 5.4 %collective-permute-start.2 = (f32[3,104,128]{2,1,0:T(8,128)S(1)}, f32[3,104,128]{2,1,0:T(8,128)S(1)}, u32[]{:S(2)}, u32[]{:S(2)}) collective-permute-start(f32[3,104,128]{2,1,0:T(8,128)S(1)} %get-tuple-element.37), channel_id=1, source_target_pairs={{0,16},{16,32},{32,48},{48,0},{1,17},{17,33},{33,49},{49,1},{2,18}... | collective-permute-start | bytes 479240 | tf_op jit(solution)/shard_map/ppermute | solution.py:806
  15.5 4.1 %collective-permute-start.3 = (f32[3,104,128]{2,1,0:T(8,128)S(1)}, f32[3,104,128]{2,1,0:T(8,128)S(1)}, u32[]{:S(2)}, u32[]{:S(2)}) collective-permute-start(f32[3,104,128]{2,1,0:T(8,128)S(1)} %get-tuple-element.36.dn), channel_id=1, source_target_pairs={{0,48},{16,0},{32,16},{48,32},{1,49},{17,1},{33,17},{49,33},{2,50}... | collective-permute-start | bytes 479240 | tf_op jit(solution)/shard_map/ppermute | solution.py:807
  19.7 4.6 %collective-permute-start.4 = (f32[6,3,32,128]{3,2,1,0:T(8,128)S(1)}, f32[6,3,32,128]{3,2,1,0:T(8,128)S(1)}, u32[]{:S(2)}, u32[]{:S(2)}) collective-permute-start(f32[6,3,32,128]{3,2,1,0:T(8,128)S(1)} %shard_map.55), channel_id=1, source_target_pairs={{0,64},{64,0},{1,65},{65,1},{2,66},{66,2},{3,67},{67,3},{4,68},{68... | collective-permute-start | bytes 884744 | tf_op jit(solution)/shard_map/ppermute | solution.py:815
  26.4 7.3 %collective-permute-start.5 = (f32[6,24,128]{2,1,0:T(8,128)S(1)}, f32[6,24,128]{2,1,0:T(8,128)S(1)}, u32[]{:S(2)}, u32[]{:S(2)}) collective-permute-start(f32[6,24,128]{2,1,0:T(8,128)S(1)} %get-tuple-element.45), channel_id=1, source_target_pairs={{0,1},{1,2},{2,3},{3,4},{4,5},{5,6},{6,7},{7,8},{8,9},{9,10},{10,1... | collective-permute-start | bytes 221192 | tf_op jit(solution)/shard_map/ppermute | solution.py:806
  26.4 7.2 %collective-permute-start.6 = (f32[6,24,128]{2,1,0:T(8,128)S(1)}, f32[6,24,128]{2,1,0:T(8,128)S(1)}, u32[]{:S(2)}, u32[]{:S(2)}) collective-permute-start(f32[6,24,128]{2,1,0:T(8,128)S(1)} %get-tuple-element.46), channel_id=1, source_target_pairs={{0,15},{1,0},{2,1},{3,2},{4,3},{5,4},{6,5},{7,6},{8,7},{9,8},{10,9... | collective-permute-start | bytes 221192 | tf_op jit(solution)/shard_map/ppermute | solution.py:807
  33.9 5.6 %collective-permute-start.7 = (f32[12,24,128]{2,1,0:T(8,128)S(1)}, f32[12,24,128]{2,1,0:T(8,128)S(1)}, u32[]{:S(2)}, u32[]{:S(2)}) collective-permute-start(f32[12,24,128]{2,1,0:T(8,128)S(1)} %get-tuple-element.47), channel_id=1, source_target_pairs={{0,16},{16,32},{32,48},{48,0},{1,17},{17,33},{33,49},{49,1},{2,18}... | collective-permute-start | bytes 442376 | tf_op jit(solution)/shard_map/ppermute | solution.py:806
  35.2 4.3 %collective-permute-start.8 = (f32[12,24,128]{2,1,0:T(8,128)S(1)}, f32[12,24,128]{2,1,0:T(8,128)S(1)}, u32[]{:S(2)}, u32[]{:S(2)}) collective-permute-start(f32[12,24,128]{2,1,0:T(8,128)S(1)} %get-tuple-element.48), channel_id=1, source_target_pairs={{0,48},{16,0},{32,16},{48,32},{1,49},{17,1},{33,17},{49,33},{2,50}... | collective-permute-start | bytes 442376 | tf_op jit(solution)/shard_map/ppermute | solution.py:807
  39.8 3.5 %collective-permute-start.9 = (f32[12,2,24,128]{3,2,1,0:T(8,128)S(1)}, f32[12,2,24,128]{3,2,1,0:T(8,128)S(1)}, u32[]{:S(2)}, u32[]{:S(2)}) collective-permute-start(f32[12,2,24,128]{3,2,1,0:T(8,128)S(1)} %shard_map.59), channel_id=1, source_target_pairs={{0,64},{64,0},{1,65},{65,1},{2,66},{66,2},{3,67},{67,3},{4,68},{68... | collective-permute-start | bytes 884744 | tf_op jit(solution)/shard_map/ppermute | solution.py:815
